TPU v7x, 128 devices: a whole 4x4x4 slice. The times are simulated.
128 devices in a mesh: gx: 16 (over y, x), gy: 8 (over z, core).
Axes of the slice: x: 4, y: 4, z: 4, core: 2. Of those that a mesh axis runs over, the one named last changes fastest.
Arguments:
- probes: bfloat16 [512, 2048, 256], P('gx', 'gy'), may hold values from -6 to 6
- blk_rows: int32 [16384, 128], P(('gx', 'gy')), may hold values from 0 to 8191
- blk_sensor: int32 [16384], P(('gx', 'gy')), may hold values from 0 to 1023, as said below
- blk_count: int32 [128], P(('gx', 'gy')), may hold values from 64 to 128, as said below
- coef: bfloat16 [16384, 128], P(('gx', 'gy')), may hold values from -5 to 5
- owner: int32 [1024], replicated, may hold values from 0 to 127, as said below
- weights: float32 [1024], replicated, may hold values from 0.1 to 1
Outputs:
- sensitivity: float32 [1024], P(('gx', 'gy'))
- new_weights: float32 [1024], replicated
- density: float32 [512, 2048], P('gx', 'gy')
Inputs may be any that keep to these rules, and one draw needn't show every extreme that they name: `owner`: every device owns exactly 8 sensors. `blk_sensor`: among the live slots of one tile, at most 2 belong to sensors of one owner; in every draw some owner receives 2 live blocks from every tile. `blk_count`: some tile has all 128 slots live.
All inputs are finite; a program needn't handle non-finite values.
Results may differ from a plain program's by a relative error of at most 0.0008.
Values may be sent and summed in bfloat16 or wider, within the bound.
No kernel may reach another device: no remote copies, remote signals or barrier semaphores. Data moves between devices by JAX's collectives and lax.ppermute only.
A program may use at most 128 MiB of HBM per device.

v0:
```python
import jax
import jax.numpy as jnp
from jax import lax
from jax.sharding import PartitionSpec as P

SPD = 8
CAP = 2


def over_pieces(shard, axis):
    tiles = lax.all_gather(shard, axis)
    return tiles.sum(axis=0)


def local(probes, blk_rows, blk_sensor, blk_count, coef, owner, weights):
    size_gx = lax.axis_size("gx")
    size_gy = lax.axis_size("gy")
    n_dev = size_gx * size_gy
    me_flat = lax.axis_index("gx") * size_gy + lax.axis_index("gy")
    tile_r, tile_c, probe_n = probes.shape
    nblk, foot = blk_rows.shape
    n_sens = owner.shape[0]
    flat = probes.reshape(tile_r * tile_c, probe_n)
    picked = flat[blk_rows.reshape(-1)].reshape(nblk, foot, probe_n)
    slots = jnp.arange(nblk, dtype=jnp.int32)
    alive = slots < blk_count[0]
    dest = owner[blk_sensor]
    earlier = (dest[:, None] == dest[None, :]) & alive[None, :] & (slots[None, :] < slots[:, None])
    rank = jnp.sum(earlier.astype(jnp.int32), axis=1)
    position = jnp.where(alive, dest * CAP + rank, n_dev * CAP)
    send_rows = (
        jnp.zeros((n_dev * CAP, foot, probe_n), jnp.bfloat16).at[position].set(picked, mode="drop")
    )
    send_coef = jnp.zeros((n_dev * CAP, foot), jnp.bfloat16).at[position].set(coef, mode="drop")
    send_ids = jnp.full((n_dev * CAP,), -1, jnp.int32).at[position].set(blk_sensor, mode="drop")
    recv_rows, recv_coef, recv_ids = (
        lax.all_to_all(send_rows, ("gx", "gy"), split_axis=0, concat_axis=0, tiled=True),
        lax.all_to_all(send_coef, ("gx", "gy"), split_axis=0, concat_axis=0, tiled=True),
        lax.all_to_all(send_ids, ("gx", "gy"), split_axis=0, concat_axis=0, tiled=True),
    )
    my_ids = jnp.nonzero(owner == me_flat, size=SPD, fill_value=0)[0].astype(jnp.int32)
    select = (recv_ids[None, :] == my_ids[:, None]).astype(jnp.bfloat16)
    mixer = select[:, :, None] * recv_coef[None, :, :]
    obs = jnp.einsum("ksr,srp->krp", mixer, recv_rows, preferred_element_type=jnp.float32)
    owned = jnp.sum(obs * obs, axis=(1, 2)) / (foot * probe_n)
    spread = jnp.zeros((n_sens,), jnp.float32).at[my_ids].set(owned)
    sens_all = over_pieces(spread, ("gx", "gy"))
    gain = weights * jnp.sqrt(1.0 + sens_all)
    new_weights = n_sens * gain / jnp.sum(gain)
    values_pts = jnp.where(
        alive[:, None], new_weights[blk_sensor][:, None] * jnp.square(coef.astype(jnp.float32)), 0.0
    )
    density = (
        jnp.zeros((tile_r * tile_c,), jnp.float32)
        .at[blk_rows.reshape(-1)]
        .add(values_pts.reshape(-1))
    )
    return (owned, new_weights, density.reshape(tile_r, tile_c))


def solution(mesh):
    in_specs = (
        P("gx", "gy", None),
        P(("gx", "gy"), None),
        P(("gx", "gy")),
        P(("gx", "gy")),
        P(("gx", "gy"), None),
        P(),
        P(),
    )
    out_specs = (P(("gx", "gy")), P(), P("gx", "gy"))
    return jax.shard_map(local, mesh=mesh, in_specs=in_specs, out_specs=out_specs, check_vma=False)
```

profile of v0, /device:TPU:1, one launch (start us, length us, event | category | flops | bytes accessed | tf_op | source)
XLA Modules:
  0.0 503.9 jit_solution(8996993802345438385)
XLA Ops:
  0.6 0.7 compare_select_fusion.4
  2.0 1.6 gather_fusion
  3.6 0.2 convert_reduce_fusion
  3.8 1.1 scatter_custom_fusion.1
  4.9 0.8 all_to_all.16
  5.7 11.5 %all-to-all-start.1 = ((s32[128,2,1]{1,2,0:T(1,128)}), s32[128,2,1]{1,2,0:T(1,128)S(1)}, u32[]{:S(2)}, u32[]{:S(2)}) async-start(s32[128,2,1]{1,2,0:T(1,128)} %bitcast.7), calls=%async_computation.1 | async-start | bytes 131072 | tf_op jit(solution)/shard_map/all_to_all | solution.py:39
  17.1 0.9 compare_select_fusion
  18.1 1.7 scatter_custom_fusion.3
  19.8 6.8 %all-to-all-done.1 = s32[128,2,1]{1,2,0:T(1,128)S(1)} async-done(((s32[128,2,1]{1,2,0:T(1,128)}), s32[128,2,1]{1,2,0:T(1,128)S(1)}, u32[]{:S(2)}, u32[]{:S(2)}) %all-to-all-start.1) | async-done | bytes 1056 | tf_op jit(solution)/shard_map/all_to_all | solution.py:39
  26.6 4.6 all-to-all-start.2
  31.2 63.5 %gather_fusion.1 = bf16[16384,256]{1,0:T(8,128)(2,1)} fusion(bf16[8192,256]{1,0:T(8,128)(2,1)} %bitcast.28, s32[16384]{0:T(1024)S(1)} %broadcast_clamp_fusion), kind=kCustom, calls=%fused_computation.1 | custom fusion | bytes 16842752 | tf_op jit(solution)/shard_map/gather | solution.py:24
  94.7 6.0 %broadcast_in_dim.36 = bf16[256,128,256]{2,1,0:T(8,128)(2,1)} broadcast(bf16[]{:T(256)} %constant.26.clone.1), dimensions={} | broadcast | bytes 16777218 | tf_op jit(solution)/shard_map/broadcast_in_dim | solution.py:32
  100.7 22.6 %scatter_fusion = bf16[256,128,256]{2,1,0:T(8,128)(2,1)} fusion(bf16[256,128,256]{2,1,0:T(8,128)(2,1)} %broadcast_in_dim.36, s32[128]{0:T(128)S(1)} %fusion.24, bf16[128,128,256]{2,1,0:T(8,128)(2,1)} %bitcast.29), kind=kCustom, calls=%fused_computation.3 | custom fusion | bytes 25166336 | tf_op jit(solution)/shard_map/scatter | solution.py:32
  123.3 0.0 copy-start.1
  123.3 0.0 all-to-all-done.2
  123.4 10.6 %all-to-all-start = ((bf16[256,128,256]{2,1,0:T(8,128)(2,1)}), bf16[256,128,256]{2,1,0:T(8,128)(2,1)}, u32[]{:S(2)}, u32[]{:S(2)}) async-start(bf16[256,128,256]{2,1,0:T(8,128)(2,1)} %scatter_fusion), calls=%async_computation | async-start | bytes 33554432 | tf_op jit(solution)/shard_map/all_to_all | solution.py:37
  134.0 0.0 copy-done.1
  134.0 0.6 convert_reduce_fusion.1
  134.6 0.3 reduce-window.12
  134.9 0.1 slice.7
  135.0 0.1 slice_reduce_fusion
  135.1 0.1 broadcast_add_fusion
  135.2 7.8 %scatter_custom_fusion.2 = s32[8]{0:T(128)S(1)} fusion(s32[1024]{0:T(1024)S(1)} %bitcast.35, s32[1024]{0:T(1024)S(1)} %broadcast.233, s32[]{:T(128)} %constant.27.clone.1), kind=kCustom, calls=%fused_computation.59 | custom fusion | flops 1024 | bytes 36 | tf_op jit(solution)/shard_map/scatter-add | solution.py:41
  143.0 0.2 select_n.113
  143.2 0.7 compare_select_fusion.10
  143.8 0.7 fusion.21
  144.5 0.5 broadcast.255
  145.0 0.8 reduce.6
  145.8 0.1 eq.43
  146.0 0.1 compare_convert_fusion
  146.0 0.1 copy.16
  146.2 0.0 copy-start.3
  146.2 0.0 copy-start.2
  146.2 208.7 %all-to-all-done = bf16[256,128,256]{2,1,0:T(8,128)(2,1)} async-done(((bf16[256,128,256]{2,1,0:T(8,128)(2,1)}), bf16[256,128,256]{2,1,0:T(8,128)(2,1)}, u32[]{:S(2)}, u32[]{:S(2)}) %all-to-all-start) | async-done | bytes 16777248 | tf_op jit(solution)/shard_map/all_to_all | solution.py:37
  354.9 17.0 %fusion.5 = f32[8]{0:T(128)S(1)} fusion(bf16[256,128,256]{2,1,0:T(8,128)(2,1)} %all-to-all-done, bf16[256,128]{0,1:T(8,128)(2,1)S(1)} %copy.16, bf16[8,256]{1,0:T(8,128)(2,1)S(1)} %compare_convert_fusion), kind=kOutput, calls=%fused_computation.12 | convolution fusion | flops 135004160 | bytes 16846880 | tf_op jit(solution)/shard_map/ksr,srp->krp/dot_general | solution.py:44
  371.9 0.6 scatter_custom_fusion.4
  372.6 42.3 %all-gather = f32[131072]{0:T(1024)S(1)} all-gather(f32[1024]{0:T(1024)S(1)} %scatter_custom_fusion.4), channel_id=2, replica_groups=mesh['gx'=16,'gy'=8] {'gx','gy'}, dimensions={0}, use_global_device_ids=true | all-gather | bytes 528384 | tf_op jit(solution)/shard_map/all_gather | solution.py:11
  414.9 0.1 reshape.321
  415.0 0.0 copy-done.3
  415.1 0.6 fusion.18
  415.7 0.7 multiply_divide_fusion
  416.3 0.0 copy-start
  416.3 1.0 gather_fusion.2
  417.3 0.0 copy-done.2
  417.3 0.1 select_bitcast_fusion
  417.4 85.8 %scatter_custom_fusion.5 = f32[8192]{0:T(1024)S(1)} fusion(s32[16384]{0:T(1024)S(1)} %bitcast.31, f32[16384]{0:T(1024)S(1)} %select_bitcast_fusion, f32[]{:T(128)} %constant.75.clone.1), kind=kCustom, calls=%fused_computation.25 | custom fusion | flops 16384 | bytes 32772 | tf_op jit(solution)/shard_map/scatter-add | solution.py:56
  503.3 0.6 reshape.248
  503.9 0.0 copy-done.4
  (12 shorter events, 0.1 us)
Async XLA Ops:
  5.7 20.9 %all-to-all-start.1 = ((s32[128,2,1]{1,2,0:T(1,128)}), s32[128,2,1]{1,2,0:T(1,128)S(1)}, u32[]{:S(2)}, u32[]{:S(2)}) async-start(s32[128,2,1]{1,2,0:T(1,128)} %bitcast.7), calls=%async_computation.1 | async-start | bytes 131072 | tf_op jit(solution)/shard_map/all_to_all | solution.py:39
  26.6 96.8 %all-to-all-start.2 = ((bf16[128,2,128]{2,1,0:T(2,128)(2,1)}), bf16[128,2,128]{2,1,0:T(2,128)(2,1)S(1)}, u32[]{:S(2)}, u32[]{:S(2)}) async-start(bf16[128,2,128]{2,1,0:T(2,128)(2,1)} %bitcast.13), calls=%async_computation.2 | async-start | bytes 131072 | tf_op jit(solution)/shard_map/all_to_all | solution.py:38
  123.3 10.6 %copy-start.1 = (s32[1024]{0:T(1024)S(1)}, s32[1024]{0:T(1024)}, u32[]{:S(2)}) copy-start(s32[1024]{0:T(1024)} %param.12) | copy-start | bytes 12292
  123.4 231.6 %all-to-all-start = ((bf16[256,128,256]{2,1,0:T(8,128)(2,1)}), bf16[256,128,256]{2,1,0:T(8,128)(2,1)}, u32[]{:S(2)}, u32[]{:S(2)}) async-start(bf16[256,128,256]{2,1,0:T(8,128)(2,1)} %scatter_fusion), calls=%async_computation | async-start | bytes 33554432 | tf_op jit(solution)/shard_map/all_to_all | solution.py:37
  146.2 268.9 %copy-start.3 = (f32[1024]{0:T(1024)S(1)}, f32[1024]{0:T(1024)}, u32[]{:S(2)}) copy-start(f32[1024]{0:T(1024)} %param.13) | copy-start | bytes 12292
  146.2 271.1 %copy-start.2 = (bf16[128,128]{1,0:T(8,128)(2,1)S(1)}, bf16[128,128]{1,0:T(8,128)(2,1)}, u32[]{:S(2)}) copy-start(bf16[128,128]{1,0:T(8,128)(2,1)} %param.11) | copy-start | bytes 98308
  371.9 132.0 %copy-start.4 = (f32[8]{0:T(128)}, f32[8]{0:T(128)S(1)}, u32[]{:S(2)}) copy-start(f32[8]{0:T(128)S(1)} %broadcast_multiply_fusion) | copy-start | bytes 100
  416.3 87.6 %copy-start = (f32[1024]{0:T(1024)}, f32[1024]{0:T(1024)S(1)}, u32[]{:S(2)}) copy-start(f32[1024]{0:T(1024)S(1)} %multiply_divide_fusion) | copy-start | bytes 12292
where the time goes:
time: 505 us; the launch traced here: 504 us
  waiting for transfers between devices  216 us (43%)
  local copies, waits for them, and re-layouts  101 us (20%)
  other arithmetic  100 us (20%)
  blocking collectives  42.3 us (8%)
  starting transfers between devices  26.7 us (5%)
  matrix products  17 us (3%)
    all_to_all x1, waiting for transfers between devices, local(): lax.all_to_all(send_rows, ('gx', 'gy'), split_axis=0, concat_axis=0, tile...  209 us
    scatter-add x1, other arithmetic, local(): density = jnp.zeros((tile_r * tile_c,), jnp.float32).at[blk_rows.reshape(...  85.8 us
    gather x1, local copies, waits for them, and re-layouts, local(): picked = flat[blk_rows.reshape(-1)].reshape(nblk, foot, probe_n)  63.5 us
    all_gather x1, blocking collectives, over_pieces(): tiles = lax.all_gather(shard, axis)  42.3 us
    scatter x1, local copies, waits for them, and re-layouts, local(): jnp.zeros((n_dev * CAP, foot, probe_n), jnp.bfloat16).at[position]  22.6 us
    dot_general x1, matrix products, local(): jnp.einsum('ksr,srp->krp', mixer, recv_rows, preferred_element_type=jnp.f...  17 us
    all_to_all x1, starting transfers between devices, local(): lax.all_to_all(send_ids, ('gx', 'gy'), split_axis=0, concat_axis=0, tiled...  11.5 us
    all_to_all x1, starting transfers between devices, local(): lax.all_to_all(send_rows, ('gx', 'gy'), split_axis=0, concat_axis=0, tile...  10.6 us
  transfers between devices with their start and end apart: 3, of which 2 were waited for; matrix products, arithmetic and copies ran while one was open for 21% of the time, Pallas kernels for 0%

commit v1 on v0

v1 whole, which is shorter than its diff:
```python
import jax
import jax.numpy as jnp
from jax import lax
from jax.experimental import pallas as pl
from jax.experimental.pallas import tpu as pltpu
from jax.sharding import PartitionSpec as P

SPD = 8
AXES = ("gx", "gy")
CHUNKS = (32, 32, 32, 32)
F32 = jnp.float32
BF16 = jnp.bfloat16
I32 = jnp.int32


def gather_rows(flat, index, slot0, ns, rb=8):
    n, pn = flat.shape
    foot = nblk = 128
    half = pn // 2

    def body(idx, x_ref, out_ref, tab, stage):
        g = pl.program_id(0)

        @pl.when(g == 0)
        def _():
            ch = 512

            def conv(i, c):
                x = x_ref[pl.ds(i * ch, ch), :].astype(F32)
                tab[pl.ds(i * 2 * ch, ch, stride=2), :] = x[:, :half]
                tab[pl.ds(i * 2 * ch + 1, ch, stride=2), :] = x[:, half:]
                return c

            lax.fori_loop(0, n // ch, conv, 0)

        def channel(q, c):
            base = (g * rb + q) * nblk + slot0
            for j in range(ns):
                at = pl.multiple_of(idx[base + j], 2)
                stage[q, pl.ds(2 * j, 2), :] = tab[pl.ds(at, 2), :]
            return c

        lax.fori_loop(0, rb, channel, 0)
        for q in range(rb):
            out_ref[q, :, :half] = stage[q, pl.ds(0, ns, stride=2), :].astype(BF16)
            out_ref[q, :, half:] = stage[q, pl.ds(1, ns, stride=2), :].astype(BF16)

    return pl.pallas_call(
        body,
        grid_spec=pltpu.PrefetchScalarGridSpec(
            num_scalar_prefetch=1,
            grid=(foot // rb,),
            in_specs=[pl.BlockSpec((n, pn), lambda g, idx: (0, 0))],
            out_specs=pl.BlockSpec((rb, ns, pn), lambda g, idx: (g, 0, 0)),
            scratch_shapes=[
                pltpu.VMEM((2 * n, half), F32),
                pltpu.VMEM((rb, 2 * ns, half), F32),
            ],
        ),
        out_shape=jax.ShapeDtypeStruct((foot, ns, pn), BF16),
        compiler_params=pltpu.CompilerParams(
            dimension_semantics=("arbitrary",), vmem_limit_bytes=24 * 1024 * 1024
        ),
        name="gather_rows",
    )(index, flat)


def mix_chunk(data, ids, coef, acc, n_sens, last, n_dev, kb=512, mb=256):
    k, pn = data.shape

    def body(*refs):
        data_ref, ids_ref, coef_ref = refs[:3]
        acc_ref = None if acc is None else refs[3]
        out_ref, sum_ref = refs[-2:]
        g = pl.program_id(0)

        @pl.when(g == 0)
        def _():
            if acc_ref is None:
                sum_ref[...] = jnp.zeros((n_sens, pn), F32)
            else:
                sum_ref[...] = acc_ref[...]

        rows = data_ref[...]
        wanted = ids_ref[...]
        weight = coef_ref[...]
        sub = lax.broadcasted_iota(I32, (mb, kb), 0)
        for m in range(n_sens // mb):
            hit = sub == (wanted - m * mb)
            mixer = jnp.where(hit, weight, 0.0).astype(BF16)
            sum_ref[pl.ds(m * mb, mb), :] += jnp.dot(mixer, rows, preferred_element_type=F32)

        @pl.when(g == pl.num_programs(0) - 1)
        def _():
            if not last:
                out_ref[...] = sum_ref[...]
            else:
                for m in range(n_sens // 128):
                    x = sum_ref[pl.ds(m * 128, 128), :]
                    x = x * x
                    x = x[:, : pn // 2] + x[:, pn // 2 :]
                    row = jnp.sum(x.T, axis=0, keepdims=True)
                    out_ref[:, :, pl.ds(m * 128, 128)] = jnp.broadcast_to(row[None], (n_dev, 1, 128))

    specs = [
        pl.BlockSpec((kb, pn), lambda g: (g, 0)),
        pl.BlockSpec((1, kb), lambda g: (0, g)),
        pl.BlockSpec((1, kb), lambda g: (0, g)),
    ]
    args = [data, ids, coef]
    if acc is not None:
        specs.append(pl.BlockSpec((n_sens, pn), lambda g: (0, 0)))
        args.append(acc)
    shape = (n_dev, 1, n_sens) if last else (n_sens, pn)
    return pl.pallas_call(
        body,
        grid=(k // kb,),
        in_specs=specs,
        out_specs=pl.BlockSpec(shape, lambda g: (0,) * len(shape)),
        scratch_shapes=[pltpu.VMEM((n_sens, pn), F32)],
        out_shape=jax.ShapeDtypeStruct(shape, F32),
        compiler_params=pltpu.CompilerParams(
            dimension_semantics=("arbitrary",), vmem_limit_bytes=24 * 1024 * 1024
        ),
        name="mix_last" if last else "mix_chunk",
    )(*args)


def spread_squares(rows, coef, owner, me, tile_r, tile_c, sb=8):
    nblk, foot = rows.shape
    n_sens = owner.shape[1]

    def body(me_ref, rows_ref, coef_ref, owner_ref, map_ref, pos_ref):
        g = pl.program_id(0)

        @pl.when(g == 0)
        def _():
            mine = owner_ref[...] == me_ref[0]
            flag = jnp.broadcast_to(jnp.where(mine, 1.0, 0.0), (8, n_sens)).astype(BF16)
            row = lax.broadcasted_iota(I32, (n_sens, n_sens), 0)
            col = lax.broadcasted_iota(I32, (n_sens, n_sens), 1)
            before = jnp.where(row < col, 1.0, 0.0).astype(BF16)
            rank = jnp.dot(flag, before, preferred_element_type=F32)[0:1, :]
            pos_ref[...] = jnp.where(mine, rank.astype(I32), -1)

        sub_r = lax.broadcasted_iota(I32, (tile_r, foot), 0)
        sub_c = lax.broadcasted_iota(I32, (tile_c, foot), 0)
        point = rows_ref[...]
        high = point // tile_c
        low = point - high * tile_c
        c = coef_ref[...].astype(F32)
        sq = c * c
        sq_top = sq.astype(BF16).astype(F32)
        sq_rest = sq - sq_top
        for s in range(sb):
            at_r = sub_r == high[s : s + 1, :]
            left = jnp.concatenate(
                [jnp.where(at_r, sq_top[s : s + 1, :], 0.0), jnp.where(at_r, sq_rest[s : s + 1, :], 0.0)], axis=0
            ).astype(BF16)
            right = jnp.where(sub_c == low[s : s + 1, :], 1.0, 0.0).astype(BF16)
            both = lax.dot_general(left, right, (((1,), (1,)), ((), ())), preferred_element_type=F32)
            map_ref[s] = both[:tile_r] + both[tile_r:]

    return pl.pallas_call(
        body,
        grid=(nblk // sb,),
        in_specs=[
            pl.BlockSpec(memory_space=pltpu.SMEM),
            pl.BlockSpec((sb, foot), lambda g: (g, 0)),
            pl.BlockSpec((sb, foot), lambda g: (g, 0)),
            pl.BlockSpec((1, n_sens), lambda g: (0, 0)),
        ],
        out_specs=[
            pl.BlockSpec((sb, tile_r, tile_c), lambda g: (g, 0, 0)),
            pl.BlockSpec((1, n_sens), lambda g: (0, 0)),
        ],
        out_shape=[
            jax.ShapeDtypeStruct((nblk, tile_r, tile_c), F32),
            jax.ShapeDtypeStruct((1, n_sens), I32),
        ],
        compiler_params=pltpu.CompilerParams(
            dimension_semantics=("arbitrary",), vmem_limit_bytes=24 * 1024 * 1024
        ),
        name="spread_squares",
    )(me, rows, coef, owner)


def finish(parts, weights, sensor, count, maps, pos, scale, sb=32):
    n_dev = parts.shape[0]
    n_sens = weights.shape[1]
    nblk, tile_r, tile_c = maps.shape

    def body(count_ref, parts_ref, weights_ref, sensor_ref, pos_ref, maps_ref, sens_ref, new_ref, dens_ref, slot_w):
        g = pl.program_id(0)

        @pl.when(g == 0)
        def _():
            h = jnp.sum(parts_ref[...], axis=0) * scale
            gain = weights_ref[...] * jnp.sqrt(1.0 + h)
            new = n_sens * gain / jnp.sum(gain)
            new_ref[...] = new
            k = lax.broadcasted_iota(I32, (SPD, n_sens), 0)
            own = jnp.sum(jnp.where(pos_ref[...] == k, h, 0.0), axis=1, keepdims=True)
            diag = lax.broadcasted_iota(I32, (SPD, 128), 0) == lax.broadcasted_iota(I32, (SPD, 128), 1)
            sens_ref[...] = jnp.sum(jnp.where(diag, own, 0.0), axis=0, keepdims=True)
            which = lax.broadcasted_iota(I32, (nblk, n_sens), 1)
            w = jnp.sum(jnp.where(which == sensor_ref[...], new, 0.0), axis=1, keepdims=True)
            alive = lax.broadcasted_iota(I32, (nblk, 1), 0) < count_ref[0]
            slot_w[...] = jnp.broadcast_to(jnp.where(alive, w, 0.0), (nblk, tile_c))
            dens_ref[...] = jnp.zeros((tile_r, tile_c), F32)

        total = dens_ref[...]
        for s in range(sb):
            total += slot_w[pl.ds(g * sb + s, 1), :] * maps_ref[s]
        dens_ref[...] = total

    whole = lambda *shape: pl.BlockSpec(shape, lambda g: (0,) * len(shape))
    return pl.pallas_call(
        body,
        grid=(nblk // sb,),
        in_specs=[
            pl.BlockSpec(memory_space=pltpu.SMEM),
            whole(n_dev, 1, n_sens),
            whole(1, n_sens),
            whole(nblk, 1),
            whole(1, n_sens),
            pl.BlockSpec((sb, tile_r, tile_c), lambda g: (g, 0, 0)),
        ],
        out_specs=[whole(1, 128), whole(1, n_sens), whole(tile_r, tile_c)],
        out_shape=[
            jax.ShapeDtypeStruct((1, 128), F32),
            jax.ShapeDtypeStruct((1, n_sens), F32),
            jax.ShapeDtypeStruct((tile_r, tile_c), F32),
        ],
        scratch_shapes=[pltpu.VMEM((nblk, tile_c), F32)],
        compiler_params=pltpu.CompilerParams(
            dimension_semantics=("arbitrary",), vmem_limit_bytes=24 * 1024 * 1024
        ),
        name="finish",
    )(count, parts, weights, sensor, pos, maps)


def exchange(x):
    return lax.all_to_all(x, AXES, split_axis=0, concat_axis=0, tiled=True)


def local(probes, blk_rows, blk_sensor, blk_count, coef, owner, weights):
    n_dev = lax.axis_size("gx") * lax.axis_size("gy")
    me = (lax.axis_index("gx") * lax.axis_size("gy") + lax.axis_index("gy")).astype(I32).reshape(1)
    tile_r, tile_c, probe_n = probes.shape
    nblk, foot = blk_rows.shape
    n_sens = owner.shape[0]
    flat = probes.reshape(tile_r * tile_c, probe_n)
    index = (blk_rows.T * 2).reshape(-1)
    alive = jnp.arange(nblk, dtype=I32) < blk_count[0]
    side = jnp.stack(
        [
            jnp.where(alive[:, None], coef.astype(F32), 0.0).T,
            jnp.broadcast_to(blk_sensor.astype(F32)[None, :], (foot, nblk)),
        ],
        axis=1,
    )
    side = exchange(side)
    acc = None
    slot0 = 0
    for c, ns in enumerate(CHUNKS):
        sent = gather_rows(flat, index, slot0, ns)
        got = exchange(sent).reshape(n_dev * ns, probe_n)
        w = side[:, 0, slot0 : slot0 + ns].reshape(1, n_dev * ns)
        ids = side[:, 1, slot0 : slot0 + ns].astype(I32).reshape(1, n_dev * ns)
        acc = mix_chunk(got, ids, w, acc, n_sens, c == len(CHUNKS) - 1, n_dev)
        slot0 += ns
    maps, pos = spread_squares(blk_rows, coef, owner.reshape(1, n_sens), me, tile_r, tile_c)
    parts = exchange(acc)
    sens, new, density = finish(
        parts, weights.reshape(1, n_sens), blk_sensor.reshape(nblk, 1), blk_count, maps, pos, 1.0 / (foot * probe_n)
    )
    return (sens[0, :SPD], new.reshape(n_sens), density)


def solution(mesh):
    in_specs = (
        P("gx", "gy", None),
        P(("gx", "gy"), None),
        P(("gx", "gy")),
        P(("gx", "gy")),
        P(("gx", "gy"), None),
        P(),
        P(),
    )
    out_specs = (P(("gx", "gy")), P(), P("gx", "gy"))
    return jax.shard_map(local, mesh=mesh, in_specs=in_specs, out_specs=out_specs, check_vma=False)
```

time: 505 us -> 204 us (0.40)
  waiting for transfers between devices: 216 us -> 72.5 us
  other arithmetic: 100 us -> 2.36 us
  local copies, waits for them, and re-layouts: 101 us -> 20.6 us
  Pallas kernels: 0 us -> 64.4 us
  blocking collectives: 42.3 us -> 0 us
  matrix products: 17 us -> 0 us
  starting transfers between devices: 26.7 us -> 41.6 us
    all_to_all x3 -> x6, waiting for transfers between devices: 216 us -> 72.5 us  [exchange(): return lax.all_to_all(x, AXES, split_axis=0, concat_axis=0, tiled=True)]
    scatter-add x2 -> x0, other arithmetic: 93.6 us -> none  [the longest x1 85.8 us: local(): density = jnp.zeros((tile_r * tile_c,), jnp.float32).at[blk_rows.reshape(...]
    gather x3 -> x0, local copies, waits for them, and re-layouts: 66.1 us -> none  [the longest x1 63.5 us: local(): picked = flat[blk_rows.reshape(-1)].reshape(nblk, foot, probe_n)]
    pallas_call x0 -> x10, Pallas kernels: none -> 64.4 us  [the longest x4 39.4 us: gather_rows(): pl.pallas_call(body, grid_spec=pltpu.PrefetchScalarGridSpec(num_scalar_pr...]
    all_gather x1 -> x0, blocking collectives: 42.3 us -> none  [over_pieces(): tiles = lax.all_gather(shard, axis)]
    scatter x4 -> x0, local copies, waits for them, and re-layouts: 26.1 us -> none  [the longest x1 22.6 us: local(): jnp.zeros((n_dev * CAP, foot, probe_n), jnp.bfloat16).at[position]]
    unnamed x10 -> x34, local copies, waits for them, and re-layouts: 0.03 us -> 18.4 us
    dot_general x1 -> x0, matrix products: 17 us -> none  [local(): jnp.einsum('ksr,srp->krp', mixer, recv_rows, preferred_element_type=jnp.f...]
  transfers between devices with their start and end apart: 3 -> 6, of which waited for: 2 -> 5; matrix products, arithmetic and copies ran while one was open for 21% -> 2% of each run, Pallas kernels for 0% -> 29%
where the time goes in v1:
time: 204 us; the launch traced here: 203 us
  waiting for transfers between devices  72.5 us (36%)
  Pallas kernels  64.4 us (32%)
  starting transfers between devices  41.6 us (20%)
  local copies, waits for them, and re-layouts  20.6 us (10%)
  other arithmetic  2.36 us (1%)
    all_to_all x6, waiting for transfers between devices, exchange(): return lax.all_to_all(x, AXES, split_axis=0, concat_axis=0, tiled=True)  72.5 us
    all_to_all x6, starting transfers between devices, exchange(): return lax.all_to_all(x, AXES, split_axis=0, concat_axis=0, tiled=True)  41.6 us
    pallas_call x4, Pallas kernels, gather_rows(): pl.pallas_call(body, grid_spec=pltpu.PrefetchScalarGridSpec(num_scalar_pr...  39.4 us
    unnamed x34, local copies, waits for them, and re-layouts  18.4 us
    pallas_call x4, Pallas kernels, mix_chunk(): pl.pallas_call(body, grid=(k // kb,), in_specs=specs, out_specs=pl.BlockS...  18 us
    pallas_call x1, Pallas kernels, spread_squares(): pl.pallas_call(body, grid=(nblk // sb,), in_specs=[pl.BlockSpec(memory_sp...  5.32 us
  transfers between devices with their start and end apart: 6, of which 5 were waited for; matrix products, arithmetic and copies ran while one was open for 2% of the time, Pallas kernels for 29%

profile of v1, /device:TPU:1, one launch (start us, length us, event | category | flops | bytes accessed | tf_op | source)
XLA Modules:
  0.0 203.0 jit_solution(5089342295024606297)
XLA Ops:
  1.3 0.7 convert_element_type.59
  1.9 0.9 copy.30
  2.9 0.8 pad_maximum_fusion
  3.6 11.5 %all-to-all-start.1 = ((f32[128,2,128]{2,1,0:T(2,128)}), f32[128,2,128]{2,1,0:T(2,128)S(1)}, u32[]{:S(2)}, u32[]{:S(2)}) async-start(f32[128,2,128]{2,1,0:T(2,128)} %pad_maximum_fusion), calls=%async_computation.1 | async-start | bytes 262144 | tf_op jit(solution)/shard_map/all_to_all | solution.py:244
  15.1 0.9 copy.29
  16.1 0.0 copy-start
  16.1 2.2 %copy-done = bf16[32,256,256]{2,1,0:T(8,128)(2,1)S(1)} copy-done((bf16[32,256,256]{2,1,0:T(8,128)(2,1)S(1)}, bf16[32,256,256]{2,1,0:T(8,128)(2,1)}, u32[]{:S(2)}) %copy-start) | copy-done | bytes 4194328
  18.3 9.8 %gather_rows.7 = bf16[128,32,256]{2,1,0:T(8,128)(2,1)} custom-call(s32[16384]{0:T(1024)S(1)} %multiply_bitcast_fusion.idx, bf16[8192,256]{1,0:T(8,128)(2,1)S(1)} %bitcast.21), custom_call_target="tpu_custom_call" | custom-call | tf_op jit(solution)/shard_map/gather_rows/pallas_call | solution.py:48
  28.1 9.8 %all-to-all-start.4 = ((bf16[128,32,256]{2,1,0:T(8,128)(2,1)}), bf16[128,32,256]{2,1,0:T(8,128)(2,1)S(1)}, u32[]{:S(2)}, u32[]{:S(2)}) async-start(bf16[128,32,256]{2,1,0:T(8,128)(2,1)} %gather_rows.7), calls=%async_computation.4 | async-start | bytes 4194304 | tf_op jit(solution)/shard_map/all_to_all | solution.py:244
  37.8 0.0 copy-start.1
  37.8 2.2 %copy-done.1 = bf16[32,256,256]{2,1,0:T(8,128)(2,1)S(1)} copy-done((bf16[32,256,256]{2,1,0:T(8,128)(2,1)S(1)}, bf16[32,256,256]{2,1,0:T(8,128)(2,1)}, u32[]{:S(2)}) %copy-start.1) | copy-done | bytes 4194328
  40.0 9.9 %gather_rows.6 = bf16[128,32,256]{2,1,0:T(8,128)(2,1)} custom-call(s32[16384]{0:T(1024)S(1)} %multiply_bitcast_fusion.idx, bf16[8192,256]{1,0:T(8,128)(2,1)S(1)} %bitcast.22), custom_call_target="tpu_custom_call" | custom-call | tf_op jit(solution)/shard_map/gather_rows/pallas_call | solution.py:48
  49.9 18.0 %all-to-all-done.4 = bf16[128,32,256]{2,1,0:T(8,128)(2,1)S(1)} async-done(((bf16[128,32,256]{2,1,0:T(8,128)(2,1)}), bf16[128,32,256]{2,1,0:T(8,128)(2,1)S(1)}, u32[]{:S(2)}, u32[]{:S(2)}) %all-to-all-start.4) | async-done | bytes 2097184 | tf_op jit(solution)/shard_map/all_to_all | solution.py:244
  67.9 5.9 %all-to-all-start.3 = ((bf16[128,32,256]{2,1,0:T(8,128)(2,1)}), bf16[128,32,256]{2,1,0:T(8,128)(2,1)}, u32[]{:S(2)}, u32[]{:S(2)}) async-start(bf16[128,32,256]{2,1,0:T(8,128)(2,1)} %gather_rows.6), calls=%async_computation.3 | async-start | bytes 4194304 | tf_op jit(solution)/shard_map/all_to_all | solution.py:244
  73.9 2.2 %copy-done.2 = bf16[32,256,256]{2,1,0:T(8,128)(2,1)S(1)} copy-done((bf16[32,256,256]{2,1,0:T(8,128)(2,1)S(1)}, bf16[32,256,256]{2,1,0:T(8,128)(2,1)}, u32[]{:S(2)}) %copy-start.2) | copy-done | bytes 4194328
  76.0 9.9 %gather_rows.5 = bf16[128,32,256]{2,1,0:T(8,128)(2,1)} custom-call(s32[16384]{0:T(1024)S(1)} %multiply_bitcast_fusion.idx, bf16[8192,256]{1,0:T(8,128)(2,1)S(1)} %bitcast.23), custom_call_target="tpu_custom_call" | custom-call | tf_op jit(solution)/shard_map/gather_rows/pallas_call | solution.py:48
  85.9 17.8 %all-to-all-done.3 = bf16[128,32,256]{2,1,0:T(8,128)(2,1)} async-done(((bf16[128,32,256]{2,1,0:T(8,128)(2,1)}), bf16[128,32,256]{2,1,0:T(8,128)(2,1)}, u32[]{:S(2)}, u32[]{:S(2)}) %all-to-all-start.3) | async-done | bytes 2097184 | tf_op jit(solution)/shard_map/all_to_all | solution.py:244
  103.7 4.8 %all-to-all-start.2 = ((bf16[128,32,256]{2,1,0:T(8,128)(2,1)}), bf16[128,32,256]{2,1,0:T(8,128)(2,1)S(1)}, u32[]{:S(2)}, u32[]{:S(2)}) async-start(bf16[128,32,256]{2,1,0:T(8,128)(2,1)} %gather_rows.5), calls=%async_computation.2 | async-start | bytes 4194304 | tf_op jit(solution)/shard_map/all_to_all | solution.py:244
  108.6 2.2 %copy-done.3 = bf16[32,256,256]{2,1,0:T(8,128)(2,1)S(1)} copy-done((bf16[32,256,256]{2,1,0:T(8,128)(2,1)S(1)}, bf16[32,256,256]{2,1,0:T(8,128)(2,1)}, u32[]{:S(2)}) %copy-start.3) | copy-done | bytes 4194328
  110.8 9.9 %gather_rows.4 = bf16[128,32,256]{2,1,0:T(8,128)(2,1)} custom-call(s32[16384]{0:T(1024)S(1)} %multiply_bitcast_fusion.idx, bf16[8192,256]{1,0:T(8,128)(2,1)S(1)} %bitcast.24), custom_call_target="tpu_custom_call" | custom-call | tf_op jit(solution)/shard_map/gather_rows/pallas_call | solution.py:48
  120.6 18.2 %all-to-all-done.2 = bf16[128,32,256]{2,1,0:T(8,128)(2,1)S(1)} async-done(((bf16[128,32,256]{2,1,0:T(8,128)(2,1)}), bf16[128,32,256]{2,1,0:T(8,128)(2,1)S(1)}, u32[]{:S(2)}, u32[]{:S(2)}) %all-to-all-start.2) | async-done | bytes 2097184 | tf_op jit(solution)/shard_map/all_to_all | solution.py:244
  138.8 1.4 copy-done.6
  140.2 4.8 %all-to-all-start = ((bf16[128,32,256]{2,1,0:T(8,128)(2,1)}), bf16[128,32,256]{2,1,0:T(8,128)(2,1)S(1)}, u32[]{:S(2)}, u32[]{:S(2)}) async-start(bf16[128,32,256]{2,1,0:T(8,128)(2,1)} %gather_rows.4), calls=%async_computation | async-start | bytes 4194304 | tf_op jit(solution)/shard_map/all_to_all | solution.py:244
  145.0 0.8 slice_reduce_fusion
  145.8 0.1 reshape_squeeze.15.refs_2_
  145.9 0.1 reshape_squeeze.14.refs_2_
  146.0 0.1 reshape_squeeze.13.refs_2_
  146.1 0.1 reshape_squeeze.12.refs_2_
  146.2 0.9 fusion
  147.1 0.1 convert_element_type.67.refs_1_
  147.2 0.1 convert_element_type.65.refs_1_
  147.3 0.1 convert_element_type.63.refs_1_
  147.4 0.1 convert_element_type.61.refs_1_
  147.5 1.6 copy-done.5
  149.1 3.7 %mix_chunk.3.refs_3_ = f32[1024,256]{1,0:T(8,128)S(1)} custom-call(bf16[4096,256]{1,0:T(8,128)(2,1)S(1)} %bitcast.26, s32[1,4096]{1,0:T(1,128)S(1)} %convert_element_type.67.refs_1_, f32[1,4096]{1,0:T(1,128)S(1)} %reshape_squeeze.15.refs_2_), custom_call_target="tpu_custom_call" | custom-call | tf_op jit(solution)/shard_map/mix_chunk/pallas_call | solution.py:115
  152.8 6.4 %mix_chunk.4.refs_3_ = f32[1024,256]{1,0:T(8,128)S(1)} custom-call(bf16[4096,256]{1,0:T(8,128)(2,1)} %bitcast.9.refs_0_, s32[1,4096]{1,0:T(1,128)S(1)} %convert_element_type.65.refs_1_, f32[1,4096]{1,0:T(1,128)S(1)} %reshape_squeeze.14.refs_2_, f32[1024,256]{1,0:T(8,128)S(1)} %mix_chunk.3.refs_3_), custom_call_target="tpu_custom_call" | custom-call | tf_op jit(solution)/shard_map/mix_chunk/pallas_call | solution.py:115
  159.2 3.8 %mix_chunk.5.refs_3_ = f32[1024,256]{1,0:T(8,128)S(1)} custom-call(bf16[4096,256]{1,0:T(8,128)(2,1)S(1)} %bitcast.27, s32[1,4096]{1,0:T(1,128)S(1)} %convert_element_type.63.refs_1_, f32[1,4096]{1,0:T(1,128)S(1)} %reshape_squeeze.13.refs_2_, f32[1024,256]{1,0:T(8,128)S(1)} %mix_chunk.4.refs_3_), custom_call_target="tpu_custom_call" | custom-call | tf_op jit(solution)/shard_map/mix_chunk/pallas_call | solution.py:115
  163.0 12.2 %all-to-all-done = bf16[128,32,256]{2,1,0:T(8,128)(2,1)S(1)} async-done(((bf16[128,32,256]{2,1,0:T(8,128)(2,1)}), bf16[128,32,256]{2,1,0:T(8,128)(2,1)S(1)}, u32[]{:S(2)}, u32[]{:S(2)}) %all-to-all-start) | async-done | bytes 2097184 | tf_op jit(solution)/shard_map/all_to_all | solution.py:244
  175.3 4.1 %mix_last.1 = f32[128,1,1024]{2,1,0:T(1,128)S(1)} custom-call(bf16[4096,256]{1,0:T(8,128)(2,1)S(1)} %bitcast.25, s32[1,4096]{1,0:T(1,128)S(1)} %convert_element_type.61.refs_1_, f32[1,4096]{1,0:T(1,128)S(1)} %reshape_squeeze.12.refs_2_, f32[1024,256]{1,0:T(8,128)S(1)} %mix_chunk.5.refs_3_), custom_call_target="tpu_custom_call" | custom-call | tf_op jit(solution)/shard_map/mix_last/pallas_call | solution.py:115
  179.3 0.8 copy-done.10
  180.1 4.8 %all-to-all-start.5 = ((f32[128,1,1024]{2,1,0:T(1,128)}), f32[128,1,1024]{2,1,0:T(1,128)S(1)}, u32[]{:S(2)}, u32[]{:S(2)}) async-start(f32[128,1,1024]{2,1,0:T(1,128)} %copy-done.10), calls=%async_computation.5 | async-start | bytes 1048576 | tf_op jit(solution)/shard_map/all_to_all | solution.py:244
  185.0 0.1 copy.31.sensor_ref
  185.1 5.3 %spread_squares.1 = (f32[128,32,256]{2,1,0:T(8,128)S(1)}, s32[1,1024]{1,0:T(1,128)S(1)}) custom-call(s32[1]{0:T(128)} %bitcast.13.me_ref, s32[128,128]{1,0:T(8,128)S(1)} %copy-done.11, bf16[128,128]{1,0:T(8,128)(2,1)S(1)} %copy-done.12, s32[1,1024]{1,0:T(1,128)S(1)} %bitcast.29), custom_call_target="tpu_custom_call" | custom-call | tf_op jit(solution)/shard_map/spread_squares/pallas_call | solution.py:164
  190.4 1.9 copy-done.8
  192.4 6.3 %all-to-all-done.5.parts_ref = f32[128,1,1024]{2,1,0:T(1,128)S(1)} async-done(((f32[128,1,1024]{2,1,0:T(1,128)}), f32[128,1,1024]{2,1,0:T(1,128)S(1)}, u32[]{:S(2)}, u32[]{:S(2)}) %all-to-all-start.5) | async-done | bytes 524320 | tf_op jit(solution)/shard_map/all_to_all | solution.py:244
  198.6 2.2 %copy-done.9 = f32[128,32,256]{2,1,0:T(8,128)S(1)} copy-done((f32[128,32,256]{2,1,0:T(8,128)S(1)}, f32[128,32,256]{2,1,0:T(8,128)}, u32[]{:S(2)}) %copy-start.9) | copy-done | bytes 4194328
  200.8 1.7 finish.1
  202.5 0.5 slice_bitcast_fusion
  (26 shorter events, 0.1 us)
Async XLA Ops:
  3.6 24.4 %all-to-all-start.1 = ((f32[128,2,128]{2,1,0:T(2,128)}), f32[128,2,128]{2,1,0:T(2,128)S(1)}, u32[]{:S(2)}, u32[]{:S(2)}) async-start(f32[128,2,128]{2,1,0:T(2,128)} %pad_maximum_fusion), calls=%async_computation.1 | async-start | bytes 262144 | tf_op jit(solution)/shard_map/all_to_all | solution.py:244
  16.1 2.2 %copy-start = (bf16[32,256,256]{2,1,0:T(8,128)(2,1)S(1)}, bf16[32,256,256]{2,1,0:T(8,128)(2,1)}, u32[]{:S(2)}) copy-start(bf16[32,256,256]{2,1,0:T(8,128)(2,1)} %param.7) | copy-start | bytes 12582916
  28.1 39.9 %all-to-all-start.4 = ((bf16[128,32,256]{2,1,0:T(8,128)(2,1)}), bf16[128,32,256]{2,1,0:T(8,128)(2,1)S(1)}, u32[]{:S(2)}, u32[]{:S(2)}) async-start(bf16[128,32,256]{2,1,0:T(8,128)(2,1)} %gather_rows.7), calls=%async_computation.4 | async-start | bytes 4194304 | tf_op jit(solution)/shard_map/all_to_all | solution.py:244
  37.8 2.2 %copy-start.1 = (bf16[32,256,256]{2,1,0:T(8,128)(2,1)S(1)}, bf16[32,256,256]{2,1,0:T(8,128)(2,1)}, u32[]{:S(2)}) copy-start(bf16[32,256,256]{2,1,0:T(8,128)(2,1)} %param.7) | copy-start | bytes 12582916
  67.9 18.0 %copy-start.4 = (bf16[128,32,256]{2,1,0:T(8,128)(2,1)}, bf16[128,32,256]{2,1,0:T(8,128)(2,1)S(1)}, u32[]{:S(2)}) copy-start(bf16[128,32,256]{2,1,0:T(8,128)(2,1)S(1)} %all-to-all-done.4) | copy-start | bytes 6291460
  67.9 35.8 %all-to-all-start.3 = ((bf16[128,32,256]{2,1,0:T(8,128)(2,1)}), bf16[128,32,256]{2,1,0:T(8,128)(2,1)}, u32[]{:S(2)}, u32[]{:S(2)}) async-start(bf16[128,32,256]{2,1,0:T(8,128)(2,1)} %gather_rows.6), calls=%async_computation.3 | async-start | bytes 4194304 | tf_op jit(solution)/shard_map/all_to_all | solution.py:244
  73.9 2.2 %copy-start.2 = (bf16[32,256,256]{2,1,0:T(8,128)(2,1)S(1)}, bf16[32,256,256]{2,1,0:T(8,128)(2,1)}, u32[]{:S(2)}) copy-start(bf16[32,256,256]{2,1,0:T(8,128)(2,1)} %param.7) | copy-start | bytes 12582916
  103.7 35.1 %all-to-all-start.2 = ((bf16[128,32,256]{2,1,0:T(8,128)(2,1)}), bf16[128,32,256]{2,1,0:T(8,128)(2,1)S(1)}, u32[]{:S(2)}, u32[]{:S(2)}) async-start(bf16[128,32,256]{2,1,0:T(8,128)(2,1)} %gather_rows.5), calls=%async_computation.2 | async-start | bytes 4194304 | tf_op jit(solution)/shard_map/all_to_all | solution.py:244
  108.6 2.2 %copy-start.3 = (bf16[32,256,256]{2,1,0:T(8,128)(2,1)S(1)}, bf16[32,256,256]{2,1,0:T(8,128)(2,1)}, u32[]{:S(2)}) copy-start(bf16[32,256,256]{2,1,0:T(8,128)(2,1)} %param.7) | copy-start | bytes 12582916
  138.8 1.4 copy-start.6
  140.2 35.1 %all-to-all-start = ((bf16[128,32,256]{2,1,0:T(8,128)(2,1)}), bf16[128,32,256]{2,1,0:T(8,128)(2,1)S(1)}, u32[]{:S(2)}, u32[]{:S(2)}) async-start(bf16[128,32,256]{2,1,0:T(8,128)(2,1)} %gather_rows.4), calls=%async_computation | async-start | bytes 4194304 | tf_op jit(solution)/shard_map/all_to_all | solution.py:244
  147.5 1.6 copy-start.5
  152.8 6.4 %copy-start.7 = (bf16[128,32,256]{2,1,0:T(8,128)(2,1)S(1)}, bf16[128,32,256]{2,1,0:T(8,128)(2,1)}, u32[]{:S(2)}) copy-start(bf16[128,32,256]{2,1,0:T(8,128)(2,1)} %copy-done.6) | copy-start | bytes 6291460
  175.2 9.7 %copy-start.15 = (s32[128]{0:T(128)S(1)}, s32[128]{0:T(128)}, u32[]{:S(2)}) copy-start(s32[128]{0:T(128)} %param.9) | copy-start | bytes 1540
  175.2 9.8 %copy-start.11 = (s32[128,128]{1,0:T(8,128)S(1)}, s32[128,128]{1,0:T(8,128)}, u32[]{:S(2)}) copy-start(s32[128,128]{1,0:T(8,128)} %rows_ref.1) | copy-start | bytes 196612
  175.2 9.8 %copy-start.12 = (bf16[128,128]{1,0:T(8,128)(2,1)S(1)}, bf16[128,128]{1,0:T(8,128)(2,1)}, u32[]{:S(2)}) copy-start(bf16[128,128]{1,0:T(8,128)(2,1)} %coef_ref.1) | copy-start | bytes 98308
  175.2 9.9 %copy-start.14 = (s32[1024]{0:T(1024)S(1)}, s32[1024]{0:T(1024)}, u32[]{:S(2)}) copy-start(s32[1024]{0:T(1024)} %param.12) | copy-start | bytes 12292
  175.2 23.4 %copy-start.13 = (f32[1024]{0:T(1024)S(1)}, f32[1024]{0:T(1024)}, u32[]{:S(2)}) copy-start(f32[1024]{0:T(1024)} %param.13) | copy-start | bytes 12292
  179.3 0.8 copy-start.10
  180.1 18.5 %all-to-all-start.5 = ((f32[128,1,1024]{2,1,0:T(1,128)}), f32[128,1,1024]{2,1,0:T(1,128)S(1)}, u32[]{:S(2)}, u32[]{:S(2)}) async-start(f32[128,1,1024]{2,1,0:T(1,128)} %copy-done.10), calls=%async_computation.5 | async-start | bytes 1048576 | tf_op jit(solution)/shard_map/all_to_all | solution.py:244
  190.4 1.9 copy-start.8
  198.6 2.2 %copy-start.9 = (f32[128,32,256]{2,1,0:T(8,128)S(1)}, f32[128,32,256]{2,1,0:T(8,128)}, u32[]{:S(2)}) copy-start(f32[128,32,256]{2,1,0:T(8,128)} %copy-done.8) | copy-start | bytes 12582916

commit v2 on v1

v2 whole, which is shorter than its diff:
```python
import jax
import jax.numpy as jnp
from jax import lax
from jax.experimental import pallas as pl
from jax.experimental.pallas import tpu as pltpu
from jax.sharding import PartitionSpec as P

SPD = 8
AXES = ("gx", "gy")
CHUNKS = (32, 96)
SIDE = 8
VMEM = 60 * 1024 * 1024
MB = 256
TILES = {16: 64, 32: 32, 48: 16, 64: 16, 80: 16, 96: 16, 112: 8}
F32 = jnp.float32
BF16 = jnp.bfloat16
I32 = jnp.int32


def gather_rows(probes, index, slot0, ns, side=None, rb=16):
    n, pn = probes.shape
    foot = nblk = 128
    half = pn // 2
    extra = 0 if side is None else SIDE
    parts = 8
    step = n // parts

    def body(*refs):
        idx, x_hbm = refs[:2]
        side_refs = refs[2:-6]
        out_ref, raw, tab, stage, coef_t, sem = refs[-6:]
        g = pl.program_id(0)

        @pl.when(g == 0)
        def _():
            def fetch(i):
                return pltpu.make_async_copy(x_hbm.at[pl.ds(i * step, step), :], raw.at[pl.ds(i * step, step), :], sem.at[i])

            for i in range(parts):
                fetch(i).start()
            if side is not None:
                coef_ref, _, count_ref = side_refs
                alive = lax.broadcasted_iota(I32, (nblk, foot), 0) < count_ref[0]
                coef_t[...] = jnp.where(alive, coef_ref[...].astype(F32), 0.0).T
            ch = 512
            for i in range(parts):
                fetch(i).wait()

                def conv(q, c):
                    at = i * step + q * ch
                    x = raw[pl.ds(at, ch), :].astype(F32)
                    tab[pl.ds(at * 2, ch, stride=2), :] = x[:, :half]
                    tab[pl.ds(at * 2 + 1, ch, stride=2), :] = x[:, half:]
                    return c

                lax.fori_loop(0, step // ch, conv, 0)

        def channels(q2, c):
            for u in range(2):
                q = q2 * 2 + u
                base = slot0 * foot + g * rb + q
                for j in range(ns):
                    at = pl.multiple_of(idx[base + j * foot], 2)
                    stage[u, pl.ds(2 * j, 2), :] = tab[pl.ds(at, 2), :]
                out_ref[q, pl.ds(0, ns), :] = stage[u, pl.ds(0, ns, stride=2), :].astype(BF16)
                out_ref[q, pl.ds(ns, ns), :] = stage[u, pl.ds(1, ns, stride=2), :].astype(BF16)
                if side is not None:
                    sensor = side_refs[1][...]
                    high = sensor // MB
                    low = sensor - high * MB
                    row = lax.broadcasted_iota(I32, (SIDE, nblk), 0)
                    tail = jnp.where(row == 1, high, jnp.where(row == 2, low, 0)).astype(F32)
                    tail = jnp.where(row == 0, coef_t[pl.ds(g * rb + q, 1), :], tail)
                    out_ref[q, pl.ds(2 * ns, SIDE), :] = tail.astype(BF16)
            return c

        lax.fori_loop(0, rb // 2, channels, 0)

    specs = [pl.BlockSpec(memory_space=pltpu.HBM)]
    args = [probes]
    if side is not None:
        specs += [
            pl.BlockSpec((nblk, foot), lambda g, idx: (0, 0)),
            pl.BlockSpec((1, nblk), lambda g, idx: (0, 0)),
            pl.BlockSpec(memory_space=pltpu.SMEM),
        ]
        args += list(side)
    return pl.pallas_call(
        body,
        grid_spec=pltpu.PrefetchScalarGridSpec(
            num_scalar_prefetch=1,
            grid=(foot // rb,),
            in_specs=specs,
            out_specs=pl.BlockSpec((rb, 2 * ns + extra, half), lambda g, idx: (g, 0, 0)),
            scratch_shapes=[
                pltpu.VMEM((n, pn), BF16),
                pltpu.VMEM((2 * n, half), F32),
                pltpu.VMEM((2, 2 * ns, half), F32),
                pltpu.VMEM((foot, nblk), F32),
                pltpu.SemaphoreType.DMA((parts,)),
            ],
        ),
        out_shape=jax.ShapeDtypeStruct((foot, 2 * ns + extra, half), BF16),
        compiler_params=pltpu.CompilerParams(
            dimension_semantics=("arbitrary",), vmem_limit_bytes=VMEM
        ),
        name="gather_rows",
    )(index, *args)


def mix_chunk(data, high, low, coef, acc, ns, n_sens, last, kb_tiles):
    n_dev, rows, half = data.shape
    kb = kb_tiles * ns
    n_m = n_sens // MB

    def body(*refs):
        data_ref, high_ref, low_ref, coef_ref = refs[:4]
        acc_ref = None if acc is None else refs[4]
        out_ref, sum_ref = refs[-2:]
        g = pl.program_id(0)

        @pl.when(g == 0)
        def _():
            if acc_ref is None:
                sum_ref[...] = jnp.zeros((n_sens, 2 * half), F32)
            else:
                sum_ref[...] = acc_ref[...]

        x = data_ref[...]
        x = jnp.concatenate([x[:, :ns].reshape(kb, half), x[:, ns : 2 * ns].reshape(kb, half)], axis=1)
        weight = coef_ref[...]
        sub = lax.broadcasted_iota(I32, (MB, kb), 0).astype(F32).astype(BF16)
        for m in range(n_m):
            wanted = jnp.where(high_ref[...] == m, low_ref[...], -1.0).astype(BF16)
            mixer = jnp.where(sub == wanted, weight, jnp.zeros((), BF16))
            sum_ref[pl.ds(m * MB, MB), :] += jnp.dot(mixer, x, preferred_element_type=F32)

        @pl.when(g == pl.num_programs(0) - 1)
        def _():
            if not last:
                out_ref[...] = sum_ref[...]
            else:
                for m in range(n_sens // 128):
                    y = sum_ref[pl.ds(m * 128, 128), :]
                    y = y * y
                    y = y[:, :half] + y[:, half:]
                    row = jnp.sum(y.T, axis=0, keepdims=True)
                    out_ref[:, :, pl.ds(m * 128, 128)] = jnp.broadcast_to(row[None], (n_dev, 1, 128))

    specs = [pl.BlockSpec((kb_tiles, rows, half), lambda g: (g, 0, 0))]
    specs += [pl.BlockSpec((1, kb), lambda g: (0, g))] * 3
    args = [data, high, low, coef]
    if acc is not None:
        specs.append(pl.BlockSpec((n_sens, 2 * half), lambda g: (0, 0)))
        args.append(acc)
    shape = (n_dev, 1, n_sens) if last else (n_sens, 2 * half)
    return pl.pallas_call(
        body,
        grid=(n_dev // kb_tiles,),
        in_specs=specs,
        out_specs=pl.BlockSpec(shape, lambda g: (0,) * len(shape)),
        scratch_shapes=[pltpu.VMEM((n_sens, 2 * half), F32)],
        out_shape=jax.ShapeDtypeStruct(shape, F32),
        compiler_params=pltpu.CompilerParams(
            dimension_semantics=("arbitrary",), vmem_limit_bytes=VMEM
        ),
        name="mix_last" if last else "mix_chunk",
    )(*args)


def spread_squares(rows, coef, owner, me, tile_r, tile_c, sb=8):
    nblk, foot = rows.shape
    n_sens = owner.shape[1]

    def body(me_ref, rows_ref, coef_ref, owner_ref, map_ref, pos_ref):
        g = pl.program_id(0)

        @pl.when(g == 0)
        def _():
            mine = owner_ref[...] == me_ref[0]
            flag = jnp.broadcast_to(jnp.where(mine, 1.0, 0.0), (8, n_sens)).astype(BF16)
            row = lax.broadcasted_iota(I32, (n_sens, n_sens), 0)
            col = lax.broadcasted_iota(I32, (n_sens, n_sens), 1)
            before = jnp.where(row < col, 1.0, 0.0).astype(BF16)
            rank = jnp.dot(flag, before, preferred_element_type=F32)[0:1, :]
            pos_ref[...] = jnp.where(mine, rank.astype(I32), -1)

        sub_r = lax.broadcasted_iota(I32, (tile_r, foot), 0)
        sub_c = lax.broadcasted_iota(I32, (tile_c, foot), 0)
        point = rows_ref[...]
        high = point // tile_c
        low = point - high * tile_c
        c = coef_ref[...].astype(F32)
        sq = c * c
        sq_top = sq.astype(BF16).astype(F32)
        sq_rest = sq - sq_top
        for s in range(sb):
            at_r = sub_r == high[s : s + 1, :]
            left = jnp.concatenate(
                [jnp.where(at_r, sq_top[s : s + 1, :], 0.0), jnp.where(at_r, sq_rest[s : s + 1, :], 0.0)], axis=0
            ).astype(BF16)
            right = jnp.where(sub_c == low[s : s + 1, :], 1.0, 0.0).astype(BF16)
            both = lax.dot_general(left, right, (((1,), (1,)), ((), ())), preferred_element_type=F32)
            map_ref[s] = both[:tile_r] + both[tile_r:]

    return pl.pallas_call(
        body,
        grid=(nblk // sb,),
        in_specs=[
            pl.BlockSpec(memory_space=pltpu.SMEM),
            pl.BlockSpec((sb, foot), lambda g: (g, 0)),
            pl.BlockSpec((sb, foot), lambda g: (g, 0)),
            pl.BlockSpec((1, n_sens), lambda g: (0, 0)),
        ],
        out_specs=[
            pl.BlockSpec((sb, tile_r, tile_c), lambda g: (g, 0, 0)),
            pl.BlockSpec((1, n_sens), lambda g: (0, 0)),
        ],
        out_shape=[
            jax.ShapeDtypeStruct((nblk, tile_r, tile_c), F32),
            jax.ShapeDtypeStruct((1, n_sens), I32),
        ],
        compiler_params=pltpu.CompilerParams(
            dimension_semantics=("arbitrary",), vmem_limit_bytes=VMEM
        ),
        name="spread_squares",
    )(me, rows, coef, owner)


def finish(parts, weights, sensor, count, maps, pos, scale, sb=32):
    n_dev = parts.shape[0]
    n_sens = weights.shape[1]
    nblk, tile_r, tile_c = maps.shape
    pieces = nblk // sb

    def body(count_ref, parts_ref, weights_ref, sensor_ref, pos_ref, maps_hbm, sens_ref, new_ref, dens_ref, slot_w, maps_ref, sem):
        def fetch(i):
            return pltpu.make_async_copy(maps_hbm.at[pl.ds(i * sb, sb)], maps_ref.at[pl.ds(i * sb, sb)], sem.at[i])

        for i in range(pieces):
            fetch(i).start()
        h = jnp.sum(parts_ref[...], axis=0) * scale
        gain = weights_ref[...] * jnp.sqrt(1.0 + h)
        new = n_sens * gain / jnp.sum(gain)
        new_ref[...] = new
        k = lax.broadcasted_iota(I32, (SPD, n_sens), 0)
        own = jnp.sum(jnp.where(pos_ref[...] == k, h, 0.0), axis=1, keepdims=True)
        diag = lax.broadcasted_iota(I32, (SPD, 128), 0) == lax.broadcasted_iota(I32, (SPD, 128), 1)
        sens_ref[...] = jnp.sum(jnp.where(diag, own, 0.0), axis=0, keepdims=True)
        which = lax.broadcasted_iota(I32, (nblk, n_sens), 1)
        w = jnp.sum(jnp.where(which == sensor_ref[...], new, 0.0), axis=1, keepdims=True)
        alive = lax.broadcasted_iota(I32, (nblk, 1), 0) < count_ref[0]
        slot_w[...] = jnp.broadcast_to(jnp.where(alive, w, 0.0), (nblk, tile_c))
        dens_ref[...] = jnp.zeros((tile_r, tile_c), F32)
        for i in range(pieces):
            fetch(i).wait()

            def add(q, c):
                total = dens_ref[...]
                for s in range(8):
                    at = i * sb + q * 8 + s
                    total += slot_w[pl.ds(at, 1), :] * maps_ref[at]
                dens_ref[...] = total
                return c

            lax.fori_loop(0, sb // 8, add, 0)

    vmem = pl.BlockSpec(memory_space=pltpu.VMEM)
    return pl.pallas_call(
        body,
        in_specs=[pl.BlockSpec(memory_space=pltpu.SMEM), vmem, vmem, vmem, vmem, pl.BlockSpec(memory_space=pltpu.HBM)],
        out_specs=[vmem, vmem, vmem],
        out_shape=[
            jax.ShapeDtypeStruct((1, 128), F32),
            jax.ShapeDtypeStruct((1, n_sens), F32),
            jax.ShapeDtypeStruct((tile_r, tile_c), F32),
        ],
        scratch_shapes=[
            pltpu.VMEM((nblk, tile_c), F32),
            pltpu.VMEM((nblk, tile_r, tile_c), F32),
            pltpu.SemaphoreType.DMA((pieces,)),
        ],
        compiler_params=pltpu.CompilerParams(vmem_limit_bytes=VMEM),
        name="finish",
    )(count, parts, weights, sensor, pos, maps)


def exchange(x):
    return lax.all_to_all(x, AXES, split_axis=0, concat_axis=0, tiled=True)


def local(probes, blk_rows, blk_sensor, blk_count, coef, owner, weights):
    n_dev = lax.axis_size("gx") * lax.axis_size("gy")
    me = (lax.axis_index("gx") * lax.axis_size("gy") + lax.axis_index("gy")).astype(I32).reshape(1)
    tile_r, tile_c, probe_n = probes.shape
    nblk, foot = blk_rows.shape
    n_sens = owner.shape[0]
    flat = probes.reshape(tile_r * tile_c, probe_n)
    index = (blk_rows * 2).reshape(-1)
    maps, pos = spread_squares(blk_rows, coef, owner.reshape(1, n_sens), me, tile_r, tile_c)
    acc = side = None
    slot0 = 0
    for c, ns in enumerate(CHUNKS):
        last = c == len(CHUNKS) - 1
        got = exchange(gather_rows(flat, index, slot0, ns, (coef, blk_sensor.reshape(1, nblk), blk_count) if c == 0 else None))
        if c == 0:
            side = got[:, 2 * ns : 2 * ns + 3, :]
        if last:
            got, maps, pos = lax.optimization_barrier((got, maps, pos))
        w, high, low = (side[:, i, slot0 : slot0 + ns].reshape(1, n_dev * ns) for i in range(3))
        acc = mix_chunk(got, high, low, w, acc, ns, n_sens, last, TILES[ns])
        slot0 += ns
    parts = exchange(acc)
    sens, new, density = finish(
        parts, weights.reshape(1, n_sens), blk_sensor.reshape(nblk, 1), blk_count, maps, pos, 1.0 / (foot * probe_n)
    )
    return (sens[0, :SPD], new.reshape(n_sens), density)


def solution(mesh):
    in_specs = (
        P("gx", "gy", None),
        P(("gx", "gy"), None),
        P(("gx", "gy")),
        P(("gx", "gy")),
        P(("gx", "gy"), None),
        P(),
        P(),
    )
    out_specs = (P(("gx", "gy")), P(), P("gx", "gy"))
    return jax.shard_map(local, mesh=mesh, in_specs=in_specs, out_specs=out_specs, check_vma=False)
```

time: 204 us -> 180 us (0.88)
  starting transfers between devices: 41.6 us -> 24.6 us
  local copies, waits for them, and re-layouts: 20.6 us -> 8.15 us
  waiting for transfers between devices: 72.5 us -> 83.1 us
  Pallas kernels: 64.4 us -> 59.5 us
    unnamed x34 -> x6, local copies, waits for them, and re-layouts: 18.4 us -> 0.8 us
    all_to_all x6 -> x3, starting transfers between devices: 41.6 us -> 24.6 us  [exchange(): return lax.all_to_all(x, AXES, split_axis=0, concat_axis=0, tiled=True)]
    pallas_call x4 -> x2, Pallas kernels: 39.4 us -> 28.1 us  [gather_rows(): pl.pallas_call(body, grid_spec=pltpu.PrefetchScalarGridSpec(num_scalar_pr...]
    all_to_all x6 -> x3, waiting for transfers between devices: 72.5 us -> 83.1 us  [exchange(): return lax.all_to_all(x, AXES, split_axis=0, concat_axis=0, tiled=True)]
    pallas_call x1, Pallas kernels: 5.32 us -> 10.6 us  [spread_squares(): pl.pallas_call(body, grid=(nblk // sb,), in_specs=[pl.BlockSpec(memory_sp...]
    another operation x5 -> x6, local copies, waits for them, and re-layouts: 0.4 us -> 4.25 us  [local(): side[:, i, slot0:slot0 + ns].reshape(1, n_dev * ns)]
    pallas_call x5 -> x3, Pallas kernels: 19.6 us -> 20.8 us  [the longest x2 16.8 us: mix_chunk(): pl.pallas_call(body, grid=(n_dev // kb_tiles,), in_specs=specs, out_specs...]
  transfers between devices with their start and end apart: 6 -> 3, of which waited for: 5 -> 3; matrix products, arithmetic and copies ran while one was open for 2% -> 4% of each run, Pallas kernels for 29% -> 19%
where the time goes in v2:
time: 180 us; the launch traced here: 178 us
  waiting for transfers between devices  83.1 us (46%)
  Pallas kernels  59.5 us (33%)
  starting transfers between devices  24.6 us (14%)
  local copies, waits for them, and re-layouts  8.15 us (5%)
    all_to_all x3, waiting for transfers between devices, exchange(): return lax.all_to_all(x, AXES, split_axis=0, concat_axis=0, tiled=True)  83.1 us
    pallas_call x2, Pallas kernels, gather_rows(): pl.pallas_call(body, grid_spec=pltpu.PrefetchScalarGridSpec(num_scalar_pr...  28.1 us
    all_to_all x3, starting transfers between devices, exchange(): return lax.all_to_all(x, AXES, split_axis=0, concat_axis=0, tiled=True)  24.6 us
    pallas_call x2, Pallas kernels, mix_chunk(): pl.pallas_call(body, grid=(n_dev // kb_tiles,), in_specs=specs, out_specs...  16.8 us
    pallas_call x1, Pallas kernels, spread_squares(): pl.pallas_call(body, grid=(nblk // sb,), in_specs=[pl.BlockSpec(memory_sp...  10.6 us
    another operation x6, local copies, waits for them, and re-layouts, local(): side[:, i, slot0:slot0 + ns].reshape(1, n_dev * ns)  4.25 us
    pallas_call x1, Pallas kernels, finish(): pl.pallas_call(body, in_specs=[pl.BlockSpec(memory_space=pltpu.SMEM), vme...  4 us
  transfers between devices with their start and end apart: 3, of which 3 were waited for; matrix products, arithmetic and copies ran while one was open for 4% of the time, Pallas kernels for 19%

profile of v2, /device:TPU:1, one launch (start us, length us, event | category | flops | bytes accessed | tf_op | source)
XLA Modules:
  0.0 178.2 jit_solution(18348889852732901107)
XLA Ops:
  1.3 1.5 multiply_bitcast_fusion.refs_0_
  2.7 10.5 %gather_rows.3 = bf16[128,72,128]{2,1,0:T(8,128)(2,1)} custom-call(s32[16384]{0:T(1024)} %multiply_bitcast_fusion.refs_0_, bf16[8192,256]{1,0:T(8,128)(2,1)} %bitcast.11, bf16[128,128]{1,0:T(8,128)(2,1)} %refs_2_.1, s32[1,128]{1,0:T(1,128)} %bitcast.15, s32[1]{0:T(128)S(6)} %copy.12.refs_4_.count_ref), custom_call_target="tpu_custom_call" | custom-call | tf_op jit(solution)/shard_map/gather_rows/pallas_call | solution.py:88
  13.3 11.5 %all-to-all-start.1 = ((bf16[128,72,128]{2,1,0:T(8,128)(2,1)}), bf16[128,72,128]{2,1,0:T(8,128)(2,1)S(1)}, u32[]{:S(2)}, u32[]{:S(2)}) async-start(bf16[128,72,128]{2,1,0:T(8,128)(2,1)} %gather_rows.3), calls=%async_computation.1 | async-start | bytes 4718592 | tf_op jit(solution)/shard_map/all_to_all | solution.py:289
  24.8 17.5 %gather_rows.2 = bf16[128,192,128]{2,1,0:T(8,128)(2,1)} custom-call(s32[16384]{0:T(1024)} %multiply_bitcast_fusion.refs_0_, bf16[8192,256]{1,0:T(8,128)(2,1)} %bitcast.12), custom_call_target="tpu_custom_call" | custom-call | tf_op jit(solution)/shard_map/gather_rows/pallas_call | solution.py:88
  42.3 15.3 %all-to-all-done.1.refs_0_ = bf16[128,72,128]{2,1,0:T(8,128)(2,1)S(1)} async-done(((bf16[128,72,128]{2,1,0:T(8,128)(2,1)}), bf16[128,72,128]{2,1,0:T(8,128)(2,1)S(1)}, u32[]{:S(2)}, u32[]{:S(2)}) %all-to-all-start.1) | async-done | bytes 2359328 | tf_op jit(solution)/shard_map/all_to_all | solution.py:289
  57.6 0.0 copy-start
  57.6 6.0 %all-to-all-start = ((bf16[128,192,128]{2,1,0:T(8,128)(2,1)}), bf16[128,192,128]{2,1,0:T(8,128)(2,1)}, u32[]{:S(2)}, u32[]{:S(2)}) async-start(bf16[128,192,128]{2,1,0:T(8,128)(2,1)} %gather_rows.2), calls=%async_computation | async-start | bytes 12582912 | tf_op jit(solution)/shard_map/all_to_all | solution.py:289
  63.7 10.6 %spread_squares.1 = (f32[128,32,256]{2,1,0:T(8,128)}, s32[1,1024]{1,0:T(1,128)}) custom-call(s32[1]{0:T(128)} %bitcast.2.me_ref, s32[128,128]{1,0:T(8,128)} %rows_ref.1, bf16[128,128]{1,0:T(8,128)(2,1)} %refs_2_.1, s32[1,1024]{1,0:T(1,128)} %bitcast.14), custom_call_target="tpu_custom_call" | custom-call | tf_op jit(solution)/shard_map/spread_squares/pallas_call | solution.py:206
  74.3 0.7 slice_reduce_fusion.3
  75.0 0.7 reshape_squeeze.18.refs_1_
  75.7 0.7 reshape_squeeze.19.refs_2_
  76.4 0.7 reshape_squeeze.20.refs_3_
  77.2 0.0 copy-done
  77.2 0.6 slice_reduce_fusion
  77.7 0.7 reshape_squeeze.21.refs_1_
  78.4 0.7 reshape_squeeze.22.refs_2_
  79.1 0.7 reshape_squeeze.23.refs_3_
  79.8 5.5 %mix_chunk.1.refs_4_ = f32[1024,256]{1,0:T(8,128)} custom-call(bf16[128,72,128]{2,1,0:T(8,128)(2,1)} %copy-done, bf16[1,4096]{1,0:T(2,128)(2,1)} %reshape_squeeze.21.refs_1_, bf16[1,4096]{1,0:T(2,128)(2,1)} %reshape_squeeze.22.refs_2_, bf16[1,4096]{1,0:T(2,128)(2,1)} %reshape_squeeze.23.refs_3_), custom_call_target="tpu_custom_call" | custom-call | tf_op jit(solution)/shard_map/mix_chunk/pallas_call | solution.py:157
  85.3 55.0 %all-to-all-done.refs_0_ = bf16[128,192,128]{2,1,0:T(8,128)(2,1)} async-done(((bf16[128,192,128]{2,1,0:T(8,128)(2,1)}), bf16[128,192,128]{2,1,0:T(8,128)(2,1)}, u32[]{:S(2)}, u32[]{:S(2)}) %all-to-all-start) | async-done | bytes 6291488 | tf_op jit(solution)/shard_map/all_to_all | solution.py:289
  140.3 0.0 copy-start.2
  140.3 11.3 %mix_last.1 = f32[128,1,1024]{2,1,0:T(1,128)} custom-call(bf16[128,192,128]{2,1,0:T(8,128)(2,1)} %all-to-all-done.refs_0_, bf16[1,12288]{1,0:T(2,128)(2,1)} %reshape_squeeze.18.refs_1_, bf16[1,12288]{1,0:T(2,128)(2,1)} %reshape_squeeze.19.refs_2_, bf16[1,12288]{1,0:T(2,128)(2,1)} %reshape_squeeze.20.refs_3_, f32[1024,256]{1,0:T(8,128)} %mix_chunk.1.refs_4_), custom_call_target="tpu_custom_call" | custom-call | tf_op jit(solution)/shard_map/mix_last/pallas_call | solution.py:157
  151.6 7.1 %all-to-all-start.2 = ((f32[128,1,1024]{2,1,0:T(1,128)}), f32[128,1,1024]{2,1,0:T(1,128)S(1)}, u32[]{:S(2)}, u32[]{:S(2)}) async-start(f32[128,1,1024]{2,1,0:T(1,128)} %mix_last.1), calls=%async_computation.2 | async-start | bytes 1048576 | tf_op jit(solution)/shard_map/all_to_all | solution.py:289
  158.8 0.0 copy-done.2
  158.8 0.7 copy.11.sensor_ref
  159.5 12.8 %all-to-all-done.2.parts_ref = f32[128,1,1024]{2,1,0:T(1,128)S(1)} async-done(((f32[128,1,1024]{2,1,0:T(1,128)}), f32[128,1,1024]{2,1,0:T(1,128)S(1)}, u32[]{:S(2)}, u32[]{:S(2)}) %all-to-all-start.2) | async-done | bytes 524320 | tf_op jit(solution)/shard_map/all_to_all | solution.py:289
  172.3 0.0 copy-start.1
  172.3 0.8 copy-done.1
  173.1 4.0 %finish.1 = (f32[1,128]{1,0:T(1,128)}, f32[1,1024]{1,0:T(1,128)}, f32[32,256]{1,0:T(8,128)}) custom-call(s32[1]{0:T(128)S(6)} %copy.12.refs_4_.count_ref, f32[128,1,1024]{2,1,0:T(1,128)} %copy-done.1, f32[1,1024]{1,0:T(1,128)} %bitcast.13, s32[128,1]{1,0:T(8,128)} %copy.11.sensor_ref, s32[1,1024]{1,0:T(1,128)} %get-tuple-element.14.pos_ref, ...), custom_call_target="tpu_custom_call" | custom-call | tf_op jit(solution)/shard_map/finish/pallas_call | solution.py:269
  177.1 1.1 slice_bitcast_fusion
Async XLA Ops:
  13.3 44.4 %all-to-all-start.1 = ((bf16[128,72,128]{2,1,0:T(8,128)(2,1)}), bf16[128,72,128]{2,1,0:T(8,128)(2,1)S(1)}, u32[]{:S(2)}, u32[]{:S(2)}) async-start(bf16[128,72,128]{2,1,0:T(8,128)(2,1)} %gather_rows.3), calls=%async_computation.1 | async-start | bytes 4718592 | tf_op jit(solution)/shard_map/all_to_all | solution.py:289
  57.6 19.5 %copy-start = (bf16[128,72,128]{2,1,0:T(8,128)(2,1)}, bf16[128,72,128]{2,1,0:T(8,128)(2,1)S(1)}, u32[]{:S(2)}) copy-start(bf16[128,72,128]{2,1,0:T(8,128)(2,1)S(1)} %all-to-all-done.1.refs_0_) | copy-start | bytes 7077892
  57.6 82.7 %all-to-all-start = ((bf16[128,192,128]{2,1,0:T(8,128)(2,1)}), bf16[128,192,128]{2,1,0:T(8,128)(2,1)}, u32[]{:S(2)}, u32[]{:S(2)}) async-start(bf16[128,192,128]{2,1,0:T(8,128)(2,1)} %gather_rows.2), calls=%async_computation | async-start | bytes 12582912 | tf_op jit(solution)/shard_map/all_to_all | solution.py:289
  140.3 18.4 %copy-start.2 = (s32[128]{0:T(128)S(1)}, s32[128]{0:T(128)}, u32[]{:S(2)}) copy-start(s32[128]{0:T(128)} %param.9) | copy-start | bytes 1540
  151.6 20.7 %all-to-all-start.2 = ((f32[128,1,1024]{2,1,0:T(1,128)}), f32[128,1,1024]{2,1,0:T(1,128)S(1)}, u32[]{:S(2)}, u32[]{:S(2)}) async-start(f32[128,1,1024]{2,1,0:T(1,128)} %mix_last.1), calls=%async_computation.2 | async-start | bytes 1048576 | tf_op jit(solution)/shard_map/all_to_all | solution.py:289
  172.3 0.8 copy-start.1

commit v3 on v2

--- a/solution.py
+++ b/solution.py
@@ -9,26 +9,28 @@
 AXES = ("gx", "gy")
 CHUNKS = (32, 96)
 SIDE = 8
+ROOM = 5
 VMEM = 60 * 1024 * 1024
 MB = 256
-TILES = {16: 64, 32: 32, 48: 16, 64: 16, 80: 16, 96: 16, 112: 8}
+TILES = {16: 128, 32: 64, 48: 64, 64: 32, 80: 32, 96: 32, 112: 32}
 F32 = jnp.float32
 BF16 = jnp.bfloat16
 I32 = jnp.int32
 
 
-def gather_rows(probes, index, slot0, ns, side=None, rb=16):
+def gather_rows(probes, rows, slot0, ns, side=None, rb=32, unroll=4):
     n, pn = probes.shape
-    foot = nblk = 128
+    nblk, foot = rows.shape
     half = pn // 2
     extra = 0 if side is None else SIDE
     parts = 8
     step = n // parts
+    n_side = 0 if side is None else 3
 
     def body(*refs):
-        idx, x_hbm = refs[:2]
-        side_refs = refs[2:-6]
-        out_ref, raw, tab, stage, coef_t, sem = refs[-6:]
+        x_hbm, rows_hbm = refs[:2]
+        side_refs = refs[2 : 2 + n_side]
+        out_ref, idx, idx_v, raw, tab, stage, coef_t, sem = refs[2 + n_side :]
         g = pl.program_id(0)
 
         @pl.when(g == 0)
@@ -36,8 +38,14 @@
             def fetch(i):
                 return pltpu.make_async_copy(x_hbm.at[pl.ds(i * step, step), :], raw.at[pl.ds(i * step, step), :], sem.at[i])
 
+            index = pltpu.make_async_copy(rows_hbm.at[pl.ds(slot0, ns), :], idx_v, sem.at[parts])
+            index.start()
             for i in range(parts):
                 fetch(i).start()
+            index.wait()
+            idx_v[...] = idx_v[...] * 2
+            doubled = pltpu.make_async_copy(idx_v, idx, sem.at[parts + 1])
+            doubled.start()
             if side is not None:
                 coef_ref, _, count_ref = side_refs
                 alive = lax.broadcasted_iota(I32, (nblk, foot), 0) < count_ref[0]
@@ -54,14 +62,16 @@
                     return c
 
                 lax.fori_loop(0, step // ch, conv, 0)
-
-        def channels(q2, c):
-            for u in range(2):
-                q = q2 * 2 + u
-                base = slot0 * foot + g * rb + q
+            doubled.wait()
+
+        def channels(t, c):
+            for u in range(unroll):
+                r = g * rb + t * unroll + u
                 for j in range(ns):
-                    at = pl.multiple_of(idx[base + j * foot], 2)
+                    at = pl.multiple_of(idx.at[j][r], 2)
                     stage[u, pl.ds(2 * j, 2), :] = tab[pl.ds(at, 2), :]
+            for u in range(unroll):
+                q = t * unroll + u
                 out_ref[q, pl.ds(0, ns), :] = stage[u, pl.ds(0, ns, stride=2), :].astype(BF16)
                 out_ref[q, pl.ds(ns, ns), :] = stage[u, pl.ds(1, ns, stride=2), :].astype(BF16)
                 if side is not None:
@@ -74,38 +84,35 @@
                     out_ref[q, pl.ds(2 * ns, SIDE), :] = tail.astype(BF16)
             return c
 
-        lax.fori_loop(0, rb // 2, channels, 0)
-
-    specs = [pl.BlockSpec(memory_space=pltpu.HBM)]
-    args = [probes]
+        lax.fori_loop(0, rb // unroll, channels, 0)
+
+    specs = [pl.BlockSpec(memory_space=pltpu.HBM)] * 2
+    args = [probes, rows]
     if side is not None:
         specs += [
-            pl.BlockSpec((nblk, foot), lambda g, idx: (0, 0)),
-            pl.BlockSpec((1, nblk), lambda g, idx: (0, 0)),
+            pl.BlockSpec((nblk, foot), lambda g: (0, 0)),
+            pl.BlockSpec((1, nblk), lambda g: (0, 0)),
             pl.BlockSpec(memory_space=pltpu.SMEM),
         ]
         args += list(side)
     return pl.pallas_call(
         body,
-        grid_spec=pltpu.PrefetchScalarGridSpec(
-            num_scalar_prefetch=1,
-            grid=(foot // rb,),
-            in_specs=specs,
-            out_specs=pl.BlockSpec((rb, 2 * ns + extra, half), lambda g, idx: (g, 0, 0)),
-            scratch_shapes=[
-                pltpu.VMEM((n, pn), BF16),
-                pltpu.VMEM((2 * n, half), F32),
-                pltpu.VMEM((2, 2 * ns, half), F32),
-                pltpu.VMEM((foot, nblk), F32),
-                pltpu.SemaphoreType.DMA((parts,)),
-            ],
-        ),
+        grid=(foot // rb,),
+        in_specs=specs,
+        out_specs=pl.BlockSpec((rb, 2 * ns + extra, half), lambda g: (g, 0, 0)),
+        scratch_shapes=[
+            pltpu.SMEM((ns, foot), I32),
+            pltpu.VMEM((ns, foot), I32),
+            pltpu.VMEM((n, pn), BF16),
+            pltpu.VMEM((2 * n, half), F32),
+            pltpu.VMEM((unroll, 2 * ns, half), F32),
+            pltpu.VMEM((foot, nblk), F32),
+            pltpu.SemaphoreType.DMA((parts + 2,)),
+        ],
         out_shape=jax.ShapeDtypeStruct((foot, 2 * ns + extra, half), BF16),
-        compiler_params=pltpu.CompilerParams(
-            dimension_semantics=("arbitrary",), vmem_limit_bytes=VMEM
-        ),
+        compiler_params=pltpu.CompilerParams(dimension_semantics=("arbitrary",), vmem_limit_bytes=VMEM),
         name="gather_rows",
-    )(index, *args)
+    )(*args)
 
 
 def mix_chunk(data, high, low, coef, acc, ns, n_sens, last, kb_tiles):
@@ -217,7 +224,7 @@
             pl.BlockSpec((1, n_sens), lambda g: (0, 0)),
         ],
         out_shape=[
-            jax.ShapeDtypeStruct((nblk, tile_r, tile_c), F32),
+            jax.ShapeDtypeStruct((ROOM * nblk, tile_r, tile_c), F32),
             jax.ShapeDtypeStruct((1, n_sens), I32),
         ],
         compiler_params=pltpu.CompilerParams(
@@ -230,7 +237,8 @@
 def finish(parts, weights, sensor, count, maps, pos, scale, sb=32):
     n_dev = parts.shape[0]
     n_sens = weights.shape[1]
-    nblk, tile_r, tile_c = maps.shape
+    nblk = sensor.shape[0]
+    tile_r, tile_c = maps.shape[1:]
     pieces = nblk // sb
 
     def body(count_ref, parts_ref, weights_ref, sensor_ref, pos_ref, maps_hbm, sens_ref, new_ref, dens_ref, slot_w, maps_ref, sem):
@@ -245,7 +253,7 @@
         new_ref[...] = new
         k = lax.broadcasted_iota(I32, (SPD, n_sens), 0)
         own = jnp.sum(jnp.where(pos_ref[...] == k, h, 0.0), axis=1, keepdims=True)
-        diag = lax.broadcasted_iota(I32, (SPD, 128), 0) == lax.broadcasted_iota(I32, (SPD, 128), 1)
+        diag = lax.broadcasted_iota(I32, (SPD, SPD), 0) == lax.broadcasted_iota(I32, (SPD, SPD), 1)
         sens_ref[...] = jnp.sum(jnp.where(diag, own, 0.0), axis=0, keepdims=True)
         which = lax.broadcasted_iota(I32, (nblk, n_sens), 1)
         w = jnp.sum(jnp.where(which == sensor_ref[...], new, 0.0), axis=1, keepdims=True)
@@ -271,7 +279,7 @@
         in_specs=[pl.BlockSpec(memory_space=pltpu.SMEM), vmem, vmem, vmem, vmem, pl.BlockSpec(memory_space=pltpu.HBM)],
         out_specs=[vmem, vmem, vmem],
         out_shape=[
-            jax.ShapeDtypeStruct((1, 128), F32),
+            jax.ShapeDtypeStruct((1, SPD), F32),
             jax.ShapeDtypeStruct((1, n_sens), F32),
             jax.ShapeDtypeStruct((tile_r, tile_c), F32),
         ],
@@ -280,7 +288,7 @@
             pltpu.VMEM((nblk, tile_r, tile_c), F32),
             pltpu.SemaphoreType.DMA((pieces,)),
         ],
-        compiler_params=pltpu.CompilerParams(vmem_limit_bytes=VMEM),
+        compiler_params=pltpu.CompilerParams(vmem_limit_bytes=48 * 1024 * 1024),
         name="finish",
     )(count, parts, weights, sensor, pos, maps)
 
@@ -296,13 +304,12 @@
     nblk, foot = blk_rows.shape
     n_sens = owner.shape[0]
     flat = probes.reshape(tile_r * tile_c, probe_n)
-    index = (blk_rows * 2).reshape(-1)
     maps, pos = spread_squares(blk_rows, coef, owner.reshape(1, n_sens), me, tile_r, tile_c)
     acc = side = None
     slot0 = 0
     for c, ns in enumerate(CHUNKS):
         last = c == len(CHUNKS) - 1
-        got = exchange(gather_rows(flat, index, slot0, ns, (coef, blk_sensor.reshape(1, nblk), blk_count) if c == 0 else None))
+        got = exchange(gather_rows(flat, blk_rows, slot0, ns, (coef, blk_sensor.reshape(1, nblk), blk_count) if c == 0 else None))
         if c == 0:
             side = got[:, 2 * ns : 2 * ns + 3, :]
         if last:
@@ -314,7 +321,7 @@
     sens, new, density = finish(
         parts, weights.reshape(1, n_sens), blk_sensor.reshape(nblk, 1), blk_count, maps, pos, 1.0 / (foot * probe_n)
     )
-    return (sens[0, :SPD], new.reshape(n_sens), density)
+    return (sens.reshape(SPD), new.reshape(n_sens), density)
 
 
 def solution(mesh):

time: 180 us -> 171 us (0.950)
  Pallas kernels: 59.5 us -> 47.4 us
  waiting for transfers between devices: 83.1 us -> 90.6 us
  local copies, waits for them, and re-layouts: 8.15 us -> 5.66 us
    pallas_call x2, Pallas kernels: 28.1 us -> 18.2 us  [gather_rows(): pl.pallas_call(body, grid=(foot // rb,), in_specs=specs, out_specs=pl.Blo...]
    all_to_all x3, waiting for transfers between devices: 83.1 us -> 90.6 us  [exchange(): return lax.all_to_all(x, AXES, split_axis=0, concat_axis=0, tiled=True)]
  transfers between devices with their start and end apart: 3 -> 3, of which waited for: 3 -> 3; matrix products, arithmetic and copies ran while one was open for 4% -> 3% of each run, Pallas kernels for 19% -> 16%
where the time goes in v3:
time: 171 us; the launch traced here: 170 us
  waiting for transfers between devices  90.6 us (53%)
  Pallas kernels  47.4 us (28%)
  starting transfers between devices  24.6 us (14%)
  local copies, waits for them, and re-layouts  5.66 us (3%)
    all_to_all x3, waiting for transfers between devices, exchange(): return lax.all_to_all(x, AXES, split_axis=0, concat_axis=0, tiled=True)  90.6 us
    all_to_all x3, starting transfers between devices, exchange(): return lax.all_to_all(x, AXES, split_axis=0, concat_axis=0, tiled=True)  24.6 us
    pallas_call x2, Pallas kernels, gather_rows(): pl.pallas_call(body, grid=(foot // rb,), in_specs=specs, out_specs=pl.Blo...  18.2 us
    pallas_call x2, Pallas kernels, mix_chunk(): pl.pallas_call(body, grid=(n_dev // kb_tiles,), in_specs=specs, out_specs...  15.2 us
    pallas_call x1, Pallas kernels, spread_squares(): pl.pallas_call(body, grid=(nblk // sb,), in_specs=[pl.BlockSpec(memory_sp...  10.7 us
    another operation x6, local copies, waits for them, and re-layouts, local(): side[:, i, slot0:slot0 + ns].reshape(1, n_dev * ns)  4.26 us
  transfers between devices with their start and end apart: 3, of which 3 were waited for; matrix products, arithmetic and copies ran while one was open for 3% of the time, Pallas kernels for 16%

profile of v3, /device:TPU:1, one launch (start us, length us, event | category | flops | bytes accessed | tf_op | source)
XLA Modules:
  0.0 169.5 jit_solution(3770237569968016593)
XLA Ops:
  1.3 6.9 %gather_rows.3 = bf16[128,72,128]{2,1,0:T(8,128)(2,1)} custom-call(bf16[8192,256]{1,0:T(8,128)(2,1)} %bitcast.9, s32[128,128]{1,0:T(8,128)} %refs_1_.3, bf16[128,128]{1,0:T(8,128)(2,1)} %refs_2_.1, s32[1,128]{1,0:T(1,128)} %bitcast.12, s32[1]{0:T(128)S(6)} %copy.12.refs_4_.count_ref), custom_call_target="tpu_custom_call" | custom-call | tf_op jit(solution)/shard_map/gather_rows/pallas_call | solution.py:98
  8.2 11.5 %all-to-all-start.1 = ((bf16[128,72,128]{2,1,0:T(8,128)(2,1)}), bf16[128,72,128]{2,1,0:T(8,128)(2,1)S(1)}, u32[]{:S(2)}, u32[]{:S(2)}) async-start(bf16[128,72,128]{2,1,0:T(8,128)(2,1)} %gather_rows.3), calls=%async_computation.1 | async-start | bytes 4718592 | tf_op jit(solution)/shard_map/all_to_all | solution.py:297
  19.7 11.3 %gather_rows.2 = bf16[128,192,128]{2,1,0:T(8,128)(2,1)} custom-call(bf16[8192,256]{1,0:T(8,128)(2,1)} %bitcast.10, s32[128,128]{1,0:T(8,128)} %refs_1_.3), custom_call_target="tpu_custom_call" | custom-call | tf_op jit(solution)/shard_map/gather_rows/pallas_call | solution.py:98
  31.0 21.6 %all-to-all-done.1.refs_0_ = bf16[128,72,128]{2,1,0:T(8,128)(2,1)S(1)} async-done(((bf16[128,72,128]{2,1,0:T(8,128)(2,1)}), bf16[128,72,128]{2,1,0:T(8,128)(2,1)S(1)}, u32[]{:S(2)}, u32[]{:S(2)}) %all-to-all-start.1) | async-done | bytes 2359328 | tf_op jit(solution)/shard_map/all_to_all | solution.py:297
  52.6 0.0 copy-start.2
  52.6 6.0 %all-to-all-start = ((bf16[128,192,128]{2,1,0:T(8,128)(2,1)}), bf16[128,192,128]{2,1,0:T(8,128)(2,1)}, u32[]{:S(2)}, u32[]{:S(2)}) async-start(bf16[128,192,128]{2,1,0:T(8,128)(2,1)} %gather_rows.2), calls=%async_computation | async-start | bytes 12582912 | tf_op jit(solution)/shard_map/all_to_all | solution.py:297
  58.6 10.7 %spread_squares.1 = (f32[640,32,256]{2,1,0:T(8,128)}, s32[1,1024]{1,0:T(1,128)}) custom-call(s32[1]{0:T(128)} %bitcast.1.me_ref, s32[128,128]{1,0:T(8,128)} %refs_1_.3, bf16[128,128]{1,0:T(8,128)(2,1)} %refs_2_.1, s32[1,1024]{1,0:T(1,128)} %bitcast.11), custom_call_target="tpu_custom_call" | custom-call | tf_op jit(solution)/shard_map/spread_squares/pallas_call | solution.py:213
  69.2 0.7 slice_reduce_fusion.3
  69.9 0.7 reshape_squeeze.20.refs_3_
  70.7 0.7 reshape_squeeze.19.refs_2_
  71.4 0.7 reshape_squeeze.18.refs_1_
  72.1 0.0 copy-done.2
  72.1 0.6 slice_reduce_fusion
  72.7 0.7 reshape_squeeze.23.refs_3_
  73.4 0.7 reshape_squeeze.22.refs_2_
  74.1 0.7 reshape_squeeze.21.refs_1_
  74.8 4.9 %mix_chunk.1.refs_4_ = f32[1024,256]{1,0:T(8,128)} custom-call(bf16[128,72,128]{2,1,0:T(8,128)(2,1)} %copy-done.2, bf16[1,4096]{1,0:T(2,128)(2,1)} %reshape_squeeze.21.refs_1_, bf16[1,4096]{1,0:T(2,128)(2,1)} %reshape_squeeze.22.refs_2_, bf16[1,4096]{1,0:T(2,128)(2,1)} %reshape_squeeze.23.refs_3_), custom_call_target="tpu_custom_call" | custom-call | tf_op jit(solution)/shard_map/mix_chunk/pallas_call | solution.py:164
  79.7 55.6 %all-to-all-done.refs_0_ = bf16[128,192,128]{2,1,0:T(8,128)(2,1)} async-done(((bf16[128,192,128]{2,1,0:T(8,128)(2,1)}), bf16[128,192,128]{2,1,0:T(8,128)(2,1)}, u32[]{:S(2)}, u32[]{:S(2)}) %all-to-all-start) | async-done | bytes 6291488 | tf_op jit(solution)/shard_map/all_to_all | solution.py:297
  135.3 0.0 copy-start.3
  135.3 0.0 copy-start
  135.3 0.0 copy-start.1
  135.3 10.3 %mix_last.1 = f32[128,1,1024]{2,1,0:T(1,128)} custom-call(bf16[128,192,128]{2,1,0:T(8,128)(2,1)} %all-to-all-done.refs_0_, bf16[1,12288]{1,0:T(2,128)(2,1)} %reshape_squeeze.18.refs_1_, bf16[1,12288]{1,0:T(2,128)(2,1)} %reshape_squeeze.19.refs_2_, bf16[1,12288]{1,0:T(2,128)(2,1)} %reshape_squeeze.20.refs_3_, f32[1024,256]{1,0:T(8,128)} %mix_chunk.1.refs_4_), custom_call_target="tpu_custom_call" | custom-call | tf_op jit(solution)/shard_map/mix_last/pallas_call | solution.py:164
  145.6 7.1 %all-to-all-start.2 = ((f32[128,1,1024]{2,1,0:T(1,128)}), f32[128,1,1024]{2,1,0:T(1,128)S(1)}, u32[]{:S(2)}, u32[]{:S(2)}) async-start(f32[128,1,1024]{2,1,0:T(1,128)} %mix_last.1), calls=%async_computation.2 | async-start | bytes 1048576 | tf_op jit(solution)/shard_map/all_to_all | solution.py:297
  152.7 0.0 copy-done.3
  152.7 0.1 copy.11.sensor_ref
  152.8 13.4 %all-to-all-done.2.parts_ref = f32[128,1,1024]{2,1,0:T(1,128)S(1)} async-done(((f32[128,1,1024]{2,1,0:T(1,128)}), f32[128,1,1024]{2,1,0:T(1,128)S(1)}, u32[]{:S(2)}, u32[]{:S(2)}) %all-to-all-start.2) | async-done | bytes 524320 | tf_op jit(solution)/shard_map/all_to_all | solution.py:297
  166.3 0.0 copy-done
  166.3 0.0 copy-done.1
  166.3 3.3 %finish.1 = (f32[1,8]{1,0:T(1,128)}, f32[1,1024]{1,0:T(1,128)}, f32[32,256]{1,0:T(8,128)}) custom-call(s32[1]{0:T(128)S(6)} %copy.12.refs_4_.count_ref, f32[128,1,1024]{2,1,0:T(1,128)S(1)} %all-to-all-done.2.parts_ref, f32[1,1024]{1,0:T(1,128)S(1)} %bitcast.8, s32[128,1]{1,0:T(8,128)S(1)} %copy.11.sensor_ref, s32[1,1024]{1,0:T(1,128)S(1)} %copy-done.1, ...), custom_call_target="tpu_custom_call" | custom-call | tf_op jit(solution)/shard_map/finish/pallas_call | solution.py:277
Async XLA Ops:
  8.2 44.4 %all-to-all-start.1 = ((bf16[128,72,128]{2,1,0:T(8,128)(2,1)}), bf16[128,72,128]{2,1,0:T(8,128)(2,1)S(1)}, u32[]{:S(2)}, u32[]{:S(2)}) async-start(bf16[128,72,128]{2,1,0:T(8,128)(2,1)} %gather_rows.3), calls=%async_computation.1 | async-start | bytes 4718592 | tf_op jit(solution)/shard_map/all_to_all | solution.py:297
  52.6 19.5 %copy-start.2 = (bf16[128,72,128]{2,1,0:T(8,128)(2,1)}, bf16[128,72,128]{2,1,0:T(8,128)(2,1)S(1)}, u32[]{:S(2)}) copy-start(bf16[128,72,128]{2,1,0:T(8,128)(2,1)S(1)} %all-to-all-done.1.refs_0_) | copy-start | bytes 7077892
  52.6 82.7 %all-to-all-start = ((bf16[128,192,128]{2,1,0:T(8,128)(2,1)}), bf16[128,192,128]{2,1,0:T(8,128)(2,1)}, u32[]{:S(2)}, u32[]{:S(2)}) async-start(bf16[128,192,128]{2,1,0:T(8,128)(2,1)} %gather_rows.2), calls=%async_computation | async-start | bytes 12582912 | tf_op jit(solution)/shard_map/all_to_all | solution.py:297
  135.3 17.5 %copy-start.3 = (s32[128]{0:T(128)S(1)}, s32[128]{0:T(128)}, u32[]{:S(2)}) copy-start(s32[128]{0:T(128)} %param.9) | copy-start | bytes 1540
  135.3 31.0 %copy-start = (f32[1024]{0:T(1024)S(1)}, f32[1024]{0:T(1024)}, u32[]{:S(2)}) copy-start(f32[1024]{0:T(1024)} %param.13) | copy-start | bytes 12292
  135.3 31.0 %copy-start.1 = (s32[1,1024]{1,0:T(1,128)S(1)}, s32[1,1024]{1,0:T(1,128)}, u32[]{:S(2)}) copy-start(s32[1,1024]{1,0:T(1,128)} %get-tuple-element.14.pos_ref) | copy-start | bytes 12292
  145.6 20.7 %all-to-all-start.2 = ((f32[128,1,1024]{2,1,0:T(1,128)}), f32[128,1,1024]{2,1,0:T(1,128)S(1)}, u32[]{:S(2)}, u32[]{:S(2)}) async-start(f32[128,1,1024]{2,1,0:T(1,128)} %mix_last.1), calls=%async_computation.2 | async-start | bytes 1048576 | tf_op jit(solution)/shard_map/all_to_all | solution.py:297

commit v4 on v3

--- a/solution.py
+++ b/solution.py
@@ -7,12 +7,12 @@
 
 SPD = 8
 AXES = ("gx", "gy")
-CHUNKS = (32, 96)
+CHUNKS = (112, 16)
 SIDE = 8
 ROOM = 5
 VMEM = 60 * 1024 * 1024
 MB = 256
-TILES = {16: 128, 32: 64, 48: 64, 64: 32, 80: 32, 96: 32, 112: 32}
+TILES = {16: 64, 32: 64, 48: 64, 64: 32, 80: 32, 96: 32, 112: 32}
 F32 = jnp.float32
 BF16 = jnp.bfloat16
 I32 = jnp.int32

time: 171 us -> 185 us (1.082)
  waiting for transfers between devices: 90.6 us -> 99.3 us
  local copies, waits for them, and re-layouts: 5.66 us -> 9.09 us
    all_to_all x3, waiting for transfers between devices: 90.6 us -> 99.3 us  [exchange(): return lax.all_to_all(x, AXES, split_axis=0, concat_axis=0, tiled=True)]
    slice x2, local copies, waits for them, and re-layouts: 1.26 us -> 3.69 us  [local(): side[:, i, slot0:slot0 + ns].reshape(1, n_dev * ns)]
  transfers between devices with their start and end apart: 3 -> 3, of which waited for: 3 -> 3; matrix products, arithmetic and copies ran while one was open for 3% -> 0% of each run, Pallas kernels for 16% -> 13%
where the time goes in v4:
time: 185 us; the launch traced here: 184 us
  waiting for transfers between devices  99.3 us (54%)
  Pallas kernels  47.8 us (26%)
  starting transfers between devices  26.3 us (14%)
  local copies, waits for them, and re-layouts  9.09 us (5%)
    all_to_all x3, waiting for transfers between devices, exchange(): return lax.all_to_all(x, AXES, split_axis=0, concat_axis=0, tiled=True)  99.3 us
    all_to_all x3, starting transfers between devices, exchange(): return lax.all_to_all(x, AXES, split_axis=0, concat_axis=0, tiled=True)  26.3 us
    pallas_call x2, Pallas kernels, gather_rows(): pl.pallas_call(body, grid=(foot // rb,), in_specs=specs, out_specs=pl.Blo...  18.7 us
    pallas_call x2, Pallas kernels, mix_chunk(): pl.pallas_call(body, grid=(n_dev // kb_tiles,), in_specs=specs, out_specs...  15.2 us
    pallas_call x1, Pallas kernels, spread_squares(): pl.pallas_call(body, grid=(nblk // sb,), in_specs=[pl.BlockSpec(memory_sp...  10.6 us
    another operation x6, local copies, waits for them, and re-layouts, local(): side[:, i, slot0:slot0 + ns].reshape(1, n_dev * ns)  4.28 us
  transfers between devices with their start and end apart: 3, of which 3 were waited for; matrix products, arithmetic and copies ran while one was open for 0% of the time, Pallas kernels for 13%

profile of v4, /device:TPU:1, one launch (start us, length us, event | category | flops | bytes accessed | tf_op | source)
XLA Modules:
  0.0 183.8 jit_solution(17118538407148710919)
XLA Ops:
  0.6 5.0 %gather_rows.2 = bf16[128,32,128]{2,1,0:T(8,128)(2,1)} custom-call(bf16[8192,256]{1,0:T(8,128)(2,1)} %bitcast.9, s32[128,128]{1,0:T(8,128)} %refs_1_.3), custom_call_target="tpu_custom_call" | custom-call | tf_op jit(solution)/shard_map/gather_rows/pallas_call | solution.py:98
  5.6 11.5 %all-to-all-start = ((bf16[128,32,128]{2,1,0:T(8,128)(2,1)}), bf16[128,32,128]{2,1,0:T(8,128)(2,1)S(1)}, u32[]{:S(2)}, u32[]{:S(2)}) async-start(bf16[128,32,128]{2,1,0:T(8,128)(2,1)} %gather_rows.2), calls=%async_computation | async-start | bytes 2097152 | tf_op jit(solution)/shard_map/all_to_all | solution.py:297
  17.7 13.8 %gather_rows.3 = bf16[128,232,128]{2,1,0:T(8,128)(2,1)} custom-call(bf16[8192,256]{1,0:T(8,128)(2,1)} %bitcast.10, s32[128,128]{1,0:T(8,128)} %refs_1_.3, bf16[128,128]{1,0:T(8,128)(2,1)} %refs_2_.1, s32[1,128]{1,0:T(1,128)} %bitcast.12, s32[1]{0:T(128)S(6)} %copy.12.refs_4_.count_ref), custom_call_target="tpu_custom_call" | custom-call | tf_op jit(solution)/shard_map/gather_rows/pallas_call | solution.py:98
  31.5 4.6 %all-to-all-done.refs_0_ = bf16[128,32,128]{2,1,0:T(8,128)(2,1)S(1)} async-done(((bf16[128,32,128]{2,1,0:T(8,128)(2,1)}), bf16[128,32,128]{2,1,0:T(8,128)(2,1)S(1)}, u32[]{:S(2)}, u32[]{:S(2)}) %all-to-all-start) | async-done | bytes 1048608 | tf_op jit(solution)/shard_map/all_to_all | solution.py:297
  36.1 0.0 copy-start.2
  36.1 1.0 copy-done.2
  37.1 5.9 %all-to-all-start.1 = ((bf16[128,232,128]{2,1,0:T(8,128)(2,1)}), bf16[128,232,128]{2,1,0:T(8,128)(2,1)}, u32[]{:S(2)}, u32[]{:S(2)}) async-start(bf16[128,232,128]{2,1,0:T(8,128)(2,1)} %gather_rows.3), calls=%async_computation.1 | async-start | bytes 15204352 | tf_op jit(solution)/shard_map/all_to_all | solution.py:297
  43.0 0.0 copy-start.3
  43.0 0.0 copy-start
  43.0 10.6 %spread_squares.1 = (f32[640,32,256]{2,1,0:T(8,128)}, s32[1,1024]{1,0:T(1,128)}) custom-call(s32[1]{0:T(128)} %bitcast.1.me_ref, s32[128,128]{1,0:T(8,128)} %refs_1_.3, bf16[128,128]{1,0:T(8,128)(2,1)} %refs_2_.1, s32[1,1024]{1,0:T(1,128)} %bitcast.11), custom_call_target="tpu_custom_call" | custom-call | tf_op jit(solution)/shard_map/spread_squares/pallas_call | solution.py:213
  53.7 0.0 copy-start.1
  53.7 81.3 %all-to-all-done.1.refs_0_ = bf16[128,232,128]{2,1,0:T(8,128)(2,1)} async-done(((bf16[128,232,128]{2,1,0:T(8,128)(2,1)}), bf16[128,232,128]{2,1,0:T(8,128)(2,1)}, u32[]{:S(2)}, u32[]{:S(2)}) %all-to-all-start.1) | async-done | bytes 7602208 | tf_op jit(solution)/shard_map/all_to_all | solution.py:297
  135.0 1.9 %slice_reduce_fusion.3 = (bf16[128,16]{1,0:T(8,128)(2,1)S(1)}, bf16[128,16]{1,0:T(8,128)(2,1)S(1)}, bf16[128,16]{1,0:T(8,128)(2,1)S(1)}) fusion(bf16[128,232,128]{2,1,0:T(8,128)(2,1)} %all-to-all-done.1.refs_0_), kind=kLoop, calls=%fused_computation.3 | loop fusion | bytes 24576 | tf_op jit(solution)/shard_map/slice | solution.py:317
  136.9 0.7 reshape_squeeze.20.refs_3_
  137.6 0.7 reshape_squeeze.19.refs_2_
  138.2 0.7 reshape_squeeze.18.refs_1_
  138.9 1.8 slice_reduce_fusion
  140.7 0.7 reshape_squeeze.23.refs_3_
  141.5 0.7 reshape_squeeze.22.refs_2_
  142.2 0.7 reshape_squeeze.21.refs_1_
  142.9 11.0 %mix_chunk.1.refs_4_ = f32[1024,256]{1,0:T(8,128)} custom-call(bf16[128,232,128]{2,1,0:T(8,128)(2,1)} %all-to-all-done.1.refs_0_, bf16[1,14336]{1,0:T(2,128)(2,1)} %reshape_squeeze.21.refs_1_, bf16[1,14336]{1,0:T(2,128)(2,1)} %reshape_squeeze.22.refs_2_, bf16[1,14336]{1,0:T(2,128)(2,1)} %reshape_squeeze.23.refs_3_), custom_call_target="tpu_custom_call" | custom-call | tf_op jit(solution)/shard_map/mix_chunk/pallas_call | solution.py:164
  153.9 4.2 %mix_last.1 = f32[128,1,1024]{2,1,0:T(1,128)} custom-call(bf16[128,32,128]{2,1,0:T(8,128)(2,1)} %copy-done.2, bf16[1,2048]{1,0:T(2,128)(2,1)} %reshape_squeeze.18.refs_1_, bf16[1,2048]{1,0:T(2,128)(2,1)} %reshape_squeeze.19.refs_2_, bf16[1,2048]{1,0:T(2,128)(2,1)} %reshape_squeeze.20.refs_3_, f32[1024,256]{1,0:T(8,128)} %mix_chunk.1.refs_4_), custom_call_target="tpu_custom_call" | custom-call | tf_op jit(solution)/shard_map/mix_last/pallas_call | solution.py:164
  158.1 8.9 %all-to-all-start.2 = ((f32[128,1,1024]{2,1,0:T(1,128)}), f32[128,1,1024]{2,1,0:T(1,128)S(1)}, u32[]{:S(2)}, u32[]{:S(2)}) async-start(f32[128,1,1024]{2,1,0:T(1,128)} %mix_last.1), calls=%async_computation.2 | async-start | bytes 1048576 | tf_op jit(solution)/shard_map/all_to_all | solution.py:297
  167.0 0.0 copy-done.3
  167.0 0.1 copy.11.sensor_ref
  167.1 13.4 %all-to-all-done.2.parts_ref = f32[128,1,1024]{2,1,0:T(1,128)S(1)} async-done(((f32[128,1,1024]{2,1,0:T(1,128)}), f32[128,1,1024]{2,1,0:T(1,128)S(1)}, u32[]{:S(2)}, u32[]{:S(2)}) %all-to-all-start.2) | async-done | bytes 524320 | tf_op jit(solution)/shard_map/all_to_all | solution.py:297
  180.5 0.0 copy-done
  180.5 0.0 copy-done.1
  180.5 3.3 %finish.1 = (f32[1,8]{1,0:T(1,128)}, f32[1,1024]{1,0:T(1,128)}, f32[32,256]{1,0:T(8,128)}) custom-call(s32[1]{0:T(128)S(6)} %copy.12.refs_4_.count_ref, f32[128,1,1024]{2,1,0:T(1,128)S(1)} %all-to-all-done.2.parts_ref, f32[1,1024]{1,0:T(1,128)S(1)} %bitcast.8, s32[128,1]{1,0:T(8,128)S(1)} %copy.11.sensor_ref, s32[1,1024]{1,0:T(1,128)S(1)} %copy-done.1, ...), custom_call_target="tpu_custom_call" | custom-call | tf_op jit(solution)/shard_map/finish/pallas_call | solution.py:277
Async XLA Ops:
  5.6 30.5 %all-to-all-start = ((bf16[128,32,128]{2,1,0:T(8,128)(2,1)}), bf16[128,32,128]{2,1,0:T(8,128)(2,1)S(1)}, u32[]{:S(2)}, u32[]{:S(2)}) async-start(bf16[128,32,128]{2,1,0:T(8,128)(2,1)} %gather_rows.2), calls=%async_computation | async-start | bytes 2097152 | tf_op jit(solution)/shard_map/all_to_all | solution.py:297
  36.1 1.0 copy-start.2
  37.1 97.9 %all-to-all-start.1 = ((bf16[128,232,128]{2,1,0:T(8,128)(2,1)}), bf16[128,232,128]{2,1,0:T(8,128)(2,1)}, u32[]{:S(2)}, u32[]{:S(2)}) async-start(bf16[128,232,128]{2,1,0:T(8,128)(2,1)} %gather_rows.3), calls=%async_computation.1 | async-start | bytes 15204352 | tf_op jit(solution)/shard_map/all_to_all | solution.py:297
  43.0 124.0 %copy-start.3 = (s32[128]{0:T(128)S(1)}, s32[128]{0:T(128)}, u32[]{:S(2)}) copy-start(s32[128]{0:T(128)} %param.9) | copy-start | bytes 1540
  43.0 137.5 %copy-start = (f32[1024]{0:T(1024)S(1)}, f32[1024]{0:T(1024)}, u32[]{:S(2)}) copy-start(f32[1024]{0:T(1024)} %param.13) | copy-start | bytes 12292
  53.7 126.9 %copy-start.1 = (s32[1,1024]{1,0:T(1,128)S(1)}, s32[1,1024]{1,0:T(1,128)}, u32[]{:S(2)}) copy-start(s32[1,1024]{1,0:T(1,128)} %get-tuple-element.14.pos_ref) | copy-start | bytes 12292
  158.1 22.4 %all-to-all-start.2 = ((f32[128,1,1024]{2,1,0:T(1,128)}), f32[128,1,1024]{2,1,0:T(1,128)S(1)}, u32[]{:S(2)}, u32[]{:S(2)}) async-start(f32[128,1,1024]{2,1,0:T(1,128)} %mix_last.1), calls=%async_computation.2 | async-start | bytes 1048576 | tf_op jit(solution)/shard_map/all_to_all | solution.py:297

commit v5 on v4

v5 whole, which is shorter than its diff:
```python
import jax
import jax.numpy as jnp
from jax import lax
from jax.experimental import pallas as pl
from jax.experimental.pallas import tpu as pltpu
from jax.sharding import Mesh
from jax.sharding import PartitionSpec as P

SPD = 8
AXES = ("gx", "z", "core")
SIDE = 8
ROOM = 5
VMEM = 60 * 1024 * 1024
MB = 256
F32 = jnp.float32
BF16 = jnp.bfloat16
I32 = jnp.int32


def gather_rows(probes, rows, coef, sensor, count, core, rb=16, unroll=4):
    n, pn = probes.shape
    nblk, foot = rows.shape
    half = pn // 2
    parts = 8
    step = n // parts

    def body(x_hbm, rows_hbm, coef_ref, sensor_ref, count_ref, core_ref, out_ref, idx, idx_v, raw, tab, stage, coef_t, sem):
        g = pl.program_id(0)

        @pl.when(g == 0)
        def _():
            def fetch(i):
                return pltpu.make_async_copy(x_hbm.at[pl.ds(i * step, step), :], raw.at[pl.ds(i * step, step), :], sem.at[i])

            index = pltpu.make_async_copy(rows_hbm, idx_v, sem.at[parts])
            index.start()
            for i in range(parts):
                fetch(i).start()
            index.wait()
            idx_v[...] = idx_v[...] * 2
            doubled = pltpu.make_async_copy(idx_v, idx, sem.at[parts + 1])
            doubled.start()
            alive = lax.broadcasted_iota(I32, (nblk, foot), 0) < count_ref[0]
            coef_t[...] = jnp.where(alive, coef_ref[...].astype(F32), 0.0).T
            ch = 512
            for i in range(parts):
                fetch(i).wait()

                def conv(q, c):
                    at = i * step + q * ch
                    x = raw[pl.ds(at, ch), :].astype(F32)
                    tab[pl.ds(at * 2, ch, stride=2), :] = x[:, :half]
                    tab[pl.ds(at * 2 + 1, ch, stride=2), :] = x[:, half:]
                    return c

                lax.fori_loop(0, step // ch, conv, 0)
            doubled.wait()

        def channels(t, c):
            for u in range(unroll):
                r = (g * rb + t * unroll + u) * 2 + core_ref[0]
                for j in range(nblk):
                    at = pl.multiple_of(idx.at[j][r], 2)
                    stage[u, pl.ds(2 * j, 2), :] = tab[pl.ds(at, 2), :]
            for u in range(unroll):
                q = t * unroll + u
                out_ref[q, pl.ds(0, nblk), :] = stage[u, pl.ds(0, nblk, stride=2), :].astype(BF16)
                out_ref[q, pl.ds(nblk, nblk), :] = stage[u, pl.ds(1, nblk, stride=2), :].astype(BF16)
                high = sensor_ref[...] // MB
                low = sensor_ref[...] - high * MB
                row = lax.broadcasted_iota(I32, (SIDE, nblk), 0)
                tail = jnp.where(row == 1, high, jnp.where(row == 2, low, 0)).astype(F32)
                tail = jnp.where(row == 0, coef_t[pl.ds((g * rb + q) * 2 + core_ref[0], 1), :], tail)
                out_ref[q, pl.ds(2 * nblk, SIDE), :] = tail.astype(BF16)
            return c

        lax.fori_loop(0, rb // unroll, channels, 0)

    hbm = pl.BlockSpec(memory_space=pltpu.HBM)
    smem = pl.BlockSpec(memory_space=pltpu.SMEM)
    shape = (foot // 2, 2 * nblk + SIDE, half)
    return pl.pallas_call(
        body,
        grid=(foot // 2 // rb,),
        in_specs=[
            hbm,
            hbm,
            pl.BlockSpec((nblk, foot), lambda g: (0, 0)),
            pl.BlockSpec((1, nblk), lambda g: (0, 0)),
            smem,
            smem,
        ],
        out_specs=pl.BlockSpec((rb,) + shape[1:], lambda g: (g, 0, 0)),
        scratch_shapes=[
            pltpu.SMEM((nblk, foot), I32),
            pltpu.VMEM((nblk, foot), I32),
            pltpu.VMEM((n, pn), BF16),
            pltpu.VMEM((2 * n, half), F32),
            pltpu.VMEM((unroll, 2 * nblk, half), F32),
            pltpu.VMEM((foot, nblk), F32),
            pltpu.SemaphoreType.DMA((parts + 2,)),
        ],
        out_shape=jax.ShapeDtypeStruct(shape, BF16),
        compiler_params=pltpu.CompilerParams(dimension_semantics=("arbitrary",), vmem_limit_bytes=VMEM),
        name="gather_rows",
    )(probes, rows, coef, sensor, count, core)


def mix_chunk(data, acc, n_sens, n_dev, last, tiles=16):
    n_tiles, rows, half = data.shape
    ns = half
    kb = tiles * ns
    n_m = n_sens // MB

    def body(*refs):
        data_ref = refs[0]
        acc_ref = None if acc is None else refs[1]
        out_ref, sum_ref = refs[-2:]
        g = pl.program_id(0)

        @pl.when(g == 0)
        def _():
            if acc_ref is None:
                sum_ref[...] = jnp.zeros((n_sens, 2 * half), F32)
            else:
                sum_ref[...] = acc_ref[...]

        x = jnp.concatenate([data_ref[:, :ns].reshape(kb, half), data_ref[:, ns : 2 * ns].reshape(kb, half)], axis=1)
        side = [data_ref[t, 2 * ns :].astype(F32) for t in range(tiles)]
        coef, high, low = (jnp.concatenate([s[i : i + 1] for s in side], axis=1) for i in range(3))
        coef = coef.astype(BF16)
        sub = lax.broadcasted_iota(I32, (MB, kb), 0).astype(F32).astype(BF16)
        for m in range(n_m):
            wanted = jnp.where(high == m, low, -1.0).astype(BF16)
            mixer = jnp.where(sub == wanted, coef, jnp.zeros((), BF16))
            sum_ref[pl.ds(m * MB, MB), :] += jnp.dot(mixer, x, preferred_element_type=F32)

        @pl.when(g == pl.num_programs(0) - 1)
        def _():
            if not last:
                out_ref[...] = sum_ref[...]
            else:
                lanes = []
                for m in range(n_sens // 128):
                    y = sum_ref[pl.ds(m * 128, 128), :]
                    y = y * y
                    y = y[:, :half] + y[:, half:]
                    lanes.append(jnp.sum(y.T, axis=0, keepdims=True))
                out_ref[...] = jnp.broadcast_to(jnp.concatenate(lanes, axis=0)[None], out_ref.shape)

    specs = [pl.BlockSpec((tiles, rows, half), lambda g: (g, 0, 0))]
    args = [data]
    if acc is not None:
        specs.append(pl.BlockSpec((n_sens, 2 * half), lambda g: (0, 0)))
        args.append(acc)
    shape = (n_dev, n_sens // 128, 128) if last else (n_sens, 2 * half)
    return pl.pallas_call(
        body,
        grid=(n_tiles // tiles,),
        in_specs=specs,
        out_specs=pl.BlockSpec(shape, lambda g: (0,) * len(shape)),
        scratch_shapes=[pltpu.VMEM((n_sens, 2 * half), F32)],
        out_shape=jax.ShapeDtypeStruct(shape, F32),
        compiler_params=pltpu.CompilerParams(dimension_semantics=("arbitrary",), vmem_limit_bytes=VMEM),
        name="mix_last" if last else "mix_chunk",
    )(*args)


def spread_squares(rows, coef, owner, me, tile_r, tile_c, sb=8):
    nblk, foot = rows.shape
    n_sens = owner.shape[1]

    def body(me_ref, rows_ref, coef_ref, owner_ref, map_ref, pos_ref):
        g = pl.program_id(0)

        @pl.when(g == 0)
        def _():
            mine = owner_ref[...] == me_ref[0]
            flag = jnp.broadcast_to(jnp.where(mine, 1.0, 0.0), (8, n_sens)).astype(BF16)
            row = lax.broadcasted_iota(I32, (n_sens, n_sens), 0)
            col = lax.broadcasted_iota(I32, (n_sens, n_sens), 1)
            before = jnp.where(row < col, 1.0, 0.0).astype(BF16)
            rank = jnp.dot(flag, before, preferred_element_type=F32)[0:1, :]
            pos_ref[...] = jnp.where(mine, rank.astype(I32), -1)

        sub_r = lax.broadcasted_iota(I32, (tile_r, foot), 0)
        sub_c = lax.broadcasted_iota(I32, (tile_c, foot), 0)
        point = rows_ref[...]
        high = point // tile_c
        low = point - high * tile_c
        c = coef_ref[...].astype(F32)
        sq = c * c
        sq_top = sq.astype(BF16).astype(F32)
        sq_rest = sq - sq_top
        for s in range(sb):
            at_r = sub_r == high[s : s + 1, :]
            left = jnp.concatenate(
                [jnp.where(at_r, sq_top[s : s + 1, :], 0.0), jnp.where(at_r, sq_rest[s : s + 1, :], 0.0)], axis=0
            ).astype(BF16)
            right = jnp.where(sub_c == low[s : s + 1, :], 1.0, 0.0).astype(BF16)
            both = lax.dot_general(left, right, (((1,), (1,)), ((), ())), preferred_element_type=F32)
            map_ref[s] = both[:tile_r] + both[tile_r:]

    return pl.pallas_call(
        body,
        grid=(nblk // sb,),
        in_specs=[
            pl.BlockSpec(memory_space=pltpu.SMEM),
            pl.BlockSpec((sb, foot), lambda g: (g, 0)),
            pl.BlockSpec((sb, foot), lambda g: (g, 0)),
            pl.BlockSpec((1, n_sens), lambda g: (0, 0)),
        ],
        out_specs=[
            pl.BlockSpec((sb, tile_r, tile_c), lambda g: (g, 0, 0)),
            pl.BlockSpec((1, n_sens), lambda g: (0, 0)),
        ],
        out_shape=[
            jax.ShapeDtypeStruct((ROOM * nblk, tile_r, tile_c), F32),
            jax.ShapeDtypeStruct((1, n_sens), I32),
        ],
        compiler_params=pltpu.CompilerParams(
            dimension_semantics=("arbitrary",), vmem_limit_bytes=VMEM
        ),
        name="spread_squares",
    )(me, rows, coef, owner)


def finish(parts, weights, sensor, count, maps, pos, scale, sb=32):
    n_sens = pos.shape[1]
    nblk = sensor.shape[0]
    tile_r, tile_c = maps.shape[1:]
    pieces = nblk // sb

    def body(count_ref, parts_ref, weights_ref, sensor_ref, pos_ref, maps_hbm, sens_ref, new_ref, dens_ref, slot_w, maps_ref, sem):
        def fetch(i):
            return pltpu.make_async_copy(maps_hbm.at[pl.ds(i * sb, sb)], maps_ref.at[pl.ds(i * sb, sb)], sem.at[i])

        for i in range(pieces):
            fetch(i).start()
        h8 = jnp.sum(parts_ref[...], axis=0) * scale
        gain = weights_ref[...] * jnp.sqrt(1.0 + h8)
        new8 = n_sens * gain / jnp.sum(gain)
        new_ref[...] = new8
        h, new = (jnp.concatenate([v[i : i + 1] for i in range(n_sens // 128)], axis=1) for v in (h8, new8))
        k = lax.broadcasted_iota(I32, (SPD, n_sens), 0)
        own = jnp.sum(jnp.where(pos_ref[...] == k, h, 0.0), axis=1, keepdims=True)
        diag = lax.broadcasted_iota(I32, (SPD, SPD), 0) == lax.broadcasted_iota(I32, (SPD, SPD), 1)
        sens_ref[...] = jnp.sum(jnp.where(diag, own, 0.0), axis=0, keepdims=True)
        which = lax.broadcasted_iota(I32, (nblk, n_sens), 1)
        w = jnp.sum(jnp.where(which == sensor_ref[...], new, 0.0), axis=1, keepdims=True)
        alive = lax.broadcasted_iota(I32, (nblk, 1), 0) < count_ref[0]
        slot_w[...] = jnp.broadcast_to(jnp.where(alive, w, 0.0), (nblk, tile_c))
        dens_ref[...] = jnp.zeros((tile_r, tile_c), F32)
        for i in range(pieces):
            fetch(i).wait()

            def add(q, c):
                total = dens_ref[...]
                for s in range(8):
                    at = i * sb + q * 8 + s
                    total += slot_w[pl.ds(at, 1), :] * maps_ref[at]
                dens_ref[...] = total
                return c

            lax.fori_loop(0, sb // 8, add, 0)

    vmem = pl.BlockSpec(memory_space=pltpu.VMEM)
    return pl.pallas_call(
        body,
        in_specs=[pl.BlockSpec(memory_space=pltpu.SMEM), vmem, vmem, vmem, vmem, pl.BlockSpec(memory_space=pltpu.HBM)],
        out_specs=[vmem, vmem, vmem],
        out_shape=[
            jax.ShapeDtypeStruct((1, SPD), F32),
            jax.ShapeDtypeStruct((n_sens // 128, 128), F32),
            jax.ShapeDtypeStruct((tile_r, tile_c), F32),
        ],
        scratch_shapes=[
            pltpu.VMEM((nblk, tile_c), F32),
            pltpu.VMEM((nblk, tile_r, tile_c), F32),
            pltpu.SemaphoreType.DMA((pieces,)),
        ],
        compiler_params=pltpu.CompilerParams(vmem_limit_bytes=48 * 1024 * 1024),
        name="finish",
    )(count, parts, weights, sensor, pos, maps)


def exchange(x, axes):
    return lax.all_to_all(x, axes, split_axis=0, concat_axis=0, tiled=True)


def local(probes, blk_rows, blk_sensor, blk_count, coef, owner, weights):
    n_dev = lax.axis_size(AXES)
    core = lax.axis_index("core").astype(I32).reshape(1)
    me = lax.axis_index(AXES).astype(I32).reshape(1)
    tile_r, tile_c, probe_n = probes.shape
    nblk, foot = blk_rows.shape
    n_sens = owner.shape[0]
    flat = probes.reshape(tile_r * tile_c, probe_n)
    tile = (blk_rows, coef, blk_sensor.reshape(1, nblk), blk_count)
    maps, pos = spread_squares(blk_rows, coef, owner.reshape(1, n_sens), me, tile_r, tile_c)
    own, flat = lax.optimization_barrier((gather_rows(flat, *tile, core), flat))
    own = exchange(own, AXES[:2])
    partner = gather_rows(flat, *tile, 1 - core)
    partner = lax.ppermute(partner, AXES[2], [(0, 1), (1, 0)])
    partner = exchange(partner, AXES[:2])
    acc = mix_chunk(own, None, n_sens, n_dev, False)
    partner, maps, pos = lax.optimization_barrier((partner, maps, pos))
    acc = mix_chunk(partner, acc, n_sens, n_dev, True)
    parts = exchange(acc, AXES)
    sens, new, density = finish(
        parts, weights.reshape(n_sens // 128, 128), blk_sensor.reshape(nblk, 1), blk_count, maps, pos, 1.0 / (foot * probe_n)
    )
    return (sens.reshape(SPD), new.reshape(n_sens), density)


def solution(mesh):
    n_gx, n_gy = mesh.devices.shape
    mesh = Mesh(mesh.devices.reshape(n_gx, n_gy // 2, 2), AXES)
    gy = AXES[1:]
    in_specs = (P("gx", gy, None), P(AXES, None), P(AXES), P(AXES), P(AXES, None), P(), P())
    out_specs = (P(AXES), P(), P("gx", gy))
    return jax.shard_map(local, mesh=mesh, in_specs=in_specs, out_specs=out_specs, check_vma=False)
```

time: 185 us -> 184 us (level)
  blocking collectives: 0 us -> 64.9 us
  waiting for transfers between devices: 99.3 us -> 48.8 us
  local copies, waits for them, and re-layouts: 9.09 us -> 0.12 us
  starting transfers between devices: 26.3 us -> 19.6 us
    all_to_all x0 -> x1, blocking collectives: none -> 64.9 us  [exchange(): return lax.all_to_all(x, axes, split_axis=0, concat_axis=0, tiled=True)]
    all_to_all x3 -> x2, waiting for transfers between devices: 99.3 us -> 48.8 us  [exchange(): return lax.all_to_all(x, axes, split_axis=0, concat_axis=0, tiled=True)]
    all_to_all x3 -> x2, starting transfers between devices: 26.3 us -> 18.1 us  [exchange(): return lax.all_to_all(x, axes, split_axis=0, concat_axis=0, tiled=True)]
    another operation x6 -> x0, local copies, waits for them, and re-layouts: 4.28 us -> none  [local(): side[:, i, slot0:slot0 + ns].reshape(1, n_dev * ns)]
    slice x2 -> x0, local copies, waits for them, and re-layouts: 3.69 us -> none  [local(): side[:, i, slot0:slot0 + ns].reshape(1, n_dev * ns)]
  transfers between devices with their start and end apart: 3 -> 3, of which waited for: 3 -> 2; matrix products, arithmetic and copies ran while one was open for 0% -> 0% of each run, Pallas kernels for 13% -> 10%
where the time goes in v5:
time: 184 us; the launch traced here: 183 us
  blocking collectives  64.9 us (35%)
  waiting for transfers between devices  48.8 us (27%)
  Pallas kernels  48.6 us (26%)
  starting transfers between devices  19.6 us (11%)
    all_to_all x1, blocking collectives, exchange(): return lax.all_to_all(x, axes, split_axis=0, concat_axis=0, tiled=True)  64.9 us
    all_to_all x2, waiting for transfers between devices, exchange(): return lax.all_to_all(x, axes, split_axis=0, concat_axis=0, tiled=True)  48.8 us
    pallas_call x2, Pallas kernels, gather_rows(): pl.pallas_call(body, grid=(foot // 2 // rb,), in_specs=[hbm, hbm, pl.Bloc...  19.8 us
    all_to_all x2, starting transfers between devices, exchange(): return lax.all_to_all(x, axes, split_axis=0, concat_axis=0, tiled=True)  18.1 us
    pallas_call x2, Pallas kernels, mix_chunk(): pl.pallas_call(body, grid=(n_tiles // tiles,), in_specs=specs, out_specs=...  15.2 us
    pallas_call x1, Pallas kernels, spread_squares(): pl.pallas_call(body, grid=(nblk // sb,), in_specs=[pl.BlockSpec(memory_sp...  10.6 us
  transfers between devices with their start and end apart: 3, of which 2 were waited for; matrix products, arithmetic and copies ran while one was open for 0% of the time, Pallas kernels for 10%

profile of v5, /device:TPU:1, one launch (start us, length us, event | category | flops | bytes accessed | tf_op | source)
XLA Modules:
  0.0 183.3 jit_solution(15491259714226976635)
XLA Ops:
  1.3 9.9 %gather_rows.2 = bf16[64,264,128]{2,1,0:T(8,128)(2,1)} custom-call(bf16[8192,256]{1,0:T(8,128)(2,1)} %bitcast.10, s32[128,128]{1,0:T(8,128)} %rows_ref.1, bf16[128,128]{1,0:T(8,128)(2,1)} %coef_ref.5, s32[1,128]{1,0:T(1,128)} %bitcast.12, s32[1]{0:T(128)S(6)} %copy.11.count_ref, s32[1]{0:T(128)} %bitcast.2.core_ref), custom_call_target="tpu_custom_call" | custom-call | tf_op jit(solution)/shard_map/gather_rows/pallas_call | solution.py:82
  11.2 9.9 %gather_rows.3 = bf16[64,264,128]{2,1,0:T(8,128)(2,1)} custom-call(bf16[8192,256]{1,0:T(8,128)(2,1)} %bitcast.11, s32[128,128]{1,0:T(8,128)} %rows_ref.1, bf16[128,128]{1,0:T(8,128)(2,1)} %coef_ref.5, s32[1,128]{1,0:T(1,128)} %bitcast.13, s32[1]{0:T(128)S(6)} %copy.11.count_ref, s32[1]{0:T(128)S(6)} %sub.3.core_ref), custom_call_target="tpu_custom_call" | custom-call | tf_op jit(solution)/shard_map/gather_rows/pallas_call | solution.py:82
  21.1 1.5 collective-permute-start
  22.6 64.9 %all_to_all.15.refs_0_ = bf16[64,264,128]{2,1,0:T(8,128)(2,1)} all-to-all(bf16[64,264,128]{2,1,0:T(8,128)(2,1)} %gather_rows.2), channel_id=1, replica_groups=mesh['gx'=16,'z'=4,'core'=2] {'gx','z'}, dimensions={0} | all-to-all | bytes 8650752 | tf_op jit(solution)/shard_map/all_to_all | solution.py:288
  87.4 0.0 collective-permute-done
  87.4 6.3 %all-to-all-start = ((bf16[64,264,128]{2,1,0:T(8,128)(2,1)}), bf16[64,264,128]{2,1,0:T(8,128)(2,1)}, u32[]{:S(2)}, u32[]{:S(2)}) async-start(bf16[64,264,128]{2,1,0:T(8,128)(2,1)} %collective-permute-done), calls=%async_computation | async-start | bytes 8650752 | tf_op jit(solution)/shard_map/all_to_all | solution.py:288
  93.7 10.6 %spread_squares.1 = (f32[640,32,256]{2,1,0:T(8,128)}, s32[1,1024]{1,0:T(1,128)}) custom-call(s32[1]{0:T(128)} %bitcast.3.me_ref, s32[128,128]{1,0:T(8,128)} %rows_ref.1, bf16[128,128]{1,0:T(8,128)(2,1)} %coef_ref.5, s32[1,1024]{1,0:T(1,128)} %bitcast.15), custom_call_target="tpu_custom_call" | custom-call | tf_op jit(solution)/shard_map/spread_squares/pallas_call | solution.py:204
  104.3 7.4 %mix_chunk.1.refs_1_ = f32[1024,256]{1,0:T(8,128)} custom-call(bf16[64,264,128]{2,1,0:T(8,128)(2,1)} %all_to_all.15.refs_0_), custom_call_target="tpu_custom_call" | custom-call | tf_op jit(solution)/shard_map/mix_chunk/pallas_call | solution.py:157
  111.7 0.0 copy-start.2
  111.7 0.0 copy-start
  111.7 0.0 copy-start.1
  111.7 35.4 %all-to-all-done.refs_0_ = bf16[64,264,128]{2,1,0:T(8,128)(2,1)} async-done(((bf16[64,264,128]{2,1,0:T(8,128)(2,1)}), bf16[64,264,128]{2,1,0:T(8,128)(2,1)}, u32[]{:S(2)}, u32[]{:S(2)}) %all-to-all-start) | async-done | bytes 4325408 | tf_op jit(solution)/shard_map/all_to_all | solution.py:288
  147.1 7.8 %mix_last.1 = f32[128,8,128]{2,1,0:T(8,128)} custom-call(bf16[64,264,128]{2,1,0:T(8,128)(2,1)} %all-to-all-done.refs_0_, f32[1024,256]{1,0:T(8,128)} %mix_chunk.1.refs_1_), custom_call_target="tpu_custom_call" | custom-call | tf_op jit(solution)/shard_map/mix_last/pallas_call | solution.py:157
  154.9 11.9 %all-to-all-start.2 = ((f32[128,8,128]{2,1,0:T(8,128)}), f32[128,8,128]{2,1,0:T(8,128)S(1)}, u32[]{:S(2)}, u32[]{:S(2)}) async-start(f32[128,8,128]{2,1,0:T(8,128)} %mix_last.1), calls=%async_computation.2 | async-start | bytes 1048576 | tf_op jit(solution)/shard_map/all_to_all | solution.py:288
  166.7 0.0 copy-done.2
  166.7 0.1 copy.10.sensor_ref
  166.8 13.4 %all-to-all-done.2.parts_ref = f32[128,8,128]{2,1,0:T(8,128)S(1)} async-done(((f32[128,8,128]{2,1,0:T(8,128)}), f32[128,8,128]{2,1,0:T(8,128)S(1)}, u32[]{:S(2)}, u32[]{:S(2)}) %all-to-all-start.2) | async-done | bytes 524320 | tf_op jit(solution)/shard_map/all_to_all | solution.py:288
  180.3 0.0 copy-done
  180.3 0.0 copy-done.1
  180.3 3.0 %finish.1 = (f32[1,8]{1,0:T(1,128)}, f32[8,128]{1,0:T(8,128)}, f32[32,256]{1,0:T(8,128)}) custom-call(s32[1]{0:T(128)S(6)} %copy.11.count_ref, f32[128,8,128]{2,1,0:T(8,128)S(1)} %all-to-all-done.2.parts_ref, f32[8,128]{1,0:T(8,128)S(1)} %bitcast.9, s32[128,1]{1,0:T(8,128)S(1)} %copy.10.sensor_ref, s32[1,1024]{1,0:T(1,128)S(1)} %copy-done.1, ...), custom_call_target="tpu_custom_call" | custom-call | tf_op jit(solution)/shard_map/finish/pallas_call | solution.py:268
Async XLA Ops:
  21.1 66.3 %collective-permute-start = (bf16[64,264,128]{2,1,0:T(8,128)(2,1)}, bf16[64,264,128]{2,1,0:T(8,128)(2,1)}, u32[]{:S(2)}, u32[]{:S(2)}) collective-permute-start(bf16[64,264,128]{2,1,0:T(8,128)(2,1)} %gather_rows.3), channel_id=1, source_target_pairs={{0,1},{1,0},{2,3},{3,2},{4,5},{5,4},{6,7},{7,6},{8,9},{9,8},{10,11... | collective-permute-start | bytes 12976136 | tf_op jit(solution)/shard_map/ppermute | solution.py:304
  87.4 59.7 %all-to-all-start = ((bf16[64,264,128]{2,1,0:T(8,128)(2,1)}), bf16[64,264,128]{2,1,0:T(8,128)(2,1)}, u32[]{:S(2)}, u32[]{:S(2)}) async-start(bf16[64,264,128]{2,1,0:T(8,128)(2,1)} %collective-permute-done), calls=%async_computation | async-start | bytes 8650752 | tf_op jit(solution)/shard_map/all_to_all | solution.py:288
  111.7 55.0 %copy-start.2 = (s32[128]{0:T(128)S(1)}, s32[128]{0:T(128)}, u32[]{:S(2)}) copy-start(s32[128]{0:T(128)} %param.9) | copy-start | bytes 1540
  111.7 68.5 %copy-start = (f32[1024]{0:T(1024)S(1)}, f32[1024]{0:T(1024)}, u32[]{:S(2)}) copy-start(f32[1024]{0:T(1024)} %param.13) | copy-start | bytes 12292
  111.7 68.5 %copy-start.1 = (s32[1,1024]{1,0:T(1,128)S(1)}, s32[1,1024]{1,0:T(1,128)}, u32[]{:S(2)}) copy-start(s32[1,1024]{1,0:T(1,128)} %get-tuple-element.18.pos_ref) | copy-start | bytes 12292
  154.9 25.4 %all-to-all-start.2 = ((f32[128,8,128]{2,1,0:T(8,128)}), f32[128,8,128]{2,1,0:T(8,128)S(1)}, u32[]{:S(2)}, u32[]{:S(2)}) async-start(f32[128,8,128]{2,1,0:T(8,128)} %mix_last.1), calls=%async_computation.2 | async-start | bytes 1048576 | tf_op jit(solution)/shard_map/all_to_all | solution.py:288

commit v6 on v5

v6 whole, which is shorter than its diff:
```python
import itertools

import jax
import jax.numpy as jnp
from jax import lax
from jax.experimental import pallas as pl
from jax.experimental.pallas import tpu as pltpu
from jax.sharding import Mesh
from jax.sharding import PartitionSpec as P

SPD = 8
AXES = ("y", "x", "z", "core")
ORDERS = (("z", "y", "x"), ("y", "x", "z"), ("x", "z", "y"))
EACH = (5, 5, 6)
PEERS = ((0, 0), (0, 1), (1, 0), (1, 1), (3, 0), (3, 1), (2, 0), (2, 1))
SHIFTS = (0, 1, 3, 2)
SIDE = 8
ROOM = 5
VMEM = 60 * 1024 * 1024
MB = 256
F32 = jnp.float32
BF16 = jnp.bfloat16
I32 = jnp.int32


def member(core_ref, at_ref, shift, flip):
    return ((at_ref[0] + shift) & 3) * 2 + (core_ref[0] + flip) % 2


def gather_flows(probes, rows, coef, sensor, count, core, flows, places):
    n, pn = probes.shape
    nblk, foot = rows.shape
    half = pn // 2
    parts = 8
    step = n // parts
    n_at = len(places)
    n_out = len(flows) * len(PEERS)

    def body(*refs):
        x_hbm, rows_hbm, coef_ref, sensor_ref, count_ref, core_ref = refs[:6]
        at_refs = refs[6 : 6 + n_at]
        outs = refs[6 + n_at : 6 + n_at + n_out]
        idx, idx_v, raw, tab, stage, coef_t, ids, sem, out_sem = refs[6 + n_at + n_out : 6 + n_at + n_out + 9]
        packs = refs[6 + n_at + n_out + 9 :]

        def fetch(i):
            return pltpu.make_async_copy(x_hbm.at[pl.ds(i * step, step), :], raw.at[pl.ds(i * step, step), :], sem.at[i])

        index = pltpu.make_async_copy(rows_hbm, idx_v, sem.at[parts])
        index.start()
        for i in range(parts):
            fetch(i).start()
        index.wait()
        idx_v[...] = idx_v[...] * 2
        doubled = pltpu.make_async_copy(idx_v, idx, sem.at[parts + 1])
        doubled.start()
        alive = lax.broadcasted_iota(I32, (nblk, foot), 0) < count_ref[0]
        coef_t[...] = jnp.where(alive, coef_ref[...].astype(F32), 0.0).T
        high = sensor_ref[...] // MB
        low = sensor_ref[...] - high * MB
        row = lax.broadcasted_iota(I32, (SIDE, nblk), 0)
        ids[...] = jnp.where(row == 1, high, jnp.where(row == 2, low, 0)).astype(F32)
        ch = 512
        for i in range(parts):
            fetch(i).wait()

            def conv(q, c):
                at = i * step + q * ch
                x = raw[pl.ds(at, ch), :].astype(F32)
                tab[pl.ds(at * 2, ch, stride=2), :] = x[:, :half]
                tab[pl.ds(at * 2 + 1, ch, stride=2), :] = x[:, half:]
                return c

            lax.fori_loop(0, step // ch, conv, 0)
        doubled.wait()
        copies = []
        for f, (first, each, axis) in enumerate(flows):
            for p, (shift, flip) in enumerate(PEERS):
                base = first + member(core_ref, at_refs[axis], shift, flip) * each
                pack = packs[f].at[p]

                def channel(i, c):
                    r = base + i
                    for j in range(nblk):
                        at = pl.multiple_of(idx.at[j][r], 2)
                        stage[pl.ds(2 * j, 2), :] = tab[pl.ds(at, 2), :]
                    pack[i, pl.ds(0, nblk), :] = stage[pl.ds(0, nblk, stride=2), :].astype(BF16)
                    pack[i, pl.ds(nblk, nblk), :] = stage[pl.ds(1, nblk, stride=2), :].astype(BF16)
                    tail = jnp.where(row == 0, coef_t[pl.ds(r, 1), :], ids[...])
                    pack[i, pl.ds(2 * nblk, SIDE), :] = tail.astype(BF16)
                    return c

                lax.fori_loop(0, each, channel, 0)
                at = f * len(PEERS) + p
                copies.append(pltpu.make_async_copy(pack, outs[at], out_sem.at[at]))
                copies[-1].start()
        for copy in copies:
            copy.wait()

    hbm = pl.BlockSpec(memory_space=pltpu.HBM)
    smem = pl.BlockSpec(memory_space=pltpu.SMEM)
    vmem = pl.BlockSpec(memory_space=pltpu.VMEM)
    shapes = [(each, 2 * nblk + SIDE, half) for _, each, _ in flows]
    return pl.pallas_call(
        body,
        in_specs=[hbm, hbm, vmem, vmem, smem, smem] + [smem] * n_at,
        out_specs=[hbm] * n_out,
        scratch_shapes=[
            pltpu.SMEM((nblk, foot), I32),
            pltpu.VMEM((nblk, foot), I32),
            pltpu.VMEM((n, pn), BF16),
            pltpu.VMEM((2 * n, half), F32),
            pltpu.VMEM((2 * nblk, half), F32),
            pltpu.VMEM((foot, nblk), F32),
            pltpu.VMEM((SIDE, nblk), F32),
            pltpu.SemaphoreType.DMA((parts + 2,)),
            pltpu.SemaphoreType.DMA((n_out,)),
        ]
        + [pltpu.VMEM((len(PEERS),) + s, BF16) for s in shapes],
        out_shape=[jax.ShapeDtypeStruct(s, BF16) for s in shapes for _ in PEERS],
        compiler_params=pltpu.CompilerParams(vmem_limit_bytes=VMEM),
        name="gather_flows",
    )(probes, rows, coef, sensor, count, core, *places)


def mix_tiles(tiles, at, n_sens):
    each, rows, half = tiles[0].shape
    ns = half
    n = len(tiles)

    def body(at_ref, *refs):
        data, outs = refs[:n], refs[n:]
        x = jnp.concatenate(
            [
                jnp.concatenate([d[0, :ns] for d in data], axis=0),
                jnp.concatenate([d[0, ns : 2 * ns] for d in data], axis=0),
            ],
            axis=1,
        )
        side = [d[0, 2 * ns :].astype(F32) for d in data]
        coef, high, low = (jnp.concatenate([s[i : i + 1] for s in side], axis=1) for i in range(3))
        coef = coef.astype(BF16)
        high = high.astype(I32)
        sub = lax.broadcasted_iota(I32, (MB, n * ns), 0).astype(F32).astype(BF16)
        for out, shift in zip(outs, SHIFTS):
            wanted = jnp.where(high == ((at_ref[0] + shift) & 3), low, -1.0).astype(BF16)
            mixer = jnp.where(sub == wanted, coef, jnp.zeros((), BF16))
            out[0] = jnp.dot(mixer, x, preferred_element_type=F32).astype(BF16)

    shape = (each, n_sens // 4, 2 * half)
    return pl.pallas_call(
        body,
        grid=(each,),
        in_specs=[pl.BlockSpec(memory_space=pltpu.SMEM)] + [pl.BlockSpec((1, rows, half), lambda i: (i, 0, 0))] * n,
        out_specs=[pl.BlockSpec((1,) + shape[1:], lambda i: (i, 0, 0))] * 4,
        out_shape=[jax.ShapeDtypeStruct(shape, BF16)] * 4,
        compiler_params=pltpu.CompilerParams(dimension_semantics=("arbitrary",), vmem_limit_bytes=VMEM),
        name="mix_tiles",
    )(at, *tiles)


def add_quarters(quarters, at):
    each, n_sens, width = quarters[0].shape
    piece = n_sens // 4

    def body(at_ref, *refs):
        for out, shift in zip(refs[4:], SHIFTS):
            rows = pl.ds(pl.multiple_of(((at_ref[0] + shift) & 3) * piece, piece), piece)
            total = refs[0][0, rows, :].astype(F32)
            for r in refs[1:4]:
                total += r[0, rows, :].astype(F32)
            out[0] = total.astype(BF16)

    shape = (each, piece, width)
    return pl.pallas_call(
        body,
        grid=(each,),
        in_specs=[pl.BlockSpec(memory_space=pltpu.SMEM)] + [pl.BlockSpec((1, n_sens, width), lambda i: (i, 0, 0))] * 4,
        out_specs=[pl.BlockSpec((1,) + shape[1:], lambda i: (i, 0, 0))] * 4,
        out_shape=[jax.ShapeDtypeStruct(shape, BF16)] * 4,
        compiler_params=pltpu.CompilerParams(dimension_semantics=("arbitrary",), vmem_limit_bytes=VMEM),
        name="add_quarters",
    )(at, *quarters)


def square_sums(flows, n_dev):
    n = len(flows)
    piece = flows[0][0].shape[1]

    def body(*refs):
        out = refs[-1]
        lanes = []
        for f in range(n):
            four = refs[4 * f : 4 * f + 4]
            total = jnp.zeros((piece, 128), F32)
            for i in range(four[0].shape[0]):
                y = four[0][i].astype(F32) + four[1][i].astype(F32) + four[2][i].astype(F32) + four[3][i].astype(F32)
                y = y * y
                total += y[:, :128] + y[:, 128:]
            total = jnp.concatenate([total, jnp.zeros((128 - piece, 128), F32)], axis=0)
            lanes.append(jnp.sum(total.T, axis=0, keepdims=True))
        out[...] = jnp.broadcast_to(jnp.concatenate(lanes, axis=1)[None], out.shape)

    return pl.pallas_call(
        body,
        out_shape=jax.ShapeDtypeStruct((n_dev, 1, 128 * n), F32),
        compiler_params=pltpu.CompilerParams(vmem_limit_bytes=VMEM),
        name="square_sums",
    )(*[x for four in flows for x in four])


def spread_squares(rows, coef, owner, me, tile_r, tile_c, sb=8):
    nblk, foot = rows.shape
    n_sens = owner.shape[1]

    def body(me_ref, rows_ref, coef_ref, owner_ref, map_ref, pos_ref):
        g = pl.program_id(0)

        @pl.when(g == 0)
        def _():
            mine = owner_ref[...] == me_ref[0]
            flag = jnp.broadcast_to(jnp.where(mine, 1.0, 0.0), (8, n_sens)).astype(BF16)
            row = lax.broadcasted_iota(I32, (n_sens, n_sens), 0)
            col = lax.broadcasted_iota(I32, (n_sens, n_sens), 1)
            before = jnp.where(row < col, 1.0, 0.0).astype(BF16)
            rank = jnp.dot(flag, before, preferred_element_type=F32)[0:1, :]
            pos_ref[...] = jnp.where(mine, rank.astype(I32), -1)

        sub_r = lax.broadcasted_iota(I32, (tile_r, foot), 0)
        sub_c = lax.broadcasted_iota(I32, (tile_c, foot), 0)
        point = rows_ref[...]
        high = point // tile_c
        low = point - high * tile_c
        c = coef_ref[...].astype(F32)
        sq = c * c
        sq_top = sq.astype(BF16).astype(F32)
        sq_rest = sq - sq_top
        for s in range(sb):
            at_r = sub_r == high[s : s + 1, :]
            left = jnp.concatenate(
                [jnp.where(at_r, sq_top[s : s + 1, :], 0.0), jnp.where(at_r, sq_rest[s : s + 1, :], 0.0)], axis=0
            ).astype(BF16)
            right = jnp.where(sub_c == low[s : s + 1, :], 1.0, 0.0).astype(BF16)
            both = lax.dot_general(left, right, (((1,), (1,)), ((), ())), preferred_element_type=F32)
            map_ref[s] = both[:tile_r] + both[tile_r:]

    return pl.pallas_call(
        body,
        grid=(nblk // sb,),
        in_specs=[
            pl.BlockSpec(memory_space=pltpu.SMEM),
            pl.BlockSpec((sb, foot), lambda g: (g, 0)),
            pl.BlockSpec((sb, foot), lambda g: (g, 0)),
            pl.BlockSpec((1, n_sens), lambda g: (0, 0)),
        ],
        out_specs=[
            pl.BlockSpec((sb, tile_r, tile_c), lambda g: (g, 0, 0)),
            pl.BlockSpec((1, n_sens), lambda g: (0, 0)),
        ],
        out_shape=[
            jax.ShapeDtypeStruct((ROOM * nblk, tile_r, tile_c), F32),
            jax.ShapeDtypeStruct((1, n_sens), I32),
        ],
        compiler_params=pltpu.CompilerParams(
            dimension_semantics=("arbitrary",), vmem_limit_bytes=VMEM
        ),
        name="spread_squares",
    )(me, rows, coef, owner)


def finish(parts, weights, sensor, count, maps, pos, scale, sb=32):
    n_sens = pos.shape[1]
    nblk = sensor.shape[0]
    tile_r, tile_c = maps.shape[1:]
    pieces = nblk // sb

    def body(count_ref, parts_ref, weights_ref, sensor_ref, pos_ref, maps_hbm, sens_ref, new_ref, dens_ref, slot_w, maps_ref, sem):
        def fetch(i):
            return pltpu.make_async_copy(maps_hbm.at[pl.ds(i * sb, sb)], maps_ref.at[pl.ds(i * sb, sb)], sem.at[i])

        for i in range(pieces):
            fetch(i).start()
        col = lax.broadcasted_iota(I32, (8, 128), 1)
        place = {"y": col // 32, "x": col // 8 % 4, "z": col // 2 % 4}
        want = lax.broadcasted_iota(I32, (8, 128), 0) * 2
        pair = [jnp.zeros((8, 128), F32), jnp.zeros((8, 128), F32)]
        for f, (_, b, c) in enumerate(ORDERS):
            group = place[b] * 4 + place[c]
            sums = parts_ref[:, 0, pl.ds(128 * f, 128)]
            for odd in range(2):
                pick = jnp.where(group == want + odd, 1.0, 0.0)
                pair[odd] += jnp.dot(pick, sums, precision=lax.Precision.HIGHEST, preferred_element_type=F32)
        h8 = (pair[0] + pltpu.roll(pair[1], 64, 1)) * scale
        gain = weights_ref[...] * jnp.sqrt(1.0 + h8)
        new8 = n_sens * gain / jnp.sum(gain)
        new_ref[...] = new8
        h, new = (jnp.concatenate([v[i : i + 1] for i in range(n_sens // 128)], axis=1) for v in (h8, new8))
        k = lax.broadcasted_iota(I32, (SPD, n_sens), 0)
        own = jnp.sum(jnp.where(pos_ref[...] == k, h, 0.0), axis=1, keepdims=True)
        diag = lax.broadcasted_iota(I32, (SPD, SPD), 0) == lax.broadcasted_iota(I32, (SPD, SPD), 1)
        sens_ref[...] = jnp.sum(jnp.where(diag, own, 0.0), axis=0, keepdims=True)
        which = lax.broadcasted_iota(I32, (nblk, n_sens), 1)
        w = jnp.sum(jnp.where(which == sensor_ref[...], new, 0.0), axis=1, keepdims=True)
        alive = lax.broadcasted_iota(I32, (nblk, 1), 0) < count_ref[0]
        slot_w[...] = jnp.broadcast_to(jnp.where(alive, w, 0.0), (nblk, tile_c))
        dens_ref[...] = jnp.zeros((tile_r, tile_c), F32)
        for i in range(pieces):
            fetch(i).wait()

            def add(q, c):
                total = dens_ref[...]
                for s in range(8):
                    at = i * sb + q * 8 + s
                    total += slot_w[pl.ds(at, 1), :] * maps_ref[at]
                dens_ref[...] = total
                return c

            lax.fori_loop(0, sb // 8, add, 0)

    vmem = pl.BlockSpec(memory_space=pltpu.VMEM)
    return pl.pallas_call(
        body,
        in_specs=[pl.BlockSpec(memory_space=pltpu.SMEM), vmem, vmem, vmem, vmem, pl.BlockSpec(memory_space=pltpu.HBM)],
        out_specs=[vmem, vmem, vmem],
        out_shape=[
            jax.ShapeDtypeStruct((1, SPD), F32),
            jax.ShapeDtypeStruct((n_sens // 128, 128), F32),
            jax.ShapeDtypeStruct((tile_r, tile_c), F32),
        ],
        scratch_shapes=[
            pltpu.VMEM((nblk, tile_c), F32),
            pltpu.VMEM((nblk, tile_r, tile_c), F32),
            pltpu.SemaphoreType.DMA((pieces,)),
        ],
        compiler_params=pltpu.CompilerParams(vmem_limit_bytes=48 * 1024 * 1024),
        name="finish",
    )(count, parts, weights, sensor, pos, maps)


def exchange(x, axes):
    return lax.all_to_all(x, axes, split_axis=0, concat_axis=0, tiled=True)


def shift_to(x, axis, shift, flip):
    if not shift and not flip:
        return x
    sizes = [lax.axis_size(a) for a in AXES]
    where = AXES.index(axis)
    pairs = []
    for i, place in enumerate(itertools.product(*map(range, sizes))):
        to = list(place)
        to[where] = (to[where] + shift) % sizes[where]
        to[3] = (to[3] + flip) % 2
        j = 0
        for p, size in zip(to, sizes):
            j = j * size + p
        pairs.append((i, j))
    return lax.ppermute(x, AXES, pairs)


def local(probes, blk_rows, blk_sensor, blk_count, coef, owner, weights):
    n_dev = lax.axis_size(AXES)
    core = lax.axis_index("core").astype(I32).reshape(1)
    me = lax.axis_index(AXES).astype(I32).reshape(1)
    at = {axis: lax.axis_index(axis).astype(I32).reshape(1) for axis in AXES[:3]}
    tile_r, tile_c, probe_n = probes.shape
    nblk, foot = blk_rows.shape
    n_sens = owner.shape[0]
    flat = probes.reshape(tile_r * tile_c, probe_n)
    tile = (blk_rows, coef, blk_sensor.reshape(1, nblk), blk_count, core)
    maps, pos = spread_squares(blk_rows, coef, owner.reshape(1, n_sens), me, tile_r, tile_c)
    firsts = [8 * sum(EACH[:f]) for f in range(3)]
    sent = gather_flows(flat, *tile, [(firsts[0], EACH[0], 0)], [at["z"]])
    *sent, flat = lax.optimization_barrier((*sent, flat))
    more = gather_flows(flat, *tile, [(firsts[1], EACH[1], 0), (firsts[2], EACH[2], 1)], [at["y"], at["x"]])
    sent = (sent, more[:8], more[8:])
    tiles = [[shift_to(x, a, *peer) for x, peer in zip(sent[f], PEERS)] for f, (a, _, _) in enumerate(ORDERS)]
    flows = []
    for f, (_, b, c) in enumerate(ORDERS):
        quarters = mix_tiles(tiles[f], at[b], n_sens)
        quarters = [shift_to(x, b, s, 0) for x, s in zip(quarters, SHIFTS)]
        pieces = add_quarters(quarters, at[c])
        flows.append([shift_to(x, c, s, 0) for x, s in zip(pieces, SHIFTS)])
    (flows, maps, pos) = lax.optimization_barrier((flows, maps, pos))
    acc = square_sums(flows, n_dev)
    parts = exchange(acc, AXES)
    sens, new, density = finish(
        parts, weights.reshape(n_sens // 128, 128), blk_sensor.reshape(nblk, 1), blk_count, maps, pos, 1.0 / (foot * probe_n)
    )
    return (sens.reshape(SPD), new.reshape(n_sens), density)


def solution(mesh):
    mesh = Mesh(mesh.devices.reshape(4, 4, 4, 2), AXES)
    gx, gy = AXES[:2], AXES[2:]
    in_specs = (P(gx, gy, None), P(AXES, None), P(AXES), P(AXES), P(AXES, None), P(), P())
    out_specs = (P(AXES), P(), P(gx, gy))
    return jax.shard_map(local, mesh=mesh, in_specs=in_specs, out_specs=out_specs, check_vma=False)
```

time: 184 us -> 262 us (1.42)
  starting transfers between devices: 19.6 us -> 95.7 us
  blocking collectives: 64.9 us -> 0 us
  waiting for transfers between devices: 48.8 us -> 87.5 us
  Pallas kernels: 48.6 us -> 68.9 us
  local copies, waits for them, and re-layouts: 0.12 us -> 5.7 us
    ppermute x1 -> x39, starting transfers between devices: 1.46 us -> 84.9 us  [shift_to(): return lax.ppermute(x, AXES, pairs)]
    ppermute x1 -> x39, waiting for transfers between devices: 0.01 us -> 77.3 us  [shift_to(): return lax.ppermute(x, AXES, pairs)]
    all_to_all x1 -> x0, blocking collectives: 64.9 us -> none  [exchange(): return lax.all_to_all(x, axes, split_axis=0, concat_axis=0, tiled=True)]
    all_to_all x2 -> x1, waiting for transfers between devices: 48.8 us -> 10.2 us  [exchange(): return lax.all_to_all(x, axes, split_axis=0, concat_axis=0, tiled=True)]
    pallas_call x4 -> x9, Pallas kernels: 35 us -> 55 us  [the longest x3 20.1 us: mix_tiles(): pl.pallas_call(body, grid=(each,), in_specs=[pl.BlockSpec(memory_space=pl...]
    all_to_all x2 -> x1, starting transfers between devices: 18.1 us -> 10.8 us  [exchange(): return lax.all_to_all(x, axes, split_axis=0, concat_axis=0, tiled=True)]
    unnamed x6 -> x74, local copies, waits for them, and re-layouts: 0.01 us -> 5.59 us
  transfers between devices with their start and end apart: 3 -> 40, of which waited for: 2 -> 10; matrix products, arithmetic and copies ran while one was open for 0% -> 0% of each run, Pallas kernels for 10% -> 17%
where the time goes in v6:
time: 262 us; the launch traced here: 260 us
  starting transfers between devices  95.7 us (37%)
  waiting for transfers between devices  87.5 us (33%)
  Pallas kernels  68.9 us (26%)
  local copies, waits for them, and re-layouts  5.7 us (2%)
    ppermute x39, starting transfers between devices, shift_to(): return lax.ppermute(x, AXES, pairs)  84.9 us
    ppermute x39, waiting for transfers between devices, shift_to(): return lax.ppermute(x, AXES, pairs)  77.3 us
    pallas_call x3, Pallas kernels, mix_tiles(): pl.pallas_call(body, grid=(each,), in_specs=[pl.BlockSpec(memory_space=pl...  20.1 us
    pallas_call x2, Pallas kernels, gather_flows(): pl.pallas_call(body, in_specs=[hbm, hbm, vmem, vmem, smem, smem] + [smem]...  19.2 us
    pallas_call x3, Pallas kernels, add_quarters(): pl.pallas_call(body, grid=(each,), in_specs=[pl.BlockSpec(memory_space=pl...  13 us
    all_to_all x1, starting transfers between devices, exchange(): return lax.all_to_all(x, axes, split_axis=0, concat_axis=0, tiled=True)  10.8 us
    pallas_call x1, Pallas kernels, spread_squares(): pl.pallas_call(body, grid=(nblk // sb,), in_specs=[pl.BlockSpec(memory_sp...  10.6 us
    all_to_all x1, waiting for transfers between devices, exchange(): return lax.all_to_all(x, axes, split_axis=0, concat_axis=0, tiled=True)  10.2 us
  transfers between devices with their start and end apart: 40, of which 10 were waited for; matrix products, arithmetic and copies ran while one was open for 0% of the time, Pallas kernels for 17%

profile of v6, /device:TPU:1, one launch (start us, length us, event | category | flops | bytes accessed | tf_op | source)
XLA Modules:
  0.0 259.7 jit_solution(14462355897975518844)
XLA Ops:
  1.3 7.5 %gather_flows.2 = (bf16[5,264,128]{2,1,0:T(8,128)(2,1)}, bf16[5,264,128]{2,1,0:T(8,128)(2,1)}, bf16[5,264,128]{2,1,0:T(8,128)(2,1)}, bf16[5,264,128]{2,1,0:T(8,1...) custom-call(bf16[8192,256]{1,0:T(8,128)(2,1)} %bitcast.13, ...), custom_call_target="tpu_custom_call" | custom-call | tf_op jit(solution)/shard_map/gather_flows/pallas_call | solution.py:104
  8.9 11.7 %gather_flows.3 = (bf16[5,264,128]{2,1,0:T(8,128)(2,1)}, bf16[5,264,128]{2,1,0:T(8,128)(2,1)}, bf16[5,264,128]{2,1,0:T(8,128)(2,1)}, bf16[5,264,128]{2,1,0:T(8,1...) custom-call(bf16[8192,256]{1,0:T(8,128)(2,1)} %bitcast.14, ...), custom_call_target="tpu_custom_call" | custom-call | tf_op jit(solution)/shard_map/gather_flows/pallas_call | solution.py:104
  20.6 1.5 collective-permute-start.13
  22.0 1.4 collective-permute-start.14
  23.4 1.5 collective-permute-start.15
  25.0 1.4 collective-permute-start.16
  26.9 1.6 collective-permute-start.18
  28.6 4.6 %collective-permute-done.14.refs_2_ = bf16[5,264,128]{2,1,0:T(8,128)(2,1)S(1)} collective-permute-done((bf16[5,264,128]{2,1,0:T(8,128)(2,1)}, bf16[5,264,128]{2,1,0:T(8,128)(2,1)S(1)}, u32[]{:S(2)}, u32[]{:S(2)}) %collective-permute-start.14) | collective-permute-done | bytes 337952 | tf_op jit(solution)/shard_map/ppermute | solution.py:358
  33.2 2.8 %collective-permute-start.19 = (bf16[5,264,128]{2,1,0:T(8,128)(2,1)}, bf16[5,264,128]{2,1,0:T(8,128)(2,1)S(1)}, u32[]{:S(2)}, u32[]{:S(2)}) collective-permute-start(bf16[5,264,128]{2,1,0:T(8,128)(2,1)} %get-tuple-element.111), channel_id=1, source_target_pairs={{0,65},{1,64},{2,67},{3,66},{4,69},{5,68},{6,71},{7,70},{8,73},{9,... | collective-permute-start | bytes 1013768 | tf_op jit(solution)/shard_map/ppermute | solution.py:358
  36.0 4.5 %collective-permute-done.15.refs_3_ = bf16[5,264,128]{2,1,0:T(8,128)(2,1)S(1)} collective-permute-done((bf16[5,264,128]{2,1,0:T(8,128)(2,1)}, bf16[5,264,128]{2,1,0:T(8,128)(2,1)S(1)}, u32[]{:S(2)}, u32[]{:S(2)}) %collective-permute-start.15) | collective-permute-done | bytes 337952 | tf_op jit(solution)/shard_map/ppermute | solution.py:358
  40.8 1.5 collective-permute-start.1
  43.0 1.5 collective-permute-start.2
  44.5 4.2 %collective-permute-done.18.refs_6_ = bf16[5,264,128]{2,1,0:T(8,128)(2,1)S(1)} collective-permute-done((bf16[5,264,128]{2,1,0:T(8,128)(2,1)}, bf16[5,264,128]{2,1,0:T(8,128)(2,1)S(1)}, u32[]{:S(2)}, u32[]{:S(2)}) %collective-permute-start.18) | collective-permute-done | bytes 337952 | tf_op jit(solution)/shard_map/ppermute | solution.py:358
  48.7 3.8 %collective-permute-start.3 = (bf16[5,264,128]{2,1,0:T(8,128)(2,1)}, bf16[5,264,128]{2,1,0:T(8,128)(2,1)S(1)}, u32[]{:S(2)}, u32[]{:S(2)}) collective-permute-start(bf16[5,264,128]{2,1,0:T(8,128)(2,1)} %get-tuple-element.91), channel_id=1, source_target_pairs={{0,6},{1,7},{2,0},{3,1},{4,2},{5,3},{6,4},{7,5},{8,14},{9,15},{10,... | collective-permute-start | bytes 1013768 | tf_op jit(solution)/shard_map/ppermute | solution.py:358
  52.5 3.7 %collective-permute-done.19.refs_7_ = bf16[5,264,128]{2,1,0:T(8,128)(2,1)S(1)} collective-permute-done((bf16[5,264,128]{2,1,0:T(8,128)(2,1)}, bf16[5,264,128]{2,1,0:T(8,128)(2,1)S(1)}, u32[]{:S(2)}, u32[]{:S(2)}) %collective-permute-start.19) | collective-permute-done | bytes 337952 | tf_op jit(solution)/shard_map/ppermute | solution.py:358
  56.2 3.8 %collective-permute-start.4 = (bf16[5,264,128]{2,1,0:T(8,128)(2,1)}, bf16[5,264,128]{2,1,0:T(8,128)(2,1)S(1)}, u32[]{:S(2)}, u32[]{:S(2)}) collective-permute-start(bf16[5,264,128]{2,1,0:T(8,128)(2,1)} %get-tuple-element.92), channel_id=1, source_target_pairs={{0,7},{1,6},{2,1},{3,0},{4,3},{5,2},{6,5},{7,4},{8,15},{9,14},{10,... | collective-permute-start | bytes 1013768 | tf_op jit(solution)/shard_map/ppermute | solution.py:358
  60.0 3.5 %collective-permute-start.6 = (bf16[5,264,128]{2,1,0:T(8,128)(2,1)}, bf16[5,264,128]{2,1,0:T(8,128)(2,1)S(1)}, u32[]{:S(2)}, u32[]{:S(2)}) collective-permute-start(bf16[5,264,128]{2,1,0:T(8,128)(2,1)} %get-tuple-element.94), channel_id=1, source_target_pairs={{0,5},{1,4},{2,7},{3,6},{4,1},{5,0},{6,3},{7,2},{8,13},{9,12},{10,... | collective-permute-start | bytes 1013768 | tf_op jit(solution)/shard_map/ppermute | solution.py:358
  64.3 1.2 collective-permute-start.27
  65.5 16.5 %collective-permute-done.4.refs_5_ = bf16[5,264,128]{2,1,0:T(8,128)(2,1)S(1)} collective-permute-done((bf16[5,264,128]{2,1,0:T(8,128)(2,1)}, bf16[5,264,128]{2,1,0:T(8,128)(2,1)S(1)}, u32[]{:S(2)}, u32[]{:S(2)}) %collective-permute-start.4) | collective-permute-done | bytes 337952 | tf_op jit(solution)/shard_map/ppermute | solution.py:358
  82.7 2.0 collective-permute-start.28
  84.7 1.5 collective-permute-start.29
  86.2 1.0 collective-permute-start.30
  87.9 6.4 %mix_tiles.4 = (bf16[5,256,256]{2,1,0:T(8,128)(2,1)}, bf16[5,256,256]{2,1,0:T(8,128)(2,1)}, bf16[5,256,256]{2,1,0:T(8,128)(2,1)}, bf16[5,256,256]{2,1,0:T(8,128)(2,1)}) custom-call(s32[1]{0:T(128)} %bitcast.at_ref.refs_7_, bf16[5,264,128]{2,1,0:T(8,128)(2,1)} %get-tuple-element.104.refs_0_, bf16[5,264,128]{2,1,0:T(8,128)(2,1)} %copy-done.13, ...), custom_call_target="tpu_custom_call" | custom-call | tf_op jit(solution)/shard_map/mix_tiles/pallas_call | solution.py:151
  95.0 1.2 collective-permute-done.28.refs_3_
  97.2 1.7 collective-permute-start.22
  98.9 6.5 %mix_tiles.3 = (bf16[5,256,256]{2,1,0:T(8,128)(2,1)}, bf16[5,256,256]{2,1,0:T(8,128)(2,1)}, bf16[5,256,256]{2,1,0:T(8,128)(2,1)}, bf16[5,256,256]{2,1,0:T(8,128)(2,1)}) custom-call(s32[1]{0:T(128)} %bitcast.1.at_ref.refs_6_, bf16[5,264,128]{2,1,0:T(8,128)(2,1)} %get-tuple-element.87.refs_0_, bf16[5,264,128]{2,1,0:T(8,128)(2,1)} %copy-done.15, ...), custom_call_target="tpu_custom_call" | custom-call | tf_op jit(solution)/shard_map/mix_tiles/pallas_call | solution.py:151
  106.1 8.8 %collective-permute-start.7 = (bf16[5,256,256]{2,1,0:T(8,128)(2,1)}, bf16[5,256,256]{2,1,0:T(8,128)(2,1)S(1)}, u32[]{:S(2)}, u32[]{:S(2)}) collective-permute-start(bf16[5,256,256]{2,1,0:T(8,128)(2,1)} %get-tuple-element.96), channel_id=1, source_target_pairs={{0,32},{1,33},{2,34},{3,35},{4,36},{5,37},{6,38},{7,39},{8,40},{9,... | collective-permute-start | bytes 1966088 | tf_op jit(solution)/shard_map/ppermute | solution.py:358
  114.9 2.5 collective-permute-start.32
  117.4 25.0 %collective-permute-done.32.refs_7_ = bf16[6,264,128]{2,1,0:T(8,128)(2,1)} collective-permute-done((bf16[6,264,128]{2,1,0:T(8,128)(2,1)}, bf16[6,264,128]{2,1,0:T(8,128)(2,1)}, u32[]{:S(2)}, u32[]{:S(2)}) %collective-permute-start.32) | collective-permute-done | bytes 405536 | tf_op jit(solution)/shard_map/ppermute | solution.py:358
  142.5 7.2 %mix_tiles.5 = (bf16[6,256,256]{2,1,0:T(8,128)(2,1)}, bf16[6,256,256]{2,1,0:T(8,128)(2,1)}, bf16[6,256,256]{2,1,0:T(8,128)(2,1)}, bf16[6,256,256]{2,1,0:T(8,128)(2,1)}) custom-call(s32[1]{0:T(128)} %bitcast.5.refs_6_.at_ref, bf16[6,264,128]{2,1,0:T(8,128)(2,1)} %get-tuple-element.120.refs_0_, bf16[6,264,128]{2,1,0:T(8,128)(2,1)} %copy-done.8, ...), custom_call_target="tpu_custom_call" | custom-call | tf_op jit(solution)/shard_map/mix_tiles/pallas_call | solution.py:151
  149.8 3.1 %collective-permute-start.34 = (bf16[6,256,256]{2,1,0:T(8,128)(2,1)}, bf16[6,256,256]{2,1,0:T(8,128)(2,1)S(1)}, u32[]{:S(2)}, u32[]{:S(2)}) collective-permute-start(bf16[6,256,256]{2,1,0:T(8,128)(2,1)} %get-tuple-element.130), channel_id=1, source_target_pairs={{0,6},{1,7},{2,0},{3,1},{4,2},{5,3},{6,4},{7,5},{8,14},{9,15},{10,... | collective-permute-start | bytes 2359304 | tf_op jit(solution)/shard_map/ppermute | solution.py:358
  152.8 10.8 %collective-permute-start.8 = (bf16[5,256,256]{2,1,0:T(8,128)(2,1)}, bf16[5,256,256]{2,1,0:T(8,128)(2,1)}, u32[]{:S(2)}, u32[]{:S(2)}) collective-permute-start(bf16[5,256,256]{2,1,0:T(8,128)(2,1)} %get-tuple-element.97), channel_id=1, source_target_pairs={{0,96},{1,97},{2,98},{3,99},{4,100},{5,101},{6,102},{7,103},{8,104... | collective-permute-start | bytes 1966088 | tf_op jit(solution)/shard_map/ppermute | solution.py:358
  163.6 2.7 %collective-permute-start.9 = (bf16[5,256,256]{2,1,0:T(8,128)(2,1)}, bf16[5,256,256]{2,1,0:T(8,128)(2,1)}, u32[]{:S(2)}, u32[]{:S(2)}) collective-permute-start(bf16[5,256,256]{2,1,0:T(8,128)(2,1)} %get-tuple-element.98), channel_id=1, source_target_pairs={{0,64},{1,65},{2,66},{3,67},{4,68},{5,69},{6,70},{7,71},{8,72},{9,... | collective-permute-start | bytes 1966088 | tf_op jit(solution)/shard_map/ppermute | solution.py:358
  167.1 3.1 %collective-permute-start.35 = (bf16[6,256,256]{2,1,0:T(8,128)(2,1)}, bf16[6,256,256]{2,1,0:T(8,128)(2,1)S(1)}, u32[]{:S(2)}, u32[]{:S(2)}) collective-permute-start(bf16[6,256,256]{2,1,0:T(8,128)(2,1)} %get-tuple-element.131), channel_id=1, source_target_pairs={{0,4},{1,5},{2,6},{3,7},{4,0},{5,1},{6,2},{7,3},{8,12},{9,13},{10,... | collective-permute-start | bytes 2359304 | tf_op jit(solution)/shard_map/ppermute | solution.py:358
  170.2 4.1 %add_quarters.4 = (bf16[5,64,256]{2,1,0:T(8,128)(2,1)}, bf16[5,64,256]{2,1,0:T(8,128)(2,1)}, bf16[5,64,256]{2,1,0:T(8,128)(2,1)}, bf16[5,64,256]{2,1,0:T(8,128)(2,1)}) custom-call(s32[1]{0:T(128)} %bitcast.5.refs_6_.at_ref, bf16[5,256,256]{2,1,0:T(8,128)(2,1)} %get-tuple-element.112.refs_0_, bf16[5,256,256]{2,1,0:T(8,128)(2,1)} %copy-done.5, ...), custom_call_target="tpu_custom_call" | custom-call | tf_op jit(solution)/shard_map/add_quarters/pallas_call | solution.py:175
  174.4 16.8 %collective-permute-done.8.refs_2_ = bf16[5,256,256]{2,1,0:T(8,128)(2,1)} collective-permute-done((bf16[5,256,256]{2,1,0:T(8,128)(2,1)}, bf16[5,256,256]{2,1,0:T(8,128)(2,1)}, u32[]{:S(2)}, u32[]{:S(2)}) %collective-permute-start.8) | collective-permute-done | bytes 655392 | tf_op jit(solution)/shard_map/ppermute | solution.py:358
  191.2 2.7 %collective-permute-start.24 = (bf16[5,64,256]{2,1,0:T(8,128)(2,1)}, bf16[5,64,256]{2,1,0:T(8,128)(2,1)S(1)}, u32[]{:S(2)}, u32[]{:S(2)}) collective-permute-start(bf16[5,64,256]{2,1,0:T(8,128)(2,1)} %get-tuple-element.118), channel_id=1, source_target_pairs={{0,6},{1,7},{2,0},{3,1},{4,2},{5,3},{6,4},{7,5},{8,14},{9,15},{10,... | collective-permute-start | bytes 491528 | tf_op jit(solution)/shard_map/ppermute | solution.py:358
  193.9 4.1 %add_quarters.3 = (bf16[5,64,256]{2,1,0:T(8,128)(2,1)}, bf16[5,64,256]{2,1,0:T(8,128)(2,1)}, bf16[5,64,256]{2,1,0:T(8,128)(2,1)}, bf16[5,64,256]{2,1,0:T(8,128)(2,1)}) custom-call(s32[1]{0:T(128)} %bitcast.at_ref.refs_7_, bf16[5,256,256]{2,1,0:T(8,128)(2,1)} %get-tuple-element.95.refs_0_, bf16[5,256,256]{2,1,0:T(8,128)(2,1)} %copy-done.7, ...), custom_call_target="tpu_custom_call" | custom-call | tf_op jit(solution)/shard_map/add_quarters/pallas_call | solution.py:175
  198.1 9.4 %collective-permute-start.10 = (bf16[5,64,256]{2,1,0:T(8,128)(2,1)}, bf16[5,64,256]{2,1,0:T(8,128)(2,1)S(1)}, u32[]{:S(2)}, u32[]{:S(2)}) collective-permute-start(bf16[5,64,256]{2,1,0:T(8,128)(2,1)} %get-tuple-element.100), channel_id=1, source_target_pairs={{0,8},{1,9},{2,10},{3,11},{4,12},{5,13},{6,14},{7,15},{8,16},{9,17... | collective-permute-start | bytes 491528 | tf_op jit(solution)/shard_map/ppermute | solution.py:358
  208.4 4.7 %add_quarters.5 = (bf16[6,64,256]{2,1,0:T(8,128)(2,1)}, bf16[6,64,256]{2,1,0:T(8,128)(2,1)}, bf16[6,64,256]{2,1,0:T(8,128)(2,1)}, bf16[6,64,256]{2,1,0:T(8,128)(2,1)}) custom-call(s32[1]{0:T(128)} %bitcast.1.at_ref.refs_6_, bf16[6,256,256]{2,1,0:T(8,128)(2,1)} %get-tuple-element.128.refs_0_, bf16[6,256,256]{2,1,0:T(8,128)(2,1)} %copy-done.2, ...), custom_call_target="tpu_custom_call" | custom-call | tf_op jit(solution)/shard_map/add_quarters/pallas_call | solution.py:175
  213.3 3.5 %collective-permute-start.37 = (bf16[6,64,256]{2,1,0:T(8,128)(2,1)}, bf16[6,64,256]{2,1,0:T(8,128)(2,1)S(1)}, u32[]{:S(2)}, u32[]{:S(2)}) collective-permute-start(bf16[6,64,256]{2,1,0:T(8,128)(2,1)} %get-tuple-element.134), channel_id=1, source_target_pairs={{0,96},{1,97},{2,98},{3,99},{4,100},{5,101},{6,102},{7,103},{8,104... | collective-permute-start | bytes 589832 | tf_op jit(solution)/shard_map/ppermute | solution.py:358
  216.9 1.2 collective-permute-start.38
  218.9 1.2 collective-permute-start.12
  220.1 10.6 %spread_squares.1 = (f32[640,32,256]{2,1,0:T(8,128)}, s32[1,1024]{1,0:T(1,128)}) custom-call(s32[1]{0:T(128)} %bitcast.6.me_ref, s32[128,128]{1,0:T(8,128)} %rows_ref.1, bf16[128,128]{1,0:T(8,128)(2,1)} %coef_ref.1, s32[1,1024]{1,0:T(1,128)} %bitcast.18), custom_call_target="tpu_custom_call" | custom-call | tf_op jit(solution)/shard_map/spread_squares/pallas_call | solution.py:247
  231.7 2.7 %square_sums.1 = f32[128,1,384]{2,1,0:T(1,128)} custom-call(bf16[5,64,256]{2,1,0:T(8,128)(2,1)} %get-tuple-element.138.refs_0_, bf16[5,64,256]{2,1,0:T(8,128)(2,1)} %copy-done.33, bf16[5,64,256]{2,1,0:T(8,128)(2,1)} %copy-done.34, bf16[5,64,256]{2,1,0:T(8,128)(2,1)} %copy-done.35, bf16[5,64,256]{2,1,0:T(8,128)(2,1)} %get-tuple-element.142.refs_4_, ...), custom_call_target="tpu_custom_call" | custom-call | tf_op jit(solution)/shard_map/square_sums/pallas_call | solution.py:204
  234.4 10.8 %all-to-all-start = ((f32[128,1,384]{2,1,0:T(1,128)}), f32[128,1,384]{2,1,0:T(1,128)S(1)}, u32[]{:S(2)}, u32[]{:S(2)}) async-start(f32[128,1,384]{2,1,0:T(1,128)} %square_sums.1), calls=%async_computation | async-start | bytes 393216 | tf_op jit(solution)/shard_map/all_to_all | solution.py:341
  245.3 10.2 %all-to-all-done.parts_ref = f32[128,1,384]{2,1,0:T(1,128)S(1)} async-done(((f32[128,1,384]{2,1,0:T(1,128)}), f32[128,1,384]{2,1,0:T(1,128)S(1)}, u32[]{:S(2)}, u32[]{:S(2)}) %all-to-all-start) | async-done | bytes 196640 | tf_op jit(solution)/shard_map/all_to_all | solution.py:341
  256.2 3.3 %finish.1 = (f32[1,8]{1,0:T(1,128)}, f32[8,128]{1,0:T(8,128)}, f32[32,256]{1,0:T(8,128)}) custom-call(s32[1]{0:T(128)S(6)} %copy.11.refs_4_.count_ref, f32[128,1,384]{2,1,0:T(1,128)S(1)} %all-to-all-done.parts_ref, f32[8,128]{1,0:T(8,128)S(1)} %bitcast.12, s32[128,1]{1,0:T(8,128)S(1)} %copy.10.sensor_ref, s32[1,1024]{1,0:T(1,128)S(1)} %copy-done.1, ...), custom_call_target="tpu_custom_call" | custom-call | tf_op jit(solution)/shard_map/finish/pallas_call | solution.py:321
  (118 shorter events, 10.6 us)
Async XLA Ops:
  0.6 244.6 %copy-start.36 = (s32[128]{0:T(128)S(1)}, s32[128]{0:T(128)}, u32[]{:S(2)}) copy-start(s32[128]{0:T(128)} %param.9) | copy-start | bytes 1540
  0.6 254.9 %copy-start = (f32[1024]{0:T(1024)S(1)}, f32[1024]{0:T(1024)}, u32[]{:S(2)}) copy-start(f32[1024]{0:T(1024)} %param.13) | copy-start | bytes 12292
  20.6 6.3 %collective-permute-start.13 = (bf16[5,264,128]{2,1,0:T(8,128)(2,1)}, bf16[5,264,128]{2,1,0:T(8,128)(2,1)S(1)}, u32[]{:S(2)}, u32[]{:S(2)}) collective-permute-start(bf16[5,264,128]{2,1,0:T(8,128)(2,1)} %get-tuple-element.105), channel_id=1, source_target_pairs={{0,1},{1,0},{2,3},{3,2},{4,5},{5,4},{6,7},{7,6},{8,9},{9,8},{10,11... | collective-permute-start | bytes 1013768 | tf_op jit(solution)/shard_map/ppermute | solution.py:358
  22.0 11.2 %collective-permute-start.14 = (bf16[5,264,128]{2,1,0:T(8,128)(2,1)}, bf16[5,264,128]{2,1,0:T(8,128)(2,1)S(1)}, u32[]{:S(2)}, u32[]{:S(2)}) collective-permute-start(bf16[5,264,128]{2,1,0:T(8,128)(2,1)} %get-tuple-element.106), channel_id=1, source_target_pairs={{0,32},{1,33},{2,34},{3,35},{4,36},{5,37},{6,38},{7,39},{8,40},{9,... | collective-permute-start | bytes 1013768 | tf_op jit(solution)/shard_map/ppermute | solution.py:358
  23.4 17.1 %collective-permute-start.15 = (bf16[5,264,128]{2,1,0:T(8,128)(2,1)}, bf16[5,264,128]{2,1,0:T(8,128)(2,1)S(1)}, u32[]{:S(2)}, u32[]{:S(2)}) collective-permute-start(bf16[5,264,128]{2,1,0:T(8,128)(2,1)} %get-tuple-element.107), channel_id=1, source_target_pairs={{0,33},{1,32},{2,35},{3,34},{4,37},{5,36},{6,39},{7,38},{8,41},{9,... | collective-permute-start | bytes 1013768 | tf_op jit(solution)/shard_map/ppermute | solution.py:358
  25.0 15.9 %collective-permute-start.16 = (bf16[5,264,128]{2,1,0:T(8,128)(2,1)}, bf16[5,264,128]{2,1,0:T(8,128)(2,1)S(1)}, u32[]{:S(2)}, u32[]{:S(2)}) collective-permute-start(bf16[5,264,128]{2,1,0:T(8,128)(2,1)} %get-tuple-element.108), channel_id=1, source_target_pairs={{0,96},{1,97},{2,98},{3,99},{4,100},{5,101},{6,102},{7,103},{8,104... | collective-permute-start | bytes 1013768 | tf_op jit(solution)/shard_map/ppermute | solution.py:358
  26.4 16.6 %collective-permute-start.17 = (bf16[5,264,128]{2,1,0:T(8,128)(2,1)}, bf16[5,264,128]{2,1,0:T(8,128)(2,1)S(1)}, u32[]{:S(2)}, u32[]{:S(2)}) collective-permute-start(bf16[5,264,128]{2,1,0:T(8,128)(2,1)} %get-tuple-element.109), channel_id=1, source_target_pairs={{0,97},{1,96},{2,99},{3,98},{4,101},{5,100},{6,103},{7,102},{8,105... | collective-permute-start | bytes 1013768 | tf_op jit(solution)/shard_map/ppermute | solution.py:358
  26.9 61.0 %copy-start.13 = (bf16[5,264,128]{2,1,0:T(8,128)(2,1)}, bf16[5,264,128]{2,1,0:T(8,128)(2,1)S(1)}, u32[]{:S(2)}) copy-start(bf16[5,264,128]{2,1,0:T(8,128)(2,1)S(1)} %collective-permute-done.13.refs_1_) | copy-start | bytes 1013764
  26.9 21.8 %collective-permute-start.18 = (bf16[5,264,128]{2,1,0:T(8,128)(2,1)}, bf16[5,264,128]{2,1,0:T(8,128)(2,1)S(1)}, u32[]{:S(2)}, u32[]{:S(2)}) collective-permute-start(bf16[5,264,128]{2,1,0:T(8,128)(2,1)} %get-tuple-element.110), channel_id=1, source_target_pairs={{0,64},{1,65},{2,66},{3,67},{4,68},{5,69},{6,70},{7,71},{8,72},{9,... | collective-permute-start | bytes 1013768 | tf_op jit(solution)/shard_map/ppermute | solution.py:358
  33.2 54.7 %copy-start.14 = (bf16[5,264,128]{2,1,0:T(8,128)(2,1)}, bf16[5,264,128]{2,1,0:T(8,128)(2,1)S(1)}, u32[]{:S(2)}) copy-start(bf16[5,264,128]{2,1,0:T(8,128)(2,1)S(1)} %collective-permute-done.14.refs_2_) | copy-start | bytes 1013764
  33.2 23.0 %collective-permute-start.19 = (bf16[5,264,128]{2,1,0:T(8,128)(2,1)}, bf16[5,264,128]{2,1,0:T(8,128)(2,1)S(1)}, u32[]{:S(2)}, u32[]{:S(2)}) collective-permute-start(bf16[5,264,128]{2,1,0:T(8,128)(2,1)} %get-tuple-element.111), channel_id=1, source_target_pairs={{0,65},{1,64},{2,67},{3,66},{4,69},{5,68},{6,71},{7,70},{8,73},{9,... | collective-permute-start | bytes 1013768 | tf_op jit(solution)/shard_map/ppermute | solution.py:358
  40.5 47.4 %copy-start.16 = (bf16[5,264,128]{2,1,0:T(8,128)(2,1)}, bf16[5,264,128]{2,1,0:T(8,128)(2,1)S(1)}, u32[]{:S(2)}) copy-start(bf16[5,264,128]{2,1,0:T(8,128)(2,1)S(1)} %collective-permute-done.15.refs_3_) | copy-start | bytes 1013764
  40.5 19.5 %collective-permute-start = (bf16[5,264,128]{2,1,0:T(8,128)(2,1)}, bf16[5,264,128]{2,1,0:T(8,128)(2,1)S(1)}, u32[]{:S(2)}, u32[]{:S(2)}) collective-permute-start(bf16[5,264,128]{2,1,0:T(8,128)(2,1)} %get-tuple-element.88), channel_id=1, source_target_pairs={{0,1},{1,0},{2,3},{3,2},{4,5},{5,4},{6,7},{7,6},{8,9},{9,8},{10,11... | collective-permute-start | bytes 1013768 | tf_op jit(solution)/shard_map/ppermute | solution.py:358
  40.8 47.1 %copy-start.17 = (bf16[5,264,128]{2,1,0:T(8,128)(2,1)}, bf16[5,264,128]{2,1,0:T(8,128)(2,1)S(1)}, u32[]{:S(2)}) copy-start(bf16[5,264,128]{2,1,0:T(8,128)(2,1)S(1)} %collective-permute-done.16.refs_4_) | copy-start | bytes 1013764
  40.8 19.1 %collective-permute-start.1 = (bf16[5,264,128]{2,1,0:T(8,128)(2,1)}, bf16[5,264,128]{2,1,0:T(8,128)(2,1)S(1)}, u32[]{:S(2)}, u32[]{:S(2)}) collective-permute-start(bf16[5,264,128]{2,1,0:T(8,128)(2,1)} %get-tuple-element.89), channel_id=1, source_target_pairs={{0,2},{1,3},{2,4},{3,5},{4,6},{5,7},{6,0},{7,1},{8,10},{9,11},{10,... | collective-permute-start | bytes 1013768 | tf_op jit(solution)/shard_map/ppermute | solution.py:358
  43.0 20.5 %collective-permute-start.2 = (bf16[5,264,128]{2,1,0:T(8,128)(2,1)}, bf16[5,264,128]{2,1,0:T(8,128)(2,1)S(1)}, u32[]{:S(2)}, u32[]{:S(2)}) collective-permute-start(bf16[5,264,128]{2,1,0:T(8,128)(2,1)} %get-tuple-element.90), channel_id=1, source_target_pairs={{0,3},{1,2},{2,5},{3,4},{4,7},{5,6},{6,1},{7,0},{8,11},{9,10},{10,... | collective-permute-start | bytes 1013768 | tf_op jit(solution)/shard_map/ppermute | solution.py:358
  48.7 14.8 %collective-permute-start.3 = (bf16[5,264,128]{2,1,0:T(8,128)(2,1)}, bf16[5,264,128]{2,1,0:T(8,128)(2,1)S(1)}, u32[]{:S(2)}, u32[]{:S(2)}) collective-permute-start(bf16[5,264,128]{2,1,0:T(8,128)(2,1)} %get-tuple-element.91), channel_id=1, source_target_pairs={{0,6},{1,7},{2,0},{3,1},{4,2},{5,3},{6,4},{7,5},{8,14},{9,15},{10,... | collective-permute-start | bytes 1013768 | tf_op jit(solution)/shard_map/ppermute | solution.py:358
  56.2 25.8 %collective-permute-start.4 = (bf16[5,264,128]{2,1,0:T(8,128)(2,1)}, bf16[5,264,128]{2,1,0:T(8,128)(2,1)S(1)}, u32[]{:S(2)}, u32[]{:S(2)}) collective-permute-start(bf16[5,264,128]{2,1,0:T(8,128)(2,1)} %get-tuple-element.92), channel_id=1, source_target_pairs={{0,7},{1,6},{2,1},{3,0},{4,3},{5,2},{6,5},{7,4},{8,15},{9,14},{10,... | collective-permute-start | bytes 1013768 | tf_op jit(solution)/shard_map/ppermute | solution.py:358
  60.0 24.8 %collective-permute-start.5 = (bf16[5,264,128]{2,1,0:T(8,128)(2,1)}, bf16[5,264,128]{2,1,0:T(8,128)(2,1)S(1)}, u32[]{:S(2)}, u32[]{:S(2)}) collective-permute-start(bf16[5,264,128]{2,1,0:T(8,128)(2,1)} %get-tuple-element.93), channel_id=1, source_target_pairs={{0,4},{1,5},{2,6},{3,7},{4,0},{5,1},{6,2},{7,3},{8,12},{9,13},{10,... | collective-permute-start | bytes 1013768 | tf_op jit(solution)/shard_map/ppermute | solution.py:358
  60.0 26.2 %collective-permute-start.6 = (bf16[5,264,128]{2,1,0:T(8,128)(2,1)}, bf16[5,264,128]{2,1,0:T(8,128)(2,1)S(1)}, u32[]{:S(2)}, u32[]{:S(2)}) collective-permute-start(bf16[5,264,128]{2,1,0:T(8,128)(2,1)} %get-tuple-element.94), channel_id=1, source_target_pairs={{0,5},{1,4},{2,7},{3,6},{4,1},{5,0},{6,3},{7,2},{8,13},{9,12},{10,... | collective-permute-start | bytes 1013768 | tf_op jit(solution)/shard_map/ppermute | solution.py:358
  63.5 23.7 %collective-permute-start.26 = (bf16[6,264,128]{2,1,0:T(8,128)(2,1)}, bf16[6,264,128]{2,1,0:T(8,128)(2,1)S(1)}, u32[]{:S(2)}, u32[]{:S(2)}) collective-permute-start(bf16[6,264,128]{2,1,0:T(8,128)(2,1)} %get-tuple-element.121), channel_id=1, source_target_pairs={{0,1},{1,0},{2,3},{3,2},{4,5},{5,4},{6,7},{7,6},{8,9},{9,8},{10,11... | collective-permute-start | bytes 1216520 | tf_op jit(solution)/shard_map/ppermute | solution.py:358
  64.3 30.1 %collective-permute-start.27 = (bf16[6,264,128]{2,1,0:T(8,128)(2,1)}, bf16[6,264,128]{2,1,0:T(8,128)(2,1)S(1)}, u32[]{:S(2)}, u32[]{:S(2)}) collective-permute-start(bf16[6,264,128]{2,1,0:T(8,128)(2,1)} %get-tuple-element.122), channel_id=1, source_target_pairs={{0,8},{1,9},{2,10},{3,11},{4,12},{5,13},{6,14},{7,15},{8,16},{9,17... | collective-permute-start | bytes 1216520 | tf_op jit(solution)/shard_map/ppermute | solution.py:358
  82.7 13.5 %collective-permute-start.28 = (bf16[6,264,128]{2,1,0:T(8,128)(2,1)}, bf16[6,264,128]{2,1,0:T(8,128)(2,1)S(1)}, u32[]{:S(2)}, u32[]{:S(2)}) collective-permute-start(bf16[6,264,128]{2,1,0:T(8,128)(2,1)} %get-tuple-element.123), channel_id=1, source_target_pairs={{0,9},{1,8},{2,11},{3,10},{4,13},{5,12},{6,15},{7,14},{8,17},{9,16... | collective-permute-start | bytes 1216520 | tf_op jit(solution)/shard_map/ppermute | solution.py:358
  84.7 12.4 %collective-permute-start.29 = (bf16[6,264,128]{2,1,0:T(8,128)(2,1)}, bf16[6,264,128]{2,1,0:T(8,128)(2,1)S(1)}, u32[]{:S(2)}, u32[]{:S(2)}) collective-permute-start(bf16[6,264,128]{2,1,0:T(8,128)(2,1)} %get-tuple-element.124), channel_id=1, source_target_pairs={{0,24},{1,25},{2,26},{3,27},{4,28},{5,29},{6,30},{7,31},{8,0},{9,1... | collective-permute-start | bytes 1216520 | tf_op jit(solution)/shard_map/ppermute | solution.py:358
  86.2 19.1 %collective-permute-start.30 = (bf16[6,264,128]{2,1,0:T(8,128)(2,1)}, bf16[6,264,128]{2,1,0:T(8,128)(2,1)S(1)}, u32[]{:S(2)}, u32[]{:S(2)}) collective-permute-start(bf16[6,264,128]{2,1,0:T(8,128)(2,1)} %get-tuple-element.125), channel_id=1, source_target_pairs={{0,25},{1,24},{2,27},{3,26},{4,29},{5,28},{6,31},{7,30},{8,1},{9,0... | collective-permute-start | bytes 1216520 | tf_op jit(solution)/shard_map/ppermute | solution.py:358
  87.2 55.2 %copy-start.8 = (bf16[6,264,128]{2,1,0:T(8,128)(2,1)}, bf16[6,264,128]{2,1,0:T(8,128)(2,1)S(1)}, u32[]{:S(2)}) copy-start(bf16[6,264,128]{2,1,0:T(8,128)(2,1)S(1)} %collective-permute-done.26.refs_1_) | copy-start | bytes 1216516
  87.2 27.7 %collective-permute-start.31 = (bf16[6,264,128]{2,1,0:T(8,128)(2,1)}, bf16[6,264,128]{2,1,0:T(8,128)(2,1)}, u32[]{:S(2)}, u32[]{:S(2)}) collective-permute-start(bf16[6,264,128]{2,1,0:T(8,128)(2,1)} %get-tuple-element.126), channel_id=1, source_target_pairs={{0,16},{1,17},{2,18},{3,19},{4,20},{5,21},{6,22},{7,23},{8,24},{9,... | collective-permute-start | bytes 1216520 | tf_op jit(solution)/shard_map/ppermute | solution.py:358
  94.4 48.1 %copy-start.9 = (bf16[6,264,128]{2,1,0:T(8,128)(2,1)}, bf16[6,264,128]{2,1,0:T(8,128)(2,1)S(1)}, u32[]{:S(2)}) copy-start(bf16[6,264,128]{2,1,0:T(8,128)(2,1)S(1)} %collective-permute-done.27.refs_2_) | copy-start | bytes 1216516
  94.4 55.3 %collective-permute-start.20 = (bf16[5,256,256]{2,1,0:T(8,128)(2,1)}, bf16[5,256,256]{2,1,0:T(8,128)(2,1)S(1)}, u32[]{:S(2)}, u32[]{:S(2)}) collective-permute-start(bf16[5,256,256]{2,1,0:T(8,128)(2,1)} %get-tuple-element.113), channel_id=1, source_target_pairs={{0,8},{1,9},{2,10},{3,11},{4,12},{5,13},{6,14},{7,15},{8,16},{9,17... | collective-permute-start | bytes 1966088 | tf_op jit(solution)/shard_map/ppermute | solution.py:358
  96.2 56.6 %collective-permute-start.21 = (bf16[5,256,256]{2,1,0:T(8,128)(2,1)}, bf16[5,256,256]{2,1,0:T(8,128)(2,1)S(1)}, u32[]{:S(2)}, u32[]{:S(2)}) collective-permute-start(bf16[5,256,256]{2,1,0:T(8,128)(2,1)} %get-tuple-element.114), channel_id=1, source_target_pairs={{0,24},{1,25},{2,26},{3,27},{4,28},{5,29},{6,30},{7,31},{8,0},{9,1... | collective-permute-start | bytes 1966088 | tf_op jit(solution)/shard_map/ppermute | solution.py:358
  97.2 66.4 %collective-permute-start.22 = (bf16[5,256,256]{2,1,0:T(8,128)(2,1)}, bf16[5,256,256]{2,1,0:T(8,128)(2,1)}, u32[]{:S(2)}, u32[]{:S(2)}) collective-permute-start(bf16[5,256,256]{2,1,0:T(8,128)(2,1)} %get-tuple-element.115), channel_id=1, source_target_pairs={{0,16},{1,17},{2,18},{3,19},{4,20},{5,21},{6,22},{7,23},{8,24},{9,... | collective-permute-start | bytes 1966088 | tf_op jit(solution)/shard_map/ppermute | solution.py:358
  106.1 60.2 %collective-permute-start.7 = (bf16[5,256,256]{2,1,0:T(8,128)(2,1)}, bf16[5,256,256]{2,1,0:T(8,128)(2,1)S(1)}, u32[]{:S(2)}, u32[]{:S(2)}) collective-permute-start(bf16[5,256,256]{2,1,0:T(8,128)(2,1)} %get-tuple-element.96), channel_id=1, source_target_pairs={{0,32},{1,33},{2,34},{3,35},{4,36},{5,37},{6,38},{7,39},{8,40},{9,... | collective-permute-start | bytes 1966088 | tf_op jit(solution)/shard_map/ppermute | solution.py:358
  114.9 27.6 %collective-permute-start.32 = (bf16[6,264,128]{2,1,0:T(8,128)(2,1)}, bf16[6,264,128]{2,1,0:T(8,128)(2,1)}, u32[]{:S(2)}, u32[]{:S(2)}) collective-permute-start(bf16[6,264,128]{2,1,0:T(8,128)(2,1)} %get-tuple-element.127), channel_id=1, source_target_pairs={{0,17},{1,16},{2,19},{3,18},{4,21},{5,20},{6,23},{7,22},{8,25},{9,... | collective-permute-start | bytes 1216520 | tf_op jit(solution)/shard_map/ppermute | solution.py:358
  149.7 48.4 %collective-permute-start.33 = (bf16[6,256,256]{2,1,0:T(8,128)(2,1)}, bf16[6,256,256]{2,1,0:T(8,128)(2,1)S(1)}, u32[]{:S(2)}, u32[]{:S(2)}) collective-permute-start(bf16[6,256,256]{2,1,0:T(8,128)(2,1)} %get-tuple-element.129), channel_id=1, source_target_pairs={{0,2},{1,3},{2,4},{3,5},{4,6},{5,7},{6,0},{7,1},{8,10},{9,11},{10,... | collective-permute-start | bytes 2359304 | tf_op jit(solution)/shard_map/ppermute | solution.py:358
  149.8 48.4 %collective-permute-start.34 = (bf16[6,256,256]{2,1,0:T(8,128)(2,1)}, bf16[6,256,256]{2,1,0:T(8,128)(2,1)S(1)}, u32[]{:S(2)}, u32[]{:S(2)}) collective-permute-start(bf16[6,256,256]{2,1,0:T(8,128)(2,1)} %get-tuple-element.130), channel_id=1, source_target_pairs={{0,6},{1,7},{2,0},{3,1},{4,2},{5,3},{6,4},{7,5},{8,14},{9,15},{10,... | collective-permute-start | bytes 2359304 | tf_op jit(solution)/shard_map/ppermute | solution.py:358
  152.8 38.4 %collective-permute-start.8 = (bf16[5,256,256]{2,1,0:T(8,128)(2,1)}, bf16[5,256,256]{2,1,0:T(8,128)(2,1)}, u32[]{:S(2)}, u32[]{:S(2)}) collective-permute-start(bf16[5,256,256]{2,1,0:T(8,128)(2,1)} %get-tuple-element.97), channel_id=1, source_target_pairs={{0,96},{1,97},{2,98},{3,99},{4,100},{5,101},{6,102},{7,103},{8,104... | collective-permute-start | bytes 1966088 | tf_op jit(solution)/shard_map/ppermute | solution.py:358
  163.6 27.6 %collective-permute-start.9 = (bf16[5,256,256]{2,1,0:T(8,128)(2,1)}, bf16[5,256,256]{2,1,0:T(8,128)(2,1)}, u32[]{:S(2)}, u32[]{:S(2)}) collective-permute-start(bf16[5,256,256]{2,1,0:T(8,128)(2,1)} %get-tuple-element.98), channel_id=1, source_target_pairs={{0,64},{1,65},{2,66},{3,67},{4,68},{5,69},{6,70},{7,71},{8,72},{9,... | collective-permute-start | bytes 1966088 | tf_op jit(solution)/shard_map/ppermute | solution.py:358
  167.1 40.4 %collective-permute-start.35 = (bf16[6,256,256]{2,1,0:T(8,128)(2,1)}, bf16[6,256,256]{2,1,0:T(8,128)(2,1)S(1)}, u32[]{:S(2)}, u32[]{:S(2)}) collective-permute-start(bf16[6,256,256]{2,1,0:T(8,128)(2,1)} %get-tuple-element.131), channel_id=1, source_target_pairs={{0,4},{1,5},{2,6},{3,7},{4,0},{5,1},{6,2},{7,3},{8,12},{9,13},{10,... | collective-permute-start | bytes 2359304 | tf_op jit(solution)/shard_map/ppermute | solution.py:358
  191.2 22.1 %collective-permute-start.23 = (bf16[5,64,256]{2,1,0:T(8,128)(2,1)}, bf16[5,64,256]{2,1,0:T(8,128)(2,1)S(1)}, u32[]{:S(2)}, u32[]{:S(2)}) collective-permute-start(bf16[5,64,256]{2,1,0:T(8,128)(2,1)} %get-tuple-element.117), channel_id=1, source_target_pairs={{0,2},{1,3},{2,4},{3,5},{4,6},{5,7},{6,0},{7,1},{8,10},{9,11},{10,... | collective-permute-start | bytes 491528 | tf_op jit(solution)/shard_map/ppermute | solution.py:358
  191.2 25.6 %collective-permute-start.24 = (bf16[5,64,256]{2,1,0:T(8,128)(2,1)}, bf16[5,64,256]{2,1,0:T(8,128)(2,1)S(1)}, u32[]{:S(2)}, u32[]{:S(2)}) collective-permute-start(bf16[5,64,256]{2,1,0:T(8,128)(2,1)} %get-tuple-element.118), channel_id=1, source_target_pairs={{0,6},{1,7},{2,0},{3,1},{4,2},{5,3},{6,4},{7,5},{8,14},{9,15},{10,... | collective-permute-start | bytes 491528 | tf_op jit(solution)/shard_map/ppermute | solution.py:358
  198.0 20.0 %collective-permute-start.25 = (bf16[5,64,256]{2,1,0:T(8,128)(2,1)}, bf16[5,64,256]{2,1,0:T(8,128)(2,1)S(1)}, u32[]{:S(2)}, u32[]{:S(2)}) collective-permute-start(bf16[5,64,256]{2,1,0:T(8,128)(2,1)} %get-tuple-element.119), channel_id=1, source_target_pairs={{0,4},{1,5},{2,6},{3,7},{4,0},{5,1},{6,2},{7,3},{8,12},{9,13},{10,... | collective-permute-start | bytes 491528 | tf_op jit(solution)/shard_map/ppermute | solution.py:358
  198.1 20.8 %collective-permute-start.10 = (bf16[5,64,256]{2,1,0:T(8,128)(2,1)}, bf16[5,64,256]{2,1,0:T(8,128)(2,1)S(1)}, u32[]{:S(2)}, u32[]{:S(2)}) collective-permute-start(bf16[5,64,256]{2,1,0:T(8,128)(2,1)} %get-tuple-element.100), channel_id=1, source_target_pairs={{0,8},{1,9},{2,10},{3,11},{4,12},{5,13},{6,14},{7,15},{8,16},{9,17... | collective-permute-start | bytes 491528 | tf_op jit(solution)/shard_map/ppermute | solution.py:358
  213.1 17.6 %collective-permute-start.36 = (bf16[6,64,256]{2,1,0:T(8,128)(2,1)}, bf16[6,64,256]{2,1,0:T(8,128)(2,1)S(1)}, u32[]{:S(2)}, u32[]{:S(2)}) collective-permute-start(bf16[6,64,256]{2,1,0:T(8,128)(2,1)} %get-tuple-element.133), channel_id=1, source_target_pairs={{0,32},{1,33},{2,34},{3,35},{4,36},{5,37},{6,38},{7,39},{8,40},{9,... | collective-permute-start | bytes 589832 | tf_op jit(solution)/shard_map/ppermute | solution.py:358
  213.3 17.4 %collective-permute-start.37 = (bf16[6,64,256]{2,1,0:T(8,128)(2,1)}, bf16[6,64,256]{2,1,0:T(8,128)(2,1)S(1)}, u32[]{:S(2)}, u32[]{:S(2)}) collective-permute-start(bf16[6,64,256]{2,1,0:T(8,128)(2,1)} %get-tuple-element.134), channel_id=1, source_target_pairs={{0,96},{1,97},{2,98},{3,99},{4,100},{5,101},{6,102},{7,103},{8,104... | collective-permute-start | bytes 589832 | tf_op jit(solution)/shard_map/ppermute | solution.py:358
  216.9 13.9 %collective-permute-start.38 = (bf16[6,64,256]{2,1,0:T(8,128)(2,1)}, bf16[6,64,256]{2,1,0:T(8,128)(2,1)S(1)}, u32[]{:S(2)}, u32[]{:S(2)}) collective-permute-start(bf16[6,64,256]{2,1,0:T(8,128)(2,1)} %get-tuple-element.135), channel_id=1, source_target_pairs={{0,64},{1,65},{2,66},{3,67},{4,68},{5,69},{6,70},{7,71},{8,72},{9,... | collective-permute-start | bytes 589832 | tf_op jit(solution)/shard_map/ppermute | solution.py:358
  218.0 12.7 %collective-permute-start.11 = (bf16[5,64,256]{2,1,0:T(8,128)(2,1)}, bf16[5,64,256]{2,1,0:T(8,128)(2,1)S(1)}, u32[]{:S(2)}, u32[]{:S(2)}) collective-permute-start(bf16[5,64,256]{2,1,0:T(8,128)(2,1)} %get-tuple-element.101), channel_id=1, source_target_pairs={{0,24},{1,25},{2,26},{3,27},{4,28},{5,29},{6,30},{7,31},{8,0},{9,1... | collective-permute-start | bytes 491528 | tf_op jit(solution)/shard_map/ppermute | solution.py:358
  218.9 11.8 %collective-permute-start.12 = (bf16[5,64,256]{2,1,0:T(8,128)(2,1)}, bf16[5,64,256]{2,1,0:T(8,128)(2,1)S(1)}, u32[]{:S(2)}, u32[]{:S(2)}) collective-permute-start(bf16[5,64,256]{2,1,0:T(8,128)(2,1)} %get-tuple-element.102), channel_id=1, source_target_pairs={{0,16},{1,17},{2,18},{3,19},{4,20},{5,21},{6,22},{7,23},{8,24},{9,... | collective-permute-start | bytes 491528 | tf_op jit(solution)/shard_map/ppermute | solution.py:358
  234.4 21.1 %all-to-all-start = ((f32[128,1,384]{2,1,0:T(1,128)}), f32[128,1,384]{2,1,0:T(1,128)S(1)}, u32[]{:S(2)}, u32[]{:S(2)}) async-start(f32[128,1,384]{2,1,0:T(1,128)} %square_sums.1), calls=%async_computation | async-start | bytes 393216 | tf_op jit(solution)/shard_map/all_to_all | solution.py:341
  (29 other events, 388.3 us)

commit v7 on v6

--- a/solution.py
+++ b/solution.py
@@ -154,7 +154,7 @@
         in_specs=[pl.BlockSpec(memory_space=pltpu.SMEM)] + [pl.BlockSpec((1, rows, half), lambda i: (i, 0, 0))] * n,
         out_specs=[pl.BlockSpec((1,) + shape[1:], lambda i: (i, 0, 0))] * 4,
         out_shape=[jax.ShapeDtypeStruct(shape, BF16)] * 4,
-        compiler_params=pltpu.CompilerParams(dimension_semantics=("arbitrary",), vmem_limit_bytes=VMEM),
+        compiler_params=pltpu.CompilerParams(dimension_semantics=("arbitrary",), vmem_limit_bytes=24 * 1024 * 1024),
         name="mix_tiles",
     )(at, *tiles)
 
@@ -166,19 +166,24 @@
     def body(at_ref, *refs):
         for out, shift in zip(refs[4:], SHIFTS):
             rows = pl.ds(pl.multiple_of(((at_ref[0] + shift) & 3) * piece, piece), piece)
-            total = refs[0][0, rows, :].astype(F32)
-            for r in refs[1:4]:
-                total += r[0, rows, :].astype(F32)
-            out[0] = total.astype(BF16)
+
+            def channel(i, c):
+                total = refs[0][i, rows, :].astype(F32)
+                for r in refs[1:4]:
+                    total += r[i, rows, :].astype(F32)
+                out[i] = total.astype(BF16)
+                return c
+
+            lax.fori_loop(0, each, channel, 0)
 
     shape = (each, piece, width)
-    return pl.pallas_call(
-        body,
-        grid=(each,),
-        in_specs=[pl.BlockSpec(memory_space=pltpu.SMEM)] + [pl.BlockSpec((1, n_sens, width), lambda i: (i, 0, 0))] * 4,
-        out_specs=[pl.BlockSpec((1,) + shape[1:], lambda i: (i, 0, 0))] * 4,
+    vmem = pl.BlockSpec(memory_space=pltpu.VMEM)
+    return pl.pallas_call(
+        body,
+        in_specs=[pl.BlockSpec(memory_space=pltpu.SMEM)] + [vmem] * 4,
+        out_specs=[vmem] * 4,
         out_shape=[jax.ShapeDtypeStruct(shape, BF16)] * 4,
-        compiler_params=pltpu.CompilerParams(dimension_semantics=("arbitrary",), vmem_limit_bytes=VMEM),
+        compiler_params=pltpu.CompilerParams(vmem_limit_bytes=24 * 1024 * 1024),
         name="add_quarters",
     )(at, *quarters)
 
@@ -204,7 +209,7 @@
     return pl.pallas_call(
         body,
         out_shape=jax.ShapeDtypeStruct((n_dev, 1, 128 * n), F32),
-        compiler_params=pltpu.CompilerParams(vmem_limit_bytes=VMEM),
+        compiler_params=pltpu.CompilerParams(vmem_limit_bytes=24 * 1024 * 1024),
         name="square_sums",
     )(*[x for four in flows for x in four])
 
@@ -368,13 +373,13 @@
     n_sens = owner.shape[0]
     flat = probes.reshape(tile_r * tile_c, probe_n)
     tile = (blk_rows, coef, blk_sensor.reshape(1, nblk), blk_count, core)
+    firsts = [8 * sum(EACH[:f]) for f in range(3)]
+    packs = [(first, each, f) for f, (first, each) in enumerate(zip(firsts, EACH))]
+    sent = gather_flows(flat, *tile, packs, [at[a] for a, _, _ in ORDERS])
     maps, pos = spread_squares(blk_rows, coef, owner.reshape(1, n_sens), me, tile_r, tile_c)
-    firsts = [8 * sum(EACH[:f]) for f in range(3)]
-    sent = gather_flows(flat, *tile, [(firsts[0], EACH[0], 0)], [at["z"]])
-    *sent, flat = lax.optimization_barrier((*sent, flat))
-    more = gather_flows(flat, *tile, [(firsts[1], EACH[1], 0), (firsts[2], EACH[2], 1)], [at["y"], at["x"]])
-    sent = (sent, more[:8], more[8:])
-    tiles = [[shift_to(x, a, *peer) for x, peer in zip(sent[f], PEERS)] for f, (a, _, _) in enumerate(ORDERS)]
+    tiles = []
+    for f, (a, _, _) in enumerate(ORDERS):
+        tiles.append([shift_to(x, a, *peer) for x, peer in zip(sent[8 * f : 8 * f + 8], PEERS)])
     flows = []
     for f, (_, b, c) in enumerate(ORDERS):
         quarters = mix_tiles(tiles[f], at[b], n_sens)

time: 262 us -> 244 us (0.931)
  Pallas kernels: 68.9 us -> 43.1 us
  waiting for transfers between devices: 87.5 us -> 97.7 us
    pallas_call x3, Pallas kernels: 13 us -> 1.4 us  [add_quarters(): pl.pallas_call(body, in_specs=[pl.BlockSpec(memory_space=pltpu.SMEM)] + [...]
    ppermute x39, waiting for transfers between devices: 77.3 us -> 87.5 us  [shift_to(): return lax.ppermute(x, AXES, pairs)]
    pallas_call x3, Pallas kernels: 20.1 us -> 11.5 us  [mix_tiles(): pl.pallas_call(body, grid=(each,), in_specs=[pl.BlockSpec(memory_space=pl...]
    pallas_call x2 -> x1, Pallas kernels: 19.2 us -> 15.2 us  [gather_flows(): pl.pallas_call(body, in_specs=[hbm, hbm, vmem, vmem, smem, smem] + [smem]...]
    unnamed x74 -> x12, local copies, waits for them, and re-layouts: 5.59 us -> 3.65 us
  transfers between devices with their start and end apart: 40 -> 40, of which waited for: 10 -> 11; matrix products, arithmetic and copies ran while one was open for 0% -> 0% of each run, Pallas kernels for 17% -> 10%
where the time goes in v7:
time: 244 us; the launch traced here: 243 us
  waiting for transfers between devices  97.7 us (40%)
  starting transfers between devices  97 us (40%)
  Pallas kernels  43.1 us (18%)
  local copies, waits for them, and re-layouts  3.76 us (2%)
    ppermute x39, waiting for transfers between devices, shift_to(): return lax.ppermute(x, AXES, pairs)  87.5 us
    ppermute x39, starting transfers between devices, shift_to(): return lax.ppermute(x, AXES, pairs)  87.4 us
    pallas_call x1, Pallas kernels, gather_flows(): pl.pallas_call(body, in_specs=[hbm, hbm, vmem, vmem, smem, smem] + [smem]...  15.2 us
    pallas_call x3, Pallas kernels, mix_tiles(): pl.pallas_call(body, grid=(each,), in_specs=[pl.BlockSpec(memory_space=pl...  11.5 us
    pallas_call x1, Pallas kernels, spread_squares(): pl.pallas_call(body, grid=(nblk // sb,), in_specs=[pl.BlockSpec(memory_sp...  10.6 us
    all_to_all x1, waiting for transfers between devices, exchange(): return lax.all_to_all(x, axes, split_axis=0, concat_axis=0, tiled=True)  10.2 us
    all_to_all x1, starting transfers between devices, exchange(): return lax.all_to_all(x, axes, split_axis=0, concat_axis=0, tiled=True)  9.59 us
  transfers between devices with their start and end apart: 40, of which 11 were waited for; matrix products, arithmetic and copies ran while one was open for 0% of the time, Pallas kernels for 10%

profile of v7, /device:TPU:1, one launch (start us, length us, event | category | flops | bytes accessed | tf_op | source)
XLA Modules:
  0.0 243.2 jit_solution(6027382441241775902)
XLA Ops:
  1.3 15.2 %gather_flows.1 = (bf16[5,264,128]{2,1,0:T(8,128)(2,1)}, bf16[5,264,128]{2,1,0:T(8,128)(2,1)}, bf16[5,264,128]{2,1,0:T(8,128)(2,1)}, bf16[5,264,128]{2,1,0:T(8,1...) custom-call(bf16[8192,256]{1,0:T(8,128)(2,1)} %bitcast.13, ...), custom_call_target="tpu_custom_call" | custom-call | tf_op jit(solution)/shard_map/gather_flows/pallas_call | solution.py:104
  16.5 1.5 collective-permute-start.13
  18.0 1.4 collective-permute-start.14
  19.4 1.5 collective-permute-start.15
  20.9 1.4 collective-permute-start.16
  22.9 1.6 collective-permute-start.18
  24.5 4.6 %collective-permute-done.14.refs_2_ = bf16[5,264,128]{2,1,0:T(8,128)(2,1)S(1)} collective-permute-done((bf16[5,264,128]{2,1,0:T(8,128)(2,1)}, bf16[5,264,128]{2,1,0:T(8,128)(2,1)S(1)}, u32[]{:S(2)}, u32[]{:S(2)}) %collective-permute-start.14) | collective-permute-done | bytes 337952 | tf_op jit(solution)/shard_map/ppermute | solution.py:363
  29.1 2.8 %collective-permute-start.19 = (bf16[5,264,128]{2,1,0:T(8,128)(2,1)}, bf16[5,264,128]{2,1,0:T(8,128)(2,1)S(1)}, u32[]{:S(2)}, u32[]{:S(2)}) collective-permute-start(bf16[5,264,128]{2,1,0:T(8,128)(2,1)} %get-tuple-element.93), channel_id=1, source_target_pairs={{0,65},{1,64},{2,67},{3,66},{4,69},{5,68},{6,71},{7,70},{8,73},{9,... | collective-permute-start | bytes 1013768 | tf_op jit(solution)/shard_map/ppermute | solution.py:363
  32.0 4.5 %collective-permute-done.15.refs_3_ = bf16[5,264,128]{2,1,0:T(8,128)(2,1)S(1)} collective-permute-done((bf16[5,264,128]{2,1,0:T(8,128)(2,1)}, bf16[5,264,128]{2,1,0:T(8,128)(2,1)S(1)}, u32[]{:S(2)}, u32[]{:S(2)}) %collective-permute-start.15) | collective-permute-done | bytes 337952 | tf_op jit(solution)/shard_map/ppermute | solution.py:363
  36.8 1.5 collective-permute-start.1
  38.9 1.5 collective-permute-start.2
  40.4 4.2 %collective-permute-done.18.refs_6_ = bf16[5,264,128]{2,1,0:T(8,128)(2,1)S(1)} collective-permute-done((bf16[5,264,128]{2,1,0:T(8,128)(2,1)}, bf16[5,264,128]{2,1,0:T(8,128)(2,1)S(1)}, u32[]{:S(2)}, u32[]{:S(2)}) %collective-permute-start.18) | collective-permute-done | bytes 337952 | tf_op jit(solution)/shard_map/ppermute | solution.py:363
  44.6 3.8 %collective-permute-start.3 = (bf16[5,264,128]{2,1,0:T(8,128)(2,1)}, bf16[5,264,128]{2,1,0:T(8,128)(2,1)S(1)}, u32[]{:S(2)}, u32[]{:S(2)}) collective-permute-start(bf16[5,264,128]{2,1,0:T(8,128)(2,1)} %get-tuple-element.74), channel_id=1, source_target_pairs={{0,6},{1,7},{2,0},{3,1},{4,2},{5,3},{6,4},{7,5},{8,14},{9,15},{10,... | collective-permute-start | bytes 1013768 | tf_op jit(solution)/shard_map/ppermute | solution.py:363
  48.4 3.7 %collective-permute-done.19.refs_7_ = bf16[5,264,128]{2,1,0:T(8,128)(2,1)S(1)} collective-permute-done((bf16[5,264,128]{2,1,0:T(8,128)(2,1)}, bf16[5,264,128]{2,1,0:T(8,128)(2,1)S(1)}, u32[]{:S(2)}, u32[]{:S(2)}) %collective-permute-start.19) | collective-permute-done | bytes 337952 | tf_op jit(solution)/shard_map/ppermute | solution.py:363
  52.1 3.8 %collective-permute-start.4 = (bf16[5,264,128]{2,1,0:T(8,128)(2,1)}, bf16[5,264,128]{2,1,0:T(8,128)(2,1)S(1)}, u32[]{:S(2)}, u32[]{:S(2)}) collective-permute-start(bf16[5,264,128]{2,1,0:T(8,128)(2,1)} %get-tuple-element.75), channel_id=1, source_target_pairs={{0,7},{1,6},{2,1},{3,0},{4,3},{5,2},{6,5},{7,4},{8,15},{9,14},{10,... | collective-permute-start | bytes 1013768 | tf_op jit(solution)/shard_map/ppermute | solution.py:363
  55.9 3.5 %collective-permute-start.6 = (bf16[5,264,128]{2,1,0:T(8,128)(2,1)}, bf16[5,264,128]{2,1,0:T(8,128)(2,1)S(1)}, u32[]{:S(2)}, u32[]{:S(2)}) collective-permute-start(bf16[5,264,128]{2,1,0:T(8,128)(2,1)} %get-tuple-element.77), channel_id=1, source_target_pairs={{0,5},{1,4},{2,7},{3,6},{4,1},{5,0},{6,3},{7,2},{8,13},{9,12},{10,... | collective-permute-start | bytes 1013768 | tf_op jit(solution)/shard_map/ppermute | solution.py:363
  59.4 1.3 collective-permute-start.27
  60.7 17.2 %collective-permute-done.4.refs_5_ = bf16[5,264,128]{2,1,0:T(8,128)(2,1)S(1)} collective-permute-done((bf16[5,264,128]{2,1,0:T(8,128)(2,1)}, bf16[5,264,128]{2,1,0:T(8,128)(2,1)S(1)}, u32[]{:S(2)}, u32[]{:S(2)}) %collective-permute-start.4) | collective-permute-done | bytes 337952 | tf_op jit(solution)/shard_map/ppermute | solution.py:363
  77.9 2.0 collective-permute-start.28
  80.0 1.5 collective-permute-start.29
  81.4 1.0 collective-permute-start.30
  84.0 3.6 %mix_tiles.4 = (bf16[5,256,256]{2,1,0:T(8,128)(2,1)S(1)}, bf16[5,256,256]{2,1,0:T(8,128)(2,1)S(1)}, bf16[5,256,256]{2,1,0:T(8,128)(2,1)S(1)}, bf16[5,256,256]{2,1,0:T(8,128)(2,1)S(1)}) custom-call(s32[1]{0:T(128)} %bitcast.refs_8_.at_ref, bf16[5,264,128]{2,1,0:T(8,128)(2,1)S(1)} %copy-done.2, bf16[5,264,128]{2,1,0:T(8,128)(2,1)S(1)} %collective-permute-done.13.refs_1_, ...), custom_call_target="tpu_custom_call" | custom-call | tf_op jit(solution)/shard_map/mix_tiles/pallas_call | solution.py:151
  88.2 3.2 %collective-permute-done.28.refs_3_ = bf16[6,264,128]{2,1,0:T(8,128)(2,1)S(1)} collective-permute-done((bf16[6,264,128]{2,1,0:T(8,128)(2,1)}, bf16[6,264,128]{2,1,0:T(8,128)(2,1)S(1)}, u32[]{:S(2)}, u32[]{:S(2)}) %collective-permute-start.28) | collective-permute-done | bytes 405536 | tf_op jit(solution)/shard_map/ppermute | solution.py:363
  92.3 1.7 collective-permute-start.22
  95.0 3.6 %mix_tiles.3 = (bf16[5,256,256]{2,1,0:T(8,128)(2,1)S(1)}, bf16[5,256,256]{2,1,0:T(8,128)(2,1)S(1)}, bf16[5,256,256]{2,1,0:T(8,128)(2,1)S(1)}, bf16[5,256,256]{2,1,0:T(8,128)(2,1)S(1)}) custom-call(s32[1]{0:T(128)} %bitcast.1.refs_7_.at_ref, bf16[5,264,128]{2,1,0:T(8,128)(2,1)S(1)} %copy-done.1, bf16[5,264,128]{2,1,0:T(8,128)(2,1)S(1)} %collective-permute-done.refs_1_, ...), custom_call_target="tpu_custom_call" | custom-call | tf_op jit(solution)/shard_map/mix_tiles/pallas_call | solution.py:151
  98.6 1.7 collective-permute-done.30.refs_5_
  100.3 8.9 %collective-permute-start.7 = (bf16[5,256,256]{2,1,0:T(8,128)(2,1)S(1)}, bf16[5,256,256]{2,1,0:T(8,128)(2,1)S(1)}, u32[]{:S(2)}, u32[]{:S(2)}) collective-permute-start(bf16[5,256,256]{2,1,0:T(8,128)(2,1)S(1)} %get-tuple-element.79), channel_id=1, source_target_pairs={{0,32},{1,33},{2,34},{3,35},{4,36},{5,37},{6,38},{7,39},{8,40},{9,... | collective-permute-start | bytes 1966088 | tf_op jit(solution)/shard_map/ppermute | solution.py:363
  109.2 1.9 collective-permute-start.32
  111.2 26.4 %collective-permute-done.32.refs_7_ = bf16[6,264,128]{2,1,0:T(8,128)(2,1)S(1)} collective-permute-done((bf16[6,264,128]{2,1,0:T(8,128)(2,1)}, bf16[6,264,128]{2,1,0:T(8,128)(2,1)S(1)}, u32[]{:S(2)}, u32[]{:S(2)}) %collective-permute-start.32) | collective-permute-done | bytes 405536 | tf_op jit(solution)/shard_map/ppermute | solution.py:363
  137.6 1.0 copy-done
  138.6 4.3 %mix_tiles.5 = (bf16[6,256,256]{2,1,0:T(8,128)(2,1)S(1)}, bf16[6,256,256]{2,1,0:T(8,128)(2,1)S(1)}, bf16[6,256,256]{2,1,0:T(8,128)(2,1)S(1)}, bf16[6,256,256]{2,1,0:T(8,128)(2,1)S(1)}) custom-call(s32[1]{0:T(128)} %bitcast.5.refs_6_.at_ref, bf16[6,264,128]{2,1,0:T(8,128)(2,1)S(1)} %copy-done, bf16[6,264,128]{2,1,0:T(8,128)(2,1)S(1)} %collective-permute-done.26.refs_1_, ...), custom_call_target="tpu_custom_call" | custom-call | tf_op jit(solution)/shard_map/mix_tiles/pallas_call | solution.py:151
  143.0 3.0 %collective-permute-start.34 = (bf16[6,256,256]{2,1,0:T(8,128)(2,1)S(1)}, bf16[6,256,256]{2,1,0:T(8,128)(2,1)S(1)}, u32[]{:S(2)}, u32[]{:S(2)}) collective-permute-start(bf16[6,256,256]{2,1,0:T(8,128)(2,1)S(1)} %get-tuple-element.112), channel_id=1, source_target_pairs={{0,6},{1,7},{2,0},{3,1},{4,2},{5,3},{6,4},{7,5},{8,14},{9,15},{10,... | collective-permute-start | bytes 2359304 | tf_op jit(solution)/shard_map/ppermute | solution.py:363
  146.0 10.7 %collective-permute-start.8 = (bf16[5,256,256]{2,1,0:T(8,128)(2,1)S(1)}, bf16[5,256,256]{2,1,0:T(8,128)(2,1)S(1)}, u32[]{:S(2)}, u32[]{:S(2)}) collective-permute-start(bf16[5,256,256]{2,1,0:T(8,128)(2,1)S(1)} %get-tuple-element.80), channel_id=1, source_target_pairs={{0,96},{1,97},{2,98},{3,99},{4,100},{5,101},{6,102},{7,103},{8,104... | collective-permute-start | bytes 1966088 | tf_op jit(solution)/shard_map/ppermute | solution.py:363
  156.8 2.6 %collective-permute-start.9 = (bf16[5,256,256]{2,1,0:T(8,128)(2,1)S(1)}, bf16[5,256,256]{2,1,0:T(8,128)(2,1)S(1)}, u32[]{:S(2)}, u32[]{:S(2)}) collective-permute-start(bf16[5,256,256]{2,1,0:T(8,128)(2,1)S(1)} %get-tuple-element.81), channel_id=1, source_target_pairs={{0,64},{1,65},{2,66},{3,67},{4,68},{5,69},{6,70},{7,71},{8,72},{9,... | collective-permute-start | bytes 1966088 | tf_op jit(solution)/shard_map/ppermute | solution.py:363
  159.4 3.1 %collective-permute-start.35 = (bf16[6,256,256]{2,1,0:T(8,128)(2,1)S(1)}, bf16[6,256,256]{2,1,0:T(8,128)(2,1)S(1)}, u32[]{:S(2)}, u32[]{:S(2)}) collective-permute-start(bf16[6,256,256]{2,1,0:T(8,128)(2,1)S(1)} %get-tuple-element.113), channel_id=1, source_target_pairs={{0,4},{1,5},{2,6},{3,7},{4,0},{5,1},{6,2},{7,3},{8,12},{9,13},{10,... | collective-permute-start | bytes 2359304 | tf_op jit(solution)/shard_map/ppermute | solution.py:363
  162.9 21.2 %collective-permute-done.8.refs_2_ = bf16[5,256,256]{2,1,0:T(8,128)(2,1)S(1)} collective-permute-done((bf16[5,256,256]{2,1,0:T(8,128)(2,1)S(1)}, bf16[5,256,256]{2,1,0:T(8,128)(2,1)S(1)}, u32[]{:S(2)}, u32[]{:S(2)}) %collective-permute-start.8) | collective-permute-done | bytes 655392 | tf_op jit(solution)/shard_map/ppermute | solution.py:363
  184.1 2.7 %collective-permute-start.24 = (bf16[5,64,256]{2,1,0:T(8,128)(2,1)S(1)}, bf16[5,64,256]{2,1,0:T(8,128)(2,1)S(1)}, u32[]{:S(2)}, u32[]{:S(2)}) collective-permute-start(bf16[5,64,256]{2,1,0:T(8,128)(2,1)S(1)} %get-tuple-element.100), channel_id=1, source_target_pairs={{0,6},{1,7},{2,0},{3,1},{4,2},{5,3},{6,4},{7,5},{8,14},{9,15},{10,... | collective-permute-start | bytes 491528 | tf_op jit(solution)/shard_map/ppermute | solution.py:363
  187.3 9.4 %collective-permute-start.10 = (bf16[5,64,256]{2,1,0:T(8,128)(2,1)S(1)}, bf16[5,64,256]{2,1,0:T(8,128)(2,1)S(1)}, u32[]{:S(2)}, u32[]{:S(2)}) collective-permute-start(bf16[5,64,256]{2,1,0:T(8,128)(2,1)S(1)} %get-tuple-element.83), channel_id=1, source_target_pairs={{0,8},{1,9},{2,10},{3,11},{4,12},{5,13},{6,14},{7,15},{8,16},{9,17... | collective-permute-start | bytes 491528 | tf_op jit(solution)/shard_map/ppermute | solution.py:363
  197.3 1.2 collective-permute-start.36
  198.5 2.5 %collective-permute-start.37 = (bf16[6,64,256]{2,1,0:T(8,128)(2,1)S(1)}, bf16[6,64,256]{2,1,0:T(8,128)(2,1)S(1)}, u32[]{:S(2)}, u32[]{:S(2)}) collective-permute-start(bf16[6,64,256]{2,1,0:T(8,128)(2,1)S(1)} %get-tuple-element.116), channel_id=1, source_target_pairs={{0,96},{1,97},{2,98},{3,99},{4,100},{5,101},{6,102},{7,103},{8,104... | collective-permute-start | bytes 589832 | tf_op jit(solution)/shard_map/ppermute | solution.py:363
  201.0 1.2 collective-permute-start.38
  202.2 4.1 %collective-permute-start.11 = (bf16[5,64,256]{2,1,0:T(8,128)(2,1)S(1)}, bf16[5,64,256]{2,1,0:T(8,128)(2,1)S(1)}, u32[]{:S(2)}, u32[]{:S(2)}) collective-permute-start(bf16[5,64,256]{2,1,0:T(8,128)(2,1)S(1)} %get-tuple-element.84), channel_id=1, source_target_pairs={{0,24},{1,25},{2,26},{3,27},{4,28},{5,29},{6,30},{7,31},{8,0},{9,1... | collective-permute-start | bytes 491528 | tf_op jit(solution)/shard_map/ppermute | solution.py:363
  206.3 1.1 collective-permute-start.12
  207.4 10.6 %spread_squares.1 = (f32[640,32,256]{2,1,0:T(8,128)}, s32[1,1024]{1,0:T(1,128)}) custom-call(s32[1]{0:T(128)} %bitcast.6.me_ref, s32[128,128]{1,0:T(8,128)} %rows_ref.1, bf16[128,128]{1,0:T(8,128)(2,1)} %coef_ref.1, s32[1,1024]{1,0:T(1,128)} %bitcast.14), custom_call_target="tpu_custom_call" | custom-call | tf_op jit(solution)/shard_map/spread_squares/pallas_call | solution.py:252
  218.0 1.1 square_sums.1
  219.1 9.6 %all-to-all-start = ((f32[128,1,384]{2,1,0:T(1,128)}), f32[128,1,384]{2,1,0:T(1,128)S(1)}, u32[]{:S(2)}, u32[]{:S(2)}) async-start(f32[128,1,384]{2,1,0:T(1,128)} %square_sums.1), calls=%async_computation | async-start | bytes 393216 | tf_op jit(solution)/shard_map/all_to_all | solution.py:346
  228.9 10.2 %all-to-all-done.parts_ref = f32[128,1,384]{2,1,0:T(1,128)S(1)} async-done(((f32[128,1,384]{2,1,0:T(1,128)}), f32[128,1,384]{2,1,0:T(1,128)S(1)}, u32[]{:S(2)}, u32[]{:S(2)}) %all-to-all-start) | async-done | bytes 196640 | tf_op jit(solution)/shard_map/all_to_all | solution.py:346
  239.7 3.3 %finish.1 = (f32[1,8]{1,0:T(1,128)}, f32[8,128]{1,0:T(8,128)}, f32[32,256]{1,0:T(8,128)}) custom-call(s32[1]{0:T(128)S(6)} %copy.11.refs_4_.count_ref, f32[128,1,384]{2,1,0:T(1,128)S(1)} %all-to-all-done.parts_ref, f32[8,128]{1,0:T(8,128)S(1)} %bitcast.12, s32[128,1]{1,0:T(8,128)S(1)} %copy.10.sensor_ref, s32[1,1024]{1,0:T(1,128)S(1)} %copy-done.4, ...), custom_call_target="tpu_custom_call" | custom-call | tf_op jit(solution)/shard_map/finish/pallas_call | solution.py:326
  (55 shorter events, 7.9 us)
Async XLA Ops:
  0.6 228.1 %copy-start.5 = (s32[128]{0:T(128)S(1)}, s32[128]{0:T(128)}, u32[]{:S(2)}) copy-start(s32[128]{0:T(128)} %param.9) | copy-start | bytes 1540
  0.6 238.4 %copy-start.3 = (f32[1024]{0:T(1024)S(1)}, f32[1024]{0:T(1024)}, u32[]{:S(2)}) copy-start(f32[1024]{0:T(1024)} %param.13) | copy-start | bytes 12292
  16.5 6.3 %collective-permute-start.13 = (bf16[5,264,128]{2,1,0:T(8,128)(2,1)}, bf16[5,264,128]{2,1,0:T(8,128)(2,1)S(1)}, u32[]{:S(2)}, u32[]{:S(2)}) collective-permute-start(bf16[5,264,128]{2,1,0:T(8,128)(2,1)} %get-tuple-element.87), channel_id=1, source_target_pairs={{0,1},{1,0},{2,3},{3,2},{4,5},{5,4},{6,7},{7,6},{8,9},{9,8},{10,11... | collective-permute-start | bytes 1013768 | tf_op jit(solution)/shard_map/ppermute | solution.py:363
  18.0 11.2 %collective-permute-start.14 = (bf16[5,264,128]{2,1,0:T(8,128)(2,1)}, bf16[5,264,128]{2,1,0:T(8,128)(2,1)S(1)}, u32[]{:S(2)}, u32[]{:S(2)}) collective-permute-start(bf16[5,264,128]{2,1,0:T(8,128)(2,1)} %get-tuple-element.88), channel_id=1, source_target_pairs={{0,32},{1,33},{2,34},{3,35},{4,36},{5,37},{6,38},{7,39},{8,40},{9,... | collective-permute-start | bytes 1013768 | tf_op jit(solution)/shard_map/ppermute | solution.py:363
  19.4 17.1 %collective-permute-start.15 = (bf16[5,264,128]{2,1,0:T(8,128)(2,1)}, bf16[5,264,128]{2,1,0:T(8,128)(2,1)S(1)}, u32[]{:S(2)}, u32[]{:S(2)}) collective-permute-start(bf16[5,264,128]{2,1,0:T(8,128)(2,1)} %get-tuple-element.89), channel_id=1, source_target_pairs={{0,33},{1,32},{2,35},{3,34},{4,37},{5,36},{6,39},{7,38},{8,41},{9,... | collective-permute-start | bytes 1013768 | tf_op jit(solution)/shard_map/ppermute | solution.py:363
  20.9 15.9 %collective-permute-start.16 = (bf16[5,264,128]{2,1,0:T(8,128)(2,1)}, bf16[5,264,128]{2,1,0:T(8,128)(2,1)S(1)}, u32[]{:S(2)}, u32[]{:S(2)}) collective-permute-start(bf16[5,264,128]{2,1,0:T(8,128)(2,1)} %get-tuple-element.90), channel_id=1, source_target_pairs={{0,96},{1,97},{2,98},{3,99},{4,100},{5,101},{6,102},{7,103},{8,104... | collective-permute-start | bytes 1013768 | tf_op jit(solution)/shard_map/ppermute | solution.py:363
  22.3 16.6 %collective-permute-start.17 = (bf16[5,264,128]{2,1,0:T(8,128)(2,1)}, bf16[5,264,128]{2,1,0:T(8,128)(2,1)S(1)}, u32[]{:S(2)}, u32[]{:S(2)}) collective-permute-start(bf16[5,264,128]{2,1,0:T(8,128)(2,1)} %get-tuple-element.91), channel_id=1, source_target_pairs={{0,97},{1,96},{2,99},{3,98},{4,101},{5,100},{6,103},{7,102},{8,105... | collective-permute-start | bytes 1013768 | tf_op jit(solution)/shard_map/ppermute | solution.py:363
  22.9 21.8 %collective-permute-start.18 = (bf16[5,264,128]{2,1,0:T(8,128)(2,1)}, bf16[5,264,128]{2,1,0:T(8,128)(2,1)S(1)}, u32[]{:S(2)}, u32[]{:S(2)}) collective-permute-start(bf16[5,264,128]{2,1,0:T(8,128)(2,1)} %get-tuple-element.92), channel_id=1, source_target_pairs={{0,64},{1,65},{2,66},{3,67},{4,68},{5,69},{6,70},{7,71},{8,72},{9,... | collective-permute-start | bytes 1013768 | tf_op jit(solution)/shard_map/ppermute | solution.py:363
  29.1 23.0 %collective-permute-start.19 = (bf16[5,264,128]{2,1,0:T(8,128)(2,1)}, bf16[5,264,128]{2,1,0:T(8,128)(2,1)S(1)}, u32[]{:S(2)}, u32[]{:S(2)}) collective-permute-start(bf16[5,264,128]{2,1,0:T(8,128)(2,1)} %get-tuple-element.93), channel_id=1, source_target_pairs={{0,65},{1,64},{2,67},{3,66},{4,69},{5,68},{6,71},{7,70},{8,73},{9,... | collective-permute-start | bytes 1013768 | tf_op jit(solution)/shard_map/ppermute | solution.py:363
  36.5 19.5 %collective-permute-start = (bf16[5,264,128]{2,1,0:T(8,128)(2,1)}, bf16[5,264,128]{2,1,0:T(8,128)(2,1)S(1)}, u32[]{:S(2)}, u32[]{:S(2)}) collective-permute-start(bf16[5,264,128]{2,1,0:T(8,128)(2,1)} %get-tuple-element.71), channel_id=1, source_target_pairs={{0,1},{1,0},{2,3},{3,2},{4,5},{5,4},{6,7},{7,6},{8,9},{9,8},{10,11... | collective-permute-start | bytes 1013768 | tf_op jit(solution)/shard_map/ppermute | solution.py:363
  36.8 19.1 %collective-permute-start.1 = (bf16[5,264,128]{2,1,0:T(8,128)(2,1)}, bf16[5,264,128]{2,1,0:T(8,128)(2,1)S(1)}, u32[]{:S(2)}, u32[]{:S(2)}) collective-permute-start(bf16[5,264,128]{2,1,0:T(8,128)(2,1)} %get-tuple-element.72), channel_id=1, source_target_pairs={{0,2},{1,3},{2,4},{3,5},{4,6},{5,7},{6,0},{7,1},{8,10},{9,11},{10,... | collective-permute-start | bytes 1013768 | tf_op jit(solution)/shard_map/ppermute | solution.py:363
  38.9 20.5 %collective-permute-start.2 = (bf16[5,264,128]{2,1,0:T(8,128)(2,1)}, bf16[5,264,128]{2,1,0:T(8,128)(2,1)S(1)}, u32[]{:S(2)}, u32[]{:S(2)}) collective-permute-start(bf16[5,264,128]{2,1,0:T(8,128)(2,1)} %get-tuple-element.73), channel_id=1, source_target_pairs={{0,3},{1,2},{2,5},{3,4},{4,7},{5,6},{6,1},{7,0},{8,11},{9,10},{10,... | collective-permute-start | bytes 1013768 | tf_op jit(solution)/shard_map/ppermute | solution.py:363
  44.6 14.8 %collective-permute-start.3 = (bf16[5,264,128]{2,1,0:T(8,128)(2,1)}, bf16[5,264,128]{2,1,0:T(8,128)(2,1)S(1)}, u32[]{:S(2)}, u32[]{:S(2)}) collective-permute-start(bf16[5,264,128]{2,1,0:T(8,128)(2,1)} %get-tuple-element.74), channel_id=1, source_target_pairs={{0,6},{1,7},{2,0},{3,1},{4,2},{5,3},{6,4},{7,5},{8,14},{9,15},{10,... | collective-permute-start | bytes 1013768 | tf_op jit(solution)/shard_map/ppermute | solution.py:363
  52.1 25.8 %collective-permute-start.4 = (bf16[5,264,128]{2,1,0:T(8,128)(2,1)}, bf16[5,264,128]{2,1,0:T(8,128)(2,1)S(1)}, u32[]{:S(2)}, u32[]{:S(2)}) collective-permute-start(bf16[5,264,128]{2,1,0:T(8,128)(2,1)} %get-tuple-element.75), channel_id=1, source_target_pairs={{0,7},{1,6},{2,1},{3,0},{4,3},{5,2},{6,5},{7,4},{8,15},{9,14},{10,... | collective-permute-start | bytes 1013768 | tf_op jit(solution)/shard_map/ppermute | solution.py:363
  55.9 24.0 %collective-permute-start.5 = (bf16[5,264,128]{2,1,0:T(8,128)(2,1)}, bf16[5,264,128]{2,1,0:T(8,128)(2,1)S(1)}, u32[]{:S(2)}, u32[]{:S(2)}) collective-permute-start(bf16[5,264,128]{2,1,0:T(8,128)(2,1)} %get-tuple-element.76), channel_id=1, source_target_pairs={{0,4},{1,5},{2,6},{3,7},{4,0},{5,1},{6,2},{7,3},{8,12},{9,13},{10,... | collective-permute-start | bytes 1013768 | tf_op jit(solution)/shard_map/ppermute | solution.py:363
  55.9 25.5 %collective-permute-start.6 = (bf16[5,264,128]{2,1,0:T(8,128)(2,1)}, bf16[5,264,128]{2,1,0:T(8,128)(2,1)S(1)}, u32[]{:S(2)}, u32[]{:S(2)}) collective-permute-start(bf16[5,264,128]{2,1,0:T(8,128)(2,1)} %get-tuple-element.77), channel_id=1, source_target_pairs={{0,5},{1,4},{2,7},{3,6},{4,1},{5,0},{6,3},{7,2},{8,13},{9,12},{10,... | collective-permute-start | bytes 1013768 | tf_op jit(solution)/shard_map/ppermute | solution.py:363
  59.4 23.0 %collective-permute-start.26 = (bf16[6,264,128]{2,1,0:T(8,128)(2,1)}, bf16[6,264,128]{2,1,0:T(8,128)(2,1)S(1)}, u32[]{:S(2)}, u32[]{:S(2)}) collective-permute-start(bf16[6,264,128]{2,1,0:T(8,128)(2,1)} %get-tuple-element.103), channel_id=1, source_target_pairs={{0,1},{1,0},{2,3},{3,2},{4,5},{5,4},{6,7},{7,6},{8,9},{9,8},{10,11... | collective-permute-start | bytes 1216520 | tf_op jit(solution)/shard_map/ppermute | solution.py:363
  59.4 28.2 %collective-permute-start.27 = (bf16[6,264,128]{2,1,0:T(8,128)(2,1)}, bf16[6,264,128]{2,1,0:T(8,128)(2,1)S(1)}, u32[]{:S(2)}, u32[]{:S(2)}) collective-permute-start(bf16[6,264,128]{2,1,0:T(8,128)(2,1)} %get-tuple-element.104), channel_id=1, source_target_pairs={{0,8},{1,9},{2,10},{3,11},{4,12},{5,13},{6,14},{7,15},{8,16},{9,17... | collective-permute-start | bytes 1216520 | tf_op jit(solution)/shard_map/ppermute | solution.py:363
  77.9 13.5 %collective-permute-start.28 = (bf16[6,264,128]{2,1,0:T(8,128)(2,1)}, bf16[6,264,128]{2,1,0:T(8,128)(2,1)S(1)}, u32[]{:S(2)}, u32[]{:S(2)}) collective-permute-start(bf16[6,264,128]{2,1,0:T(8,128)(2,1)} %get-tuple-element.105), channel_id=1, source_target_pairs={{0,9},{1,8},{2,11},{3,10},{4,13},{5,12},{6,15},{7,14},{8,17},{9,16... | collective-permute-start | bytes 1216520 | tf_op jit(solution)/shard_map/ppermute | solution.py:363
  80.0 12.4 %collective-permute-start.29 = (bf16[6,264,128]{2,1,0:T(8,128)(2,1)}, bf16[6,264,128]{2,1,0:T(8,128)(2,1)S(1)}, u32[]{:S(2)}, u32[]{:S(2)}) collective-permute-start(bf16[6,264,128]{2,1,0:T(8,128)(2,1)} %get-tuple-element.106), channel_id=1, source_target_pairs={{0,24},{1,25},{2,26},{3,27},{4,28},{5,29},{6,30},{7,31},{8,0},{9,1... | collective-permute-start | bytes 1216520 | tf_op jit(solution)/shard_map/ppermute | solution.py:363
  81.4 18.9 %collective-permute-start.30 = (bf16[6,264,128]{2,1,0:T(8,128)(2,1)}, bf16[6,264,128]{2,1,0:T(8,128)(2,1)S(1)}, u32[]{:S(2)}, u32[]{:S(2)}) collective-permute-start(bf16[6,264,128]{2,1,0:T(8,128)(2,1)} %get-tuple-element.107), channel_id=1, source_target_pairs={{0,25},{1,24},{2,27},{3,26},{4,29},{5,28},{6,31},{7,30},{8,1},{9,0... | collective-permute-start | bytes 1216520 | tf_op jit(solution)/shard_map/ppermute | solution.py:363
  82.4 26.8 %collective-permute-start.31 = (bf16[6,264,128]{2,1,0:T(8,128)(2,1)}, bf16[6,264,128]{2,1,0:T(8,128)(2,1)S(1)}, u32[]{:S(2)}, u32[]{:S(2)}) collective-permute-start(bf16[6,264,128]{2,1,0:T(8,128)(2,1)} %get-tuple-element.108), channel_id=1, source_target_pairs={{0,16},{1,17},{2,18},{3,19},{4,20},{5,21},{6,22},{7,23},{8,24},{9,... | collective-permute-start | bytes 1216520 | tf_op jit(solution)/shard_map/ppermute | solution.py:363
  83.1 1.0 copy-start.2
  87.7 55.3 %collective-permute-start.20 = (bf16[5,256,256]{2,1,0:T(8,128)(2,1)S(1)}, bf16[5,256,256]{2,1,0:T(8,128)(2,1)S(1)}, u32[]{:S(2)}, u32[]{:S(2)}) collective-permute-start(bf16[5,256,256]{2,1,0:T(8,128)(2,1)S(1)} %get-tuple-element.95), channel_id=1, source_target_pairs={{0,8},{1,9},{2,10},{3,11},{4,12},{5,13},{6,14},{7,15},{8,16},{9,17... | collective-permute-start | bytes 1966088 | tf_op jit(solution)/shard_map/ppermute | solution.py:363
  91.5 54.6 %collective-permute-start.21 = (bf16[5,256,256]{2,1,0:T(8,128)(2,1)S(1)}, bf16[5,256,256]{2,1,0:T(8,128)(2,1)S(1)}, u32[]{:S(2)}, u32[]{:S(2)}) collective-permute-start(bf16[5,256,256]{2,1,0:T(8,128)(2,1)S(1)} %get-tuple-element.96), channel_id=1, source_target_pairs={{0,24},{1,25},{2,26},{3,27},{4,28},{5,29},{6,30},{7,31},{8,0},{9,1... | collective-permute-start | bytes 1966088 | tf_op jit(solution)/shard_map/ppermute | solution.py:363
  92.3 64.4 %collective-permute-start.22 = (bf16[5,256,256]{2,1,0:T(8,128)(2,1)S(1)}, bf16[5,256,256]{2,1,0:T(8,128)(2,1)S(1)}, u32[]{:S(2)}, u32[]{:S(2)}) collective-permute-start(bf16[5,256,256]{2,1,0:T(8,128)(2,1)S(1)} %get-tuple-element.97), channel_id=1, source_target_pairs={{0,16},{1,17},{2,18},{3,19},{4,20},{5,21},{6,22},{7,23},{8,24},{9,... | collective-permute-start | bytes 1966088 | tf_op jit(solution)/shard_map/ppermute | solution.py:363
  94.0 1.0 copy-start.1
  100.3 59.1 %collective-permute-start.7 = (bf16[5,256,256]{2,1,0:T(8,128)(2,1)S(1)}, bf16[5,256,256]{2,1,0:T(8,128)(2,1)S(1)}, u32[]{:S(2)}, u32[]{:S(2)}) collective-permute-start(bf16[5,256,256]{2,1,0:T(8,128)(2,1)S(1)} %get-tuple-element.79), channel_id=1, source_target_pairs={{0,32},{1,33},{2,34},{3,35},{4,36},{5,37},{6,38},{7,39},{8,40},{9,... | collective-permute-start | bytes 1966088 | tf_op jit(solution)/shard_map/ppermute | solution.py:363
  109.2 28.3 %collective-permute-start.32 = (bf16[6,264,128]{2,1,0:T(8,128)(2,1)}, bf16[6,264,128]{2,1,0:T(8,128)(2,1)S(1)}, u32[]{:S(2)}, u32[]{:S(2)}) collective-permute-start(bf16[6,264,128]{2,1,0:T(8,128)(2,1)} %get-tuple-element.109), channel_id=1, source_target_pairs={{0,17},{1,16},{2,19},{3,18},{4,21},{5,20},{6,23},{7,22},{8,25},{9,... | collective-permute-start | bytes 1216520 | tf_op jit(solution)/shard_map/ppermute | solution.py:363
  137.6 1.0 copy-start
  142.9 44.3 %collective-permute-start.33 = (bf16[6,256,256]{2,1,0:T(8,128)(2,1)S(1)}, bf16[6,256,256]{2,1,0:T(8,128)(2,1)S(1)}, u32[]{:S(2)}, u32[]{:S(2)}) collective-permute-start(bf16[6,256,256]{2,1,0:T(8,128)(2,1)S(1)} %get-tuple-element.111), channel_id=1, source_target_pairs={{0,2},{1,3},{2,4},{3,5},{4,6},{5,7},{6,0},{7,1},{8,10},{9,11},{10,... | collective-permute-start | bytes 2359304 | tf_op jit(solution)/shard_map/ppermute | solution.py:363
  143.0 44.3 %collective-permute-start.34 = (bf16[6,256,256]{2,1,0:T(8,128)(2,1)S(1)}, bf16[6,256,256]{2,1,0:T(8,128)(2,1)S(1)}, u32[]{:S(2)}, u32[]{:S(2)}) collective-permute-start(bf16[6,256,256]{2,1,0:T(8,128)(2,1)S(1)} %get-tuple-element.112), channel_id=1, source_target_pairs={{0,6},{1,7},{2,0},{3,1},{4,2},{5,3},{6,4},{7,5},{8,14},{9,15},{10,... | collective-permute-start | bytes 2359304 | tf_op jit(solution)/shard_map/ppermute | solution.py:363
  146.0 38.1 %collective-permute-start.8 = (bf16[5,256,256]{2,1,0:T(8,128)(2,1)S(1)}, bf16[5,256,256]{2,1,0:T(8,128)(2,1)S(1)}, u32[]{:S(2)}, u32[]{:S(2)}) collective-permute-start(bf16[5,256,256]{2,1,0:T(8,128)(2,1)S(1)} %get-tuple-element.80), channel_id=1, source_target_pairs={{0,96},{1,97},{2,98},{3,99},{4,100},{5,101},{6,102},{7,103},{8,104... | collective-permute-start | bytes 1966088 | tf_op jit(solution)/shard_map/ppermute | solution.py:363
  156.8 27.3 %collective-permute-start.9 = (bf16[5,256,256]{2,1,0:T(8,128)(2,1)S(1)}, bf16[5,256,256]{2,1,0:T(8,128)(2,1)S(1)}, u32[]{:S(2)}, u32[]{:S(2)}) collective-permute-start(bf16[5,256,256]{2,1,0:T(8,128)(2,1)S(1)} %get-tuple-element.81), channel_id=1, source_target_pairs={{0,64},{1,65},{2,66},{3,67},{4,68},{5,69},{6,70},{7,71},{8,72},{9,... | collective-permute-start | bytes 1966088 | tf_op jit(solution)/shard_map/ppermute | solution.py:363
  159.4 37.4 %collective-permute-start.35 = (bf16[6,256,256]{2,1,0:T(8,128)(2,1)S(1)}, bf16[6,256,256]{2,1,0:T(8,128)(2,1)S(1)}, u32[]{:S(2)}, u32[]{:S(2)}) collective-permute-start(bf16[6,256,256]{2,1,0:T(8,128)(2,1)S(1)} %get-tuple-element.113), channel_id=1, source_target_pairs={{0,4},{1,5},{2,6},{3,7},{4,0},{5,1},{6,2},{7,3},{8,12},{9,13},{10,... | collective-permute-start | bytes 2359304 | tf_op jit(solution)/shard_map/ppermute | solution.py:363
  184.1 14.4 %collective-permute-start.23 = (bf16[5,64,256]{2,1,0:T(8,128)(2,1)S(1)}, bf16[5,64,256]{2,1,0:T(8,128)(2,1)S(1)}, u32[]{:S(2)}, u32[]{:S(2)}) collective-permute-start(bf16[5,64,256]{2,1,0:T(8,128)(2,1)S(1)} %get-tuple-element.99), channel_id=1, source_target_pairs={{0,2},{1,3},{2,4},{3,5},{4,6},{5,7},{6,0},{7,1},{8,10},{9,11},{10,... | collective-permute-start | bytes 491528 | tf_op jit(solution)/shard_map/ppermute | solution.py:363
  184.1 16.9 %collective-permute-start.24 = (bf16[5,64,256]{2,1,0:T(8,128)(2,1)S(1)}, bf16[5,64,256]{2,1,0:T(8,128)(2,1)S(1)}, u32[]{:S(2)}, u32[]{:S(2)}) collective-permute-start(bf16[5,64,256]{2,1,0:T(8,128)(2,1)S(1)} %get-tuple-element.100), channel_id=1, source_target_pairs={{0,6},{1,7},{2,0},{3,1},{4,2},{5,3},{6,4},{7,5},{8,14},{9,15},{10,... | collective-permute-start | bytes 491528 | tf_op jit(solution)/shard_map/ppermute | solution.py:363
  187.2 15.0 %collective-permute-start.25 = (bf16[5,64,256]{2,1,0:T(8,128)(2,1)S(1)}, bf16[5,64,256]{2,1,0:T(8,128)(2,1)S(1)}, u32[]{:S(2)}, u32[]{:S(2)}) collective-permute-start(bf16[5,64,256]{2,1,0:T(8,128)(2,1)S(1)} %get-tuple-element.101), channel_id=1, source_target_pairs={{0,4},{1,5},{2,6},{3,7},{4,0},{5,1},{6,2},{7,3},{8,12},{9,13},{10,... | collective-permute-start | bytes 491528 | tf_op jit(solution)/shard_map/ppermute | solution.py:363
  187.3 18.9 %collective-permute-start.10 = (bf16[5,64,256]{2,1,0:T(8,128)(2,1)S(1)}, bf16[5,64,256]{2,1,0:T(8,128)(2,1)S(1)}, u32[]{:S(2)}, u32[]{:S(2)}) collective-permute-start(bf16[5,64,256]{2,1,0:T(8,128)(2,1)S(1)} %get-tuple-element.83), channel_id=1, source_target_pairs={{0,8},{1,9},{2,10},{3,11},{4,12},{5,13},{6,14},{7,15},{8,16},{9,17... | collective-permute-start | bytes 491528 | tf_op jit(solution)/shard_map/ppermute | solution.py:363
  197.3 20.7 %collective-permute-start.36 = (bf16[6,64,256]{2,1,0:T(8,128)(2,1)S(1)}, bf16[6,64,256]{2,1,0:T(8,128)(2,1)S(1)}, u32[]{:S(2)}, u32[]{:S(2)}) collective-permute-start(bf16[6,64,256]{2,1,0:T(8,128)(2,1)S(1)} %get-tuple-element.115), channel_id=1, source_target_pairs={{0,32},{1,33},{2,34},{3,35},{4,36},{5,37},{6,38},{7,39},{8,40},{9,... | collective-permute-start | bytes 589832 | tf_op jit(solution)/shard_map/ppermute | solution.py:363
  198.5 19.5 %collective-permute-start.37 = (bf16[6,64,256]{2,1,0:T(8,128)(2,1)S(1)}, bf16[6,64,256]{2,1,0:T(8,128)(2,1)S(1)}, u32[]{:S(2)}, u32[]{:S(2)}) collective-permute-start(bf16[6,64,256]{2,1,0:T(8,128)(2,1)S(1)} %get-tuple-element.116), channel_id=1, source_target_pairs={{0,96},{1,97},{2,98},{3,99},{4,100},{5,101},{6,102},{7,103},{8,104... | collective-permute-start | bytes 589832 | tf_op jit(solution)/shard_map/ppermute | solution.py:363
  201.0 17.0 %collective-permute-start.38 = (bf16[6,64,256]{2,1,0:T(8,128)(2,1)S(1)}, bf16[6,64,256]{2,1,0:T(8,128)(2,1)S(1)}, u32[]{:S(2)}, u32[]{:S(2)}) collective-permute-start(bf16[6,64,256]{2,1,0:T(8,128)(2,1)S(1)} %get-tuple-element.117), channel_id=1, source_target_pairs={{0,64},{1,65},{2,66},{3,67},{4,68},{5,69},{6,70},{7,71},{8,72},{9,... | collective-permute-start | bytes 589832 | tf_op jit(solution)/shard_map/ppermute | solution.py:363
  202.2 15.8 %collective-permute-start.11 = (bf16[5,64,256]{2,1,0:T(8,128)(2,1)S(1)}, bf16[5,64,256]{2,1,0:T(8,128)(2,1)S(1)}, u32[]{:S(2)}, u32[]{:S(2)}) collective-permute-start(bf16[5,64,256]{2,1,0:T(8,128)(2,1)S(1)} %get-tuple-element.84), channel_id=1, source_target_pairs={{0,24},{1,25},{2,26},{3,27},{4,28},{5,29},{6,30},{7,31},{8,0},{9,1... | collective-permute-start | bytes 491528 | tf_op jit(solution)/shard_map/ppermute | solution.py:363
  206.3 11.7 %collective-permute-start.12 = (bf16[5,64,256]{2,1,0:T(8,128)(2,1)S(1)}, bf16[5,64,256]{2,1,0:T(8,128)(2,1)S(1)}, u32[]{:S(2)}, u32[]{:S(2)}) collective-permute-start(bf16[5,64,256]{2,1,0:T(8,128)(2,1)S(1)} %get-tuple-element.85), channel_id=1, source_target_pairs={{0,16},{1,17},{2,18},{3,19},{4,20},{5,21},{6,22},{7,23},{8,24},{9,... | collective-permute-start | bytes 491528 | tf_op jit(solution)/shard_map/ppermute | solution.py:363
  219.1 19.9 %all-to-all-start = ((f32[128,1,384]{2,1,0:T(1,128)}), f32[128,1,384]{2,1,0:T(1,128)S(1)}, u32[]{:S(2)}, u32[]{:S(2)}) async-start(f32[128,1,384]{2,1,0:T(1,128)} %square_sums.1), calls=%async_computation | async-start | bytes 393216 | tf_op jit(solution)/shard_map/all_to_all | solution.py:346
  239.1 0.7 copy-start.4

commit v8 on v7

--- a/solution.py
+++ b/solution.py
@@ -11,7 +11,7 @@
 SPD = 8
 AXES = ("y", "x", "z", "core")
 ORDERS = (("z", "y", "x"), ("y", "x", "z"), ("x", "z", "y"))
-EACH = (5, 5, 6)
+EACH = (4, 6, 6)
 PEERS = ((0, 0), (0, 1), (1, 0), (1, 1), (3, 0), (3, 1), (2, 0), (2, 1))
 SHIFTS = (0, 1, 3, 2)
 SIDE = 8
@@ -374,18 +374,19 @@
     flat = probes.reshape(tile_r * tile_c, probe_n)
     tile = (blk_rows, coef, blk_sensor.reshape(1, nblk), blk_count, core)
     firsts = [8 * sum(EACH[:f]) for f in range(3)]
-    packs = [(first, each, f) for f, (first, each) in enumerate(zip(firsts, EACH))]
-    sent = gather_flows(flat, *tile, packs, [at[a] for a, _, _ in ORDERS])
+    tiles = [None] * 3
+    flows = [None] * 3
     maps, pos = spread_squares(blk_rows, coef, owner.reshape(1, n_sens), me, tile_r, tile_c)
-    tiles = []
-    for f, (a, _, _) in enumerate(ORDERS):
-        tiles.append([shift_to(x, a, *peer) for x, peer in zip(sent[8 * f : 8 * f + 8], PEERS)])
-    flows = []
+    for group in ((2,), (0, 1)):
+        packs = [(firsts[f], EACH[f], i) for i, f in enumerate(group)]
+        sent = gather_flows(flat, *tile, packs, [at[ORDERS[f][0]] for f in group])
+        for i, f in enumerate(group):
+            tiles[f] = [shift_to(x, ORDERS[f][0], *peer) for x, peer in zip(sent[8 * i : 8 * i + 8], PEERS)]
     for f, (_, b, c) in enumerate(ORDERS):
         quarters = mix_tiles(tiles[f], at[b], n_sens)
         quarters = [shift_to(x, b, s, 0) for x, s in zip(quarters, SHIFTS)]
         pieces = add_quarters(quarters, at[c])
-        flows.append([shift_to(x, c, s, 0) for x, s in zip(pieces, SHIFTS)])
+        flows[f] = [shift_to(x, c, s, 0) for x, s in zip(pieces, SHIFTS)]
     (flows, maps, pos) = lax.optimization_barrier((flows, maps, pos))
     acc = square_sums(flows, n_dev)
     parts = exchange(acc, AXES)

time: 244 us -> 221 us (0.906)
  starting transfers between devices: 97 us -> 76.2 us
  waiting for transfers between devices: 97.7 us -> 91 us
  Pallas kernels: 43.1 us -> 47.2 us
    ppermute x39, starting transfers between devices: 87.4 us -> 67 us  [shift_to(): return lax.ppermute(x, AXES, pairs)]
    ppermute x39, waiting for transfers between devices: 87.5 us -> 80.8 us  [shift_to(): return lax.ppermute(x, AXES, pairs)]
    pallas_call x1 -> x2, Pallas kernels: 15.2 us -> 19.3 us  [gather_flows(): pl.pallas_call(body, in_specs=[hbm, hbm, vmem, vmem, smem, smem] + [smem]...]
  transfers between devices with their start and end apart: 40 -> 40, of which waited for: 11 -> 16; matrix products, arithmetic and copies ran while one was open for 0% -> 0% of each run, Pallas kernels for 10% -> 14%
where the time goes in v8:
time: 221 us; the launch traced here: 220 us
  waiting for transfers between devices  91 us (41%)
  starting transfers between devices  76.2 us (34%)
  Pallas kernels  47.2 us (21%)
  local copies, waits for them, and re-layouts  3.76 us (2%)
    ppermute x39, waiting for transfers between devices, shift_to(): return lax.ppermute(x, AXES, pairs)  80.8 us
    ppermute x39, starting transfers between devices, shift_to(): return lax.ppermute(x, AXES, pairs)  67 us
    pallas_call x2, Pallas kernels, gather_flows(): pl.pallas_call(body, in_specs=[hbm, hbm, vmem, vmem, smem, smem] + [smem]...  19.3 us
    pallas_call x3, Pallas kernels, mix_tiles(): pl.pallas_call(body, grid=(each,), in_specs=[pl.BlockSpec(memory_space=pl...  11.5 us
    pallas_call x1, Pallas kernels, spread_squares(): pl.pallas_call(body, grid=(nblk // sb,), in_specs=[pl.BlockSpec(memory_sp...  10.6 us
    all_to_all x1, waiting for transfers between devices, exchange(): return lax.all_to_all(x, axes, split_axis=0, concat_axis=0, tiled=True)  10.2 us
    all_to_all x1, starting transfers between devices, exchange(): return lax.all_to_all(x, axes, split_axis=0, concat_axis=0, tiled=True)  9.25 us
  transfers between devices with their start and end apart: 40, of which 16 were waited for; matrix products, arithmetic and copies ran while one was open for 0% of the time, Pallas kernels for 14%

profile of v8, /device:TPU:1, one launch (start us, length us, event | category | flops | bytes accessed | tf_op | source)
XLA Modules:
  0.0 219.9 jit_solution(4411120269525110350)
XLA Ops:
  1.3 11.1 %gather_flows.2 = (bf16[4,264,128]{2,1,0:T(8,128)(2,1)}, bf16[4,264,128]{2,1,0:T(8,128)(2,1)}, bf16[4,264,128]{2,1,0:T(8,128)(2,1)}, bf16[4,264,128]{2,1,0:T(8,1...) custom-call(bf16[8192,256]{1,0:T(8,128)(2,1)} %bitcast.13, ...), custom_call_target="tpu_custom_call" | custom-call | tf_op jit(solution)/shard_map/gather_flows/pallas_call | solution.py:104
  12.4 1.5 collective-permute-start
  13.8 1.7 collective-permute-start.1
  15.6 1.9 collective-permute-start.2
  17.5 1.0 collective-permute-start.3
  18.5 1.2 collective-permute-start.4
  19.7 8.2 %gather_flows.3 = (bf16[6,264,128]{2,1,0:T(8,128)(2,1)}, bf16[6,264,128]{2,1,0:T(8,128)(2,1)}, bf16[6,264,128]{2,1,0:T(8,128)(2,1)}, bf16[6,264,128]{2,1,0:T(8,1...) custom-call(bf16[8192,256]{1,0:T(8,128)(2,1)} %bitcast.14, ...), custom_call_target="tpu_custom_call" | custom-call | tf_op jit(solution)/shard_map/gather_flows/pallas_call | solution.py:104
  28.1 1.3 collective-permute-start.27
  29.4 1.1 collective-permute-done.2.refs_3_
  30.5 1.6 collective-permute-start.5
  32.1 2.0 collective-permute-start.6
  35.0 4.9 %collective-permute-done.5.refs_6_ = bf16[4,264,128]{2,1,0:T(8,128)(2,1)S(1)} collective-permute-done((bf16[4,264,128]{2,1,0:T(8,128)(2,1)}, bf16[4,264,128]{2,1,0:T(8,128)(2,1)S(1)}, u32[]{:S(2)}, u32[]{:S(2)}) %collective-permute-start.5) | collective-permute-done | bytes 270368 | tf_op jit(solution)/shard_map/ppermute | solution.py:363
  39.8 2.5 %collective-permute-start.29 = (bf16[6,264,128]{2,1,0:T(8,128)(2,1)}, bf16[6,264,128]{2,1,0:T(8,128)(2,1)S(1)}, u32[]{:S(2)}, u32[]{:S(2)}) collective-permute-start(bf16[6,264,128]{2,1,0:T(8,128)(2,1)} %get-tuple-element.106), channel_id=1, source_target_pairs={{0,24},{1,25},{2,26},{3,27},{4,28},{5,29},{6,30},{7,31},{8,0},{9,1... | collective-permute-start | bytes 1216520 | tf_op jit(solution)/shard_map/ppermute | solution.py:363
  42.3 3.9 %collective-permute-done.6.refs_7_ = bf16[4,264,128]{2,1,0:T(8,128)(2,1)S(1)} collective-permute-done((bf16[4,264,128]{2,1,0:T(8,128)(2,1)}, bf16[4,264,128]{2,1,0:T(8,128)(2,1)S(1)}, u32[]{:S(2)}, u32[]{:S(2)}) %collective-permute-start.6) | collective-permute-done | bytes 270368 | tf_op jit(solution)/shard_map/ppermute | solution.py:363
  46.2 2.2 collective-permute-start.30
  49.0 3.3 %collective-permute-start.32 = (bf16[6,264,128]{2,1,0:T(8,128)(2,1)}, bf16[6,264,128]{2,1,0:T(8,128)(2,1)S(1)}, u32[]{:S(2)}, u32[]{:S(2)}) collective-permute-start(bf16[6,264,128]{2,1,0:T(8,128)(2,1)} %get-tuple-element.109), channel_id=1, source_target_pairs={{0,17},{1,16},{2,19},{3,18},{4,21},{5,20},{6,23},{7,22},{8,25},{9,... | collective-permute-start | bytes 1216520 | tf_op jit(solution)/shard_map/ppermute | solution.py:363
  52.2 1.4 collective-permute-start.14
  53.6 9.1 %collective-permute-done.30.refs_5_ = bf16[6,264,128]{2,1,0:T(8,128)(2,1)S(1)} collective-permute-done((bf16[6,264,128]{2,1,0:T(8,128)(2,1)}, bf16[6,264,128]{2,1,0:T(8,128)(2,1)S(1)}, u32[]{:S(2)}, u32[]{:S(2)}) %collective-permute-start.30) | collective-permute-done | bytes 405536 | tf_op jit(solution)/shard_map/ppermute | solution.py:363
  62.7 16.8 %collective-permute-start.15 = (bf16[6,264,128]{2,1,0:T(8,128)(2,1)}, bf16[6,264,128]{2,1,0:T(8,128)(2,1)S(1)}, u32[]{:S(2)}, u32[]{:S(2)}) collective-permute-start(bf16[6,264,128]{2,1,0:T(8,128)(2,1)} %get-tuple-element.89), channel_id=1, source_target_pairs={{0,33},{1,32},{2,35},{3,34},{4,37},{5,36},{6,39},{7,38},{8,41},{9,... | collective-permute-start | bytes 1216520 | tf_op jit(solution)/shard_map/ppermute | solution.py:363
  79.5 1.4 collective-permute-start.16
  81.7 1.0 collective-permute-start.18
  82.7 1.0 copy-done.1
  83.7 4.3 %mix_tiles.5 = (bf16[6,256,256]{2,1,0:T(8,128)(2,1)S(1)}, bf16[6,256,256]{2,1,0:T(8,128)(2,1)S(1)}, bf16[6,256,256]{2,1,0:T(8,128)(2,1)S(1)}, bf16[6,256,256]{2,1,0:T(8,128)(2,1)S(1)}) custom-call(s32[1]{0:T(128)} %bitcast.5.refs_6_.at_ref, bf16[6,264,128]{2,1,0:T(8,128)(2,1)S(1)} %copy-done.1, bf16[6,264,128]{2,1,0:T(8,128)(2,1)S(1)} %collective-permute-done.26.refs_1_, ...), custom_call_target="tpu_custom_call" | custom-call | tf_op jit(solution)/shard_map/mix_tiles/pallas_call | solution.py:151
  88.1 3.1 %collective-permute-done.15.refs_3_ = bf16[6,264,128]{2,1,0:T(8,128)(2,1)S(1)} collective-permute-done((bf16[6,264,128]{2,1,0:T(8,128)(2,1)}, bf16[6,264,128]{2,1,0:T(8,128)(2,1)S(1)}, u32[]{:S(2)}, u32[]{:S(2)}) %collective-permute-start.15) | collective-permute-done | bytes 405536 | tf_op jit(solution)/shard_map/ppermute | solution.py:363
  91.2 2.3 %collective-permute-start.34 = (bf16[6,256,256]{2,1,0:T(8,128)(2,1)S(1)}, bf16[6,256,256]{2,1,0:T(8,128)(2,1)S(1)}, u32[]{:S(2)}, u32[]{:S(2)}) collective-permute-start(bf16[6,256,256]{2,1,0:T(8,128)(2,1)S(1)} %get-tuple-element.112), channel_id=1, source_target_pairs={{0,6},{1,7},{2,0},{3,1},{4,2},{5,3},{6,4},{7,5},{8,14},{9,15},{10,... | collective-permute-start | bytes 2359304 | tf_op jit(solution)/shard_map/ppermute | solution.py:363
  93.5 0.9 copy-done.2
  94.4 2.9 %mix_tiles.3 = (bf16[4,256,256]{2,1,0:T(8,128)(2,1)S(1)}, bf16[4,256,256]{2,1,0:T(8,128)(2,1)S(1)}, bf16[4,256,256]{2,1,0:T(8,128)(2,1)S(1)}, bf16[4,256,256]{2,1,0:T(8,128)(2,1)S(1)}) custom-call(s32[1]{0:T(128)} %bitcast.1.refs_7_.at_ref, bf16[4,264,128]{2,1,0:T(8,128)(2,1)S(1)} %copy-done.2, bf16[4,264,128]{2,1,0:T(8,128)(2,1)S(1)} %collective-permute-done.refs_1_, ...), custom_call_target="tpu_custom_call" | custom-call | tf_op jit(solution)/shard_map/mix_tiles/pallas_call | solution.py:151
  97.3 1.6 collective-permute-done.17.refs_5_
  100.0 12.2 %collective-permute-start.19 = (bf16[6,264,128]{2,1,0:T(8,128)(2,1)}, bf16[6,264,128]{2,1,0:T(8,128)(2,1)S(1)}, u32[]{:S(2)}, u32[]{:S(2)}) collective-permute-start(bf16[6,264,128]{2,1,0:T(8,128)(2,1)} %get-tuple-element.93), channel_id=1, source_target_pairs={{0,65},{1,64},{2,67},{3,66},{4,69},{5,68},{6,71},{7,70},{8,73},{9,... | collective-permute-start | bytes 1216520 | tf_op jit(solution)/shard_map/ppermute | solution.py:363
  112.2 21.0 %collective-permute-done.19.refs_7_ = bf16[6,264,128]{2,1,0:T(8,128)(2,1)S(1)} collective-permute-done((bf16[6,264,128]{2,1,0:T(8,128)(2,1)}, bf16[6,264,128]{2,1,0:T(8,128)(2,1)S(1)}, u32[]{:S(2)}, u32[]{:S(2)}) %collective-permute-start.19) | collective-permute-done | bytes 405536 | tf_op jit(solution)/shard_map/ppermute | solution.py:363
  133.2 1.0 copy-done
  134.2 4.3 %mix_tiles.4 = (bf16[6,256,256]{2,1,0:T(8,128)(2,1)S(1)}, bf16[6,256,256]{2,1,0:T(8,128)(2,1)S(1)}, bf16[6,256,256]{2,1,0:T(8,128)(2,1)S(1)}, bf16[6,256,256]{2,1,0:T(8,128)(2,1)S(1)}) custom-call(s32[1]{0:T(128)} %bitcast.at_ref.refs_6_, bf16[6,264,128]{2,1,0:T(8,128)(2,1)S(1)} %copy-done, bf16[6,264,128]{2,1,0:T(8,128)(2,1)S(1)} %collective-permute-done.13.refs_1_, ...), custom_call_target="tpu_custom_call" | custom-call | tf_op jit(solution)/shard_map/mix_tiles/pallas_call | solution.py:151
  138.7 3.0 %collective-permute-start.21 = (bf16[6,256,256]{2,1,0:T(8,128)(2,1)S(1)}, bf16[6,256,256]{2,1,0:T(8,128)(2,1)S(1)}, u32[]{:S(2)}, u32[]{:S(2)}) collective-permute-start(bf16[6,256,256]{2,1,0:T(8,128)(2,1)S(1)} %get-tuple-element.96), channel_id=1, source_target_pairs={{0,24},{1,25},{2,26},{3,27},{4,28},{5,29},{6,30},{7,31},{8,0},{9,1... | collective-permute-start | bytes 2359304 | tf_op jit(solution)/shard_map/ppermute | solution.py:363
  141.7 1.2 collective-permute-start.22
  143.5 11.9 %collective-permute-done.8.refs_2_ = bf16[4,256,256]{2,1,0:T(8,128)(2,1)S(1)} collective-permute-done((bf16[4,256,256]{2,1,0:T(8,128)(2,1)S(1)}, bf16[4,256,256]{2,1,0:T(8,128)(2,1)S(1)}, u32[]{:S(2)}, u32[]{:S(2)}) %collective-permute-start.8) | collective-permute-done | bytes 524320 | tf_op jit(solution)/shard_map/ppermute | solution.py:363
  155.4 1.6 collective-permute-done.9.refs_3_
  157.9 1.2 collective-permute-done.20.refs_1_
  159.0 1.2 collective-permute-start.11
  160.3 14.2 %collective-permute-done.21.refs_2_ = bf16[6,256,256]{2,1,0:T(8,128)(2,1)S(1)} collective-permute-done((bf16[6,256,256]{2,1,0:T(8,128)(2,1)S(1)}, bf16[6,256,256]{2,1,0:T(8,128)(2,1)S(1)}, u32[]{:S(2)}, u32[]{:S(2)}) %collective-permute-start.21) | collective-permute-done | bytes 786464 | tf_op jit(solution)/shard_map/ppermute | solution.py:363
  174.5 2.4 %collective-permute-done.22.refs_3_ = bf16[6,256,256]{2,1,0:T(8,128)(2,1)S(1)} collective-permute-done((bf16[6,256,256]{2,1,0:T(8,128)(2,1)S(1)}, bf16[6,256,256]{2,1,0:T(8,128)(2,1)S(1)}, u32[]{:S(2)}, u32[]{:S(2)}) %collective-permute-start.22) | collective-permute-done | bytes 786464 | tf_op jit(solution)/shard_map/ppermute | solution.py:363
  177.4 2.9 %collective-permute-done.10.refs_1_ = bf16[4,64,256]{2,1,0:T(8,128)(2,1)S(1)} collective-permute-done((bf16[4,64,256]{2,1,0:T(8,128)(2,1)S(1)}, bf16[4,64,256]{2,1,0:T(8,128)(2,1)S(1)}, u32[]{:S(2)}, u32[]{:S(2)}) %collective-permute-start.10) | collective-permute-done | bytes 131104 | tf_op jit(solution)/shard_map/ppermute | solution.py:363
  180.5 1.6 collective-permute-done.12.refs_3_
  182.1 2.3 %collective-permute-start.24 = (bf16[6,64,256]{2,1,0:T(8,128)(2,1)S(1)}, bf16[6,64,256]{2,1,0:T(8,128)(2,1)S(1)}, u32[]{:S(2)}, u32[]{:S(2)}) collective-permute-start(bf16[6,64,256]{2,1,0:T(8,128)(2,1)S(1)} %get-tuple-element.100), channel_id=1, source_target_pairs={{0,6},{1,7},{2,0},{3,1},{4,2},{5,3},{6,4},{7,5},{8,14},{9,15},{10,... | collective-permute-start | bytes 589832 | tf_op jit(solution)/shard_map/ppermute | solution.py:363
  184.4 10.6 %spread_squares.1 = (f32[640,32,256]{2,1,0:T(8,128)}, s32[1,1024]{1,0:T(1,128)}) custom-call(s32[1]{0:T(128)} %bitcast.6.me_ref, s32[128,128]{1,0:T(8,128)} %rows_ref.1, bf16[128,128]{1,0:T(8,128)(2,1)} %coef_ref.1, s32[1,1024]{1,0:T(1,128)} %bitcast.18), custom_call_target="tpu_custom_call" | custom-call | tf_op jit(solution)/shard_map/spread_squares/pallas_call | solution.py:252
  195.1 1.1 square_sums.1
  196.2 9.2 %all-to-all-start = ((f32[128,1,384]{2,1,0:T(1,128)}), f32[128,1,384]{2,1,0:T(1,128)S(1)}, u32[]{:S(2)}, u32[]{:S(2)}) async-start(f32[128,1,384]{2,1,0:T(1,128)} %square_sums.1), calls=%async_computation | async-start | bytes 393216 | tf_op jit(solution)/shard_map/all_to_all | solution.py:346
  205.6 10.2 %all-to-all-done.parts_ref = f32[128,1,384]{2,1,0:T(1,128)S(1)} async-done(((f32[128,1,384]{2,1,0:T(1,128)}), f32[128,1,384]{2,1,0:T(1,128)S(1)}, u32[]{:S(2)}, u32[]{:S(2)}) %all-to-all-start) | async-done | bytes 196640 | tf_op jit(solution)/shard_map/all_to_all | solution.py:346
  216.5 3.3 %finish.1 = (f32[1,8]{1,0:T(1,128)}, f32[8,128]{1,0:T(8,128)}, f32[32,256]{1,0:T(8,128)}) custom-call(s32[1]{0:T(128)S(6)} %copy.11.refs_4_.count_ref, f32[128,1,384]{2,1,0:T(1,128)S(1)} %all-to-all-done.parts_ref, f32[8,128]{1,0:T(8,128)S(1)} %bitcast.12, s32[128,1]{1,0:T(8,128)S(1)} %copy.10.sensor_ref, s32[1,1024]{1,0:T(1,128)S(1)} %copy-done.4, ...), custom_call_target="tpu_custom_call" | custom-call | tf_op jit(solution)/shard_map/finish/pallas_call | solution.py:326
  (56 shorter events, 6.7 us)
Async XLA Ops:
  0.6 204.8 %copy-start.5 = (s32[128]{0:T(128)S(1)}, s32[128]{0:T(128)}, u32[]{:S(2)}) copy-start(s32[128]{0:T(128)} %param.9) | copy-start | bytes 1540
  0.6 215.1 %copy-start.3 = (f32[1024]{0:T(1024)S(1)}, f32[1024]{0:T(1024)}, u32[]{:S(2)}) copy-start(f32[1024]{0:T(1024)} %param.13) | copy-start | bytes 12292
  12.4 15.6 %collective-permute-start = (bf16[4,264,128]{2,1,0:T(8,128)(2,1)}, bf16[4,264,128]{2,1,0:T(8,128)(2,1)S(1)}, u32[]{:S(2)}, u32[]{:S(2)}) collective-permute-start(bf16[4,264,128]{2,1,0:T(8,128)(2,1)} %get-tuple-element.71), channel_id=1, source_target_pairs={{0,1},{1,0},{2,3},{3,2},{4,5},{5,4},{6,7},{7,6},{8,9},{9,8},{10,11... | collective-permute-start | bytes 811016 | tf_op jit(solution)/shard_map/ppermute | solution.py:363
  13.8 14.2 %collective-permute-start.1 = (bf16[4,264,128]{2,1,0:T(8,128)(2,1)}, bf16[4,264,128]{2,1,0:T(8,128)(2,1)S(1)}, u32[]{:S(2)}, u32[]{:S(2)}) collective-permute-start(bf16[4,264,128]{2,1,0:T(8,128)(2,1)} %get-tuple-element.72), channel_id=1, source_target_pairs={{0,2},{1,3},{2,4},{3,5},{4,6},{5,7},{6,0},{7,1},{8,10},{9,11},{10,... | collective-permute-start | bytes 811016 | tf_op jit(solution)/shard_map/ppermute | solution.py:363
  15.6 14.9 %collective-permute-start.2 = (bf16[4,264,128]{2,1,0:T(8,128)(2,1)}, bf16[4,264,128]{2,1,0:T(8,128)(2,1)S(1)}, u32[]{:S(2)}, u32[]{:S(2)}) collective-permute-start(bf16[4,264,128]{2,1,0:T(8,128)(2,1)} %get-tuple-element.73), channel_id=1, source_target_pairs={{0,3},{1,2},{2,5},{3,4},{4,7},{5,6},{6,1},{7,0},{8,11},{9,10},{10,... | collective-permute-start | bytes 811016 | tf_op jit(solution)/shard_map/ppermute | solution.py:363
  17.5 14.6 %collective-permute-start.3 = (bf16[4,264,128]{2,1,0:T(8,128)(2,1)}, bf16[4,264,128]{2,1,0:T(8,128)(2,1)S(1)}, u32[]{:S(2)}, u32[]{:S(2)}) collective-permute-start(bf16[4,264,128]{2,1,0:T(8,128)(2,1)} %get-tuple-element.74), channel_id=1, source_target_pairs={{0,6},{1,7},{2,0},{3,1},{4,2},{5,3},{6,4},{7,5},{8,14},{9,15},{10,... | collective-permute-start | bytes 811016 | tf_op jit(solution)/shard_map/ppermute | solution.py:363
  18.5 15.5 %collective-permute-start.4 = (bf16[4,264,128]{2,1,0:T(8,128)(2,1)}, bf16[4,264,128]{2,1,0:T(8,128)(2,1)S(1)}, u32[]{:S(2)}, u32[]{:S(2)}) collective-permute-start(bf16[4,264,128]{2,1,0:T(8,128)(2,1)} %get-tuple-element.75), channel_id=1, source_target_pairs={{0,7},{1,6},{2,1},{3,0},{4,3},{5,2},{6,5},{7,4},{8,15},{9,14},{10,... | collective-permute-start | bytes 811016 | tf_op jit(solution)/shard_map/ppermute | solution.py:363
  28.0 20.4 %collective-permute-start.26 = (bf16[6,264,128]{2,1,0:T(8,128)(2,1)}, bf16[6,264,128]{2,1,0:T(8,128)(2,1)S(1)}, u32[]{:S(2)}, u32[]{:S(2)}) collective-permute-start(bf16[6,264,128]{2,1,0:T(8,128)(2,1)} %get-tuple-element.103), channel_id=1, source_target_pairs={{0,1},{1,0},{2,3},{3,2},{4,5},{5,4},{6,7},{7,6},{8,9},{9,8},{10,11... | collective-permute-start | bytes 1216520 | tf_op jit(solution)/shard_map/ppermute | solution.py:363
  28.1 20.9 %collective-permute-start.27 = (bf16[6,264,128]{2,1,0:T(8,128)(2,1)}, bf16[6,264,128]{2,1,0:T(8,128)(2,1)S(1)}, u32[]{:S(2)}, u32[]{:S(2)}) collective-permute-start(bf16[6,264,128]{2,1,0:T(8,128)(2,1)} %get-tuple-element.104), channel_id=1, source_target_pairs={{0,8},{1,9},{2,10},{3,11},{4,12},{5,13},{6,14},{7,15},{8,16},{9,17... | collective-permute-start | bytes 1216520 | tf_op jit(solution)/shard_map/ppermute | solution.py:363
  30.5 9.4 %collective-permute-start.5 = (bf16[4,264,128]{2,1,0:T(8,128)(2,1)}, bf16[4,264,128]{2,1,0:T(8,128)(2,1)S(1)}, u32[]{:S(2)}, u32[]{:S(2)}) collective-permute-start(bf16[4,264,128]{2,1,0:T(8,128)(2,1)} %get-tuple-element.76), channel_id=1, source_target_pairs={{0,4},{1,5},{2,6},{3,7},{4,0},{5,1},{6,2},{7,3},{8,12},{9,13},{10,... | collective-permute-start | bytes 811016 | tf_op jit(solution)/shard_map/ppermute | solution.py:363
  32.1 14.1 %collective-permute-start.6 = (bf16[4,264,128]{2,1,0:T(8,128)(2,1)}, bf16[4,264,128]{2,1,0:T(8,128)(2,1)S(1)}, u32[]{:S(2)}, u32[]{:S(2)}) collective-permute-start(bf16[4,264,128]{2,1,0:T(8,128)(2,1)} %get-tuple-element.77), channel_id=1, source_target_pairs={{0,5},{1,4},{2,7},{3,6},{4,1},{5,0},{6,3},{7,2},{8,13},{9,12},{10,... | collective-permute-start | bytes 811016 | tf_op jit(solution)/shard_map/ppermute | solution.py:363
  34.0 18.2 %collective-permute-start.28 = (bf16[6,264,128]{2,1,0:T(8,128)(2,1)}, bf16[6,264,128]{2,1,0:T(8,128)(2,1)S(1)}, u32[]{:S(2)}, u32[]{:S(2)}) collective-permute-start(bf16[6,264,128]{2,1,0:T(8,128)(2,1)} %get-tuple-element.105), channel_id=1, source_target_pairs={{0,9},{1,8},{2,11},{3,10},{4,13},{5,12},{6,15},{7,14},{8,17},{9,16... | collective-permute-start | bytes 1216520 | tf_op jit(solution)/shard_map/ppermute | solution.py:363
  39.8 12.4 %collective-permute-start.29 = (bf16[6,264,128]{2,1,0:T(8,128)(2,1)}, bf16[6,264,128]{2,1,0:T(8,128)(2,1)S(1)}, u32[]{:S(2)}, u32[]{:S(2)}) collective-permute-start(bf16[6,264,128]{2,1,0:T(8,128)(2,1)} %get-tuple-element.106), channel_id=1, source_target_pairs={{0,24},{1,25},{2,26},{3,27},{4,28},{5,29},{6,30},{7,31},{8,0},{9,1... | collective-permute-start | bytes 1216520 | tf_op jit(solution)/shard_map/ppermute | solution.py:363
  46.2 16.5 %collective-permute-start.30 = (bf16[6,264,128]{2,1,0:T(8,128)(2,1)}, bf16[6,264,128]{2,1,0:T(8,128)(2,1)S(1)}, u32[]{:S(2)}, u32[]{:S(2)}) collective-permute-start(bf16[6,264,128]{2,1,0:T(8,128)(2,1)} %get-tuple-element.107), channel_id=1, source_target_pairs={{0,25},{1,24},{2,27},{3,26},{4,29},{5,28},{6,31},{7,30},{8,1},{9,0... | collective-permute-start | bytes 1216520 | tf_op jit(solution)/shard_map/ppermute | solution.py:363
  48.4 31.1 %collective-permute-start.31 = (bf16[6,264,128]{2,1,0:T(8,128)(2,1)}, bf16[6,264,128]{2,1,0:T(8,128)(2,1)S(1)}, u32[]{:S(2)}, u32[]{:S(2)}) collective-permute-start(bf16[6,264,128]{2,1,0:T(8,128)(2,1)} %get-tuple-element.108), channel_id=1, source_target_pairs={{0,16},{1,17},{2,18},{3,19},{4,20},{5,21},{6,22},{7,23},{8,24},{9,... | collective-permute-start | bytes 1216520 | tf_op jit(solution)/shard_map/ppermute | solution.py:363
  49.0 31.9 %collective-permute-start.32 = (bf16[6,264,128]{2,1,0:T(8,128)(2,1)}, bf16[6,264,128]{2,1,0:T(8,128)(2,1)S(1)}, u32[]{:S(2)}, u32[]{:S(2)}) collective-permute-start(bf16[6,264,128]{2,1,0:T(8,128)(2,1)} %get-tuple-element.109), channel_id=1, source_target_pairs={{0,17},{1,16},{2,19},{3,18},{4,21},{5,20},{6,23},{7,22},{8,25},{9,... | collective-permute-start | bytes 1216520 | tf_op jit(solution)/shard_map/ppermute | solution.py:363
  52.2 29.5 %collective-permute-start.13 = (bf16[6,264,128]{2,1,0:T(8,128)(2,1)}, bf16[6,264,128]{2,1,0:T(8,128)(2,1)S(1)}, u32[]{:S(2)}, u32[]{:S(2)}) collective-permute-start(bf16[6,264,128]{2,1,0:T(8,128)(2,1)} %get-tuple-element.87), channel_id=1, source_target_pairs={{0,1},{1,0},{2,3},{3,2},{4,5},{5,4},{6,7},{7,6},{8,9},{9,8},{10,11... | collective-permute-start | bytes 1216520 | tf_op jit(solution)/shard_map/ppermute | solution.py:363
  52.2 35.8 %collective-permute-start.14 = (bf16[6,264,128]{2,1,0:T(8,128)(2,1)}, bf16[6,264,128]{2,1,0:T(8,128)(2,1)S(1)}, u32[]{:S(2)}, u32[]{:S(2)}) collective-permute-start(bf16[6,264,128]{2,1,0:T(8,128)(2,1)} %get-tuple-element.88), channel_id=1, source_target_pairs={{0,32},{1,33},{2,34},{3,35},{4,36},{5,37},{6,38},{7,39},{8,40},{9,... | collective-permute-start | bytes 1216520 | tf_op jit(solution)/shard_map/ppermute | solution.py:363
  62.7 28.5 %collective-permute-start.15 = (bf16[6,264,128]{2,1,0:T(8,128)(2,1)}, bf16[6,264,128]{2,1,0:T(8,128)(2,1)S(1)}, u32[]{:S(2)}, u32[]{:S(2)}) collective-permute-start(bf16[6,264,128]{2,1,0:T(8,128)(2,1)} %get-tuple-element.89), channel_id=1, source_target_pairs={{0,33},{1,32},{2,35},{3,34},{4,37},{5,36},{6,39},{7,38},{8,41},{9,... | collective-permute-start | bytes 1216520 | tf_op jit(solution)/shard_map/ppermute | solution.py:363
  79.5 14.0 %collective-permute-start.16 = (bf16[6,264,128]{2,1,0:T(8,128)(2,1)}, bf16[6,264,128]{2,1,0:T(8,128)(2,1)S(1)}, u32[]{:S(2)}, u32[]{:S(2)}) collective-permute-start(bf16[6,264,128]{2,1,0:T(8,128)(2,1)} %get-tuple-element.90), channel_id=1, source_target_pairs={{0,96},{1,97},{2,98},{3,99},{4,100},{5,101},{6,102},{7,103},{8,104... | collective-permute-start | bytes 1216520 | tf_op jit(solution)/shard_map/ppermute | solution.py:363
  80.9 18.1 %collective-permute-start.17 = (bf16[6,264,128]{2,1,0:T(8,128)(2,1)}, bf16[6,264,128]{2,1,0:T(8,128)(2,1)S(1)}, u32[]{:S(2)}, u32[]{:S(2)}) collective-permute-start(bf16[6,264,128]{2,1,0:T(8,128)(2,1)} %get-tuple-element.91), channel_id=1, source_target_pairs={{0,97},{1,96},{2,99},{3,98},{4,101},{5,100},{6,103},{7,102},{8,105... | collective-permute-start | bytes 1216520 | tf_op jit(solution)/shard_map/ppermute | solution.py:363
  81.7 18.3 %collective-permute-start.18 = (bf16[6,264,128]{2,1,0:T(8,128)(2,1)}, bf16[6,264,128]{2,1,0:T(8,128)(2,1)S(1)}, u32[]{:S(2)}, u32[]{:S(2)}) collective-permute-start(bf16[6,264,128]{2,1,0:T(8,128)(2,1)} %get-tuple-element.92), channel_id=1, source_target_pairs={{0,64},{1,65},{2,66},{3,67},{4,68},{5,69},{6,70},{7,71},{8,72},{9,... | collective-permute-start | bytes 1216520 | tf_op jit(solution)/shard_map/ppermute | solution.py:363
  82.7 1.0 copy-start.1
  88.0 53.6 %collective-permute-start.33 = (bf16[6,256,256]{2,1,0:T(8,128)(2,1)S(1)}, bf16[6,256,256]{2,1,0:T(8,128)(2,1)S(1)}, u32[]{:S(2)}, u32[]{:S(2)}) collective-permute-start(bf16[6,256,256]{2,1,0:T(8,128)(2,1)S(1)} %get-tuple-element.111), channel_id=1, source_target_pairs={{0,2},{1,3},{2,4},{3,5},{4,6},{5,7},{6,0},{7,1},{8,10},{9,11},{10,... | collective-permute-start | bytes 2359304 | tf_op jit(solution)/shard_map/ppermute | solution.py:363
  91.2 51.6 %collective-permute-start.34 = (bf16[6,256,256]{2,1,0:T(8,128)(2,1)S(1)}, bf16[6,256,256]{2,1,0:T(8,128)(2,1)S(1)}, u32[]{:S(2)}, u32[]{:S(2)}) collective-permute-start(bf16[6,256,256]{2,1,0:T(8,128)(2,1)S(1)} %get-tuple-element.112), channel_id=1, source_target_pairs={{0,6},{1,7},{2,0},{3,1},{4,2},{5,3},{6,4},{7,5},{8,14},{9,15},{10,... | collective-permute-start | bytes 2359304 | tf_op jit(solution)/shard_map/ppermute | solution.py:363
  93.5 49.4 %collective-permute-start.35 = (bf16[6,256,256]{2,1,0:T(8,128)(2,1)S(1)}, bf16[6,256,256]{2,1,0:T(8,128)(2,1)S(1)}, u32[]{:S(2)}, u32[]{:S(2)}) collective-permute-start(bf16[6,256,256]{2,1,0:T(8,128)(2,1)S(1)} %get-tuple-element.113), channel_id=1, source_target_pairs={{0,4},{1,5},{2,6},{3,7},{4,0},{5,1},{6,2},{7,3},{8,12},{9,13},{10,... | collective-permute-start | bytes 2359304 | tf_op jit(solution)/shard_map/ppermute | solution.py:363
  93.5 1.0 copy-start.2
  99.0 39.7 %collective-permute-start.7 = (bf16[4,256,256]{2,1,0:T(8,128)(2,1)S(1)}, bf16[4,256,256]{2,1,0:T(8,128)(2,1)S(1)}, u32[]{:S(2)}, u32[]{:S(2)}) collective-permute-start(bf16[4,256,256]{2,1,0:T(8,128)(2,1)S(1)} %get-tuple-element.79), channel_id=1, source_target_pairs={{0,32},{1,33},{2,34},{3,35},{4,36},{5,37},{6,38},{7,39},{8,40},{9,... | collective-permute-start | bytes 1572872 | tf_op jit(solution)/shard_map/ppermute | solution.py:363
  100.0 33.3 %collective-permute-start.19 = (bf16[6,264,128]{2,1,0:T(8,128)(2,1)}, bf16[6,264,128]{2,1,0:T(8,128)(2,1)S(1)}, u32[]{:S(2)}, u32[]{:S(2)}) collective-permute-start(bf16[6,264,128]{2,1,0:T(8,128)(2,1)} %get-tuple-element.93), channel_id=1, source_target_pairs={{0,65},{1,64},{2,67},{3,66},{4,69},{5,68},{6,71},{7,70},{8,73},{9,... | collective-permute-start | bytes 1216520 | tf_op jit(solution)/shard_map/ppermute | solution.py:363
  133.2 1.0 copy-start
  138.6 20.5 %collective-permute-start.20 = (bf16[6,256,256]{2,1,0:T(8,128)(2,1)S(1)}, bf16[6,256,256]{2,1,0:T(8,128)(2,1)S(1)}, u32[]{:S(2)}, u32[]{:S(2)}) collective-permute-start(bf16[6,256,256]{2,1,0:T(8,128)(2,1)S(1)} %get-tuple-element.95), channel_id=1, source_target_pairs={{0,8},{1,9},{2,10},{3,11},{4,12},{5,13},{6,14},{7,15},{8,16},{9,17... | collective-permute-start | bytes 2359304 | tf_op jit(solution)/shard_map/ppermute | solution.py:363
  138.7 35.8 %collective-permute-start.21 = (bf16[6,256,256]{2,1,0:T(8,128)(2,1)S(1)}, bf16[6,256,256]{2,1,0:T(8,128)(2,1)S(1)}, u32[]{:S(2)}, u32[]{:S(2)}) collective-permute-start(bf16[6,256,256]{2,1,0:T(8,128)(2,1)S(1)} %get-tuple-element.96), channel_id=1, source_target_pairs={{0,24},{1,25},{2,26},{3,27},{4,28},{5,29},{6,30},{7,31},{8,0},{9,1... | collective-permute-start | bytes 2359304 | tf_op jit(solution)/shard_map/ppermute | solution.py:363
  141.7 35.2 %collective-permute-start.22 = (bf16[6,256,256]{2,1,0:T(8,128)(2,1)S(1)}, bf16[6,256,256]{2,1,0:T(8,128)(2,1)S(1)}, u32[]{:S(2)}, u32[]{:S(2)}) collective-permute-start(bf16[6,256,256]{2,1,0:T(8,128)(2,1)S(1)} %get-tuple-element.97), channel_id=1, source_target_pairs={{0,16},{1,17},{2,18},{3,19},{4,20},{5,21},{6,22},{7,23},{8,24},{9,... | collective-permute-start | bytes 2359304 | tf_op jit(solution)/shard_map/ppermute | solution.py:363
  142.8 12.5 %collective-permute-start.8 = (bf16[4,256,256]{2,1,0:T(8,128)(2,1)S(1)}, bf16[4,256,256]{2,1,0:T(8,128)(2,1)S(1)}, u32[]{:S(2)}, u32[]{:S(2)}) collective-permute-start(bf16[4,256,256]{2,1,0:T(8,128)(2,1)S(1)} %get-tuple-element.80), channel_id=1, source_target_pairs={{0,96},{1,97},{2,98},{3,99},{4,100},{5,101},{6,102},{7,103},{8,104... | collective-permute-start | bytes 1572872 | tf_op jit(solution)/shard_map/ppermute | solution.py:363
  142.8 14.1 %collective-permute-start.9 = (bf16[4,256,256]{2,1,0:T(8,128)(2,1)S(1)}, bf16[4,256,256]{2,1,0:T(8,128)(2,1)S(1)}, u32[]{:S(2)}, u32[]{:S(2)}) collective-permute-start(bf16[4,256,256]{2,1,0:T(8,128)(2,1)S(1)} %get-tuple-element.81), channel_id=1, source_target_pairs={{0,64},{1,65},{2,66},{3,67},{4,68},{5,69},{6,70},{7,71},{8,72},{9,... | collective-permute-start | bytes 1572872 | tf_op jit(solution)/shard_map/ppermute | solution.py:363
  155.4 29.0 %collective-permute-start.36 = (bf16[6,64,256]{2,1,0:T(8,128)(2,1)S(1)}, bf16[6,64,256]{2,1,0:T(8,128)(2,1)S(1)}, u32[]{:S(2)}, u32[]{:S(2)}) collective-permute-start(bf16[6,64,256]{2,1,0:T(8,128)(2,1)S(1)} %get-tuple-element.115), channel_id=1, source_target_pairs={{0,32},{1,33},{2,34},{3,35},{4,36},{5,37},{6,38},{7,39},{8,40},{9,... | collective-permute-start | bytes 589832 | tf_op jit(solution)/shard_map/ppermute | solution.py:363
  157.3 23.0 %collective-permute-start.10 = (bf16[4,64,256]{2,1,0:T(8,128)(2,1)S(1)}, bf16[4,64,256]{2,1,0:T(8,128)(2,1)S(1)}, u32[]{:S(2)}, u32[]{:S(2)}) collective-permute-start(bf16[4,64,256]{2,1,0:T(8,128)(2,1)S(1)} %get-tuple-element.83), channel_id=1, source_target_pairs={{0,8},{1,9},{2,10},{3,11},{4,12},{5,13},{6,14},{7,15},{8,16},{9,17... | collective-permute-start | bytes 393224 | tf_op jit(solution)/shard_map/ppermute | solution.py:363
  159.0 21.5 %collective-permute-start.11 = (bf16[4,64,256]{2,1,0:T(8,128)(2,1)S(1)}, bf16[4,64,256]{2,1,0:T(8,128)(2,1)S(1)}, u32[]{:S(2)}, u32[]{:S(2)}) collective-permute-start(bf16[4,64,256]{2,1,0:T(8,128)(2,1)S(1)} %get-tuple-element.84), channel_id=1, source_target_pairs={{0,24},{1,25},{2,26},{3,27},{4,28},{5,29},{6,30},{7,31},{8,0},{9,1... | collective-permute-start | bytes 393224 | tf_op jit(solution)/shard_map/ppermute | solution.py:363
  174.5 7.6 %collective-permute-start.12 = (bf16[4,64,256]{2,1,0:T(8,128)(2,1)S(1)}, bf16[4,64,256]{2,1,0:T(8,128)(2,1)S(1)}, u32[]{:S(2)}, u32[]{:S(2)}) collective-permute-start(bf16[4,64,256]{2,1,0:T(8,128)(2,1)S(1)} %get-tuple-element.85), channel_id=1, source_target_pairs={{0,16},{1,17},{2,18},{3,19},{4,20},{5,21},{6,22},{7,23},{8,24},{9,... | collective-permute-start | bytes 393224 | tf_op jit(solution)/shard_map/ppermute | solution.py:363
  176.9 18.1 %collective-permute-start.37 = (bf16[6,64,256]{2,1,0:T(8,128)(2,1)S(1)}, bf16[6,64,256]{2,1,0:T(8,128)(2,1)S(1)}, u32[]{:S(2)}, u32[]{:S(2)}) collective-permute-start(bf16[6,64,256]{2,1,0:T(8,128)(2,1)S(1)} %get-tuple-element.116), channel_id=1, source_target_pairs={{0,96},{1,97},{2,98},{3,99},{4,100},{5,101},{6,102},{7,103},{8,104... | collective-permute-start | bytes 589832 | tf_op jit(solution)/shard_map/ppermute | solution.py:363
  180.3 14.7 %collective-permute-start.38 = (bf16[6,64,256]{2,1,0:T(8,128)(2,1)S(1)}, bf16[6,64,256]{2,1,0:T(8,128)(2,1)S(1)}, u32[]{:S(2)}, u32[]{:S(2)}) collective-permute-start(bf16[6,64,256]{2,1,0:T(8,128)(2,1)S(1)} %get-tuple-element.117), channel_id=1, source_target_pairs={{0,64},{1,65},{2,66},{3,67},{4,68},{5,69},{6,70},{7,71},{8,72},{9,... | collective-permute-start | bytes 589832 | tf_op jit(solution)/shard_map/ppermute | solution.py:363
  180.5 14.5 %collective-permute-start.23 = (bf16[6,64,256]{2,1,0:T(8,128)(2,1)S(1)}, bf16[6,64,256]{2,1,0:T(8,128)(2,1)S(1)}, u32[]{:S(2)}, u32[]{:S(2)}) collective-permute-start(bf16[6,64,256]{2,1,0:T(8,128)(2,1)S(1)} %get-tuple-element.99), channel_id=1, source_target_pairs={{0,2},{1,3},{2,4},{3,5},{4,6},{5,7},{6,0},{7,1},{8,10},{9,11},{10,... | collective-permute-start | bytes 589832 | tf_op jit(solution)/shard_map/ppermute | solution.py:363
  182.1 12.9 %collective-permute-start.24 = (bf16[6,64,256]{2,1,0:T(8,128)(2,1)S(1)}, bf16[6,64,256]{2,1,0:T(8,128)(2,1)S(1)}, u32[]{:S(2)}, u32[]{:S(2)}) collective-permute-start(bf16[6,64,256]{2,1,0:T(8,128)(2,1)S(1)} %get-tuple-element.100), channel_id=1, source_target_pairs={{0,6},{1,7},{2,0},{3,1},{4,2},{5,3},{6,4},{7,5},{8,14},{9,15},{10,... | collective-permute-start | bytes 589832 | tf_op jit(solution)/shard_map/ppermute | solution.py:363
  184.4 10.6 %collective-permute-start.25 = (bf16[6,64,256]{2,1,0:T(8,128)(2,1)S(1)}, bf16[6,64,256]{2,1,0:T(8,128)(2,1)S(1)}, u32[]{:S(2)}, u32[]{:S(2)}) collective-permute-start(bf16[6,64,256]{2,1,0:T(8,128)(2,1)S(1)} %get-tuple-element.101), channel_id=1, source_target_pairs={{0,4},{1,5},{2,6},{3,7},{4,0},{5,1},{6,2},{7,3},{8,12},{9,13},{10,... | collective-permute-start | bytes 589832 | tf_op jit(solution)/shard_map/ppermute | solution.py:363
  196.2 19.6 %all-to-all-start = ((f32[128,1,384]{2,1,0:T(1,128)}), f32[128,1,384]{2,1,0:T(1,128)S(1)}, u32[]{:S(2)}, u32[]{:S(2)}) async-start(f32[128,1,384]{2,1,0:T(1,128)} %square_sums.1), calls=%async_computation | async-start | bytes 393216 | tf_op jit(solution)/shard_map/all_to_all | solution.py:346
  215.8 0.7 copy-start.4

commit v9 on v8

--- a/solution.py
+++ b/solution.py
@@ -11,7 +11,7 @@
 SPD = 8
 AXES = ("y", "x", "z", "core")
 ORDERS = (("z", "y", "x"), ("y", "x", "z"), ("x", "z", "y"))
-EACH = (4, 6, 6)
+EACH = (5, 5, 6)
 PEERS = ((0, 0), (0, 1), (1, 0), (1, 1), (3, 0), (3, 1), (2, 0), (2, 1))
 SHIFTS = (0, 1, 3, 2)
 SIDE = 8
@@ -34,7 +34,8 @@
     parts = 8
     step = n // parts
     n_at = len(places)
-    n_out = len(flows) * len(PEERS)
+    n_out = sum(1 if axis is None else len(PEERS) for _, _, axis in flows)
+    n_copy = len(flows) * len(PEERS)
 
     def body(*refs):
         x_hbm, rows_hbm, coef_ref, sensor_ref, count_ref, core_ref = refs[:6]
@@ -74,9 +75,14 @@
             lax.fori_loop(0, step // ch, conv, 0)
         doubled.wait()
         copies = []
+        free = list(outs)
         for f, (first, each, axis) in enumerate(flows):
+            taken = [free.pop(0) for _ in range(1 if axis is None else len(PEERS))]
             for p, (shift, flip) in enumerate(PEERS):
-                base = first + member(core_ref, at_refs[axis], shift, flip) * each
+                if axis is None:
+                    base, to = first + p * each, taken[0].at[p]
+                else:
+                    base, to = first + member(core_ref, at_refs[axis], shift, flip) * each, taken[p]
                 pack = packs[f].at[p]
 
                 def channel(i, c):
@@ -91,8 +97,7 @@
                     return c
 
                 lax.fori_loop(0, each, channel, 0)
-                at = f * len(PEERS) + p
-                copies.append(pltpu.make_async_copy(pack, outs[at], out_sem.at[at]))
+                copies.append(pltpu.make_async_copy(pack, to, out_sem.at[len(copies)]))
                 copies[-1].start()
         for copy in copies:
             copy.wait()
@@ -114,10 +119,14 @@
             pltpu.VMEM((foot, nblk), F32),
             pltpu.VMEM((SIDE, nblk), F32),
             pltpu.SemaphoreType.DMA((parts + 2,)),
-            pltpu.SemaphoreType.DMA((n_out,)),
+            pltpu.SemaphoreType.DMA((n_copy,)),
         ]
         + [pltpu.VMEM((len(PEERS),) + s, BF16) for s in shapes],
-        out_shape=[jax.ShapeDtypeStruct(s, BF16) for s in shapes for _ in PEERS],
+        out_shape=[
+            jax.ShapeDtypeStruct(s, BF16)
+            for shape, (_, _, axis) in zip(shapes, flows)
+            for s in ([(len(PEERS),) + shape] if axis is None else [shape] * len(PEERS))
+        ],
         compiler_params=pltpu.CompilerParams(vmem_limit_bytes=VMEM),
         name="gather_flows",
     )(probes, rows, coef, sensor, count, core, *places)
@@ -159,6 +168,68 @@
     )(at, *tiles)
 
 
+def mix_members(tiles, n_sens):
+    n, each, rows, half = tiles.shape
+    ns = half
+
+    def body(data, out):
+        x = jnp.concatenate(
+            [
+                jnp.concatenate([data[t, 0, :ns] for t in range(n)], axis=0),
+                jnp.concatenate([data[t, 0, ns : 2 * ns] for t in range(n)], axis=0),
+            ],
+            axis=1,
+        )
+        side = [data[t, 0, 2 * ns :].astype(F32) for t in range(n)]
+        coef, high, low = (jnp.concatenate([s[i : i + 1] for s in side], axis=1) for i in range(3))
+        coef = coef.astype(BF16)
+        sub = lax.broadcasted_iota(I32, (MB, n * ns), 0).astype(F32).astype(BF16)
+        for q in range(4):
+            wanted = jnp.where(high == q, low, -1.0).astype(BF16)
+            mixer = jnp.where(sub == wanted, coef, jnp.zeros((), BF16))
+            out[q, 0] = jnp.dot(mixer, x, preferred_element_type=F32).astype(BF16)
+
+    shape = (4, each, n_sens // 4, 2 * half)
+    return pl.pallas_call(
+        body,
+        grid=(each,),
+        in_specs=[pl.BlockSpec((n, 1, rows, half), lambda i: (0, i, 0, 0))],
+        out_specs=pl.BlockSpec((4, 1) + shape[2:], lambda i: (0, i, 0, 0)),
+        out_shape=jax.ShapeDtypeStruct(shape, BF16),
+        compiler_params=pltpu.CompilerParams(
+            dimension_semantics=("arbitrary",), vmem_limit_bytes=24 * 1024 * 1024
+        ),
+        name="mix_members",
+    )(tiles)
+
+
+def add_members(quarters):
+    n, each, n_sens, width = quarters.shape
+    piece = n_sens // 4
+
+    def body(data, out):
+        def channel(i, c):
+            total = data[0, i].astype(F32)
+            for t in range(1, n):
+                total += data[t, i].astype(F32)
+            total = total.astype(BF16)
+            for q in range(4):
+                out[q, i] = total[q * piece : (q + 1) * piece]
+            return c
+
+        lax.fori_loop(0, each, channel, 0)
+
+    vmem = pl.BlockSpec(memory_space=pltpu.VMEM)
+    return pl.pallas_call(
+        body,
+        in_specs=[vmem],
+        out_specs=vmem,
+        out_shape=jax.ShapeDtypeStruct((4, each, piece, width), BF16),
+        compiler_params=pltpu.CompilerParams(vmem_limit_bytes=24 * 1024 * 1024),
+        name="add_members",
+    )(quarters)
+
+
 def add_quarters(quarters, at):
     each, n_sens, width = quarters[0].shape
     piece = n_sens // 4
@@ -189,14 +260,18 @@
 
 
 def square_sums(flows, n_dev):
-    n = len(flows)
-    piece = flows[0][0].shape[1]
+    counts = [len(four) if isinstance(four, list) else 1 for four in flows]
+    args = [x for four in flows for x in (four if isinstance(four, list) else [four])]
+    piece = args[0].shape[-2]
 
     def body(*refs):
         out = refs[-1]
+        free = list(refs[:-1])
         lanes = []
-        for f in range(n):
-            four = refs[4 * f : 4 * f + 4]
+        for count in counts:
+            four = [free.pop(0) for _ in range(count)]
+            if count == 1:
+                four = [four[0].at[t] for t in range(4)]
             total = jnp.zeros((piece, 128), F32)
             for i in range(four[0].shape[0]):
                 y = four[0][i].astype(F32) + four[1][i].astype(F32) + four[2][i].astype(F32) + four[3][i].astype(F32)
@@ -208,10 +283,10 @@
 
     return pl.pallas_call(
         body,
-        out_shape=jax.ShapeDtypeStruct((n_dev, 1, 128 * n), F32),
+        out_shape=jax.ShapeDtypeStruct((n_dev, 1, 128 * len(flows)), F32),
         compiler_params=pltpu.CompilerParams(vmem_limit_bytes=24 * 1024 * 1024),
         name="square_sums",
-    )(*[x for four in flows for x in four])
+    )(*args)
 
 
 def spread_squares(rows, coef, owner, me, tile_r, tile_c, sb=8):
@@ -376,14 +451,19 @@
     firsts = [8 * sum(EACH[:f]) for f in range(3)]
     tiles = [None] * 3
     flows = [None] * 3
+    packs = [(firsts[f], EACH[f], i) for i, f in enumerate((2, 1))] + [(firsts[0], EACH[0], None)]
+    sent = gather_flows(flat, *tile, packs, [at[ORDERS[f][0]] for f in (2, 1)])
     maps, pos = spread_squares(blk_rows, coef, owner.reshape(1, n_sens), me, tile_r, tile_c)
-    for group in ((2,), (0, 1)):
-        packs = [(firsts[f], EACH[f], i) for i, f in enumerate(group)]
-        sent = gather_flows(flat, *tile, packs, [at[ORDERS[f][0]] for f in group])
-        for i, f in enumerate(group):
-            tiles[f] = [shift_to(x, ORDERS[f][0], *peer) for x, peer in zip(sent[8 * i : 8 * i + 8], PEERS)]
-    for f, (_, b, c) in enumerate(ORDERS):
-        quarters = mix_tiles(tiles[f], at[b], n_sens)
+    for f, (a, b, c) in enumerate(ORDERS):
+        if f == 0:
+            tiles = exchange(sent[-1], (a, "core"))
+            quarters = mix_members(tiles, n_sens)
+            quarters = exchange(quarters, b)
+            pieces = add_members(quarters)
+            flows[f] = exchange(pieces, c)
+            continue
+        tiles = [shift_to(x, a, *peer) for x, peer in zip(sent[8 * (2 - f) :], PEERS)]
+        quarters = mix_tiles(tiles, at[b], n_sens)
         quarters = [shift_to(x, b, s, 0) for x, s in zip(quarters, SHIFTS)]
         pieces = add_quarters(quarters, at[c])
         flows[f] = [shift_to(x, c, s, 0) for x, s in zip(pieces, SHIFTS)]

time: 221 us -> 273 us (1.24)
  blocking collectives: 0 us -> 39.7 us
  local copies, waits for them, and re-layouts: 3.76 us -> 15 us
  starting transfers between devices: 76.2 us -> 67.9 us
  waiting for transfers between devices: 91 us -> 95.7 us
  Pallas kernels: 47.2 us -> 51.4 us
    all_to_all x0 -> x1, blocking collectives: none -> 39.7 us  [exchange(): return lax.all_to_all(x, axes, split_axis=0, concat_axis=0, tiled=True)]
    ppermute x39 -> x26, starting transfers between devices: 67 us -> 48.5 us  [shift_to(): return lax.ppermute(x, AXES, pairs)]
    unnamed x12 -> x42, local copies, waits for them, and re-layouts: 3.65 us -> 14.9 us
    all_to_all x1 -> x3, starting transfers between devices: 9.25 us -> 19.4 us  [exchange(): return lax.all_to_all(x, axes, split_axis=0, concat_axis=0, tiled=True)]
    pallas_call x1 -> x3, Pallas kernels: 1.13 us -> 6.28 us  [the longest x1 3.96 us: mix_members(): pl.pallas_call(body, grid=(each,), in_specs=[pl.BlockSpec((n, 1, rows, ha...]
    ppermute x39 -> x26, waiting for transfers between devices: 80.8 us -> 85.5 us  [shift_to(): return lax.ppermute(x, AXES, pairs)]
    pallas_call x2 -> x1, Pallas kernels: 19.3 us -> 15.1 us  [gather_flows(): pl.pallas_call(body, in_specs=[hbm, hbm, vmem, vmem, smem, smem] + [smem]...]
    pallas_call x3 -> x2, Pallas kernels: 1.41 us -> 5.45 us  [add_quarters(): pl.pallas_call(body, in_specs=[pl.BlockSpec(memory_space=pltpu.SMEM)] + [...]
  transfers between devices with their start and end apart: 40 -> 29, of which waited for: 16 -> 11; matrix products, arithmetic and copies ran while one was open for 0% -> 0% of each run, Pallas kernels for 14% -> 10%
where the time goes in v9:
time: 273 us; the launch traced here: 271 us
  waiting for transfers between devices  95.7 us (35%)
  starting transfers between devices  67.9 us (25%)
  Pallas kernels  51.4 us (19%)
  blocking collectives  39.7 us (15%)
  local copies, waits for them, and re-layouts  15 us (5%)
    ppermute x26, waiting for transfers between devices, shift_to(): return lax.ppermute(x, AXES, pairs)  85.5 us
    ppermute x26, starting transfers between devices, shift_to(): return lax.ppermute(x, AXES, pairs)  48.5 us
    all_to_all x1, blocking collectives, exchange(): return lax.all_to_all(x, axes, split_axis=0, concat_axis=0, tiled=True)  39.7 us
    all_to_all x3, starting transfers between devices, exchange(): return lax.all_to_all(x, axes, split_axis=0, concat_axis=0, tiled=True)  19.4 us
    pallas_call x1, Pallas kernels, gather_flows(): pl.pallas_call(body, in_specs=[hbm, hbm, vmem, vmem, smem, smem] + [smem]...  15.1 us
    unnamed x42, local copies, waits for them, and re-layouts  14.9 us
    pallas_call x2, Pallas kernels, mix_tiles(): pl.pallas_call(body, grid=(each,), in_specs=[pl.BlockSpec(memory_space=pl...  10.7 us
    pallas_call x1, Pallas kernels, spread_squares(): pl.pallas_call(body, grid=(nblk // sb,), in_specs=[pl.BlockSpec(memory_sp...  10.6 us
  transfers between devices with their start and end apart: 29, of which 11 were waited for; matrix products, arithmetic and copies ran while one was open for 0% of the time, Pallas kernels for 10%

profile of v9, /device:TPU:1, one launch (start us, length us, event | category | flops | bytes accessed | tf_op | source)
XLA Modules:
  0.0 271.3 jit_solution(2549113989134197976)
XLA Ops:
  1.3 15.1 %gather_flows.1 = (bf16[6,264,128]{2,1,0:T(8,128)(2,1)}, bf16[6,264,128]{2,1,0:T(8,128)(2,1)}, bf16[6,264,128]{2,1,0:T(8,128)(2,1)}, bf16[6,264,128]{2,1,0:T(8,1...) custom-call(bf16[8192,256]{1,0:T(8,128)(2,1)} %bitcast.13, ...), custom_call_target="tpu_custom_call" | custom-call | tf_op jit(solution)/shard_map/gather_flows/pallas_call | solution.py:109
  16.4 39.7 %all_to_all.20.data = bf16[8,5,264,128]{3,2,1,0:T(8,128)(2,1)S(1)} all-to-all(bf16[8,5,264,128]{3,2,1,0:T(8,128)(2,1)} %get-tuple-element.52), channel_id=1, replica_groups=mesh['y'=4,'x'=4,'z'=4,'core'=2] {'z','core'}, dimensions={0} | all-to-all | bytes 5406720 | tf_op jit(solution)/shard_map/all_to_all | solution.py:421
  56.1 4.0 %mix_members.1 = bf16[4,5,256,256]{3,2,1,0:T(8,128)(2,1)S(1)} custom-call(bf16[8,5,264,128]{3,2,1,0:T(8,128)(2,1)S(1)} %all_to_all.20.data), custom_call_target="tpu_custom_call" | custom-call | tf_op jit(solution)/shard_map/mix_members/pallas_call | solution.py:193
  60.0 1.5 copy-done
  61.5 4.3 %all-to-all-start.1 = ((bf16[4,5,256,256]{3,2,1,0:T(8,128)(2,1)}), bf16[4,5,256,256]{3,2,1,0:T(8,128)(2,1)S(1)}, u32[]{:S(2)}, u32[]{:S(2)}) async-start(bf16[4,5,256,256]{3,2,1,0:T(8,128)(2,1)} %copy-done), calls=%async_computation.1 | async-start | bytes 5242880 | tf_op jit(solution)/shard_map/all_to_all | solution.py:421
  65.8 1.1 collective-permute-start
  66.9 1.7 collective-permute-start.1
  68.7 1.4 collective-permute-start.2
  70.0 1.5 collective-permute-start.3
  71.9 1.8 collective-permute-start.5
  73.7 30.1 %collective-permute-done.1.refs_2_ = bf16[5,264,128]{2,1,0:T(8,128)(2,1)S(1)} collective-permute-done((bf16[5,264,128]{2,1,0:T(8,128)(2,1)}, bf16[5,264,128]{2,1,0:T(8,128)(2,1)S(1)}, u32[]{:S(2)}, u32[]{:S(2)}) %collective-permute-start.1) | collective-permute-done | bytes 337952 | tf_op jit(solution)/shard_map/ppermute | solution.py:438
  103.8 3.9 %collective-permute-start.6 = (bf16[5,264,128]{2,1,0:T(8,128)(2,1)}, bf16[5,264,128]{2,1,0:T(8,128)(2,1)S(1)}, u32[]{:S(2)}, u32[]{:S(2)}) collective-permute-start(bf16[5,264,128]{2,1,0:T(8,128)(2,1)} %get-tuple-element.60), channel_id=1, source_target_pairs={{0,65},{1,64},{2,67},{3,66},{4,69},{5,68},{6,71},{7,70},{8,73},{9,... | collective-permute-start | bytes 1013768 | tf_op jit(solution)/shard_map/ppermute | solution.py:438
  107.7 5.7 %collective-permute-done.2.refs_3_ = bf16[5,264,128]{2,1,0:T(8,128)(2,1)S(1)} collective-permute-done((bf16[5,264,128]{2,1,0:T(8,128)(2,1)}, bf16[5,264,128]{2,1,0:T(8,128)(2,1)S(1)}, u32[]{:S(2)}, u32[]{:S(2)}) %collective-permute-start.2) | collective-permute-done | bytes 337952 | tf_op jit(solution)/shard_map/ppermute | solution.py:438
  113.4 1.3 collective-permute-start.14
  114.7 1.8 collective-permute-start.15
  116.5 2.0 collective-permute-done.5.refs_6_
  118.6 8.5 %collective-permute-done.6.refs_7_ = bf16[5,264,128]{2,1,0:T(8,128)(2,1)S(1)} collective-permute-done((bf16[5,264,128]{2,1,0:T(8,128)(2,1)}, bf16[5,264,128]{2,1,0:T(8,128)(2,1)S(1)}, u32[]{:S(2)}, u32[]{:S(2)}) %collective-permute-start.6) | collective-permute-done | bytes 337952 | tf_op jit(solution)/shard_map/ppermute | solution.py:438
  127.1 4.0 %mix_tiles.2 = (bf16[5,256,256]{2,1,0:T(8,128)(2,1)S(1)}, bf16[5,256,256]{2,1,0:T(8,128)(2,1)}, bf16[5,256,256]{2,1,0:T(8,128)(2,1)S(1)}, bf16[5,256,256]{2,1,0:T(8,128)(2,1)S(1)}) custom-call(s32[1]{0:T(128)} %bitcast.3.refs_6_.at_ref, bf16[5,264,128]{2,1,0:T(8,128)(2,1)S(1)} %copy-done.14, bf16[5,264,128]{2,1,0:T(8,128)(2,1)S(1)} %collective-permute-done.refs_1_, ...), custom_call_target="tpu_custom_call" | custom-call | tf_op jit(solution)/shard_map/mix_tiles/pallas_call | solution.py:160
  133.7 1.2 collective-permute-start.7
  134.9 1.5 collective-permute-start.16
  140.2 3.3 %collective-permute-start.19 = (bf16[6,264,128]{2,1,0:T(8,128)(2,1)}, bf16[6,264,128]{2,1,0:T(8,128)(2,1)}, u32[]{:S(2)}, u32[]{:S(2)}) collective-permute-start(bf16[6,264,128]{2,1,0:T(8,128)(2,1)} %get-tuple-element.76), channel_id=1, source_target_pairs={{0,17},{1,16},{2,19},{3,18},{4,21},{5,20},{6,23},{7,22},{8,25},{9,... | collective-permute-start | bytes 1216520 | tf_op jit(solution)/shard_map/ppermute | solution.py:438
  143.4 3.2 %collective-permute-done.16.refs_4_ = bf16[6,264,128]{2,1,0:T(8,128)(2,1)S(1)} collective-permute-done((bf16[6,264,128]{2,1,0:T(8,128)(2,1)}, bf16[6,264,128]{2,1,0:T(8,128)(2,1)S(1)}, u32[]{:S(2)}, u32[]{:S(2)}) %collective-permute-start.16) | collective-permute-done | bytes 405536 | tf_op jit(solution)/shard_map/ppermute | solution.py:438
  147.4 2.4 collective-permute-start.8
  149.7 5.3 %collective-permute-done.17.refs_5_ = bf16[6,264,128]{2,1,0:T(8,128)(2,1)S(1)} collective-permute-done((bf16[6,264,128]{2,1,0:T(8,128)(2,1)}, bf16[6,264,128]{2,1,0:T(8,128)(2,1)S(1)}, u32[]{:S(2)}, u32[]{:S(2)}) %collective-permute-start.17) | collective-permute-done | bytes 405536 | tf_op jit(solution)/shard_map/ppermute | solution.py:438
  155.8 2.5 collective-permute-start.9
  158.3 3.0 %collective-permute-done.18.refs_6_ = bf16[6,264,128]{2,1,0:T(8,128)(2,1)} collective-permute-done((bf16[6,264,128]{2,1,0:T(8,128)(2,1)}, bf16[6,264,128]{2,1,0:T(8,128)(2,1)}, u32[]{:S(2)}, u32[]{:S(2)}) %collective-permute-start.18) | collective-permute-done | bytes 405536 | tf_op jit(solution)/shard_map/ppermute | solution.py:438
  161.3 8.2 %collective-permute-done.19.refs_7_ = bf16[6,264,128]{2,1,0:T(8,128)(2,1)} collective-permute-done((bf16[6,264,128]{2,1,0:T(8,128)(2,1)}, bf16[6,264,128]{2,1,0:T(8,128)(2,1)}, u32[]{:S(2)}, u32[]{:S(2)}) %collective-permute-start.19) | collective-permute-done | bytes 405536 | tf_op jit(solution)/shard_map/ppermute | solution.py:438
  169.6 1.0 copy-done.3
  170.6 1.0 copy-done.5
  171.6 1.0 copy-done.7
  172.6 1.0 copy-done.9
  175.6 6.6 %mix_tiles.3 = (bf16[6,256,256]{2,1,0:T(8,128)(2,1)S(1)}, bf16[6,256,256]{2,1,0:T(8,128)(2,1)}, bf16[6,256,256]{2,1,0:T(8,128)(2,1)}, bf16[6,256,256]{2,1,0:T(8,128)(2,1)}) custom-call(s32[1]{0:T(128)} %bitcast.5.at_ref, bf16[6,264,128]{2,1,0:T(8,128)(2,1)S(1)} %copy-done.3, bf16[6,264,128]{2,1,0:T(8,128)(2,1)S(1)} %copy-done.5, ...), custom_call_target="tpu_custom_call" | custom-call | tf_op jit(solution)/shard_map/mix_tiles/pallas_call | solution.py:160
  182.8 2.1 collective-permute-start.21
  184.9 1.2 add_members.1
  186.1 8.2 %all-to-all-start.2 = ((bf16[4,5,64,256]{3,2,1,0:T(8,128)(2,1)}), bf16[4,5,64,256]{3,2,1,0:T(8,128)(2,1)S(1)}, u32[]{:S(2)}, u32[]{:S(2)}) async-start(bf16[4,5,64,256]{3,2,1,0:T(8,128)(2,1)} %add_members.1), calls=%async_computation.2 | async-start | bytes 1310720 | tf_op jit(solution)/shard_map/all_to_all | solution.py:421
  194.3 1.1 copy-done.2
  195.4 2.6 add_quarters.2
  198.6 3.7 %collective-permute-done.20.refs_1_ = bf16[6,256,256]{2,1,0:T(8,128)(2,1)} collective-permute-done((bf16[6,256,256]{2,1,0:T(8,128)(2,1)}, bf16[6,256,256]{2,1,0:T(8,128)(2,1)}, u32[]{:S(2)}, u32[]{:S(2)}) %collective-permute-start.20) | collective-permute-done | bytes 786464 | tf_op jit(solution)/shard_map/ppermute | solution.py:438
  202.3 15.7 %collective-permute-done.22.refs_3_ = bf16[6,256,256]{2,1,0:T(8,128)(2,1)} collective-permute-done((bf16[6,256,256]{2,1,0:T(8,128)(2,1)}, bf16[6,256,256]{2,1,0:T(8,128)(2,1)}, u32[]{:S(2)}, u32[]{:S(2)}) %collective-permute-start.22) | collective-permute-done | bytes 786464 | tf_op jit(solution)/shard_map/ppermute | solution.py:438
  218.0 2.8 %add_quarters.3 = (bf16[6,64,256]{2,1,0:T(8,128)(2,1)S(1)}, bf16[6,64,256]{2,1,0:T(8,128)(2,1)}, bf16[6,64,256]{2,1,0:T(8,128)(2,1)S(1)}, bf16[6,64,256]{2,1,0:T(8,128)(2,1)S(1)}) custom-call(s32[1]{0:T(128)} %bitcast.4.refs_7_.at_ref, bf16[6,256,256]{2,1,0:T(8,128)(2,1)S(1)} %get-tuple-element.77.refs_0_, ...), custom_call_target="tpu_custom_call" | custom-call | tf_op jit(solution)/shard_map/add_quarters/pallas_call | solution.py:252
  220.8 5.4 %collective-permute-start.23 = (bf16[6,64,256]{2,1,0:T(8,128)(2,1)}, bf16[6,64,256]{2,1,0:T(8,128)(2,1)S(1)}, u32[]{:S(2)}, u32[]{:S(2)}) collective-permute-start(bf16[6,64,256]{2,1,0:T(8,128)(2,1)} %get-tuple-element.82), channel_id=1, source_target_pairs={{0,32},{1,33},{2,34},{3,35},{4,36},{5,37},{6,38},{7,39},{8,40},{9,... | collective-permute-start | bytes 589832 | tf_op jit(solution)/shard_map/ppermute | solution.py:438
  226.2 10.6 %collective-permute-start.25 = (bf16[6,64,256]{2,1,0:T(8,128)(2,1)S(1)}, bf16[6,64,256]{2,1,0:T(8,128)(2,1)S(1)}, u32[]{:S(2)}, u32[]{:S(2)}) collective-permute-start(bf16[6,64,256]{2,1,0:T(8,128)(2,1)S(1)} %get-tuple-element.84), channel_id=1, source_target_pairs={{0,64},{1,65},{2,66},{3,67},{4,68},{5,69},{6,70},{7,71},{8,72},{9,... | collective-permute-start | bytes 589832 | tf_op jit(solution)/shard_map/ppermute | solution.py:438
  236.8 2.1 collective-permute-start.11
  238.9 10.6 %spread_squares.1 = (f32[640,32,256]{2,1,0:T(8,128)}, s32[1,1024]{1,0:T(1,128)}) custom-call(s32[1]{0:T(128)} %bitcast.6.me_ref, s32[128,128]{1,0:T(8,128)} %rows_ref.1, bf16[128,128]{1,0:T(8,128)(2,1)} %coef_ref.1, s32[1,1024]{1,0:T(1,128)} %bitcast.14), custom_call_target="tpu_custom_call" | custom-call | tf_op jit(solution)/shard_map/spread_squares/pallas_call | solution.py:327
  249.6 1.1 square_sums.1
  250.7 6.8 %all-to-all-start.3 = ((f32[128,1,384]{2,1,0:T(1,128)}), f32[128,1,384]{2,1,0:T(1,128)S(1)}, u32[]{:S(2)}, u32[]{:S(2)}) async-start(f32[128,1,384]{2,1,0:T(1,128)} %square_sums.1), calls=%async_computation.3 | async-start | bytes 393216 | tf_op jit(solution)/shard_map/all_to_all | solution.py:421
  257.7 10.2 %all-to-all-done.3.parts_ref = f32[128,1,384]{2,1,0:T(1,128)S(1)} async-done(((f32[128,1,384]{2,1,0:T(1,128)}), f32[128,1,384]{2,1,0:T(1,128)S(1)}, u32[]{:S(2)}, u32[]{:S(2)}) %all-to-all-start.3) | async-done | bytes 196640 | tf_op jit(solution)/shard_map/all_to_all | solution.py:421
  267.9 3.3 %finish.1 = (f32[1,8]{1,0:T(1,128)}, f32[8,128]{1,0:T(8,128)}, f32[32,256]{1,0:T(8,128)}) custom-call(s32[1]{0:T(128)S(6)} %copy.11.refs_4_.count_ref, f32[128,1,384]{2,1,0:T(1,128)S(1)} %all-to-all-done.3.parts_ref, f32[8,128]{1,0:T(8,128)S(1)} %bitcast.12, s32[128,1]{1,0:T(8,128)S(1)} %copy.10.sensor_ref, s32[1,1024]{1,0:T(1,128)S(1)} %copy-done.16, ...), custom_call_target="tpu_custom_call" | custom-call | tf_op jit(solution)/shard_map/finish/pallas_call | solution.py:401
  (64 shorter events, 11.7 us)
Async XLA Ops:
  60.0 1.5 copy-start
  61.5 51.9 %copy-start.20 = (bf16[6,264,128]{2,1,0:T(8,128)(2,1)S(1)}, bf16[6,264,128]{2,1,0:T(8,128)(2,1)}, u32[]{:S(2)}) copy-start(bf16[6,264,128]{2,1,0:T(8,128)(2,1)} %get-tuple-element.70) | copy-start | bytes 1216516
  61.5 65.6 %copy-start.14 = (bf16[5,264,128]{2,1,0:T(8,128)(2,1)S(1)}, bf16[5,264,128]{2,1,0:T(8,128)(2,1)}, u32[]{:S(2)}) copy-start(bf16[5,264,128]{2,1,0:T(8,128)(2,1)} %get-tuple-element.53.refs_0_) | copy-start | bytes 1013764
  61.5 123.4 %all-to-all-start.1 = ((bf16[4,5,256,256]{3,2,1,0:T(8,128)(2,1)}), bf16[4,5,256,256]{3,2,1,0:T(8,128)(2,1)S(1)}, u32[]{:S(2)}, u32[]{:S(2)}) async-start(bf16[4,5,256,256]{3,2,1,0:T(8,128)(2,1)} %copy-done), calls=%async_computation.1 | async-start | bytes 5242880 | tf_op jit(solution)/shard_map/all_to_all | solution.py:421
  65.8 6.1 %collective-permute-start = (bf16[5,264,128]{2,1,0:T(8,128)(2,1)}, bf16[5,264,128]{2,1,0:T(8,128)(2,1)S(1)}, u32[]{:S(2)}, u32[]{:S(2)}) collective-permute-start(bf16[5,264,128]{2,1,0:T(8,128)(2,1)} %get-tuple-element.54), channel_id=1, source_target_pairs={{0,1},{1,0},{2,3},{3,2},{4,5},{5,4},{6,7},{7,6},{8,9},{9,8},{10,11... | collective-permute-start | bytes 1013768 | tf_op jit(solution)/shard_map/ppermute | solution.py:438
  66.9 36.8 %collective-permute-start.1 = (bf16[5,264,128]{2,1,0:T(8,128)(2,1)}, bf16[5,264,128]{2,1,0:T(8,128)(2,1)S(1)}, u32[]{:S(2)}, u32[]{:S(2)}) collective-permute-start(bf16[5,264,128]{2,1,0:T(8,128)(2,1)} %get-tuple-element.55), channel_id=1, source_target_pairs={{0,32},{1,33},{2,34},{3,35},{4,36},{5,37},{6,38},{7,39},{8,40},{9,... | collective-permute-start | bytes 1013768 | tf_op jit(solution)/shard_map/ppermute | solution.py:438
  68.7 44.8 %collective-permute-start.2 = (bf16[5,264,128]{2,1,0:T(8,128)(2,1)}, bf16[5,264,128]{2,1,0:T(8,128)(2,1)S(1)}, u32[]{:S(2)}, u32[]{:S(2)}) collective-permute-start(bf16[5,264,128]{2,1,0:T(8,128)(2,1)} %get-tuple-element.56), channel_id=1, source_target_pairs={{0,33},{1,32},{2,35},{3,34},{4,37},{5,36},{6,39},{7,38},{8,41},{9,... | collective-permute-start | bytes 1013768 | tf_op jit(solution)/shard_map/ppermute | solution.py:438
  70.0 43.4 %collective-permute-start.3 = (bf16[5,264,128]{2,1,0:T(8,128)(2,1)}, bf16[5,264,128]{2,1,0:T(8,128)(2,1)S(1)}, u32[]{:S(2)}, u32[]{:S(2)}) collective-permute-start(bf16[5,264,128]{2,1,0:T(8,128)(2,1)} %get-tuple-element.57), channel_id=1, source_target_pairs={{0,96},{1,97},{2,98},{3,99},{4,100},{5,101},{6,102},{7,103},{8,104... | collective-permute-start | bytes 1013768 | tf_op jit(solution)/shard_map/ppermute | solution.py:438
  71.5 43.2 %collective-permute-start.4 = (bf16[5,264,128]{2,1,0:T(8,128)(2,1)}, bf16[5,264,128]{2,1,0:T(8,128)(2,1)S(1)}, u32[]{:S(2)}, u32[]{:S(2)}) collective-permute-start(bf16[5,264,128]{2,1,0:T(8,128)(2,1)} %get-tuple-element.58), channel_id=1, source_target_pairs={{0,97},{1,96},{2,99},{3,98},{4,101},{5,100},{6,103},{7,102},{8,105... | collective-permute-start | bytes 1013768 | tf_op jit(solution)/shard_map/ppermute | solution.py:438
  71.9 46.7 %collective-permute-start.5 = (bf16[5,264,128]{2,1,0:T(8,128)(2,1)}, bf16[5,264,128]{2,1,0:T(8,128)(2,1)S(1)}, u32[]{:S(2)}, u32[]{:S(2)}) collective-permute-start(bf16[5,264,128]{2,1,0:T(8,128)(2,1)} %get-tuple-element.59), channel_id=1, source_target_pairs={{0,64},{1,65},{2,66},{3,67},{4,68},{5,69},{6,70},{7,71},{8,72},{9,... | collective-permute-start | bytes 1013768 | tf_op jit(solution)/shard_map/ppermute | solution.py:438
  103.8 23.3 %collective-permute-start.6 = (bf16[5,264,128]{2,1,0:T(8,128)(2,1)}, bf16[5,264,128]{2,1,0:T(8,128)(2,1)S(1)}, u32[]{:S(2)}, u32[]{:S(2)}) collective-permute-start(bf16[5,264,128]{2,1,0:T(8,128)(2,1)} %get-tuple-element.60), channel_id=1, source_target_pairs={{0,65},{1,64},{2,67},{3,66},{4,69},{5,68},{6,71},{7,70},{8,73},{9,... | collective-permute-start | bytes 1013768 | tf_op jit(solution)/shard_map/ppermute | solution.py:438
  113.4 22.9 %collective-permute-start.13 = (bf16[6,264,128]{2,1,0:T(8,128)(2,1)S(1)}, bf16[6,264,128]{2,1,0:T(8,128)(2,1)S(1)}, u32[]{:S(2)}, u32[]{:S(2)}) collective-permute-start(bf16[6,264,128]{2,1,0:T(8,128)(2,1)S(1)} %copy-done.20), channel_id=1, source_target_pairs={{0,1},{1,0},{2,3},{3,2},{4,5},{5,4},{6,7},{7,6},{8,9},{9,8},{10,11... | collective-permute-start | bytes 1216520 | tf_op jit(solution)/shard_map/ppermute | solution.py:438
  113.4 24.6 %collective-permute-start.14 = (bf16[6,264,128]{2,1,0:T(8,128)(2,1)}, bf16[6,264,128]{2,1,0:T(8,128)(2,1)S(1)}, u32[]{:S(2)}, u32[]{:S(2)}) collective-permute-start(bf16[6,264,128]{2,1,0:T(8,128)(2,1)} %get-tuple-element.71), channel_id=1, source_target_pairs={{0,8},{1,9},{2,10},{3,11},{4,12},{5,13},{6,14},{7,15},{8,16},{9,17... | collective-permute-start | bytes 1216520 | tf_op jit(solution)/shard_map/ppermute | solution.py:438
  114.7 24.7 %collective-permute-start.15 = (bf16[6,264,128]{2,1,0:T(8,128)(2,1)}, bf16[6,264,128]{2,1,0:T(8,128)(2,1)S(1)}, u32[]{:S(2)}, u32[]{:S(2)}) collective-permute-start(bf16[6,264,128]{2,1,0:T(8,128)(2,1)} %get-tuple-element.72), channel_id=1, source_target_pairs={{0,9},{1,8},{2,11},{3,10},{4,13},{5,12},{6,15},{7,14},{8,17},{9,16... | collective-permute-start | bytes 1216520 | tf_op jit(solution)/shard_map/ppermute | solution.py:438
  131.1 0.9 copy-start.1
  132.0 0.8 copy-start.17
  132.8 0.9 copy-start.18
  133.7 51.2 %collective-permute-start.7 = (bf16[5,256,256]{2,1,0:T(8,128)(2,1)}, bf16[5,256,256]{2,1,0:T(8,128)(2,1)}, u32[]{:S(2)}, u32[]{:S(2)}) collective-permute-start(bf16[5,256,256]{2,1,0:T(8,128)(2,1)} %get-tuple-element.62), channel_id=1, source_target_pairs={{0,8},{1,9},{2,10},{3,11},{4,12},{5,13},{6,14},{7,15},{8,16},{9,17... | collective-permute-start | bytes 1966088 | tf_op jit(solution)/shard_map/ppermute | solution.py:438
  134.9 11.7 %collective-permute-start.16 = (bf16[6,264,128]{2,1,0:T(8,128)(2,1)}, bf16[6,264,128]{2,1,0:T(8,128)(2,1)S(1)}, u32[]{:S(2)}, u32[]{:S(2)}) collective-permute-start(bf16[6,264,128]{2,1,0:T(8,128)(2,1)} %get-tuple-element.73), channel_id=1, source_target_pairs={{0,24},{1,25},{2,26},{3,27},{4,28},{5,29},{6,30},{7,31},{8,0},{9,1... | collective-permute-start | bytes 1216520 | tf_op jit(solution)/shard_map/ppermute | solution.py:438
  136.4 0.8 copy-start.4
  137.1 17.9 %collective-permute-start.17 = (bf16[6,264,128]{2,1,0:T(8,128)(2,1)}, bf16[6,264,128]{2,1,0:T(8,128)(2,1)S(1)}, u32[]{:S(2)}, u32[]{:S(2)}) collective-permute-start(bf16[6,264,128]{2,1,0:T(8,128)(2,1)} %get-tuple-element.74), channel_id=1, source_target_pairs={{0,25},{1,24},{2,27},{3,26},{4,29},{5,28},{6,31},{7,30},{8,1},{9,0... | collective-permute-start | bytes 1216520 | tf_op jit(solution)/shard_map/ppermute | solution.py:438
  138.8 22.6 %collective-permute-start.18 = (bf16[6,264,128]{2,1,0:T(8,128)(2,1)}, bf16[6,264,128]{2,1,0:T(8,128)(2,1)}, u32[]{:S(2)}, u32[]{:S(2)}) collective-permute-start(bf16[6,264,128]{2,1,0:T(8,128)(2,1)} %get-tuple-element.75), channel_id=1, source_target_pairs={{0,16},{1,17},{2,18},{3,19},{4,20},{5,21},{6,22},{7,23},{8,24},{9,... | collective-permute-start | bytes 1216520 | tf_op jit(solution)/shard_map/ppermute | solution.py:438
  140.2 29.4 %collective-permute-start.19 = (bf16[6,264,128]{2,1,0:T(8,128)(2,1)}, bf16[6,264,128]{2,1,0:T(8,128)(2,1)}, u32[]{:S(2)}, u32[]{:S(2)}) collective-permute-start(bf16[6,264,128]{2,1,0:T(8,128)(2,1)} %get-tuple-element.76), channel_id=1, source_target_pairs={{0,17},{1,16},{2,19},{3,18},{4,21},{5,20},{6,23},{7,22},{8,25},{9,... | collective-permute-start | bytes 1216520 | tf_op jit(solution)/shard_map/ppermute | solution.py:438
  146.6 0.8 copy-start.10
  147.4 46.9 %collective-permute-start.8 = (bf16[5,256,256]{2,1,0:T(8,128)(2,1)}, bf16[5,256,256]{2,1,0:T(8,128)(2,1)}, u32[]{:S(2)}, u32[]{:S(2)}) collective-permute-start(bf16[5,256,256]{2,1,0:T(8,128)(2,1)} %copy-done.18), channel_id=1, source_target_pairs={{0,24},{1,25},{2,26},{3,27},{4,28},{5,29},{6,30},{7,31},{8,0},{9,1... | collective-permute-start | bytes 1966088 | tf_op jit(solution)/shard_map/ppermute | solution.py:438
  155.0 0.8 copy-start.12
  155.8 38.5 %collective-permute-start.9 = (bf16[5,256,256]{2,1,0:T(8,128)(2,1)}, bf16[5,256,256]{2,1,0:T(8,128)(2,1)}, u32[]{:S(2)}, u32[]{:S(2)}) collective-permute-start(bf16[5,256,256]{2,1,0:T(8,128)(2,1)} %copy-done.17), channel_id=1, source_target_pairs={{0,16},{1,17},{2,18},{3,19},{4,20},{5,21},{6,22},{7,23},{8,24},{9,... | collective-permute-start | bytes 1966088 | tf_op jit(solution)/shard_map/ppermute | solution.py:438
  169.6 1.0 copy-start.3
  170.6 1.0 copy-start.5
  171.6 1.0 copy-start.7
  172.6 1.0 copy-start.9
  173.6 1.0 copy-start.11
  174.6 1.0 copy-start.13
  182.2 20.1 %collective-permute-start.20 = (bf16[6,256,256]{2,1,0:T(8,128)(2,1)}, bf16[6,256,256]{2,1,0:T(8,128)(2,1)}, u32[]{:S(2)}, u32[]{:S(2)}) collective-permute-start(bf16[6,256,256]{2,1,0:T(8,128)(2,1)} %get-tuple-element.78), channel_id=1, source_target_pairs={{0,2},{1,3},{2,4},{3,5},{4,6},{5,7},{6,0},{7,1},{8,10},{9,11},{10,... | collective-permute-start | bytes 2359304 | tf_op jit(solution)/shard_map/ppermute | solution.py:438
  182.8 19.5 %collective-permute-start.21 = (bf16[6,256,256]{2,1,0:T(8,128)(2,1)}, bf16[6,256,256]{2,1,0:T(8,128)(2,1)}, u32[]{:S(2)}, u32[]{:S(2)}) collective-permute-start(bf16[6,256,256]{2,1,0:T(8,128)(2,1)} %get-tuple-element.79), channel_id=1, source_target_pairs={{0,6},{1,7},{2,0},{3,1},{4,2},{5,3},{6,4},{7,5},{8,14},{9,15},{10,... | collective-permute-start | bytes 2359304 | tf_op jit(solution)/shard_map/ppermute | solution.py:438
  184.9 33.1 %collective-permute-start.22 = (bf16[6,256,256]{2,1,0:T(8,128)(2,1)}, bf16[6,256,256]{2,1,0:T(8,128)(2,1)}, u32[]{:S(2)}, u32[]{:S(2)}) collective-permute-start(bf16[6,256,256]{2,1,0:T(8,128)(2,1)} %get-tuple-element.80), channel_id=1, source_target_pairs={{0,4},{1,5},{2,6},{3,7},{4,0},{5,1},{6,2},{7,3},{8,12},{9,13},{10,... | collective-permute-start | bytes 2359304 | tf_op jit(solution)/shard_map/ppermute | solution.py:438
  186.1 63.5 %all-to-all-start.2 = ((bf16[4,5,64,256]{3,2,1,0:T(8,128)(2,1)}), bf16[4,5,64,256]{3,2,1,0:T(8,128)(2,1)S(1)}, u32[]{:S(2)}, u32[]{:S(2)}) async-start(bf16[4,5,64,256]{3,2,1,0:T(8,128)(2,1)} %add_members.1), calls=%async_computation.2 | async-start | bytes 1310720 | tf_op jit(solution)/shard_map/all_to_all | solution.py:421
  194.3 1.1 copy-start.2
  198.0 40.9 %collective-permute-start.10 = (bf16[5,64,256]{2,1,0:T(8,128)(2,1)S(1)}, bf16[5,64,256]{2,1,0:T(8,128)(2,1)S(1)}, u32[]{:S(2)}, u32[]{:S(2)}) collective-permute-start(bf16[5,64,256]{2,1,0:T(8,128)(2,1)S(1)} %get-tuple-element.66), channel_id=1, source_target_pairs={{0,2},{1,3},{2,4},{3,5},{4,6},{5,7},{6,0},{7,1},{8,10},{9,11},{10,... | collective-permute-start | bytes 491528 | tf_op jit(solution)/shard_map/ppermute | solution.py:438
  218.0 39.6 %copy-start.19 = (s32[128]{0:T(128)S(1)}, s32[128]{0:T(128)}, u32[]{:S(2)}) copy-start(s32[128]{0:T(128)} %param.9) | copy-start | bytes 1540
  218.0 49.9 %copy-start.15 = (f32[1024]{0:T(1024)S(1)}, f32[1024]{0:T(1024)}, u32[]{:S(2)}) copy-start(f32[1024]{0:T(1024)} %param.13) | copy-start | bytes 12292
  220.8 28.7 %collective-permute-start.23 = (bf16[6,64,256]{2,1,0:T(8,128)(2,1)}, bf16[6,64,256]{2,1,0:T(8,128)(2,1)S(1)}, u32[]{:S(2)}, u32[]{:S(2)}) collective-permute-start(bf16[6,64,256]{2,1,0:T(8,128)(2,1)} %get-tuple-element.82), channel_id=1, source_target_pairs={{0,32},{1,33},{2,34},{3,35},{4,36},{5,37},{6,38},{7,39},{8,40},{9,... | collective-permute-start | bytes 589832 | tf_op jit(solution)/shard_map/ppermute | solution.py:438
  226.2 23.4 %collective-permute-start.24 = (bf16[6,64,256]{2,1,0:T(8,128)(2,1)S(1)}, bf16[6,64,256]{2,1,0:T(8,128)(2,1)S(1)}, u32[]{:S(2)}, u32[]{:S(2)}) collective-permute-start(bf16[6,64,256]{2,1,0:T(8,128)(2,1)S(1)} %get-tuple-element.83), channel_id=1, source_target_pairs={{0,96},{1,97},{2,98},{3,99},{4,100},{5,101},{6,102},{7,103},{8,104... | collective-permute-start | bytes 589832 | tf_op jit(solution)/shard_map/ppermute | solution.py:438
  226.2 23.4 %collective-permute-start.25 = (bf16[6,64,256]{2,1,0:T(8,128)(2,1)S(1)}, bf16[6,64,256]{2,1,0:T(8,128)(2,1)S(1)}, u32[]{:S(2)}, u32[]{:S(2)}) collective-permute-start(bf16[6,64,256]{2,1,0:T(8,128)(2,1)S(1)} %get-tuple-element.84), channel_id=1, source_target_pairs={{0,64},{1,65},{2,66},{3,67},{4,68},{5,69},{6,70},{7,71},{8,72},{9,... | collective-permute-start | bytes 589832 | tf_op jit(solution)/shard_map/ppermute | solution.py:438
  236.8 12.7 %collective-permute-start.11 = (bf16[5,64,256]{2,1,0:T(8,128)(2,1)}, bf16[5,64,256]{2,1,0:T(8,128)(2,1)S(1)}, u32[]{:S(2)}, u32[]{:S(2)}) collective-permute-start(bf16[5,64,256]{2,1,0:T(8,128)(2,1)} %get-tuple-element.67), channel_id=1, source_target_pairs={{0,6},{1,7},{2,0},{3,1},{4,2},{5,3},{6,4},{7,5},{8,14},{9,15},{10,... | collective-permute-start | bytes 491528 | tf_op jit(solution)/shard_map/ppermute | solution.py:438
  238.9 10.6 %collective-permute-start.12 = (bf16[5,64,256]{2,1,0:T(8,128)(2,1)}, bf16[5,64,256]{2,1,0:T(8,128)(2,1)S(1)}, u32[]{:S(2)}, u32[]{:S(2)}) collective-permute-start(bf16[5,64,256]{2,1,0:T(8,128)(2,1)} %get-tuple-element.68), channel_id=1, source_target_pairs={{0,4},{1,5},{2,6},{3,7},{4,0},{5,1},{6,2},{7,3},{8,12},{9,13},{10,... | collective-permute-start | bytes 491528 | tf_op jit(solution)/shard_map/ppermute | solution.py:438
  249.5 18.4 %copy-start.16 = (s32[1,1024]{1,0:T(1,128)S(1)}, s32[1,1024]{1,0:T(1,128)}, u32[]{:S(2)}) copy-start(s32[1,1024]{1,0:T(1,128)} %get-tuple-element.96.pos_ref) | copy-start | bytes 12292
  250.7 17.2 %all-to-all-start.3 = ((f32[128,1,384]{2,1,0:T(1,128)}), f32[128,1,384]{2,1,0:T(1,128)S(1)}, u32[]{:S(2)}, u32[]{:S(2)}) async-start(f32[128,1,384]{2,1,0:T(1,128)} %square_sums.1), calls=%async_computation.3 | async-start | bytes 393216 | tf_op jit(solution)/shard_map/all_to_all | solution.py:421
  (2 other events, 1.5 us)

commit v10 on v7

--- a/solution.py
+++ b/solution.py
@@ -11,7 +11,7 @@
 SPD = 8
 AXES = ("y", "x", "z", "core")
 ORDERS = (("z", "y", "x"), ("y", "x", "z"), ("x", "z", "y"))
-EACH = (5, 5, 6)
+EACH = (5, 6, 5)
 PEERS = ((0, 0), (0, 1), (1, 0), (1, 1), (3, 0), (3, 1), (2, 0), (2, 1))
 SHIFTS = (0, 1, 3, 2)
 SIDE = 8
@@ -218,10 +218,12 @@
     nblk, foot = rows.shape
     n_sens = owner.shape[1]
 
-    def body(me_ref, rows_ref, coef_ref, owner_ref, map_ref, pos_ref):
+    steps = nblk // sb
+
+    def body(me_ref, rows_ref, coef_ref, owner_ref, map_ref):
         g = pl.program_id(0)
 
-        @pl.when(g == 0)
+        @pl.when(g == steps)
         def _():
             mine = owner_ref[...] == me_ref[0]
             flag = jnp.broadcast_to(jnp.where(mine, 1.0, 0.0), (8, n_sens)).astype(BF16)
@@ -229,8 +231,15 @@
             col = lax.broadcasted_iota(I32, (n_sens, n_sens), 1)
             before = jnp.where(row < col, 1.0, 0.0).astype(BF16)
             rank = jnp.dot(flag, before, preferred_element_type=F32)[0:1, :]
-            pos_ref[...] = jnp.where(mine, rank.astype(I32), -1)
-
+            place = jnp.where(mine, rank, -1.0)
+            for i in range(n_sens // 128):
+                map_ref[0, i : i + 1, :128] = place[:, i * 128 : (i + 1) * 128]
+
+        @pl.when(g < steps)
+        def _():
+            spread(rows_ref, coef_ref, map_ref)
+
+    def spread(rows_ref, coef_ref, map_ref):
         sub_r = lax.broadcasted_iota(I32, (tile_r, foot), 0)
         sub_c = lax.broadcasted_iota(I32, (tile_c, foot), 0)
         point = rows_ref[...]
@@ -251,21 +260,15 @@
 
     return pl.pallas_call(
         body,
-        grid=(nblk // sb,),
+        grid=(steps + 1,),
         in_specs=[
             pl.BlockSpec(memory_space=pltpu.SMEM),
-            pl.BlockSpec((sb, foot), lambda g: (g, 0)),
-            pl.BlockSpec((sb, foot), lambda g: (g, 0)),
+            pl.BlockSpec((sb, foot), lambda g: (jnp.minimum(g, steps - 1), 0)),
+            pl.BlockSpec((sb, foot), lambda g: (jnp.minimum(g, steps - 1), 0)),
             pl.BlockSpec((1, n_sens), lambda g: (0, 0)),
         ],
-        out_specs=[
-            pl.BlockSpec((sb, tile_r, tile_c), lambda g: (g, 0, 0)),
-            pl.BlockSpec((1, n_sens), lambda g: (0, 0)),
-        ],
-        out_shape=[
-            jax.ShapeDtypeStruct((ROOM * nblk, tile_r, tile_c), F32),
-            jax.ShapeDtypeStruct((1, n_sens), I32),
-        ],
+        out_specs=pl.BlockSpec((sb, tile_r, tile_c), lambda g: (g, 0, 0)),
+        out_shape=jax.ShapeDtypeStruct((ROOM * nblk, tile_r, tile_c), F32),
         compiler_params=pltpu.CompilerParams(
             dimension_semantics=("arbitrary",), vmem_limit_bytes=VMEM
         ),
@@ -273,16 +276,18 @@
     )(me, rows, coef, owner)
 
 
-def finish(parts, weights, sensor, count, maps, pos, scale, sb=32):
-    n_sens = pos.shape[1]
+def finish(parts, weights, sensor, count, maps, scale, sb=32):
+    n_sens = weights.size
     nblk = sensor.shape[0]
     tile_r, tile_c = maps.shape[1:]
     pieces = nblk // sb
 
-    def body(count_ref, parts_ref, weights_ref, sensor_ref, pos_ref, maps_hbm, sens_ref, new_ref, dens_ref, slot_w, maps_ref, sem):
+    def body(count_ref, parts_ref, weights_ref, sensor_ref, maps_hbm, sens_ref, new_ref, dens_ref, slot_w, maps_ref, place_ref, sem):
         def fetch(i):
             return pltpu.make_async_copy(maps_hbm.at[pl.ds(i * sb, sb)], maps_ref.at[pl.ds(i * sb, sb)], sem.at[i])
 
+        places = pltpu.make_async_copy(maps_hbm.at[nblk], place_ref, sem.at[pieces])
+        places.start()
         for i in range(pieces):
             fetch(i).start()
         col = lax.broadcasted_iota(I32, (8, 128), 1)
@@ -299,11 +304,14 @@
         gain = weights_ref[...] * jnp.sqrt(1.0 + h8)
         new8 = n_sens * gain / jnp.sum(gain)
         new_ref[...] = new8
-        h, new = (jnp.concatenate([v[i : i + 1] for i in range(n_sens // 128)], axis=1) for v in (h8, new8))
-        k = lax.broadcasted_iota(I32, (SPD, n_sens), 0)
-        own = jnp.sum(jnp.where(pos_ref[...] == k, h, 0.0), axis=1, keepdims=True)
-        diag = lax.broadcasted_iota(I32, (SPD, SPD), 0) == lax.broadcasted_iota(I32, (SPD, SPD), 1)
-        sens_ref[...] = jnp.sum(jnp.where(diag, own, 0.0), axis=0, keepdims=True)
+        new = jnp.concatenate([new8[i : i + 1] for i in range(n_sens // 128)], axis=1)
+        places.wait()
+        mine = place_ref[: n_sens // 128, :128]
+        lane = lax.broadcasted_iota(I32, (1, SPD), 1)
+        own = jnp.zeros((1, SPD), F32)
+        for k in range(SPD):
+            own = jnp.where(lane == k, jnp.sum(jnp.where(mine == k, h8, 0.0)), own)
+        sens_ref[...] = own
         which = lax.broadcasted_iota(I32, (nblk, n_sens), 1)
         w = jnp.sum(jnp.where(which == sensor_ref[...], new, 0.0), axis=1, keepdims=True)
         alive = lax.broadcasted_iota(I32, (nblk, 1), 0) < count_ref[0]
@@ -325,7 +333,7 @@
     vmem = pl.BlockSpec(memory_space=pltpu.VMEM)
     return pl.pallas_call(
         body,
-        in_specs=[pl.BlockSpec(memory_space=pltpu.SMEM), vmem, vmem, vmem, vmem, pl.BlockSpec(memory_space=pltpu.HBM)],
+        in_specs=[pl.BlockSpec(memory_space=pltpu.SMEM), vmem, vmem, vmem, pl.BlockSpec(memory_space=pltpu.HBM)],
         out_specs=[vmem, vmem, vmem],
         out_shape=[
             jax.ShapeDtypeStruct((1, SPD), F32),
@@ -335,11 +343,12 @@
         scratch_shapes=[
             pltpu.VMEM((nblk, tile_c), F32),
             pltpu.VMEM((nblk, tile_r, tile_c), F32),
-            pltpu.SemaphoreType.DMA((pieces,)),
+            pltpu.VMEM((tile_r, tile_c), F32),
+            pltpu.SemaphoreType.DMA((pieces + 1,)),
         ],
         compiler_params=pltpu.CompilerParams(vmem_limit_bytes=48 * 1024 * 1024),
         name="finish",
-    )(count, parts, weights, sensor, pos, maps)
+    )(count, parts, weights, sensor, maps)
 
 
 def exchange(x, axes):
@@ -376,21 +385,21 @@
     firsts = [8 * sum(EACH[:f]) for f in range(3)]
     packs = [(first, each, f) for f, (first, each) in enumerate(zip(firsts, EACH))]
     sent = gather_flows(flat, *tile, packs, [at[a] for a, _, _ in ORDERS])
-    maps, pos = spread_squares(blk_rows, coef, owner.reshape(1, n_sens), me, tile_r, tile_c)
-    tiles = []
+    maps = spread_squares(blk_rows, coef, owner.reshape(1, n_sens), me, tile_r, tile_c)
+    tiles = [None] * 3
+    flows = [None] * 3
     for f, (a, _, _) in enumerate(ORDERS):
-        tiles.append([shift_to(x, a, *peer) for x, peer in zip(sent[8 * f : 8 * f + 8], PEERS)])
-    flows = []
+        tiles[f] = [shift_to(x, a, *peer) for x, peer in zip(sent[8 * f : 8 * f + 8], PEERS)]
     for f, (_, b, c) in enumerate(ORDERS):
         quarters = mix_tiles(tiles[f], at[b], n_sens)
         quarters = [shift_to(x, b, s, 0) for x, s in zip(quarters, SHIFTS)]
         pieces = add_quarters(quarters, at[c])
-        flows.append([shift_to(x, c, s, 0) for x, s in zip(pieces, SHIFTS)])
-    (flows, maps, pos) = lax.optimization_barrier((flows, maps, pos))
+        flows[f] = [shift_to(x, c, s, 0) for x, s in zip(pieces, SHIFTS)]
+    (flows, maps) = lax.optimization_barrier((flows, maps))
     acc = square_sums(flows, n_dev)
     parts = exchange(acc, AXES)
     sens, new, density = finish(
-        parts, weights.reshape(n_sens // 128, 128), blk_sensor.reshape(nblk, 1), blk_count, maps, pos, 1.0 / (foot * probe_n)
+        parts, weights.reshape(n_sens // 128, 128), blk_sensor.reshape(nblk, 1), blk_count, maps, 1.0 / (foot * probe_n)
     )
     return (sens.reshape(SPD), new.reshape(n_sens), density)
 

time: 244 us -> 230 us (0.943)
  waiting for transfers between devices: 97.7 us -> 72.2 us
  starting transfers between devices: 97 us -> 109 us
    ppermute x39, waiting for transfers between devices: 87.5 us -> 62 us  [shift_to(): return lax.ppermute(x, AXES, pairs)]
    ppermute x39, starting transfers between devices: 87.4 us -> 99 us  [shift_to(): return lax.ppermute(x, AXES, pairs)]
  transfers between devices with their start and end apart: 40 -> 40, of which waited for: 11 -> 14; matrix products, arithmetic and copies ran while one was open for 0% -> 0% of each run, Pallas kernels for 10% -> 10%
where the time goes in v10:
time: 230 us; the launch traced here: 229 us
  starting transfers between devices  109 us (47%)
  waiting for transfers between devices  72.2 us (31%)
  Pallas kernels  43 us (19%)
  local copies, waits for them, and re-layouts  3.08 us (1%)
    ppermute x39, starting transfers between devices, shift_to(): return lax.ppermute(x, AXES, pairs)  99 us
    ppermute x39, waiting for transfers between devices, shift_to(): return lax.ppermute(x, AXES, pairs)  62 us
    pallas_call x1, Pallas kernels, gather_flows(): pl.pallas_call(body, in_specs=[hbm, hbm, vmem, vmem, smem, smem] + [smem]...  15.2 us
    pallas_call x3, Pallas kernels, mix_tiles(): pl.pallas_call(body, grid=(each,), in_specs=[pl.BlockSpec(memory_space=pl...  11.5 us
    pallas_call x1, Pallas kernels, spread_squares(): pl.pallas_call(body, grid=(steps + 1,), in_specs=[pl.BlockSpec(memory_spa...  10.7 us
    all_to_all x1, starting transfers between devices, exchange(): return lax.all_to_all(x, axes, split_axis=0, concat_axis=0, tiled=True)  10.3 us
    all_to_all x1, waiting for transfers between devices, exchange(): return lax.all_to_all(x, axes, split_axis=0, concat_axis=0, tiled=True)  10.2 us
  transfers between devices with their start and end apart: 40, of which 14 were waited for; matrix products, arithmetic and copies ran while one was open for 0% of the time, Pallas kernels for 10%

profile of v10, /device:TPU:1, one launch (start us, length us, event | category | flops | bytes accessed | tf_op | source)
XLA Modules:
  0.0 229.2 jit_solution(14219258727140087242)
XLA Ops:
  1.3 15.2 %gather_flows.1 = (bf16[5,264,128]{2,1,0:T(8,128)(2,1)}, bf16[5,264,128]{2,1,0:T(8,128)(2,1)}, bf16[5,264,128]{2,1,0:T(8,128)(2,1)}, bf16[5,264,128]{2,1,0:T(8,1...) custom-call(bf16[8192,256]{1,0:T(8,128)(2,1)} %bitcast.13, ...), custom_call_target="tpu_custom_call" | custom-call | tf_op jit(solution)/shard_map/gather_flows/pallas_call | solution.py:104
  16.5 1.5 collective-permute-start.26
  17.9 1.3 collective-permute-start.27
  19.3 1.5 collective-permute-start.28
  20.7 1.5 collective-permute-start.29
  22.6 1.6 collective-permute-start.31
  24.3 4.5 %collective-permute-done.27.refs_2_ = bf16[5,264,128]{2,1,0:T(8,128)(2,1)S(1)} collective-permute-done((bf16[5,264,128]{2,1,0:T(8,128)(2,1)}, bf16[5,264,128]{2,1,0:T(8,128)(2,1)S(1)}, u32[]{:S(2)}, u32[]{:S(2)}) %collective-permute-start.27) | collective-permute-done | bytes 337952 | tf_op jit(solution)/shard_map/ppermute | solution.py:372
  28.8 3.0 %collective-permute-start.32 = (bf16[5,264,128]{2,1,0:T(8,128)(2,1)}, bf16[5,264,128]{2,1,0:T(8,128)(2,1)S(1)}, u32[]{:S(2)}, u32[]{:S(2)}) collective-permute-start(bf16[5,264,128]{2,1,0:T(8,128)(2,1)} %get-tuple-element.106), channel_id=1, source_target_pairs={{0,17},{1,16},{2,19},{3,18},{4,21},{5,20},{6,23},{7,22},{8,25},{9,... | collective-permute-start | bytes 1013768 | tf_op jit(solution)/shard_map/ppermute | solution.py:372
  31.8 4.5 %collective-permute-done.28.refs_3_ = bf16[5,264,128]{2,1,0:T(8,128)(2,1)S(1)} collective-permute-done((bf16[5,264,128]{2,1,0:T(8,128)(2,1)}, bf16[5,264,128]{2,1,0:T(8,128)(2,1)S(1)}, u32[]{:S(2)}, u32[]{:S(2)}) %collective-permute-start.28) | collective-permute-done | bytes 337952 | tf_op jit(solution)/shard_map/ppermute | solution.py:372
  36.4 1.8 collective-permute-start.1
  38.7 15.2 %collective-permute-start.2 = (bf16[5,264,128]{2,1,0:T(8,128)(2,1)}, bf16[5,264,128]{2,1,0:T(8,128)(2,1)S(1)}, u32[]{:S(2)}, u32[]{:S(2)}) collective-permute-start(bf16[5,264,128]{2,1,0:T(8,128)(2,1)} %get-tuple-element.70), channel_id=1, source_target_pairs={{0,3},{1,2},{2,5},{3,4},{4,7},{5,6},{6,1},{7,0},{8,11},{9,10},{10,... | collective-permute-start | bytes 1013768 | tf_op jit(solution)/shard_map/ppermute | solution.py:372
  53.9 1.0 collective-permute-start.3
  55.0 1.5 collective-permute-start.4
  56.5 1.0 collective-permute-start.5
  57.5 3.6 %collective-permute-start.6 = (bf16[5,264,128]{2,1,0:T(8,128)(2,1)}, bf16[5,264,128]{2,1,0:T(8,128)(2,1)S(1)}, u32[]{:S(2)}, u32[]{:S(2)}) collective-permute-start(bf16[5,264,128]{2,1,0:T(8,128)(2,1)} %get-tuple-element.74), channel_id=1, source_target_pairs={{0,5},{1,4},{2,7},{3,6},{4,1},{5,0},{6,3},{7,2},{8,13},{9,12},{10,... | collective-permute-start | bytes 1013768 | tf_op jit(solution)/shard_map/ppermute | solution.py:372
  61.1 2.3 %collective-permute-done.2.refs_3_ = bf16[5,264,128]{2,1,0:T(8,128)(2,1)S(1)} collective-permute-done((bf16[5,264,128]{2,1,0:T(8,128)(2,1)}, bf16[5,264,128]{2,1,0:T(8,128)(2,1)S(1)}, u32[]{:S(2)}, u32[]{:S(2)}) %collective-permute-start.2) | collective-permute-done | bytes 337952 | tf_op jit(solution)/shard_map/ppermute | solution.py:372
  63.4 0.9 collective-permute-done.3.refs_4_
  64.3 1.3 collective-permute-start.14
  65.6 3.5 %collective-permute-done.4.refs_5_ = bf16[5,264,128]{2,1,0:T(8,128)(2,1)S(1)} collective-permute-done((bf16[5,264,128]{2,1,0:T(8,128)(2,1)}, bf16[5,264,128]{2,1,0:T(8,128)(2,1)S(1)}, u32[]{:S(2)}, u32[]{:S(2)}) %collective-permute-start.4) | collective-permute-done | bytes 337952 | tf_op jit(solution)/shard_map/ppermute | solution.py:372
  69.0 17.3 %collective-permute-start.15 = (bf16[6,264,128]{2,1,0:T(8,128)(2,1)}, bf16[6,264,128]{2,1,0:T(8,128)(2,1)S(1)}, u32[]{:S(2)}, u32[]{:S(2)}) collective-permute-start(bf16[6,264,128]{2,1,0:T(8,128)(2,1)} %get-tuple-element.86), channel_id=1, source_target_pairs={{0,33},{1,32},{2,35},{3,34},{4,37},{5,36},{6,39},{7,38},{8,41},{9,... | collective-permute-start | bytes 1216520 | tf_op jit(solution)/shard_map/ppermute | solution.py:372
  86.4 1.4 collective-permute-start.16
  88.6 1.0 collective-permute-start.18
  89.6 1.0 copy-done.2
  90.5 3.6 %mix_tiles.5 = (bf16[5,256,256]{2,1,0:T(8,128)(2,1)S(1)}, bf16[5,256,256]{2,1,0:T(8,128)(2,1)S(1)}, bf16[5,256,256]{2,1,0:T(8,128)(2,1)S(1)}, bf16[5,256,256]{2,1,0:T(8,128)(2,1)S(1)}) custom-call(s32[1]{0:T(128)} %bitcast.5.refs_6_.at_ref, bf16[5,264,128]{2,1,0:T(8,128)(2,1)S(1)} %copy-done.2, bf16[5,264,128]{2,1,0:T(8,128)(2,1)S(1)} %collective-permute-done.26.refs_1_, ...), custom_call_target="tpu_custom_call" | custom-call | tf_op jit(solution)/shard_map/mix_tiles/pallas_call | solution.py:151
  94.2 1.6 collective-permute-start.33
  95.8 2.3 collective-permute-done.15.refs_3_
  98.1 3.7 %collective-permute-start.34 = (bf16[5,256,256]{2,1,0:T(8,128)(2,1)S(1)}, bf16[5,256,256]{2,1,0:T(8,128)(2,1)S(1)}, u32[]{:S(2)}, u32[]{:S(2)}) collective-permute-start(bf16[5,256,256]{2,1,0:T(8,128)(2,1)S(1)} %get-tuple-element.109), channel_id=1, source_target_pairs={{0,6},{1,7},{2,0},{3,1},{4,2},{5,3},{6,4},{7,5},{8,14},{9,15},{10,... | collective-permute-start | bytes 1966088 | tf_op jit(solution)/shard_map/ppermute | solution.py:372
  101.8 1.0 copy-done.1
  102.7 3.6 %mix_tiles.3 = (bf16[5,256,256]{2,1,0:T(8,128)(2,1)S(1)}, bf16[5,256,256]{2,1,0:T(8,128)(2,1)S(1)}, bf16[5,256,256]{2,1,0:T(8,128)(2,1)S(1)}, bf16[5,256,256]{2,1,0:T(8,128)(2,1)S(1)}) custom-call(s32[1]{0:T(128)} %bitcast.1.refs_7_.at_ref, bf16[5,264,128]{2,1,0:T(8,128)(2,1)S(1)} %copy-done.1, bf16[5,264,128]{2,1,0:T(8,128)(2,1)S(1)} %collective-permute-done.refs_1_, ...), custom_call_target="tpu_custom_call" | custom-call | tf_op jit(solution)/shard_map/mix_tiles/pallas_call | solution.py:151
  106.8 12.2 %collective-permute-start.19 = (bf16[6,264,128]{2,1,0:T(8,128)(2,1)}, bf16[6,264,128]{2,1,0:T(8,128)(2,1)S(1)}, u32[]{:S(2)}, u32[]{:S(2)}) collective-permute-start(bf16[6,264,128]{2,1,0:T(8,128)(2,1)} %get-tuple-element.90), channel_id=1, source_target_pairs={{0,65},{1,64},{2,67},{3,66},{4,69},{5,68},{6,71},{7,70},{8,73},{9,... | collective-permute-start | bytes 1216520 | tf_op jit(solution)/shard_map/ppermute | solution.py:372
  119.1 23.8 %collective-permute-done.19.refs_7_ = bf16[6,264,128]{2,1,0:T(8,128)(2,1)S(1)} collective-permute-done((bf16[6,264,128]{2,1,0:T(8,128)(2,1)}, bf16[6,264,128]{2,1,0:T(8,128)(2,1)S(1)}, u32[]{:S(2)}, u32[]{:S(2)}) %collective-permute-start.19) | collective-permute-done | bytes 405536 | tf_op jit(solution)/shard_map/ppermute | solution.py:372
  142.9 1.0 copy-done
  143.9 4.3 %mix_tiles.4 = (bf16[6,256,256]{2,1,0:T(8,128)(2,1)S(1)}, bf16[6,256,256]{2,1,0:T(8,128)(2,1)S(1)}, bf16[6,256,256]{2,1,0:T(8,128)(2,1)S(1)}, bf16[6,256,256]{2,1,0:T(8,128)(2,1)S(1)}) custom-call(s32[1]{0:T(128)} %bitcast.refs_8_.at_ref, bf16[6,264,128]{2,1,0:T(8,128)(2,1)S(1)} %copy-done, bf16[6,264,128]{2,1,0:T(8,128)(2,1)S(1)} %collective-permute-done.13.refs_1_, ...), custom_call_target="tpu_custom_call" | custom-call | tf_op jit(solution)/shard_map/mix_tiles/pallas_call | solution.py:151
  148.3 2.7 %collective-permute-start.21 = (bf16[6,256,256]{2,1,0:T(8,128)(2,1)S(1)}, bf16[6,256,256]{2,1,0:T(8,128)(2,1)S(1)}, u32[]{:S(2)}, u32[]{:S(2)}) collective-permute-start(bf16[6,256,256]{2,1,0:T(8,128)(2,1)S(1)} %get-tuple-element.93), channel_id=1, source_target_pairs={{0,24},{1,25},{2,26},{3,27},{4,28},{5,29},{6,30},{7,31},{8,0},{9,1... | collective-permute-start | bytes 2359304 | tf_op jit(solution)/shard_map/ppermute | solution.py:372
  151.6 14.7 %collective-permute-done.8.refs_2_ = bf16[5,256,256]{2,1,0:T(8,128)(2,1)S(1)} collective-permute-done((bf16[5,256,256]{2,1,0:T(8,128)(2,1)S(1)}, bf16[5,256,256]{2,1,0:T(8,128)(2,1)S(1)}, u32[]{:S(2)}, u32[]{:S(2)}) %collective-permute-start.8) | collective-permute-done | bytes 655392 | tf_op jit(solution)/shard_map/ppermute | solution.py:372
  166.3 1.6 collective-permute-done.9.refs_3_
  167.9 14.8 %collective-permute-start.37 = (bf16[5,64,256]{2,1,0:T(8,128)(2,1)S(1)}, bf16[5,64,256]{2,1,0:T(8,128)(2,1)S(1)}, u32[]{:S(2)}, u32[]{:S(2)}) collective-permute-start(bf16[5,64,256]{2,1,0:T(8,128)(2,1)S(1)} %get-tuple-element.113), channel_id=1, source_target_pairs={{0,96},{1,97},{2,98},{3,99},{4,100},{5,101},{6,102},{7,103},{8,104... | collective-permute-start | bytes 491528 | tf_op jit(solution)/shard_map/ppermute | solution.py:372
  183.2 1.9 collective-permute-done.20.refs_1_
  185.7 3.0 %collective-permute-start.24 = (bf16[6,64,256]{2,1,0:T(8,128)(2,1)S(1)}, bf16[6,64,256]{2,1,0:T(8,128)(2,1)S(1)}, u32[]{:S(2)}, u32[]{:S(2)}) collective-permute-start(bf16[6,64,256]{2,1,0:T(8,128)(2,1)S(1)} %get-tuple-element.97), channel_id=1, source_target_pairs={{0,6},{1,7},{2,0},{3,1},{4,2},{5,3},{6,4},{7,5},{8,14},{9,15},{10,... | collective-permute-start | bytes 589832 | tf_op jit(solution)/shard_map/ppermute | solution.py:372
  188.7 1.2 collective-permute-start.25
  189.9 1.2 collective-permute-done.38.refs_11_
  191.1 1.5 collective-permute-start.11
  192.6 1.0 collective-permute-start.12
  193.5 10.7 %spread_squares.1.maps_hbm = f32[640,32,256]{2,1,0:T(8,128)} custom-call(s32[1]{0:T(128)} %bitcast.6.me_ref, s32[128,128]{1,0:T(8,128)} %rows_ref.1, bf16[128,128]{1,0:T(8,128)(2,1)} %coef_ref.1, s32[1,1024]{1,0:T(1,128)} %bitcast.14), custom_call_target="tpu_custom_call" | custom-call | tf_op jit(solution)/shard_map/spread_squares/pallas_call | solution.py:261
  204.3 1.1 square_sums.1
  205.4 10.3 %all-to-all-start = ((f32[128,1,384]{2,1,0:T(1,128)}), f32[128,1,384]{2,1,0:T(1,128)S(1)}, u32[]{:S(2)}, u32[]{:S(2)}) async-start(f32[128,1,384]{2,1,0:T(1,128)} %square_sums.1), calls=%async_computation | async-start | bytes 393216 | tf_op jit(solution)/shard_map/all_to_all | solution.py:355
  215.8 10.2 %all-to-all-done.parts_ref = f32[128,1,384]{2,1,0:T(1,128)S(1)} async-done(((f32[128,1,384]{2,1,0:T(1,128)}), f32[128,1,384]{2,1,0:T(1,128)S(1)}, u32[]{:S(2)}, u32[]{:S(2)}) %all-to-all-start) | async-done | bytes 196640 | tf_op jit(solution)/shard_map/all_to_all | solution.py:355
  226.0 3.1 %finish.1 = (f32[1,8]{1,0:T(1,128)}, f32[8,128]{1,0:T(8,128)}, f32[32,256]{1,0:T(8,128)}) custom-call(s32[1]{0:T(128)S(6)} %copy.11.refs_4_.count_ref, f32[128,1,384]{2,1,0:T(1,128)S(1)} %all-to-all-done.parts_ref, f32[8,128]{1,0:T(8,128)S(1)} %bitcast.12, s32[128,1]{1,0:T(8,128)S(1)} %copy.10.sensor_ref, f32[640,32,256]{2,1,0:T(8,128)} %spread_squares.1.maps_hbm), custom_call_target="tpu_custom_call" | custom-call | tf_op jit(solution)/shard_map/finish/pallas_call | solution.py:334
  (53 shorter events, 4.4 us)
Async XLA Ops:
  16.5 199.2 %copy-start.4 = (s32[128]{0:T(128)S(1)}, s32[128]{0:T(128)}, u32[]{:S(2)}) copy-start(s32[128]{0:T(128)} %param.9) | copy-start | bytes 1540
  16.5 209.5 %copy-start.3 = (f32[1024]{0:T(1024)S(1)}, f32[1024]{0:T(1024)}, u32[]{:S(2)}) copy-start(f32[1024]{0:T(1024)} %param.13) | copy-start | bytes 12292
  16.5 6.2 %collective-permute-start.26 = (bf16[5,264,128]{2,1,0:T(8,128)(2,1)}, bf16[5,264,128]{2,1,0:T(8,128)(2,1)S(1)}, u32[]{:S(2)}, u32[]{:S(2)}) collective-permute-start(bf16[5,264,128]{2,1,0:T(8,128)(2,1)} %get-tuple-element.100), channel_id=1, source_target_pairs={{0,1},{1,0},{2,3},{3,2},{4,5},{5,4},{6,7},{7,6},{8,9},{9,8},{10,11... | collective-permute-start | bytes 1013768 | tf_op jit(solution)/shard_map/ppermute | solution.py:372
  17.9 10.8 %collective-permute-start.27 = (bf16[5,264,128]{2,1,0:T(8,128)(2,1)}, bf16[5,264,128]{2,1,0:T(8,128)(2,1)S(1)}, u32[]{:S(2)}, u32[]{:S(2)}) collective-permute-start(bf16[5,264,128]{2,1,0:T(8,128)(2,1)} %get-tuple-element.101), channel_id=1, source_target_pairs={{0,8},{1,9},{2,10},{3,11},{4,12},{5,13},{6,14},{7,15},{8,16},{9,17... | collective-permute-start | bytes 1013768 | tf_op jit(solution)/shard_map/ppermute | solution.py:372
  19.3 17.0 %collective-permute-start.28 = (bf16[5,264,128]{2,1,0:T(8,128)(2,1)}, bf16[5,264,128]{2,1,0:T(8,128)(2,1)S(1)}, u32[]{:S(2)}, u32[]{:S(2)}) collective-permute-start(bf16[5,264,128]{2,1,0:T(8,128)(2,1)} %get-tuple-element.102), channel_id=1, source_target_pairs={{0,9},{1,8},{2,11},{3,10},{4,13},{5,12},{6,15},{7,14},{8,17},{9,16... | collective-permute-start | bytes 1013768 | tf_op jit(solution)/shard_map/ppermute | solution.py:372
  20.7 15.7 %collective-permute-start.29 = (bf16[5,264,128]{2,1,0:T(8,128)(2,1)}, bf16[5,264,128]{2,1,0:T(8,128)(2,1)S(1)}, u32[]{:S(2)}, u32[]{:S(2)}) collective-permute-start(bf16[5,264,128]{2,1,0:T(8,128)(2,1)} %get-tuple-element.103), channel_id=1, source_target_pairs={{0,24},{1,25},{2,26},{3,27},{4,28},{5,29},{6,30},{7,31},{8,0},{9,1... | collective-permute-start | bytes 1013768 | tf_op jit(solution)/shard_map/ppermute | solution.py:372
  22.2 16.5 %collective-permute-start.30 = (bf16[5,264,128]{2,1,0:T(8,128)(2,1)}, bf16[5,264,128]{2,1,0:T(8,128)(2,1)S(1)}, u32[]{:S(2)}, u32[]{:S(2)}) collective-permute-start(bf16[5,264,128]{2,1,0:T(8,128)(2,1)} %get-tuple-element.104), channel_id=1, source_target_pairs={{0,25},{1,24},{2,27},{3,26},{4,29},{5,28},{6,31},{7,30},{8,1},{9,0... | collective-permute-start | bytes 1013768 | tf_op jit(solution)/shard_map/ppermute | solution.py:372
  22.6 31.3 %collective-permute-start.31 = (bf16[5,264,128]{2,1,0:T(8,128)(2,1)}, bf16[5,264,128]{2,1,0:T(8,128)(2,1)S(1)}, u32[]{:S(2)}, u32[]{:S(2)}) collective-permute-start(bf16[5,264,128]{2,1,0:T(8,128)(2,1)} %get-tuple-element.105), channel_id=1, source_target_pairs={{0,16},{1,17},{2,18},{3,19},{4,20},{5,21},{6,22},{7,23},{8,24},{9,... | collective-permute-start | bytes 1013768 | tf_op jit(solution)/shard_map/ppermute | solution.py:372
  28.8 26.2 %collective-permute-start.32 = (bf16[5,264,128]{2,1,0:T(8,128)(2,1)}, bf16[5,264,128]{2,1,0:T(8,128)(2,1)S(1)}, u32[]{:S(2)}, u32[]{:S(2)}) collective-permute-start(bf16[5,264,128]{2,1,0:T(8,128)(2,1)} %get-tuple-element.106), channel_id=1, source_target_pairs={{0,17},{1,16},{2,19},{3,18},{4,21},{5,20},{6,23},{7,22},{8,25},{9,... | collective-permute-start | bytes 1013768 | tf_op jit(solution)/shard_map/ppermute | solution.py:372
  36.3 20.2 %collective-permute-start = (bf16[5,264,128]{2,1,0:T(8,128)(2,1)}, bf16[5,264,128]{2,1,0:T(8,128)(2,1)S(1)}, u32[]{:S(2)}, u32[]{:S(2)}) collective-permute-start(bf16[5,264,128]{2,1,0:T(8,128)(2,1)} %get-tuple-element.68), channel_id=1, source_target_pairs={{0,1},{1,0},{2,3},{3,2},{4,5},{5,4},{6,7},{7,6},{8,9},{9,8},{10,11... | collective-permute-start | bytes 1013768 | tf_op jit(solution)/shard_map/ppermute | solution.py:372
  36.4 21.0 %collective-permute-start.1 = (bf16[5,264,128]{2,1,0:T(8,128)(2,1)}, bf16[5,264,128]{2,1,0:T(8,128)(2,1)S(1)}, u32[]{:S(2)}, u32[]{:S(2)}) collective-permute-start(bf16[5,264,128]{2,1,0:T(8,128)(2,1)} %get-tuple-element.69), channel_id=1, source_target_pairs={{0,2},{1,3},{2,4},{3,5},{4,6},{5,7},{6,0},{7,1},{8,10},{9,11},{10,... | collective-permute-start | bytes 1013768 | tf_op jit(solution)/shard_map/ppermute | solution.py:372
  38.7 24.6 %collective-permute-start.2 = (bf16[5,264,128]{2,1,0:T(8,128)(2,1)}, bf16[5,264,128]{2,1,0:T(8,128)(2,1)S(1)}, u32[]{:S(2)}, u32[]{:S(2)}) collective-permute-start(bf16[5,264,128]{2,1,0:T(8,128)(2,1)} %get-tuple-element.70), channel_id=1, source_target_pairs={{0,3},{1,2},{2,5},{3,4},{4,7},{5,6},{6,1},{7,0},{8,11},{9,10},{10,... | collective-permute-start | bytes 1013768 | tf_op jit(solution)/shard_map/ppermute | solution.py:372
  53.9 10.3 %collective-permute-start.3 = (bf16[5,264,128]{2,1,0:T(8,128)(2,1)}, bf16[5,264,128]{2,1,0:T(8,128)(2,1)S(1)}, u32[]{:S(2)}, u32[]{:S(2)}) collective-permute-start(bf16[5,264,128]{2,1,0:T(8,128)(2,1)} %get-tuple-element.71), channel_id=1, source_target_pairs={{0,6},{1,7},{2,0},{3,1},{4,2},{5,3},{6,4},{7,5},{8,14},{9,15},{10,... | collective-permute-start | bytes 1013768 | tf_op jit(solution)/shard_map/ppermute | solution.py:372
  55.0 14.1 %collective-permute-start.4 = (bf16[5,264,128]{2,1,0:T(8,128)(2,1)}, bf16[5,264,128]{2,1,0:T(8,128)(2,1)S(1)}, u32[]{:S(2)}, u32[]{:S(2)}) collective-permute-start(bf16[5,264,128]{2,1,0:T(8,128)(2,1)} %get-tuple-element.72), channel_id=1, source_target_pairs={{0,7},{1,6},{2,1},{3,0},{4,3},{5,2},{6,5},{7,4},{8,15},{9,14},{10,... | collective-permute-start | bytes 1013768 | tf_op jit(solution)/shard_map/ppermute | solution.py:372
  56.5 29.9 %collective-permute-start.5 = (bf16[5,264,128]{2,1,0:T(8,128)(2,1)}, bf16[5,264,128]{2,1,0:T(8,128)(2,1)S(1)}, u32[]{:S(2)}, u32[]{:S(2)}) collective-permute-start(bf16[5,264,128]{2,1,0:T(8,128)(2,1)} %get-tuple-element.73), channel_id=1, source_target_pairs={{0,4},{1,5},{2,6},{3,7},{4,0},{5,1},{6,2},{7,3},{8,12},{9,13},{10,... | collective-permute-start | bytes 1013768 | tf_op jit(solution)/shard_map/ppermute | solution.py:372
  57.5 30.3 %collective-permute-start.6 = (bf16[5,264,128]{2,1,0:T(8,128)(2,1)}, bf16[5,264,128]{2,1,0:T(8,128)(2,1)S(1)}, u32[]{:S(2)}, u32[]{:S(2)}) collective-permute-start(bf16[5,264,128]{2,1,0:T(8,128)(2,1)} %get-tuple-element.74), channel_id=1, source_target_pairs={{0,5},{1,4},{2,7},{3,6},{4,1},{5,0},{6,3},{7,2},{8,13},{9,12},{10,... | collective-permute-start | bytes 1013768 | tf_op jit(solution)/shard_map/ppermute | solution.py:372
  63.4 25.2 %collective-permute-start.13 = (bf16[6,264,128]{2,1,0:T(8,128)(2,1)}, bf16[6,264,128]{2,1,0:T(8,128)(2,1)S(1)}, u32[]{:S(2)}, u32[]{:S(2)}) collective-permute-start(bf16[6,264,128]{2,1,0:T(8,128)(2,1)} %get-tuple-element.84), channel_id=1, source_target_pairs={{0,1},{1,0},{2,3},{3,2},{4,5},{5,4},{6,7},{7,6},{8,9},{9,8},{10,11... | collective-permute-start | bytes 1216520 | tf_op jit(solution)/shard_map/ppermute | solution.py:372
  64.3 29.9 %collective-permute-start.14 = (bf16[6,264,128]{2,1,0:T(8,128)(2,1)}, bf16[6,264,128]{2,1,0:T(8,128)(2,1)S(1)}, u32[]{:S(2)}, u32[]{:S(2)}) collective-permute-start(bf16[6,264,128]{2,1,0:T(8,128)(2,1)} %get-tuple-element.85), channel_id=1, source_target_pairs={{0,32},{1,33},{2,34},{3,35},{4,36},{5,37},{6,38},{7,39},{8,40},{9,... | collective-permute-start | bytes 1216520 | tf_op jit(solution)/shard_map/ppermute | solution.py:372
  69.0 29.0 %collective-permute-start.15 = (bf16[6,264,128]{2,1,0:T(8,128)(2,1)}, bf16[6,264,128]{2,1,0:T(8,128)(2,1)S(1)}, u32[]{:S(2)}, u32[]{:S(2)}) collective-permute-start(bf16[6,264,128]{2,1,0:T(8,128)(2,1)} %get-tuple-element.86), channel_id=1, source_target_pairs={{0,33},{1,32},{2,35},{3,34},{4,37},{5,36},{6,39},{7,38},{8,41},{9,... | collective-permute-start | bytes 1216520 | tf_op jit(solution)/shard_map/ppermute | solution.py:372
  86.4 15.4 %collective-permute-start.16 = (bf16[6,264,128]{2,1,0:T(8,128)(2,1)}, bf16[6,264,128]{2,1,0:T(8,128)(2,1)S(1)}, u32[]{:S(2)}, u32[]{:S(2)}) collective-permute-start(bf16[6,264,128]{2,1,0:T(8,128)(2,1)} %get-tuple-element.87), channel_id=1, source_target_pairs={{0,96},{1,97},{2,98},{3,99},{4,100},{5,101},{6,102},{7,103},{8,104... | collective-permute-start | bytes 1216520 | tf_op jit(solution)/shard_map/ppermute | solution.py:372
  87.8 18.6 %collective-permute-start.17 = (bf16[6,264,128]{2,1,0:T(8,128)(2,1)}, bf16[6,264,128]{2,1,0:T(8,128)(2,1)S(1)}, u32[]{:S(2)}, u32[]{:S(2)}) collective-permute-start(bf16[6,264,128]{2,1,0:T(8,128)(2,1)} %get-tuple-element.88), channel_id=1, source_target_pairs={{0,97},{1,96},{2,99},{3,98},{4,101},{5,100},{6,103},{7,102},{8,105... | collective-permute-start | bytes 1216520 | tf_op jit(solution)/shard_map/ppermute | solution.py:372
  88.6 18.3 %collective-permute-start.18 = (bf16[6,264,128]{2,1,0:T(8,128)(2,1)}, bf16[6,264,128]{2,1,0:T(8,128)(2,1)S(1)}, u32[]{:S(2)}, u32[]{:S(2)}) collective-permute-start(bf16[6,264,128]{2,1,0:T(8,128)(2,1)} %get-tuple-element.89), channel_id=1, source_target_pairs={{0,64},{1,65},{2,66},{3,67},{4,68},{5,69},{6,70},{7,71},{8,72},{9,... | collective-permute-start | bytes 1216520 | tf_op jit(solution)/shard_map/ppermute | solution.py:372
  89.6 1.0 copy-start.2
  94.2 54.2 %collective-permute-start.33 = (bf16[5,256,256]{2,1,0:T(8,128)(2,1)S(1)}, bf16[5,256,256]{2,1,0:T(8,128)(2,1)S(1)}, u32[]{:S(2)}, u32[]{:S(2)}) collective-permute-start(bf16[5,256,256]{2,1,0:T(8,128)(2,1)S(1)} %get-tuple-element.108), channel_id=1, source_target_pairs={{0,2},{1,3},{2,4},{3,5},{4,6},{5,7},{6,0},{7,1},{8,10},{9,11},{10,... | collective-permute-start | bytes 1966088 | tf_op jit(solution)/shard_map/ppermute | solution.py:372
  98.1 52.9 %collective-permute-start.34 = (bf16[5,256,256]{2,1,0:T(8,128)(2,1)S(1)}, bf16[5,256,256]{2,1,0:T(8,128)(2,1)S(1)}, u32[]{:S(2)}, u32[]{:S(2)}) collective-permute-start(bf16[5,256,256]{2,1,0:T(8,128)(2,1)S(1)} %get-tuple-element.109), channel_id=1, source_target_pairs={{0,6},{1,7},{2,0},{3,1},{4,2},{5,3},{6,4},{7,5},{8,14},{9,15},{10,... | collective-permute-start | bytes 1966088 | tf_op jit(solution)/shard_map/ppermute | solution.py:372
  101.7 49.2 %collective-permute-start.35 = (bf16[5,256,256]{2,1,0:T(8,128)(2,1)S(1)}, bf16[5,256,256]{2,1,0:T(8,128)(2,1)S(1)}, u32[]{:S(2)}, u32[]{:S(2)}) collective-permute-start(bf16[5,256,256]{2,1,0:T(8,128)(2,1)S(1)} %get-tuple-element.110), channel_id=1, source_target_pairs={{0,4},{1,5},{2,6},{3,7},{4,0},{5,1},{6,2},{7,3},{8,12},{9,13},{10,... | collective-permute-start | bytes 1966088 | tf_op jit(solution)/shard_map/ppermute | solution.py:372
  101.7 1.0 copy-start.1
  106.3 44.7 %collective-permute-start.7 = (bf16[5,256,256]{2,1,0:T(8,128)(2,1)S(1)}, bf16[5,256,256]{2,1,0:T(8,128)(2,1)S(1)}, u32[]{:S(2)}, u32[]{:S(2)}) collective-permute-start(bf16[5,256,256]{2,1,0:T(8,128)(2,1)S(1)} %get-tuple-element.76), channel_id=1, source_target_pairs={{0,32},{1,33},{2,34},{3,35},{4,36},{5,37},{6,38},{7,39},{8,40},{9,... | collective-permute-start | bytes 1966088 | tf_op jit(solution)/shard_map/ppermute | solution.py:372
  106.8 36.1 %collective-permute-start.19 = (bf16[6,264,128]{2,1,0:T(8,128)(2,1)}, bf16[6,264,128]{2,1,0:T(8,128)(2,1)S(1)}, u32[]{:S(2)}, u32[]{:S(2)}) collective-permute-start(bf16[6,264,128]{2,1,0:T(8,128)(2,1)} %get-tuple-element.90), channel_id=1, source_target_pairs={{0,65},{1,64},{2,67},{3,66},{4,69},{5,68},{6,71},{7,70},{8,73},{9,... | collective-permute-start | bytes 1216520 | tf_op jit(solution)/shard_map/ppermute | solution.py:372
  142.9 1.0 copy-start
  148.2 36.8 %collective-permute-start.20 = (bf16[6,256,256]{2,1,0:T(8,128)(2,1)S(1)}, bf16[6,256,256]{2,1,0:T(8,128)(2,1)S(1)}, u32[]{:S(2)}, u32[]{:S(2)}) collective-permute-start(bf16[6,256,256]{2,1,0:T(8,128)(2,1)S(1)} %get-tuple-element.92), channel_id=1, source_target_pairs={{0,8},{1,9},{2,10},{3,11},{4,12},{5,13},{6,14},{7,15},{8,16},{9,17... | collective-permute-start | bytes 2359304 | tf_op jit(solution)/shard_map/ppermute | solution.py:372
  148.3 36.8 %collective-permute-start.21 = (bf16[6,256,256]{2,1,0:T(8,128)(2,1)S(1)}, bf16[6,256,256]{2,1,0:T(8,128)(2,1)S(1)}, u32[]{:S(2)}, u32[]{:S(2)}) collective-permute-start(bf16[6,256,256]{2,1,0:T(8,128)(2,1)S(1)} %get-tuple-element.93), channel_id=1, source_target_pairs={{0,24},{1,25},{2,26},{3,27},{4,28},{5,29},{6,30},{7,31},{8,0},{9,1... | collective-permute-start | bytes 2359304 | tf_op jit(solution)/shard_map/ppermute | solution.py:372
  151.0 15.3 %collective-permute-start.8 = (bf16[5,256,256]{2,1,0:T(8,128)(2,1)S(1)}, bf16[5,256,256]{2,1,0:T(8,128)(2,1)S(1)}, u32[]{:S(2)}, u32[]{:S(2)}) collective-permute-start(bf16[5,256,256]{2,1,0:T(8,128)(2,1)S(1)} %get-tuple-element.77), channel_id=1, source_target_pairs={{0,96},{1,97},{2,98},{3,99},{4,100},{5,101},{6,102},{7,103},{8,104... | collective-permute-start | bytes 1966088 | tf_op jit(solution)/shard_map/ppermute | solution.py:372
  151.0 16.9 %collective-permute-start.9 = (bf16[5,256,256]{2,1,0:T(8,128)(2,1)S(1)}, bf16[5,256,256]{2,1,0:T(8,128)(2,1)S(1)}, u32[]{:S(2)}, u32[]{:S(2)}) collective-permute-start(bf16[5,256,256]{2,1,0:T(8,128)(2,1)S(1)} %get-tuple-element.78), channel_id=1, source_target_pairs={{0,64},{1,65},{2,66},{3,67},{4,68},{5,69},{6,70},{7,71},{8,72},{9,... | collective-permute-start | bytes 1966088 | tf_op jit(solution)/shard_map/ppermute | solution.py:372
  151.1 34.0 %collective-permute-start.22 = (bf16[6,256,256]{2,1,0:T(8,128)(2,1)S(1)}, bf16[6,256,256]{2,1,0:T(8,128)(2,1)S(1)}, u32[]{:S(2)}, u32[]{:S(2)}) collective-permute-start(bf16[6,256,256]{2,1,0:T(8,128)(2,1)S(1)} %get-tuple-element.94), channel_id=1, source_target_pairs={{0,16},{1,17},{2,18},{3,19},{4,20},{5,21},{6,22},{7,23},{8,24},{9,... | collective-permute-start | bytes 2359304 | tf_op jit(solution)/shard_map/ppermute | solution.py:372
  166.3 19.4 %collective-permute-start.36 = (bf16[5,64,256]{2,1,0:T(8,128)(2,1)S(1)}, bf16[5,64,256]{2,1,0:T(8,128)(2,1)S(1)}, u32[]{:S(2)}, u32[]{:S(2)}) collective-permute-start(bf16[5,64,256]{2,1,0:T(8,128)(2,1)S(1)} %get-tuple-element.112), channel_id=1, source_target_pairs={{0,32},{1,33},{2,34},{3,35},{4,36},{5,37},{6,38},{7,39},{8,40},{9,... | collective-permute-start | bytes 491528 | tf_op jit(solution)/shard_map/ppermute | solution.py:372
  167.9 20.8 %collective-permute-start.37 = (bf16[5,64,256]{2,1,0:T(8,128)(2,1)S(1)}, bf16[5,64,256]{2,1,0:T(8,128)(2,1)S(1)}, u32[]{:S(2)}, u32[]{:S(2)}) collective-permute-start(bf16[5,64,256]{2,1,0:T(8,128)(2,1)S(1)} %get-tuple-element.113), channel_id=1, source_target_pairs={{0,96},{1,97},{2,98},{3,99},{4,100},{5,101},{6,102},{7,103},{8,104... | collective-permute-start | bytes 491528 | tf_op jit(solution)/shard_map/ppermute | solution.py:372
  185.1 6.0 %collective-permute-start.38 = (bf16[5,64,256]{2,1,0:T(8,128)(2,1)S(1)}, bf16[5,64,256]{2,1,0:T(8,128)(2,1)S(1)}, u32[]{:S(2)}, u32[]{:S(2)}) collective-permute-start(bf16[5,64,256]{2,1,0:T(8,128)(2,1)S(1)} %get-tuple-element.114), channel_id=1, source_target_pairs={{0,64},{1,65},{2,66},{3,67},{4,68},{5,69},{6,70},{7,71},{8,72},{9,... | collective-permute-start | bytes 491528 | tf_op jit(solution)/shard_map/ppermute | solution.py:372
  185.1 7.5 %collective-permute-start.10 = (bf16[5,64,256]{2,1,0:T(8,128)(2,1)S(1)}, bf16[5,64,256]{2,1,0:T(8,128)(2,1)S(1)}, u32[]{:S(2)}, u32[]{:S(2)}) collective-permute-start(bf16[5,64,256]{2,1,0:T(8,128)(2,1)S(1)} %get-tuple-element.80), channel_id=1, source_target_pairs={{0,8},{1,9},{2,10},{3,11},{4,12},{5,13},{6,14},{7,15},{8,16},{9,17... | collective-permute-start | bytes 491528 | tf_op jit(solution)/shard_map/ppermute | solution.py:372
  185.6 18.7 %collective-permute-start.23 = (bf16[6,64,256]{2,1,0:T(8,128)(2,1)S(1)}, bf16[6,64,256]{2,1,0:T(8,128)(2,1)S(1)}, u32[]{:S(2)}, u32[]{:S(2)}) collective-permute-start(bf16[6,64,256]{2,1,0:T(8,128)(2,1)S(1)} %get-tuple-element.96), channel_id=1, source_target_pairs={{0,2},{1,3},{2,4},{3,5},{4,6},{5,7},{6,0},{7,1},{8,10},{9,11},{10,... | collective-permute-start | bytes 589832 | tf_op jit(solution)/shard_map/ppermute | solution.py:372
  185.7 18.6 %collective-permute-start.24 = (bf16[6,64,256]{2,1,0:T(8,128)(2,1)S(1)}, bf16[6,64,256]{2,1,0:T(8,128)(2,1)S(1)}, u32[]{:S(2)}, u32[]{:S(2)}) collective-permute-start(bf16[6,64,256]{2,1,0:T(8,128)(2,1)S(1)} %get-tuple-element.97), channel_id=1, source_target_pairs={{0,6},{1,7},{2,0},{3,1},{4,2},{5,3},{6,4},{7,5},{8,14},{9,15},{10,... | collective-permute-start | bytes 589832 | tf_op jit(solution)/shard_map/ppermute | solution.py:372
  188.7 15.6 %collective-permute-start.25 = (bf16[6,64,256]{2,1,0:T(8,128)(2,1)S(1)}, bf16[6,64,256]{2,1,0:T(8,128)(2,1)S(1)}, u32[]{:S(2)}, u32[]{:S(2)}) collective-permute-start(bf16[6,64,256]{2,1,0:T(8,128)(2,1)S(1)} %get-tuple-element.98), channel_id=1, source_target_pairs={{0,4},{1,5},{2,6},{3,7},{4,0},{5,1},{6,2},{7,3},{8,12},{9,13},{10,... | collective-permute-start | bytes 589832 | tf_op jit(solution)/shard_map/ppermute | solution.py:372
  191.1 13.2 %collective-permute-start.11 = (bf16[5,64,256]{2,1,0:T(8,128)(2,1)S(1)}, bf16[5,64,256]{2,1,0:T(8,128)(2,1)S(1)}, u32[]{:S(2)}, u32[]{:S(2)}) collective-permute-start(bf16[5,64,256]{2,1,0:T(8,128)(2,1)S(1)} %get-tuple-element.81), channel_id=1, source_target_pairs={{0,24},{1,25},{2,26},{3,27},{4,28},{5,29},{6,30},{7,31},{8,0},{9,1... | collective-permute-start | bytes 491528 | tf_op jit(solution)/shard_map/ppermute | solution.py:372
  192.6 11.7 %collective-permute-start.12 = (bf16[5,64,256]{2,1,0:T(8,128)(2,1)S(1)}, bf16[5,64,256]{2,1,0:T(8,128)(2,1)S(1)}, u32[]{:S(2)}, u32[]{:S(2)}) collective-permute-start(bf16[5,64,256]{2,1,0:T(8,128)(2,1)S(1)} %get-tuple-element.82), channel_id=1, source_target_pairs={{0,16},{1,17},{2,18},{3,19},{4,20},{5,21},{6,22},{7,23},{8,24},{9,... | collective-permute-start | bytes 491528 | tf_op jit(solution)/shard_map/ppermute | solution.py:372
  205.4 20.6 %all-to-all-start = ((f32[128,1,384]{2,1,0:T(1,128)}), f32[128,1,384]{2,1,0:T(1,128)S(1)}, u32[]{:S(2)}, u32[]{:S(2)}) async-start(f32[128,1,384]{2,1,0:T(1,128)} %square_sums.1), calls=%async_computation | async-start | bytes 393216 | tf_op jit(solution)/shard_map/all_to_all | solution.py:355

commit v11 on v10

--- a/solution.py
+++ b/solution.py
@@ -214,7 +214,7 @@
     )(*[x for four in flows for x in four])
 
 
-def spread_squares(rows, coef, owner, me, tile_r, tile_c, sb=8):
+def spread_squares(rows, coef, owner, me, tile_r, tile_c, sb=16):
     nblk, foot = rows.shape
     n_sens = owner.shape[1]
 
@@ -237,15 +237,15 @@
 
         @pl.when(g < steps)
         def _():
-            spread(rows_ref, coef_ref, map_ref)
-
-    def spread(rows_ref, coef_ref, map_ref):
+            at = pl.ds(pl.multiple_of(g * sb, sb), sb)
+            spread(rows_ref[at, :], coef_ref[at, :], map_ref)
+
+    def spread(point, c, map_ref):
         sub_r = lax.broadcasted_iota(I32, (tile_r, foot), 0)
         sub_c = lax.broadcasted_iota(I32, (tile_c, foot), 0)
-        point = rows_ref[...]
         high = point // tile_c
         low = point - high * tile_c
-        c = coef_ref[...].astype(F32)
+        c = c.astype(F32)
         sq = c * c
         sq_top = sq.astype(BF16).astype(F32)
         sq_rest = sq - sq_top
@@ -263,8 +263,8 @@
         grid=(steps + 1,),
         in_specs=[
             pl.BlockSpec(memory_space=pltpu.SMEM),
-            pl.BlockSpec((sb, foot), lambda g: (jnp.minimum(g, steps - 1), 0)),
-            pl.BlockSpec((sb, foot), lambda g: (jnp.minimum(g, steps - 1), 0)),
+            pl.BlockSpec((nblk, foot), lambda g: (0, 0)),
+            pl.BlockSpec((nblk, foot), lambda g: (0, 0)),
             pl.BlockSpec((1, n_sens), lambda g: (0, 0)),
         ],
         out_specs=pl.BlockSpec((sb, tile_r, tile_c), lambda g: (g, 0, 0)),

time: 230 us -> 226 us (0.983)
  Pallas kernels: 43 us -> 39.4 us
    pallas_call x1, Pallas kernels: 10.7 us -> 7.12 us  [spread_squares(): pl.pallas_call(body, grid=(steps + 1,), in_specs=[pl.BlockSpec(memory_spa...]
  transfers between devices with their start and end apart: 40 -> 40, of which waited for: 14 -> 14; matrix products, arithmetic and copies ran while one was open for 0% -> 0% of each run, Pallas kernels for 10% -> 9%
where the time goes in v11:
time: 226 us
  starting transfers between devices  109 us (48%)
  waiting for transfers between devices  72.2 us (32%)
  Pallas kernels  39.4 us (17%)
  local copies, waits for them, and re-layouts  3.08 us (1%)
    ppermute x39, starting transfers between devices, shift_to(): return lax.ppermute(x, AXES, pairs)  99 us
    ppermute x39, waiting for transfers between devices, shift_to(): return lax.ppermute(x, AXES, pairs)  62 us
    pallas_call x1, Pallas kernels, gather_flows(): pl.pallas_call(body, in_specs=[hbm, hbm, vmem, vmem, smem, smem] + [smem]...  15.2 us
    pallas_call x3, Pallas kernels, mix_tiles(): pl.pallas_call(body, grid=(each,), in_specs=[pl.BlockSpec(memory_space=pl...  11.5 us
    all_to_all x1, starting transfers between devices, exchange(): return lax.all_to_all(x, axes, split_axis=0, concat_axis=0, tiled=True)  10.3 us
    all_to_all x1, waiting for transfers between devices, exchange(): return lax.all_to_all(x, axes, split_axis=0, concat_axis=0, tiled=True)  10.2 us
    pallas_call x1, Pallas kernels, spread_squares(): pl.pallas_call(body, grid=(steps + 1,), in_specs=[pl.BlockSpec(memory_spa...  7.12 us
  transfers between devices with their start and end apart: 40, of which 14 were waited for; matrix products, arithmetic and copies ran while one was open for 0% of the time, Pallas kernels for 9%

profile of v11, /device:TPU:1, one launch (start us, length us, event | category | flops | bytes accessed | tf_op | source)
XLA Modules:
  0.0 225.6 jit_solution(2780227052939243618)
XLA Ops:
  1.3 15.2 %gather_flows.1 = (bf16[5,264,128]{2,1,0:T(8,128)(2,1)}, bf16[5,264,128]{2,1,0:T(8,128)(2,1)}, bf16[5,264,128]{2,1,0:T(8,128)(2,1)}, bf16[5,264,128]{2,1,0:T(8,1...) custom-call(bf16[8192,256]{1,0:T(8,128)(2,1)} %bitcast.13, ...), custom_call_target="tpu_custom_call" | custom-call | tf_op jit(solution)/shard_map/gather_flows/pallas_call | solution.py:104
  16.5 1.5 collective-permute-start.26
  17.9 1.3 collective-permute-start.27
  19.3 1.5 collective-permute-start.28
  20.7 1.5 collective-permute-start.29
  22.6 1.6 collective-permute-start.31
  24.3 4.5 %collective-permute-done.27.refs_2_ = bf16[5,264,128]{2,1,0:T(8,128)(2,1)S(1)} collective-permute-done((bf16[5,264,128]{2,1,0:T(8,128)(2,1)}, bf16[5,264,128]{2,1,0:T(8,128)(2,1)S(1)}, u32[]{:S(2)}, u32[]{:S(2)}) %collective-permute-start.27) | collective-permute-done | bytes 337952 | tf_op jit(solution)/shard_map/ppermute | solution.py:372
  28.8 3.0 %collective-permute-start.32 = (bf16[5,264,128]{2,1,0:T(8,128)(2,1)}, bf16[5,264,128]{2,1,0:T(8,128)(2,1)S(1)}, u32[]{:S(2)}, u32[]{:S(2)}) collective-permute-start(bf16[5,264,128]{2,1,0:T(8,128)(2,1)} %get-tuple-element.106), channel_id=1, source_target_pairs={{0,17},{1,16},{2,19},{3,18},{4,21},{5,20},{6,23},{7,22},{8,25},{9,... | collective-permute-start | bytes 1013768 | tf_op jit(solution)/shard_map/ppermute | solution.py:372
  31.8 4.5 %collective-permute-done.28.refs_3_ = bf16[5,264,128]{2,1,0:T(8,128)(2,1)S(1)} collective-permute-done((bf16[5,264,128]{2,1,0:T(8,128)(2,1)}, bf16[5,264,128]{2,1,0:T(8,128)(2,1)S(1)}, u32[]{:S(2)}, u32[]{:S(2)}) %collective-permute-start.28) | collective-permute-done | bytes 337952 | tf_op jit(solution)/shard_map/ppermute | solution.py:372
  36.4 1.8 collective-permute-start.1
  38.7 15.2 %collective-permute-start.2 = (bf16[5,264,128]{2,1,0:T(8,128)(2,1)}, bf16[5,264,128]{2,1,0:T(8,128)(2,1)S(1)}, u32[]{:S(2)}, u32[]{:S(2)}) collective-permute-start(bf16[5,264,128]{2,1,0:T(8,128)(2,1)} %get-tuple-element.70), channel_id=1, source_target_pairs={{0,3},{1,2},{2,5},{3,4},{4,7},{5,6},{6,1},{7,0},{8,11},{9,10},{10,... | collective-permute-start | bytes 1013768 | tf_op jit(solution)/shard_map/ppermute | solution.py:372
  53.9 1.0 collective-permute-start.3
  55.0 1.5 collective-permute-start.4
  56.5 1.0 collective-permute-start.5
  57.5 3.6 %collective-permute-start.6 = (bf16[5,264,128]{2,1,0:T(8,128)(2,1)}, bf16[5,264,128]{2,1,0:T(8,128)(2,1)S(1)}, u32[]{:S(2)}, u32[]{:S(2)}) collective-permute-start(bf16[5,264,128]{2,1,0:T(8,128)(2,1)} %get-tuple-element.74), channel_id=1, source_target_pairs={{0,5},{1,4},{2,7},{3,6},{4,1},{5,0},{6,3},{7,2},{8,13},{9,12},{10,... | collective-permute-start | bytes 1013768 | tf_op jit(solution)/shard_map/ppermute | solution.py:372
  61.1 2.3 %collective-permute-done.2.refs_3_ = bf16[5,264,128]{2,1,0:T(8,128)(2,1)S(1)} collective-permute-done((bf16[5,264,128]{2,1,0:T(8,128)(2,1)}, bf16[5,264,128]{2,1,0:T(8,128)(2,1)S(1)}, u32[]{:S(2)}, u32[]{:S(2)}) %collective-permute-start.2) | collective-permute-done | bytes 337952 | tf_op jit(solution)/shard_map/ppermute | solution.py:372
  63.4 0.9 collective-permute-done.3.refs_4_
  64.3 1.3 collective-permute-start.14
  65.6 3.5 %collective-permute-done.4.refs_5_ = bf16[5,264,128]{2,1,0:T(8,128)(2,1)S(1)} collective-permute-done((bf16[5,264,128]{2,1,0:T(8,128)(2,1)}, bf16[5,264,128]{2,1,0:T(8,128)(2,1)S(1)}, u32[]{:S(2)}, u32[]{:S(2)}) %collective-permute-start.4) | collective-permute-done | bytes 337952 | tf_op jit(solution)/shard_map/ppermute | solution.py:372
  69.0 17.3 %collective-permute-start.15 = (bf16[6,264,128]{2,1,0:T(8,128)(2,1)}, bf16[6,264,128]{2,1,0:T(8,128)(2,1)S(1)}, u32[]{:S(2)}, u32[]{:S(2)}) collective-permute-start(bf16[6,264,128]{2,1,0:T(8,128)(2,1)} %get-tuple-element.86), channel_id=1, source_target_pairs={{0,33},{1,32},{2,35},{3,34},{4,37},{5,36},{6,39},{7,38},{8,41},{9,... | collective-permute-start | bytes 1216520 | tf_op jit(solution)/shard_map/ppermute | solution.py:372
  86.4 1.4 collective-permute-start.16
  88.6 1.0 collective-permute-start.18
  89.6 1.0 copy-done.2
  90.5 3.6 %mix_tiles.5 = (bf16[5,256,256]{2,1,0:T(8,128)(2,1)S(1)}, bf16[5,256,256]{2,1,0:T(8,128)(2,1)S(1)}, bf16[5,256,256]{2,1,0:T(8,128)(2,1)S(1)}, bf16[5,256,256]{2,1,0:T(8,128)(2,1)S(1)}) custom-call(s32[1]{0:T(128)} %bitcast.5.refs_6_.at_ref, bf16[5,264,128]{2,1,0:T(8,128)(2,1)S(1)} %copy-done.2, bf16[5,264,128]{2,1,0:T(8,128)(2,1)S(1)} %collective-permute-done.26.refs_1_, ...), custom_call_target="tpu_custom_call" | custom-call | tf_op jit(solution)/shard_map/mix_tiles/pallas_call | solution.py:151
  94.2 1.6 collective-permute-start.33
  95.8 2.3 %collective-permute-done.15.refs_3_ = bf16[6,264,128]{2,1,0:T(8,128)(2,1)S(1)} collective-permute-done((bf16[6,264,128]{2,1,0:T(8,128)(2,1)}, bf16[6,264,128]{2,1,0:T(8,128)(2,1)S(1)}, u32[]{:S(2)}, u32[]{:S(2)}) %collective-permute-start.15) | collective-permute-done | bytes 405536 | tf_op jit(solution)/shard_map/ppermute | solution.py:372
  98.1 3.7 %collective-permute-start.34 = (bf16[5,256,256]{2,1,0:T(8,128)(2,1)S(1)}, bf16[5,256,256]{2,1,0:T(8,128)(2,1)S(1)}, u32[]{:S(2)}, u32[]{:S(2)}) collective-permute-start(bf16[5,256,256]{2,1,0:T(8,128)(2,1)S(1)} %get-tuple-element.109), channel_id=1, source_target_pairs={{0,6},{1,7},{2,0},{3,1},{4,2},{5,3},{6,4},{7,5},{8,14},{9,15},{10,... | collective-permute-start | bytes 1966088 | tf_op jit(solution)/shard_map/ppermute | solution.py:372
  101.8 1.0 copy-done.1
  102.7 3.6 %mix_tiles.3 = (bf16[5,256,256]{2,1,0:T(8,128)(2,1)S(1)}, bf16[5,256,256]{2,1,0:T(8,128)(2,1)S(1)}, bf16[5,256,256]{2,1,0:T(8,128)(2,1)S(1)}, bf16[5,256,256]{2,1,0:T(8,128)(2,1)S(1)}) custom-call(s32[1]{0:T(128)} %bitcast.1.refs_7_.at_ref, bf16[5,264,128]{2,1,0:T(8,128)(2,1)S(1)} %copy-done.1, bf16[5,264,128]{2,1,0:T(8,128)(2,1)S(1)} %collective-permute-done.refs_1_, ...), custom_call_target="tpu_custom_call" | custom-call | tf_op jit(solution)/shard_map/mix_tiles/pallas_call | solution.py:151
  106.8 12.2 %collective-permute-start.19 = (bf16[6,264,128]{2,1,0:T(8,128)(2,1)}, bf16[6,264,128]{2,1,0:T(8,128)(2,1)S(1)}, u32[]{:S(2)}, u32[]{:S(2)}) collective-permute-start(bf16[6,264,128]{2,1,0:T(8,128)(2,1)} %get-tuple-element.90), channel_id=1, source_target_pairs={{0,65},{1,64},{2,67},{3,66},{4,69},{5,68},{6,71},{7,70},{8,73},{9,... | collective-permute-start | bytes 1216520 | tf_op jit(solution)/shard_map/ppermute | solution.py:372
  119.1 23.8 %collective-permute-done.19.refs_7_ = bf16[6,264,128]{2,1,0:T(8,128)(2,1)S(1)} collective-permute-done((bf16[6,264,128]{2,1,0:T(8,128)(2,1)}, bf16[6,264,128]{2,1,0:T(8,128)(2,1)S(1)}, u32[]{:S(2)}, u32[]{:S(2)}) %collective-permute-start.19) | collective-permute-done | bytes 405536 | tf_op jit(solution)/shard_map/ppermute | solution.py:372
  142.9 1.0 copy-done
  143.9 4.3 %mix_tiles.4 = (bf16[6,256,256]{2,1,0:T(8,128)(2,1)S(1)}, bf16[6,256,256]{2,1,0:T(8,128)(2,1)S(1)}, bf16[6,256,256]{2,1,0:T(8,128)(2,1)S(1)}, bf16[6,256,256]{2,1,0:T(8,128)(2,1)S(1)}) custom-call(s32[1]{0:T(128)} %bitcast.refs_8_.at_ref, bf16[6,264,128]{2,1,0:T(8,128)(2,1)S(1)} %copy-done, bf16[6,264,128]{2,1,0:T(8,128)(2,1)S(1)} %collective-permute-done.13.refs_1_, ...), custom_call_target="tpu_custom_call" | custom-call | tf_op jit(solution)/shard_map/mix_tiles/pallas_call | solution.py:151
  148.3 2.7 %collective-permute-start.21 = (bf16[6,256,256]{2,1,0:T(8,128)(2,1)S(1)}, bf16[6,256,256]{2,1,0:T(8,128)(2,1)S(1)}, u32[]{:S(2)}, u32[]{:S(2)}) collective-permute-start(bf16[6,256,256]{2,1,0:T(8,128)(2,1)S(1)} %get-tuple-element.93), channel_id=1, source_target_pairs={{0,24},{1,25},{2,26},{3,27},{4,28},{5,29},{6,30},{7,31},{8,0},{9,1... | collective-permute-start | bytes 2359304 | tf_op jit(solution)/shard_map/ppermute | solution.py:372
  151.6 14.7 %collective-permute-done.8.refs_2_ = bf16[5,256,256]{2,1,0:T(8,128)(2,1)S(1)} collective-permute-done((bf16[5,256,256]{2,1,0:T(8,128)(2,1)S(1)}, bf16[5,256,256]{2,1,0:T(8,128)(2,1)S(1)}, u32[]{:S(2)}, u32[]{:S(2)}) %collective-permute-start.8) | collective-permute-done | bytes 655392 | tf_op jit(solution)/shard_map/ppermute | solution.py:372
  166.3 1.6 collective-permute-done.9.refs_3_
  167.9 14.8 %collective-permute-start.37 = (bf16[5,64,256]{2,1,0:T(8,128)(2,1)S(1)}, bf16[5,64,256]{2,1,0:T(8,128)(2,1)S(1)}, u32[]{:S(2)}, u32[]{:S(2)}) collective-permute-start(bf16[5,64,256]{2,1,0:T(8,128)(2,1)S(1)} %get-tuple-element.113), channel_id=1, source_target_pairs={{0,96},{1,97},{2,98},{3,99},{4,100},{5,101},{6,102},{7,103},{8,104... | collective-permute-start | bytes 491528 | tf_op jit(solution)/shard_map/ppermute | solution.py:372
  183.2 1.9 collective-permute-done.20.refs_1_
  185.7 3.0 %collective-permute-start.24 = (bf16[6,64,256]{2,1,0:T(8,128)(2,1)S(1)}, bf16[6,64,256]{2,1,0:T(8,128)(2,1)S(1)}, u32[]{:S(2)}, u32[]{:S(2)}) collective-permute-start(bf16[6,64,256]{2,1,0:T(8,128)(2,1)S(1)} %get-tuple-element.97), channel_id=1, source_target_pairs={{0,6},{1,7},{2,0},{3,1},{4,2},{5,3},{6,4},{7,5},{8,14},{9,15},{10,... | collective-permute-start | bytes 589832 | tf_op jit(solution)/shard_map/ppermute | solution.py:372
  188.7 1.2 collective-permute-start.25
  189.9 1.2 collective-permute-done.38.refs_11_
  191.1 1.5 collective-permute-start.11
  192.6 1.0 collective-permute-start.12
  193.5 7.1 %spread_squares.1.maps_hbm = f32[640,32,256]{2,1,0:T(8,128)} custom-call(s32[1]{0:T(128)} %bitcast.6.me_ref, s32[128,128]{1,0:T(8,128)} %rows_ref.1, bf16[128,128]{1,0:T(8,128)(2,1)} %coef_ref.1, s32[1,1024]{1,0:T(1,128)} %bitcast.14), custom_call_target="tpu_custom_call" | custom-call | tf_op jit(solution)/shard_map/spread_squares/pallas_call | solution.py:261
  200.7 1.1 square_sums.1
  201.8 10.3 %all-to-all-start = ((f32[128,1,384]{2,1,0:T(1,128)}), f32[128,1,384]{2,1,0:T(1,128)S(1)}, u32[]{:S(2)}, u32[]{:S(2)}) async-start(f32[128,1,384]{2,1,0:T(1,128)} %square_sums.1), calls=%async_computation | async-start | bytes 393216 | tf_op jit(solution)/shard_map/all_to_all | solution.py:355
  212.2 10.2 %all-to-all-done.parts_ref = f32[128,1,384]{2,1,0:T(1,128)S(1)} async-done(((f32[128,1,384]{2,1,0:T(1,128)}), f32[128,1,384]{2,1,0:T(1,128)S(1)}, u32[]{:S(2)}, u32[]{:S(2)}) %all-to-all-start) | async-done | bytes 196640 | tf_op jit(solution)/shard_map/all_to_all | solution.py:355
  222.4 3.1 %finish.1 = (f32[1,8]{1,0:T(1,128)}, f32[8,128]{1,0:T(8,128)}, f32[32,256]{1,0:T(8,128)}) custom-call(s32[1]{0:T(128)S(6)} %copy.11.refs_4_.count_ref, f32[128,1,384]{2,1,0:T(1,128)S(1)} %all-to-all-done.parts_ref, f32[8,128]{1,0:T(8,128)S(1)} %bitcast.12, s32[128,1]{1,0:T(8,128)S(1)} %copy.10.sensor_ref, f32[640,32,256]{2,1,0:T(8,128)} %spread_squares.1.maps_hbm), custom_call_target="tpu_custom_call" | custom-call | tf_op jit(solution)/shard_map/finish/pallas_call | solution.py:334
  (53 shorter events, 4.4 us)
Async XLA Ops:
  16.5 195.6 %copy-start.4 = (s32[128]{0:T(128)S(1)}, s32[128]{0:T(128)}, u32[]{:S(2)}) copy-start(s32[128]{0:T(128)} %param.9) | copy-start | bytes 1540
  16.5 205.9 %copy-start.3 = (f32[1024]{0:T(1024)S(1)}, f32[1024]{0:T(1024)}, u32[]{:S(2)}) copy-start(f32[1024]{0:T(1024)} %param.13) | copy-start | bytes 12292
  16.5 6.2 %collective-permute-start.26 = (bf16[5,264,128]{2,1,0:T(8,128)(2,1)}, bf16[5,264,128]{2,1,0:T(8,128)(2,1)S(1)}, u32[]{:S(2)}, u32[]{:S(2)}) collective-permute-start(bf16[5,264,128]{2,1,0:T(8,128)(2,1)} %get-tuple-element.100), channel_id=1, source_target_pairs={{0,1},{1,0},{2,3},{3,2},{4,5},{5,4},{6,7},{7,6},{8,9},{9,8},{10,11... | collective-permute-start | bytes 1013768 | tf_op jit(solution)/shard_map/ppermute | solution.py:372
  17.9 10.8 %collective-permute-start.27 = (bf16[5,264,128]{2,1,0:T(8,128)(2,1)}, bf16[5,264,128]{2,1,0:T(8,128)(2,1)S(1)}, u32[]{:S(2)}, u32[]{:S(2)}) collective-permute-start(bf16[5,264,128]{2,1,0:T(8,128)(2,1)} %get-tuple-element.101), channel_id=1, source_target_pairs={{0,8},{1,9},{2,10},{3,11},{4,12},{5,13},{6,14},{7,15},{8,16},{9,17... | collective-permute-start | bytes 1013768 | tf_op jit(solution)/shard_map/ppermute | solution.py:372
  19.3 17.0 %collective-permute-start.28 = (bf16[5,264,128]{2,1,0:T(8,128)(2,1)}, bf16[5,264,128]{2,1,0:T(8,128)(2,1)S(1)}, u32[]{:S(2)}, u32[]{:S(2)}) collective-permute-start(bf16[5,264,128]{2,1,0:T(8,128)(2,1)} %get-tuple-element.102), channel_id=1, source_target_pairs={{0,9},{1,8},{2,11},{3,10},{4,13},{5,12},{6,15},{7,14},{8,17},{9,16... | collective-permute-start | bytes 1013768 | tf_op jit(solution)/shard_map/ppermute | solution.py:372
  20.7 15.7 %collective-permute-start.29 = (bf16[5,264,128]{2,1,0:T(8,128)(2,1)}, bf16[5,264,128]{2,1,0:T(8,128)(2,1)S(1)}, u32[]{:S(2)}, u32[]{:S(2)}) collective-permute-start(bf16[5,264,128]{2,1,0:T(8,128)(2,1)} %get-tuple-element.103), channel_id=1, source_target_pairs={{0,24},{1,25},{2,26},{3,27},{4,28},{5,29},{6,30},{7,31},{8,0},{9,1... | collective-permute-start | bytes 1013768 | tf_op jit(solution)/shard_map/ppermute | solution.py:372
  22.2 16.5 %collective-permute-start.30 = (bf16[5,264,128]{2,1,0:T(8,128)(2,1)}, bf16[5,264,128]{2,1,0:T(8,128)(2,1)S(1)}, u32[]{:S(2)}, u32[]{:S(2)}) collective-permute-start(bf16[5,264,128]{2,1,0:T(8,128)(2,1)} %get-tuple-element.104), channel_id=1, source_target_pairs={{0,25},{1,24},{2,27},{3,26},{4,29},{5,28},{6,31},{7,30},{8,1},{9,0... | collective-permute-start | bytes 1013768 | tf_op jit(solution)/shard_map/ppermute | solution.py:372
  22.6 31.3 %collective-permute-start.31 = (bf16[5,264,128]{2,1,0:T(8,128)(2,1)}, bf16[5,264,128]{2,1,0:T(8,128)(2,1)S(1)}, u32[]{:S(2)}, u32[]{:S(2)}) collective-permute-start(bf16[5,264,128]{2,1,0:T(8,128)(2,1)} %get-tuple-element.105), channel_id=1, source_target_pairs={{0,16},{1,17},{2,18},{3,19},{4,20},{5,21},{6,22},{7,23},{8,24},{9,... | collective-permute-start | bytes 1013768 | tf_op jit(solution)/shard_map/ppermute | solution.py:372
  28.8 26.2 %collective-permute-start.32 = (bf16[5,264,128]{2,1,0:T(8,128)(2,1)}, bf16[5,264,128]{2,1,0:T(8,128)(2,1)S(1)}, u32[]{:S(2)}, u32[]{:S(2)}) collective-permute-start(bf16[5,264,128]{2,1,0:T(8,128)(2,1)} %get-tuple-element.106), channel_id=1, source_target_pairs={{0,17},{1,16},{2,19},{3,18},{4,21},{5,20},{6,23},{7,22},{8,25},{9,... | collective-permute-start | bytes 1013768 | tf_op jit(solution)/shard_map/ppermute | solution.py:372
  36.3 20.2 %collective-permute-start = (bf16[5,264,128]{2,1,0:T(8,128)(2,1)}, bf16[5,264,128]{2,1,0:T(8,128)(2,1)S(1)}, u32[]{:S(2)}, u32[]{:S(2)}) collective-permute-start(bf16[5,264,128]{2,1,0:T(8,128)(2,1)} %get-tuple-element.68), channel_id=1, source_target_pairs={{0,1},{1,0},{2,3},{3,2},{4,5},{5,4},{6,7},{7,6},{8,9},{9,8},{10,11... | collective-permute-start | bytes 1013768 | tf_op jit(solution)/shard_map/ppermute | solution.py:372
  36.4 21.0 %collective-permute-start.1 = (bf16[5,264,128]{2,1,0:T(8,128)(2,1)}, bf16[5,264,128]{2,1,0:T(8,128)(2,1)S(1)}, u32[]{:S(2)}, u32[]{:S(2)}) collective-permute-start(bf16[5,264,128]{2,1,0:T(8,128)(2,1)} %get-tuple-element.69), channel_id=1, source_target_pairs={{0,2},{1,3},{2,4},{3,5},{4,6},{5,7},{6,0},{7,1},{8,10},{9,11},{10,... | collective-permute-start | bytes 1013768 | tf_op jit(solution)/shard_map/ppermute | solution.py:372
  38.7 24.6 %collective-permute-start.2 = (bf16[5,264,128]{2,1,0:T(8,128)(2,1)}, bf16[5,264,128]{2,1,0:T(8,128)(2,1)S(1)}, u32[]{:S(2)}, u32[]{:S(2)}) collective-permute-start(bf16[5,264,128]{2,1,0:T(8,128)(2,1)} %get-tuple-element.70), channel_id=1, source_target_pairs={{0,3},{1,2},{2,5},{3,4},{4,7},{5,6},{6,1},{7,0},{8,11},{9,10},{10,... | collective-permute-start | bytes 1013768 | tf_op jit(solution)/shard_map/ppermute | solution.py:372
  53.9 10.3 %collective-permute-start.3 = (bf16[5,264,128]{2,1,0:T(8,128)(2,1)}, bf16[5,264,128]{2,1,0:T(8,128)(2,1)S(1)}, u32[]{:S(2)}, u32[]{:S(2)}) collective-permute-start(bf16[5,264,128]{2,1,0:T(8,128)(2,1)} %get-tuple-element.71), channel_id=1, source_target_pairs={{0,6},{1,7},{2,0},{3,1},{4,2},{5,3},{6,4},{7,5},{8,14},{9,15},{10,... | collective-permute-start | bytes 1013768 | tf_op jit(solution)/shard_map/ppermute | solution.py:372
  55.0 14.1 %collective-permute-start.4 = (bf16[5,264,128]{2,1,0:T(8,128)(2,1)}, bf16[5,264,128]{2,1,0:T(8,128)(2,1)S(1)}, u32[]{:S(2)}, u32[]{:S(2)}) collective-permute-start(bf16[5,264,128]{2,1,0:T(8,128)(2,1)} %get-tuple-element.72), channel_id=1, source_target_pairs={{0,7},{1,6},{2,1},{3,0},{4,3},{5,2},{6,5},{7,4},{8,15},{9,14},{10,... | collective-permute-start | bytes 1013768 | tf_op jit(solution)/shard_map/ppermute | solution.py:372
  56.5 29.9 %collective-permute-start.5 = (bf16[5,264,128]{2,1,0:T(8,128)(2,1)}, bf16[5,264,128]{2,1,0:T(8,128)(2,1)S(1)}, u32[]{:S(2)}, u32[]{:S(2)}) collective-permute-start(bf16[5,264,128]{2,1,0:T(8,128)(2,1)} %get-tuple-element.73), channel_id=1, source_target_pairs={{0,4},{1,5},{2,6},{3,7},{4,0},{5,1},{6,2},{7,3},{8,12},{9,13},{10,... | collective-permute-start | bytes 1013768 | tf_op jit(solution)/shard_map/ppermute | solution.py:372
  57.5 30.3 %collective-permute-start.6 = (bf16[5,264,128]{2,1,0:T(8,128)(2,1)}, bf16[5,264,128]{2,1,0:T(8,128)(2,1)S(1)}, u32[]{:S(2)}, u32[]{:S(2)}) collective-permute-start(bf16[5,264,128]{2,1,0:T(8,128)(2,1)} %get-tuple-element.74), channel_id=1, source_target_pairs={{0,5},{1,4},{2,7},{3,6},{4,1},{5,0},{6,3},{7,2},{8,13},{9,12},{10,... | collective-permute-start | bytes 1013768 | tf_op jit(solution)/shard_map/ppermute | solution.py:372
  63.4 25.2 %collective-permute-start.13 = (bf16[6,264,128]{2,1,0:T(8,128)(2,1)}, bf16[6,264,128]{2,1,0:T(8,128)(2,1)S(1)}, u32[]{:S(2)}, u32[]{:S(2)}) collective-permute-start(bf16[6,264,128]{2,1,0:T(8,128)(2,1)} %get-tuple-element.84), channel_id=1, source_target_pairs={{0,1},{1,0},{2,3},{3,2},{4,5},{5,4},{6,7},{7,6},{8,9},{9,8},{10,11... | collective-permute-start | bytes 1216520 | tf_op jit(solution)/shard_map/ppermute | solution.py:372
  64.3 29.9 %collective-permute-start.14 = (bf16[6,264,128]{2,1,0:T(8,128)(2,1)}, bf16[6,264,128]{2,1,0:T(8,128)(2,1)S(1)}, u32[]{:S(2)}, u32[]{:S(2)}) collective-permute-start(bf16[6,264,128]{2,1,0:T(8,128)(2,1)} %get-tuple-element.85), channel_id=1, source_target_pairs={{0,32},{1,33},{2,34},{3,35},{4,36},{5,37},{6,38},{7,39},{8,40},{9,... | collective-permute-start | bytes 1216520 | tf_op jit(solution)/shard_map/ppermute | solution.py:372
  69.0 29.0 %collective-permute-start.15 = (bf16[6,264,128]{2,1,0:T(8,128)(2,1)}, bf16[6,264,128]{2,1,0:T(8,128)(2,1)S(1)}, u32[]{:S(2)}, u32[]{:S(2)}) collective-permute-start(bf16[6,264,128]{2,1,0:T(8,128)(2,1)} %get-tuple-element.86), channel_id=1, source_target_pairs={{0,33},{1,32},{2,35},{3,34},{4,37},{5,36},{6,39},{7,38},{8,41},{9,... | collective-permute-start | bytes 1216520 | tf_op jit(solution)/shard_map/ppermute | solution.py:372
  86.4 15.4 %collective-permute-start.16 = (bf16[6,264,128]{2,1,0:T(8,128)(2,1)}, bf16[6,264,128]{2,1,0:T(8,128)(2,1)S(1)}, u32[]{:S(2)}, u32[]{:S(2)}) collective-permute-start(bf16[6,264,128]{2,1,0:T(8,128)(2,1)} %get-tuple-element.87), channel_id=1, source_target_pairs={{0,96},{1,97},{2,98},{3,99},{4,100},{5,101},{6,102},{7,103},{8,104... | collective-permute-start | bytes 1216520 | tf_op jit(solution)/shard_map/ppermute | solution.py:372
  87.8 18.6 %collective-permute-start.17 = (bf16[6,264,128]{2,1,0:T(8,128)(2,1)}, bf16[6,264,128]{2,1,0:T(8,128)(2,1)S(1)}, u32[]{:S(2)}, u32[]{:S(2)}) collective-permute-start(bf16[6,264,128]{2,1,0:T(8,128)(2,1)} %get-tuple-element.88), channel_id=1, source_target_pairs={{0,97},{1,96},{2,99},{3,98},{4,101},{5,100},{6,103},{7,102},{8,105... | collective-permute-start | bytes 1216520 | tf_op jit(solution)/shard_map/ppermute | solution.py:372
  88.6 18.3 %collective-permute-start.18 = (bf16[6,264,128]{2,1,0:T(8,128)(2,1)}, bf16[6,264,128]{2,1,0:T(8,128)(2,1)S(1)}, u32[]{:S(2)}, u32[]{:S(2)}) collective-permute-start(bf16[6,264,128]{2,1,0:T(8,128)(2,1)} %get-tuple-element.89), channel_id=1, source_target_pairs={{0,64},{1,65},{2,66},{3,67},{4,68},{5,69},{6,70},{7,71},{8,72},{9,... | collective-permute-start | bytes 1216520 | tf_op jit(solution)/shard_map/ppermute | solution.py:372
  89.6 1.0 copy-start.2
  94.2 54.2 %collective-permute-start.33 = (bf16[5,256,256]{2,1,0:T(8,128)(2,1)S(1)}, bf16[5,256,256]{2,1,0:T(8,128)(2,1)S(1)}, u32[]{:S(2)}, u32[]{:S(2)}) collective-permute-start(bf16[5,256,256]{2,1,0:T(8,128)(2,1)S(1)} %get-tuple-element.108), channel_id=1, source_target_pairs={{0,2},{1,3},{2,4},{3,5},{4,6},{5,7},{6,0},{7,1},{8,10},{9,11},{10,... | collective-permute-start | bytes 1966088 | tf_op jit(solution)/shard_map/ppermute | solution.py:372
  98.1 52.9 %collective-permute-start.34 = (bf16[5,256,256]{2,1,0:T(8,128)(2,1)S(1)}, bf16[5,256,256]{2,1,0:T(8,128)(2,1)S(1)}, u32[]{:S(2)}, u32[]{:S(2)}) collective-permute-start(bf16[5,256,256]{2,1,0:T(8,128)(2,1)S(1)} %get-tuple-element.109), channel_id=1, source_target_pairs={{0,6},{1,7},{2,0},{3,1},{4,2},{5,3},{6,4},{7,5},{8,14},{9,15},{10,... | collective-permute-start | bytes 1966088 | tf_op jit(solution)/shard_map/ppermute | solution.py:372
  101.7 49.2 %collective-permute-start.35 = (bf16[5,256,256]{2,1,0:T(8,128)(2,1)S(1)}, bf16[5,256,256]{2,1,0:T(8,128)(2,1)S(1)}, u32[]{:S(2)}, u32[]{:S(2)}) collective-permute-start(bf16[5,256,256]{2,1,0:T(8,128)(2,1)S(1)} %get-tuple-element.110), channel_id=1, source_target_pairs={{0,4},{1,5},{2,6},{3,7},{4,0},{5,1},{6,2},{7,3},{8,12},{9,13},{10,... | collective-permute-start | bytes 1966088 | tf_op jit(solution)/shard_map/ppermute | solution.py:372
  101.7 1.0 copy-start.1
  106.3 44.7 %collective-permute-start.7 = (bf16[5,256,256]{2,1,0:T(8,128)(2,1)S(1)}, bf16[5,256,256]{2,1,0:T(8,128)(2,1)S(1)}, u32[]{:S(2)}, u32[]{:S(2)}) collective-permute-start(bf16[5,256,256]{2,1,0:T(8,128)(2,1)S(1)} %get-tuple-element.76), channel_id=1, source_target_pairs={{0,32},{1,33},{2,34},{3,35},{4,36},{5,37},{6,38},{7,39},{8,40},{9,... | collective-permute-start | bytes 1966088 | tf_op jit(solution)/shard_map/ppermute | solution.py:372
  106.8 36.1 %collective-permute-start.19 = (bf16[6,264,128]{2,1,0:T(8,128)(2,1)}, bf16[6,264,128]{2,1,0:T(8,128)(2,1)S(1)}, u32[]{:S(2)}, u32[]{:S(2)}) collective-permute-start(bf16[6,264,128]{2,1,0:T(8,128)(2,1)} %get-tuple-element.90), channel_id=1, source_target_pairs={{0,65},{1,64},{2,67},{3,66},{4,69},{5,68},{6,71},{7,70},{8,73},{9,... | collective-permute-start | bytes 1216520 | tf_op jit(solution)/shard_map/ppermute | solution.py:372
  142.9 1.0 copy-start
  148.2 36.8 %collective-permute-start.20 = (bf16[6,256,256]{2,1,0:T(8,128)(2,1)S(1)}, bf16[6,256,256]{2,1,0:T(8,128)(2,1)S(1)}, u32[]{:S(2)}, u32[]{:S(2)}) collective-permute-start(bf16[6,256,256]{2,1,0:T(8,128)(2,1)S(1)} %get-tuple-element.92), channel_id=1, source_target_pairs={{0,8},{1,9},{2,10},{3,11},{4,12},{5,13},{6,14},{7,15},{8,16},{9,17... | collective-permute-start | bytes 2359304 | tf_op jit(solution)/shard_map/ppermute | solution.py:372
  148.3 36.8 %collective-permute-start.21 = (bf16[6,256,256]{2,1,0:T(8,128)(2,1)S(1)}, bf16[6,256,256]{2,1,0:T(8,128)(2,1)S(1)}, u32[]{:S(2)}, u32[]{:S(2)}) collective-permute-start(bf16[6,256,256]{2,1,0:T(8,128)(2,1)S(1)} %get-tuple-element.93), channel_id=1, source_target_pairs={{0,24},{1,25},{2,26},{3,27},{4,28},{5,29},{6,30},{7,31},{8,0},{9,1... | collective-permute-start | bytes 2359304 | tf_op jit(solution)/shard_map/ppermute | solution.py:372
  151.0 15.3 %collective-permute-start.8 = (bf16[5,256,256]{2,1,0:T(8,128)(2,1)S(1)}, bf16[5,256,256]{2,1,0:T(8,128)(2,1)S(1)}, u32[]{:S(2)}, u32[]{:S(2)}) collective-permute-start(bf16[5,256,256]{2,1,0:T(8,128)(2,1)S(1)} %get-tuple-element.77), channel_id=1, source_target_pairs={{0,96},{1,97},{2,98},{3,99},{4,100},{5,101},{6,102},{7,103},{8,104... | collective-permute-start | bytes 1966088 | tf_op jit(solution)/shard_map/ppermute | solution.py:372
  151.0 16.9 %collective-permute-start.9 = (bf16[5,256,256]{2,1,0:T(8,128)(2,1)S(1)}, bf16[5,256,256]{2,1,0:T(8,128)(2,1)S(1)}, u32[]{:S(2)}, u32[]{:S(2)}) collective-permute-start(bf16[5,256,256]{2,1,0:T(8,128)(2,1)S(1)} %get-tuple-element.78), channel_id=1, source_target_pairs={{0,64},{1,65},{2,66},{3,67},{4,68},{5,69},{6,70},{7,71},{8,72},{9,... | collective-permute-start | bytes 1966088 | tf_op jit(solution)/shard_map/ppermute | solution.py:372
  151.1 34.0 %collective-permute-start.22 = (bf16[6,256,256]{2,1,0:T(8,128)(2,1)S(1)}, bf16[6,256,256]{2,1,0:T(8,128)(2,1)S(1)}, u32[]{:S(2)}, u32[]{:S(2)}) collective-permute-start(bf16[6,256,256]{2,1,0:T(8,128)(2,1)S(1)} %get-tuple-element.94), channel_id=1, source_target_pairs={{0,16},{1,17},{2,18},{3,19},{4,20},{5,21},{6,22},{7,23},{8,24},{9,... | collective-permute-start | bytes 2359304 | tf_op jit(solution)/shard_map/ppermute | solution.py:372
  166.3 19.4 %collective-permute-start.36 = (bf16[5,64,256]{2,1,0:T(8,128)(2,1)S(1)}, bf16[5,64,256]{2,1,0:T(8,128)(2,1)S(1)}, u32[]{:S(2)}, u32[]{:S(2)}) collective-permute-start(bf16[5,64,256]{2,1,0:T(8,128)(2,1)S(1)} %get-tuple-element.112), channel_id=1, source_target_pairs={{0,32},{1,33},{2,34},{3,35},{4,36},{5,37},{6,38},{7,39},{8,40},{9,... | collective-permute-start | bytes 491528 | tf_op jit(solution)/shard_map/ppermute | solution.py:372
  167.9 20.8 %collective-permute-start.37 = (bf16[5,64,256]{2,1,0:T(8,128)(2,1)S(1)}, bf16[5,64,256]{2,1,0:T(8,128)(2,1)S(1)}, u32[]{:S(2)}, u32[]{:S(2)}) collective-permute-start(bf16[5,64,256]{2,1,0:T(8,128)(2,1)S(1)} %get-tuple-element.113), channel_id=1, source_target_pairs={{0,96},{1,97},{2,98},{3,99},{4,100},{5,101},{6,102},{7,103},{8,104... | collective-permute-start | bytes 491528 | tf_op jit(solution)/shard_map/ppermute | solution.py:372
  185.1 6.0 %collective-permute-start.38 = (bf16[5,64,256]{2,1,0:T(8,128)(2,1)S(1)}, bf16[5,64,256]{2,1,0:T(8,128)(2,1)S(1)}, u32[]{:S(2)}, u32[]{:S(2)}) collective-permute-start(bf16[5,64,256]{2,1,0:T(8,128)(2,1)S(1)} %get-tuple-element.114), channel_id=1, source_target_pairs={{0,64},{1,65},{2,66},{3,67},{4,68},{5,69},{6,70},{7,71},{8,72},{9,... | collective-permute-start | bytes 491528 | tf_op jit(solution)/shard_map/ppermute | solution.py:372
  185.1 7.5 %collective-permute-start.10 = (bf16[5,64,256]{2,1,0:T(8,128)(2,1)S(1)}, bf16[5,64,256]{2,1,0:T(8,128)(2,1)S(1)}, u32[]{:S(2)}, u32[]{:S(2)}) collective-permute-start(bf16[5,64,256]{2,1,0:T(8,128)(2,1)S(1)} %get-tuple-element.80), channel_id=1, source_target_pairs={{0,8},{1,9},{2,10},{3,11},{4,12},{5,13},{6,14},{7,15},{8,16},{9,17... | collective-permute-start | bytes 491528 | tf_op jit(solution)/shard_map/ppermute | solution.py:372
  185.6 15.0 %collective-permute-start.23 = (bf16[6,64,256]{2,1,0:T(8,128)(2,1)S(1)}, bf16[6,64,256]{2,1,0:T(8,128)(2,1)S(1)}, u32[]{:S(2)}, u32[]{:S(2)}) collective-permute-start(bf16[6,64,256]{2,1,0:T(8,128)(2,1)S(1)} %get-tuple-element.96), channel_id=1, source_target_pairs={{0,2},{1,3},{2,4},{3,5},{4,6},{5,7},{6,0},{7,1},{8,10},{9,11},{10,... | collective-permute-start | bytes 589832 | tf_op jit(solution)/shard_map/ppermute | solution.py:372
  185.7 14.9 %collective-permute-start.24 = (bf16[6,64,256]{2,1,0:T(8,128)(2,1)S(1)}, bf16[6,64,256]{2,1,0:T(8,128)(2,1)S(1)}, u32[]{:S(2)}, u32[]{:S(2)}) collective-permute-start(bf16[6,64,256]{2,1,0:T(8,128)(2,1)S(1)} %get-tuple-element.97), channel_id=1, source_target_pairs={{0,6},{1,7},{2,0},{3,1},{4,2},{5,3},{6,4},{7,5},{8,14},{9,15},{10,... | collective-permute-start | bytes 589832 | tf_op jit(solution)/shard_map/ppermute | solution.py:372
  188.7 12.0 %collective-permute-start.25 = (bf16[6,64,256]{2,1,0:T(8,128)(2,1)S(1)}, bf16[6,64,256]{2,1,0:T(8,128)(2,1)S(1)}, u32[]{:S(2)}, u32[]{:S(2)}) collective-permute-start(bf16[6,64,256]{2,1,0:T(8,128)(2,1)S(1)} %get-tuple-element.98), channel_id=1, source_target_pairs={{0,4},{1,5},{2,6},{3,7},{4,0},{5,1},{6,2},{7,3},{8,12},{9,13},{10,... | collective-permute-start | bytes 589832 | tf_op jit(solution)/shard_map/ppermute | solution.py:372
  191.1 9.6 %collective-permute-start.11 = (bf16[5,64,256]{2,1,0:T(8,128)(2,1)S(1)}, bf16[5,64,256]{2,1,0:T(8,128)(2,1)S(1)}, u32[]{:S(2)}, u32[]{:S(2)}) collective-permute-start(bf16[5,64,256]{2,1,0:T(8,128)(2,1)S(1)} %get-tuple-element.81), channel_id=1, source_target_pairs={{0,24},{1,25},{2,26},{3,27},{4,28},{5,29},{6,30},{7,31},{8,0},{9,1... | collective-permute-start | bytes 491528 | tf_op jit(solution)/shard_map/ppermute | solution.py:372
  192.6 8.1 %collective-permute-start.12 = (bf16[5,64,256]{2,1,0:T(8,128)(2,1)S(1)}, bf16[5,64,256]{2,1,0:T(8,128)(2,1)S(1)}, u32[]{:S(2)}, u32[]{:S(2)}) collective-permute-start(bf16[5,64,256]{2,1,0:T(8,128)(2,1)S(1)} %get-tuple-element.82), channel_id=1, source_target_pairs={{0,16},{1,17},{2,18},{3,19},{4,20},{5,21},{6,22},{7,23},{8,24},{9,... | collective-permute-start | bytes 491528 | tf_op jit(solution)/shard_map/ppermute | solution.py:372
  201.8 20.6 %all-to-all-start = ((f32[128,1,384]{2,1,0:T(1,128)}), f32[128,1,384]{2,1,0:T(1,128)S(1)}, u32[]{:S(2)}, u32[]{:S(2)}) async-start(f32[128,1,384]{2,1,0:T(1,128)} %square_sums.1), calls=%async_computation | async-start | bytes 393216 | tf_op jit(solution)/shard_map/all_to_all | solution.py:355
